TPU v7x, 128 devices: a whole 4x4x4 slice. The times are simulated.
128 devices in a mesh: seq: 32 (over z, y, x_hi), dp: 4 (over x_lo, core).
Axes of the slice: x: 4 (x_hi: 2, x_lo: 2; x = x_hi * 2 + x_lo), y: 4, z: 4, core: 2. Of those that a mesh axis runs over, the one named last changes fastest.
Arguments:
- hidden: bfloat16 [4, 8192, 4608], P('dp', 'seq'), may hold values from -6 to 6
- queries: bfloat16 [4, 8192, 2048], P('dp', 'seq'), may hold values from -64 to 64
- down_weight: bfloat16 [4608, 1024], P('dp'), may hold values from -0.09375 to 0.09375
- up_weight: bfloat16 [2, 512, 1024], P(None, 'dp'), may hold values from -0.25 to 0.25
- lengths: int32 [4], P('dp'), may hold values from 2048 to 8192
Outputs:
- latent_cache: bfloat16 [4, 8192, 1024], P('dp', 'seq')
- attended: bfloat16 [4, 8192, 2048], P('dp', 'seq')
All inputs are finite; a program needn't handle non-finite values.
Results may differ from a plain program's by a relative error of at most 0.012.
The roundings to bfloat16 on the way count: a program that leaves them out, or rounds other values in their place, can miss the bound.
Values may be sent and summed in bfloat16 or wider, within the bound.
No kernel may reach another device: no remote copies, remote signals or barrier semaphores. Data moves between devices by JAX's collectives and lax.ppermute only.
A program may use at most 128 MiB of HBM per device.

v0:
```python
import functools
import itertools

import jax
import jax.numpy as jnp
from jax import lax
from jax.experimental import pallas as pl
from jax.experimental.pallas import tpu as pltpu
from jax.sharding import Mesh
from jax.sharding import PartitionSpec as P


HEAD = 128
PAIR = 2 * HEAD
BLOCK = 256
CHUNK = 2048
BLOCKS = CHUNK // BLOCK
LOW, MIDDLE = 3, 6
SIZES = {"z": 4, "y": 4, "xh": 2, "xl": 2, "core": 2}
SEQ_AXES = ("z", "y", "xh")
DP_AXES = ("xl", "core")
PLANE = ("y", "xh")

query_scale = 144.0 ** (-0.5)
soft_cap = 50.0
LOG2E = 1.4426950408889634
CONTRACT_LAST = (((1,), (1,)), ((), ()))


def x_shift(step):
    pairs = []
    for hi, lo in itertools.product(range(2), range(2)):
        to = (2 * hi + lo + step) % 4
        pairs.append((2 * hi + lo, to))
    return pairs


def to_partner(array):
    return lax.ppermute(array, "core", [(0, 1), (1, 0)])


def half_product_kernel(info, own_hidden, partner_hidden, own_weight, partner_weight, out):
    out[...] = jnp.dot(
        own_hidden[...], own_weight[...], preferred_element_type=jnp.float32
    ) + jnp.dot(partner_hidden[...], partner_weight[...], preferred_element_type=jnp.float32)


def project_kernel(
    info, partial, near_hidden, far_hidden, near_left, near_right, far_left, far_right,
    up_own, up_partner, near_keys, near_values, far_keys, far_values, cosine, sine,
    latent, pairs, uppers,
):
    mine, start, length = info[0], info[1], info[2]
    rows = partial.shape[0]
    rank = partial.shape[1] // 2
    piece = up_own.shape[1]
    live = (start + lax.broadcasted_iota(jnp.int32, (rows, rank), 0)) < length

    def place(which, shard, value):
        uppers[which, pl.ds(pl.multiple_of(shard * piece, piece), piece), :] = value

    for which, near, far in ((0, near_keys, far_keys), (1, near_values, far_values)):
        place(which, mine, up_own[which])
        place(which, mine ^ 1, up_partner[which])
        place(which, mine ^ 2, near[...])
        place(which, mine ^ 3, far[...])
    for which, near, far in ((0, near_left, far_left), (1, near_right, far_right)):
        total = (
            partial[:, which * rank : (which + 1) * rank]
            + jnp.dot(near_hidden[...], near[...], preferred_element_type=jnp.float32)
            + jnp.dot(far_hidden[...], far[...], preferred_element_type=jnp.float32)
        )
        rounded = jnp.where(live, total, 0.0).astype(jnp.bfloat16)
        latent[:, which * rank : (which + 1) * rank] = rounded
        raw = jnp.dot(rounded, uppers[which], preferred_element_type=jnp.float32)
        for head in range(raw.shape[1] // HEAD):
            entry = raw[:, head * HEAD : (head + 1) * HEAD]
            if which == 0:
                entry = entry * cosine[...] + pltpu.roll(entry, HEAD // 2, 1) * sine[...]
            pairs[head, :, which * HEAD : (which + 1) * HEAD] = entry.astype(jnp.bfloat16)


def expo(raw):
    return jnp.exp2(jnp.tanh(raw * (query_scale / soft_cap)) * (soft_cap * LOG2E))


def folded(values):
    total = values[:, :HEAD]
    for t in range(1, values.shape[1] // HEAD):
        total = total + values[:, t * HEAD : (t + 1) * HEAD]
    return total


def triangle(newer):
    row = lax.broadcasted_iota(jnp.int32, (2 * BLOCK, BLOCK), 0) % BLOCK
    col = lax.broadcasted_iota(jnp.int32, (2 * BLOCK, BLOCK), 1)
    return col <= row if newer else col > row


def stacked_rows(queries, i):
    own = queries[pl.ds(pl.multiple_of(i * BLOCK, BLOCK), BLOCK), :]
    return jnp.concatenate([own[:, :HEAD], own[:, HEAD:]], axis=0)


def over_blocks(stacked, pairs, blocks):
    numer = denom = 0.0
    for j, mask in blocks:
        at = pl.ds(j * BLOCK, BLOCK)
        raw = lax.dot_general(
            stacked, pairs[at, :HEAD], CONTRACT_LAST, preferred_element_type=jnp.float32
        )
        e = expo(raw)
        if mask is not None:
            e = jnp.where(mask, e, 0.0)
        denom = denom + folded(e)
        numer = numer + jnp.dot(
            e.astype(jnp.bfloat16), pairs[at, HEAD:], preferred_element_type=jnp.float32
        )
    return numer, denom


def state_rows(i):
    return pl.ds(pl.multiple_of(i * 2 * BLOCK, 2 * BLOCK), 2 * BLOCK)


def own_kernel(queries, pairs, numer, denom):
    mask = triangle(True)
    for i in range(BLOCKS):
        blocks = [(j, None) for j in range(i)] + [(i, mask)]
        numer[state_rows(i), :], denom[state_rows(i), :] = over_blocks(
            stacked_rows(queries, i), pairs, blocks
        )


def near_kernel(group, info, queries, pairs, numer_in, denom_in, numer, denom):
    blocks = [(j, None) for j in range(pairs.shape[0] // BLOCK)]

    @pl.when(info[0] >= 1)
    def _():
        def step(t, carry):
            for u in range(group):
                i = t * group + u
                n, d = over_blocks(stacked_rows(queries, i), pairs, blocks)
                numer[state_rows(i), :] += n
                denom[state_rows(i), :] += d
            return carry

        lax.fori_loop(0, BLOCKS // group, step, 0)


def far_kernel(first, last, info, queries, pairs, numer_in, denom_in, *outs):
    end = first + pairs.shape[0] // BLOCK
    mask = triangle(False)
    numer, denom = (numer_in, denom_in) if last else outs

    def finish(i, n, d):
        if last:
            n = n / jnp.sum(d, axis=1, keepdims=True)
            outs[0][i * BLOCK : (i + 1) * BLOCK, :] = jnp.concatenate(
                [n[:BLOCK], n[BLOCK:]], axis=1
            ).astype(jnp.bfloat16)
        else:
            numer[state_rows(i), :], denom[state_rows(i), :] = n, d

    @pl.when(info[0] >= 2)
    def _():
        for i in range(BLOCKS):
            blocks = [(j - first, mask if j == i else None) for j in range(max(i, first), end)]
            old_n, old_d = numer[state_rows(i), :], denom[state_rows(i), :]
            if blocks:
                n, d = over_blocks(stacked_rows(queries, i), pairs, blocks)
                finish(i, old_n + n, old_d + d)
            elif last:
                finish(i, old_n, old_d)

    if last:

        @pl.when(info[0] < 2)
        def _():
            for i in range(BLOCKS):
                finish(i, numer[state_rows(i), :], denom[state_rows(i), :])


IN_VMEM = pl.BlockSpec(memory_space=pltpu.VMEM)
IN_SMEM = pl.BlockSpec(memory_space=pltpu.SMEM)
STATE = jax.ShapeDtypeStruct((2 * CHUNK, HEAD), jnp.float32)
RESULT = jax.ShapeDtypeStruct((CHUNK, PAIR), jnp.bfloat16)


def attention_call(kernel, count, args, result=False, resume=True):
    single = BLOCK * 2 * BLOCK
    inputs = [IN_SMEM] + [IN_VMEM] * 4 if resume else [IN_VMEM] * 2
    return pl.pallas_call(
        kernel,
        out_shape=RESULT if result else (STATE, STATE),
        in_specs=inputs,
        out_specs=IN_VMEM if result else (IN_VMEM, IN_VMEM),
        input_output_aliases={3: 0, 4: 1} if resume and not result else {},
        compiler_params=pltpu.CompilerParams(vmem_limit_bytes=24 * 2**20),
        cost_estimate=pl.CostEstimate(
            flops=count * single * 4 * HEAD, bytes_accessed=2**22, transcendentals=2 * count * single
        ),
    )(*args)


def body(hidden, queries, down_weight, up_weight, lengths):
    _, rows, _ = hidden.shape
    rank2 = down_weight.shape[1]
    rank = rank2 // 2
    depth = down_weight.shape[0]
    kv_width = up_weight.shape[2]
    groups = kv_width // HEAD
    hidden = hidden[0]
    mine = 2 * lax.axis_index("xl") + lax.axis_index("core")
    plane = lax.axis_index("z")
    seq_index = lax.axis_index(SEQ_AXES)
    start = seq_index * rows
    info = jnp.stack([mine, start, lengths[0]]).astype(jnp.int32)

    forward, backward = x_shift(1), x_shift(-1)
    near_left = lax.ppermute(down_weight[:, :rank], ("xh", "xl"), forward)
    near_right = lax.ppermute(down_weight[:, rank:], ("xh", "xl"), backward)
    near_keys = lax.ppermute(up_weight[0], ("xh", "xl"), forward)
    near_values = lax.ppermute(up_weight[1], ("xh", "xl"), backward)
    partner_weight = to_partner(down_weight)
    up_partner = to_partner(up_weight)
    far_left, far_right = to_partner(near_left), to_partner(near_right)
    far_keys, far_values = to_partner(near_keys), to_partner(near_values)

    sent = queries[0].reshape(rows, groups, PAIR).transpose(1, 0, 2)
    my_queries = lax.all_to_all(sent, PLANE, 0, 0, tiled=True).reshape(CHUNK, PAIR)

    half = HEAD // 2
    places = (start + jnp.arange(rows, dtype=jnp.int32)).astype(jnp.float32)
    freqs = 10000.0 ** (-2.0 * jnp.arange(half, dtype=jnp.float32) / HEAD)
    angles = places[:, None] * freqs[None, :]
    cosine, sine = jnp.cos(angles), jnp.sin(angles)
    cosine = jnp.concatenate([cosine, cosine], axis=1)
    sine = jnp.concatenate([-sine, sine], axis=1)

    info, my_queries = lax.optimization_barrier((info, my_queries))

    def hidden_part(flip):
        return pl.BlockSpec((rows, depth), lambda i, s: (0, s[0] ^ flip))

    def whole(shape):
        return pl.BlockSpec(shape, lambda i, s: (0,) * len(shape))

    partial = pl.pallas_call(
        half_product_kernel,
        out_shape=jax.ShapeDtypeStruct((rows, rank2), jnp.float32),
        grid_spec=pltpu.PrefetchScalarGridSpec(
            num_scalar_prefetch=1,
            grid=(1,),
            in_specs=[hidden_part(0), hidden_part(1)] + [whole((depth, rank2))] * 2,
            out_specs=whole((rows, rank2)),
        ),
        compiler_params=pltpu.CompilerParams(vmem_limit_bytes=40 * 2**20),
        cost_estimate=pl.CostEstimate(
            flops=4 * rows * depth * rank2, bytes_accessed=8 * 2**20, transcendentals=0
        ),
        name="half_product",
    )(info, hidden, hidden, down_weight, partner_weight)

    piece = up_weight.shape[1]
    latent, pairs = pl.pallas_call(
        project_kernel,
        out_shape=(
            jax.ShapeDtypeStruct((rows, rank2), jnp.bfloat16),
            jax.ShapeDtypeStruct((groups, rows, PAIR), jnp.bfloat16),
        ),
        grid_spec=pltpu.PrefetchScalarGridSpec(
            num_scalar_prefetch=1,
            grid=(1,),
            in_specs=[whole((rows, rank2)), hidden_part(2), hidden_part(3)]
            + [whole((depth, rank))] * 4
            + [whole((2, piece, kv_width))] * 2
            + [whole((piece, kv_width))] * 4
            + [whole((rows, HEAD))] * 2,
            out_specs=[whole((rows, rank2)), whole((groups, rows, PAIR))],
            scratch_shapes=[pltpu.VMEM((2, rank, kv_width), jnp.bfloat16)],
        ),
        compiler_params=pltpu.CompilerParams(vmem_limit_bytes=48 * 2**20),
        cost_estimate=pl.CostEstimate(
            flops=4 * rows * depth * rank2, bytes_accessed=10 * 2**20, transcendentals=0
        ),
        name="project",
    )(
        info, partial, hidden, hidden, near_left, near_right, far_left, far_right,
        up_weight, up_partner, near_keys, near_values, far_keys, far_values, cosine, sine,
    )

    own_pairs = lax.all_to_all(pairs, PLANE, 0, 0, tiled=True).reshape(CHUNK, PAIR)
    low, middle = LOW * BLOCK, MIDDLE * BLOCK
    up = [(0, 1), (1, 2), (2, 3)]
    near_low = lax.ppermute(own_pairs[:low], "z", up)
    passing = lax.ppermute(own_pairs[low:], "z", [(1, 0), (0, 3)])
    near_middle = lax.ppermute(own_pairs[low:middle], "z", up)
    near_high = lax.ppermute(own_pairs[middle:], "z", up)
    far_low = lax.ppermute(near_low, "z", [(1, 2), (2, 3)])

    spot = plane.reshape(1).astype(jnp.int32)
    state = attention_call(own_kernel, 36, (my_queries, own_pairs), resume=False)
    for name, piece_pairs in (("low", near_low), ("middle", near_middle), ("high", near_high)):
        state = attention_call(
            functools.partial(near_kernel, 2),
            piece_pairs.shape[0] // BLOCK * BLOCKS,
            (spot, my_queries, piece_pairs, *state),
        )
        if name == "low":
            passing, state = lax.optimization_barrier((passing, state))
            far_high = lax.ppermute(passing, "z", [(0, 3), (3, 2)])
    state = attention_call(
        functools.partial(far_kernel, LOW, False), 30,
        (spot, my_queries, far_high, *state),
    )
    result = attention_call(
        functools.partial(far_kernel, 0, True), 6,
        (spot, my_queries, far_low, *state), result=True,
    )

    home = lax.all_to_all(result.reshape(groups, rows, PAIR), PLANE, 0, 0, tiled=True)
    home = home.transpose(1, 0, 2).reshape(rows, groups * PAIR)
    live = (start + jnp.arange(rows, dtype=jnp.int32)) < lengths[0]
    attended = jnp.where(live[:, None], home, jnp.zeros((), jnp.bfloat16))
    return latent[None], attended[None]


def solution(mesh):
    split = Mesh(mesh.devices.reshape(tuple(SIZES.values())), tuple(SIZES))
    rows = P(DP_AXES, SEQ_AXES, None)
    placed = (rows, rows, P(DP_AXES, None), P(None, DP_AXES, None), P(DP_AXES))

    return jax.shard_map(body, mesh=split, in_specs=placed, out_specs=(rows, rows), check_vma=False)
```

profile of v0, /device:TPU:96, one launch (start us, length us, event | category | flops | bytes accessed | tf_op | source)
XLA Modules:
  0.0 171.1 jit_solution(3738205306502269096)
XLA Ops:
  0.6 0.0 copy-start.4
  0.6 0.1 collective-permute-start
  0.7 1.8 %fusion.3 = (bf16[1152,512]{1,0:T(8,128)(2,1)S(1)}, bf16[1152,512]{1,0:T(8,128)(2,1)S(1)}) fusion(bf16[1152,1024]{1,0:T(8,128)(2,1)} %own_weight.1), kind=kLoop, calls=%fused_computation.14 | loop fusion | bytes 4718592 | tf_op jit(solution)/shard_map/slice | solution.py:222
  2.6 2.8 %collective-permute-start.2 = (bf16[1152,512]{1,0:T(8,128)(2,1)S(1)}, bf16[1152,512]{1,0:T(8,128)(2,1)}, u32[]{:S(2)}, u32[]{:S(2)}) collective-permute-start(bf16[1152,512]{1,0:T(8,128)(2,1)S(1)} %get-tuple-element.36), channel_id=1, source_target_pairs={{0,6},{2,0},{4,2},{6,4},{1,7},{3,1},{5,3},{7,5},{8,14},{10,8},{12,... | collective-permute-start | bytes 3538952 | tf_op jit(solution)/shard_map/ppermute | solution.py:222
  5.4 0.0 collective-permute-start.1
  5.4 25.8 %collective-permute-done.2.near_right = bf16[1152,512]{1,0:T(8,128)(2,1)} collective-permute-done((bf16[1152,512]{1,0:T(8,128)(2,1)S(1)}, bf16[1152,512]{1,0:T(8,128)(2,1)}, u32[]{:S(2)}, u32[]{:S(2)}) %collective-permute-start.2) | collective-permute-done | bytes 1179680 | tf_op jit(solution)/shard_map/ppermute | solution.py:222
  31.2 0.0 collective-permute-start.4
  31.2 3.5 %collective-permute-done.1.near_left = bf16[1152,512]{1,0:T(8,128)(2,1)} collective-permute-done((bf16[1152,512]{1,0:T(8,128)(2,1)S(1)}, bf16[1152,512]{1,0:T(8,128)(2,1)}, u32[]{:S(2)}, u32[]{:S(2)}) %collective-permute-start.1) | collective-permute-done | bytes 1179680 | tf_op jit(solution)/shard_map/ppermute | solution.py:221
  34.7 0.0 collective-permute-start.3
  34.8 0.0 copy-done.4
  34.8 0.3 copy.17
  35.1 1.2 copy.19
  36.2 0.0 copy-start
  36.2 4.6 %all-to-all-start = ((bf16[8,256,256]{2,1,0:T(8,128)(2,1)}), bf16[8,256,256]{2,1,0:T(8,128)(2,1)S(1)}, u32[]{:S(2)}, u32[]{:S(2)}) async-start(bf16[8,256,256]{2,1,0:T(8,128)(2,1)} %bitcast.36), calls=%async_computation | async-start | bytes 2097152 | tf_op jit(solution)/shard_map/all_to_all | solution.py:231
  40.8 1.9 %slice_bitcast_fusion = (bf16[128,1024]{1,0:T(8,128)(2,1)}, bf16[128,1024]{1,0:T(8,128)(2,1)}) fusion(bf16[2,128,1024]{2,1,0:T(8,128)(2,1)} %up_own.1), kind=kLoop, calls=%fused_computation.2 | loop fusion | bytes 1048576 | tf_op jit(solution)/shard_map/squeeze | solution.py:224
  42.7 3.8 %collective-permute-start.7 = (bf16[128,1024]{1,0:T(8,128)(2,1)}, bf16[128,1024]{1,0:T(8,128)(2,1)}, u32[]{:S(2)}, u32[]{:S(2)}) collective-permute-start(bf16[128,1024]{1,0:T(8,128)(2,1)} %get-tuple-element.40), channel_id=1, source_target_pairs={{0,6},{2,0},{4,2},{6,4},{1,7},{3,1},{5,3},{7,5},{8,14},{10,8},{12,... | collective-permute-start | bytes 786440 | tf_op jit(solution)/shard_map/ppermute | solution.py:224
  46.5 0.0 collective-permute-start.6
  47.1 12.6 %collective-permute-done.7.near_values = bf16[128,1024]{1,0:T(8,128)(2,1)} collective-permute-done((bf16[128,1024]{1,0:T(8,128)(2,1)}, bf16[128,1024]{1,0:T(8,128)(2,1)}, u32[]{:S(2)}, u32[]{:S(2)}) %collective-permute-start.7) | collective-permute-done | bytes 262176 | tf_op jit(solution)/shard_map/ppermute | solution.py:224
  59.7 0.0 collective-permute-start.5
  59.7 0.5 fusion
  60.3 2.1 %collective-permute-done.6.near_keys = bf16[128,1024]{1,0:T(8,128)(2,1)} collective-permute-done((bf16[128,1024]{1,0:T(8,128)(2,1)}, bf16[128,1024]{1,0:T(8,128)(2,1)}, u32[]{:S(2)}, u32[]{:S(2)}) %collective-permute-start.6) | collective-permute-done | bytes 262176 | tf_op jit(solution)/shard_map/ppermute | solution.py:223
  62.3 0.0 collective-permute-start.9
  62.3 0.0 collective-permute-done.partner_weight
  62.3 0.5 collective-permute-start.8
  62.8 0.1 pad_add_fusion.info
  62.9 0.8 pad_maximum_fusion
  63.7 0.0 all-to-all-done
  63.7 0.0 copy-done
  63.7 0.0 copy-start.1
  63.7 1.7 copy-done.1
  65.4 3.7 %half_product.1.partial = f32[256,1024]{1,0:T(8,128)S(1)} custom-call(s32[3]{0:T(128)S(1)} %pad_add_fusion.info, bf16[256,4608]{1,0:T(8,128)(2,1)S(1)} %bitcast.27, bf16[256,4608]{1,0:T(8,128)(2,1)S(1)} %bitcast.28, bf16[1152,1024]{1,0:T(8,128)(2,1)S(1)} %copy-done.1, bf16[1152,1024]{1,0:T(8,128)(2,1)} %collective-permute-done.partner_weight), custom_call_target="tpu_custom_call" | custom-call | flops 1207959552 | bytes 8388608 | tf_op jit(solution)/shard_map/half_product/pallas_call | solution.py:249
  69.1 0.0 collective-permute-done.9.far_values
  69.1 0.0 collective-permute-done.8.far_keys
  69.1 0.0 collective-permute-done.5.up_partner
  69.1 0.0 collective-permute-done.4.far_right
  69.1 0.0 collective-permute-done.3.far_left
  69.1 0.0 copy-done.2
  69.2 0.0 copy-done.3
  69.2 6.4 %project.1 = (bf16[256,1024]{1,0:T(8,128)(2,1)}, bf16[8,256,256]{2,1,0:T(8,128)(2,1)S(1)}) custom-call(s32[3]{0:T(128)S(1)} %pad_add_fusion.info, f32[256,1024]{1,0:T(8,128)S(1)} %half_product.1.partial, bf16[256,4608]{1,0:T(8,128)(2,1)} %bitcast.25, bf16[256,4608]{1,0:T(8,128)(2,1)} %bitcast.26, bf16[1152,512]{1,0:T(8,128)(2,1)} %collective-permute-done.1.near_left, ...), custom_call_target="tpu_custom_call" | custom-call | flops 1207959552 | bytes 10485760 | tf_op jit(solution)/shard_map/project/pallas_call | solution.py:266
  75.6 23.2 %all_to_all.15 = bf16[8,256,256]{2,1,0:T(8,128)(2,1)S(1)} all-to-all(bf16[8,256,256]{2,1,0:T(8,128)(2,1)S(1)} %get-tuple-element.22), channel_id=1, replica_groups=mesh['z'=4,'y'=4,'xh'=2,'xl'=2,'core'=2] {'y','xh'}, dimensions={0} | all-to-all | bytes 2097152 | tf_op jit(solution)/shard_map/all_to_all | solution.py:293
  98.8 1.3 collective-permute-start.12
  100.1 0.1 fusion.4
  100.2 1.5 collective-permute-start.10
  101.7 5.4 %shard_map.68 = (f32[4096,128]{1,0:T(8,128)S(1)}, f32[4096,128]{1,0:T(8,128)S(1)}) custom-call(bf16[2048,256]{1,0:T(8,128)(2,1)S(1)} %bitcast.30, bf16[2048,256]{1,0:T(8,128)(2,1)S(1)} %bitcast.29), custom_call_target="tpu_custom_call" | custom-call | flops 2415919104 | bytes 4194304 | tf_op jit(solution)/shard_map/pallas_call | solution.py:193
  107.0 5.3 %collective-permute-done.10.pairs = bf16[768,256]{1,0:T(8,128)(2,1)S(1)} collective-permute-done((bf16[768,256]{1,0:T(8,128)(2,1)S(1)}, bf16[768,256]{1,0:T(8,128)(2,1)S(1)}, u32[]{:S(2)}, u32[]{:S(2)}) %collective-permute-start.10) | collective-permute-done | bytes 393248 | tf_op jit(solution)/shard_map/ppermute | solution.py:296
  112.4 5.8 %shard_map.69 = (f32[4096,128]{1,0:T(8,128)S(1)}, f32[4096,128]{1,0:T(8,128)S(1)}) custom-call(s32[1]{0:T(128)} %bitcast.9.info, bf16[2048,256]{1,0:T(8,128)(2,1)S(1)} %bitcast.31, bf16[768,256]{1,0:T(8,128)(2,1)S(1)} %collective-permute-done.10.pairs, f32[4096,128]{1,0:T(8,128)S(1)} %get-tuple-element.23.numer_in, ...), custom_call_target="tpu_custom_call", output_to_operand_aliasing={{0}: (3, {}), {1}: (4, {})} | custom-call | flops 1610612736 | bytes 4194304 | tf_op jit(solution)/shard_map/pallas_call | solution.py:193
  118.2 0.0 collective-permute-done.12
  118.2 1.9 %collective-permute-start.13 = (bf16[1280,256]{1,0:T(8,128)(2,1)S(1)}, bf16[1280,256]{1,0:T(8,128)(2,1)S(1)}, u32[]{:S(2)}, u32[]{:S(2)}) collective-permute-start(bf16[1280,256]{1,0:T(8,128)(2,1)S(1)} %collective-permute-done.12), channel_id=1, source_target_pairs={{0,96},{96,64},{1,97},{97,65},{2,98},{98,66},{3,99},{99,67},{4,100... | collective-permute-start | bytes 1966088 | tf_op jit(solution)/shard_map/ppermute | solution.py:312
  120.1 1.3 collective-permute-start.15
  121.4 1.3 collective-permute-start.14
  122.7 1.3 collective-permute-start.11
  124.0 10.0 %collective-permute-done.15.pairs = bf16[768,256]{1,0:T(8,128)(2,1)S(1)} collective-permute-done((bf16[768,256]{1,0:T(8,128)(2,1)S(1)}, bf16[768,256]{1,0:T(8,128)(2,1)S(1)}, u32[]{:S(2)}, u32[]{:S(2)}) %collective-permute-start.15) | collective-permute-done | bytes 393248 | tf_op jit(solution)/shard_map/ppermute | solution.py:298
  134.0 5.8 %shard_map.70 = (f32[4096,128]{1,0:T(8,128)S(1)}, f32[4096,128]{1,0:T(8,128)S(1)}) custom-call(s32[1]{0:T(128)} %bitcast.9.info, bf16[2048,256]{1,0:T(8,128)(2,1)S(1)} %bitcast.32, bf16[768,256]{1,0:T(8,128)(2,1)S(1)} %collective-permute-done.15.pairs, f32[4096,128]{1,0:T(8,128)S(1)} %get-tuple-element.28.numer_in, ...), custom_call_target="tpu_custom_call", output_to_operand_aliasing={{0}: (3, {}), {1}: (4, {})} | custom-call | flops 1610612736 | bytes 4194304 | tf_op jit(solution)/shard_map/pallas_call | solution.py:193
  139.8 0.0 collective-permute-done.14.pairs
  139.8 4.0 %shard_map.71 = (f32[4096,128]{1,0:T(8,128)S(1)}, f32[4096,128]{1,0:T(8,128)S(1)}) custom-call(s32[1]{0:T(128)} %bitcast.9.info, bf16[2048,256]{1,0:T(8,128)(2,1)S(1)} %bitcast.33, bf16[512,256]{1,0:T(8,128)(2,1)S(1)} %collective-permute-done.14.pairs, f32[4096,128]{1,0:T(8,128)S(1)} %get-tuple-element.30.numer_in, ...), custom_call_target="tpu_custom_call", output_to_operand_aliasing={{0}: (3, {}), {1}: (4, {})} | custom-call | flops 1073741824 | bytes 4194304 | tf_op jit(solution)/shard_map/pallas_call | solution.py:193
  143.8 0.0 collective-permute-done.13.pairs
  143.8 6.0 %shard_map.72 = (f32[4096,128]{1,0:T(8,128)S(1)}, f32[4096,128]{1,0:T(8,128)S(1)}) custom-call(s32[1]{0:T(128)} %bitcast.9.info, bf16[2048,256]{1,0:T(8,128)(2,1)S(1)} %bitcast.34, bf16[1280,256]{1,0:T(8,128)(2,1)S(1)} %collective-permute-done.13.pairs, f32[4096,128]{1,0:T(8,128)S(1)} %get-tuple-element.32.numer_in, ...), custom_call_target="tpu_custom_call", output_to_operand_aliasing={{0}: (3, {}), {1}: (4, {})} | custom-call | flops 2013265920 | bytes 4194304 | tf_op jit(solution)/shard_map/pallas_call | solution.py:193
  149.8 0.0 collective-permute-done.11.pairs
  149.8 2.5 %shard_map.73 = bf16[2048,256]{1,0:T(8,128)(2,1)} custom-call(s32[1]{0:T(128)} %bitcast.9.info, bf16[2048,256]{1,0:T(8,128)(2,1)S(1)} %bitcast.35, bf16[768,256]{1,0:T(8,128)(2,1)S(1)} %collective-permute-done.11.pairs, f32[4096,128]{1,0:T(8,128)S(1)} %get-tuple-element.34.numer_in, f32[4096,128]{1,0:T(8,128)S(1)} %get-tuple-element.35.denom_in), custom_call_target="tpu_custom_call" | custom-call | flops 402653184 | bytes 4194304 | tf_op jit(solution)/shard_map/pallas_call | solution.py:193
  152.4 3.6 %all-to-all-start.2 = ((bf16[8,256,256]{2,1,0:T(8,128)(2,1)}), bf16[8,256,256]{2,1,0:T(8,128)(2,1)S(1)}, u32[]{:S(2)}, u32[]{:S(2)}) async-start(bf16[8,256,256]{2,1,0:T(8,128)(2,1)} %bitcast.15), calls=%async_computation.2 | async-start | bytes 2097152 | tf_op jit(solution)/shard_map/all_to_all | solution.py:322
  155.9 12.9 %all-to-all-done.2 = bf16[8,256,256]{2,1,0:T(8,128)(2,1)S(1)} async-done(((bf16[8,256,256]{2,1,0:T(8,128)(2,1)}), bf16[8,256,256]{2,1,0:T(8,128)(2,1)S(1)}, u32[]{:S(2)}, u32[]{:S(2)}) %all-to-all-start.2) | async-done | bytes 1048608 | tf_op jit(solution)/shard_map/all_to_all | solution.py:322
  168.9 0.6 copy.16
  169.4 0.5 reshape.69
  170.0 1.1 broadcast_select_fusion
  (7 shorter events, 0.1 us)
Async XLA Ops:
  0.6 34.1 %copy-start.4 = (bf16[1,256,2048]{2,1,0:T(8,128)(2,1)S(1)}, bf16[1,256,2048]{2,1,0:T(8,128)(2,1)}, u32[]{:S(2)}) copy-start(bf16[1,256,2048]{2,1,0:T(8,128)(2,1)} %param.6) | copy-start | bytes 3145732
  0.6 61.7 %collective-permute-start = (bf16[1152,1024]{1,0:T(8,128)(2,1)}, bf16[1152,1024]{1,0:T(8,128)(2,1)}, u32[]{:S(2)}, u32[]{:S(2)}) collective-permute-start(bf16[1152,1024]{1,0:T(8,128)(2,1)} %own_weight.1), channel_id=1, source_target_pairs={{0,1},{1,0},{2,3},{3,2},{4,5},{5,4},{6,7},{7,6},{8,9},{9,8},{10,11... | collective-permute-start | bytes 7077896 | tf_op jit(solution)/shard_map/ppermute | solution.py:39
  2.6 28.6 %collective-permute-start.2 = (bf16[1152,512]{1,0:T(8,128)(2,1)S(1)}, bf16[1152,512]{1,0:T(8,128)(2,1)}, u32[]{:S(2)}, u32[]{:S(2)}) collective-permute-start(bf16[1152,512]{1,0:T(8,128)(2,1)S(1)} %get-tuple-element.36), channel_id=1, source_target_pairs={{0,6},{2,0},{4,2},{6,4},{1,7},{3,1},{5,3},{7,5},{8,14},{10,8},{12,... | collective-permute-start | bytes 3538952 | tf_op jit(solution)/shard_map/ppermute | solution.py:222
  5.4 29.3 %collective-permute-start.1 = (bf16[1152,512]{1,0:T(8,128)(2,1)S(1)}, bf16[1152,512]{1,0:T(8,128)(2,1)}, u32[]{:S(2)}, u32[]{:S(2)}) collective-permute-start(bf16[1152,512]{1,0:T(8,128)(2,1)S(1)} %get-tuple-element.37), channel_id=1, source_target_pairs={{0,2},{2,4},{4,6},{6,0},{1,3},{3,5},{5,7},{7,1},{8,10},{10,12},{12... | collective-permute-start | bytes 3538952 | tf_op jit(solution)/shard_map/ppermute | solution.py:221
  31.2 37.9 %collective-permute-start.4 = (bf16[1152,512]{1,0:T(8,128)(2,1)}, bf16[1152,512]{1,0:T(8,128)(2,1)}, u32[]{:S(2)}, u32[]{:S(2)}) collective-permute-start(bf16[1152,512]{1,0:T(8,128)(2,1)} %collective-permute-done.2.near_right), channel_id=1, source_target_pairs={{0,1},{1,0},{2,3},{3,2},{4,5},{5,4},{6,7},{7,6},{8,9},{9,8},{10,11... | collective-permute-start | bytes 3538952 | tf_op jit(solution)/shard_map/ppermute | solution.py:39
  34.7 34.4 %collective-permute-start.3 = (bf16[1152,512]{1,0:T(8,128)(2,1)}, bf16[1152,512]{1,0:T(8,128)(2,1)}, u32[]{:S(2)}, u32[]{:S(2)}) collective-permute-start(bf16[1152,512]{1,0:T(8,128)(2,1)} %collective-permute-done.1.near_left), channel_id=1, source_target_pairs={{0,1},{1,0},{2,3},{3,2},{4,5},{5,4},{6,7},{7,6},{8,9},{9,8},{10,11... | collective-permute-start | bytes 3538952 | tf_op jit(solution)/shard_map/ppermute | solution.py:39
  36.2 27.5 %copy-start = (bf16[1,256,4608]{2,1,0:T(8,128)(2,1)S(1)}, bf16[1,256,4608]{2,1,0:T(8,128)(2,1)}, u32[]{:S(2)}) copy-start(bf16[1,256,4608]{2,1,0:T(8,128)(2,1)} %param.5) | copy-start | bytes 7077892
  36.2 27.5 %all-to-all-start = ((bf16[8,256,256]{2,1,0:T(8,128)(2,1)}), bf16[8,256,256]{2,1,0:T(8,128)(2,1)S(1)}, u32[]{:S(2)}, u32[]{:S(2)}) async-start(bf16[8,256,256]{2,1,0:T(8,128)(2,1)} %bitcast.36), calls=%async_computation | async-start | bytes 2097152 | tf_op jit(solution)/shard_map/all_to_all | solution.py:231
  42.7 17.0 %collective-permute-start.7 = (bf16[128,1024]{1,0:T(8,128)(2,1)}, bf16[128,1024]{1,0:T(8,128)(2,1)}, u32[]{:S(2)}, u32[]{:S(2)}) collective-permute-start(bf16[128,1024]{1,0:T(8,128)(2,1)} %get-tuple-element.40), channel_id=1, source_target_pairs={{0,6},{2,0},{4,2},{6,4},{1,7},{3,1},{5,3},{7,5},{8,14},{10,8},{12,... | collective-permute-start | bytes 786440 | tf_op jit(solution)/shard_map/ppermute | solution.py:224
  46.5 15.9 %collective-permute-start.6 = (bf16[128,1024]{1,0:T(8,128)(2,1)}, bf16[128,1024]{1,0:T(8,128)(2,1)}, u32[]{:S(2)}, u32[]{:S(2)}) collective-permute-start(bf16[128,1024]{1,0:T(8,128)(2,1)} %get-tuple-element.41), channel_id=1, source_target_pairs={{0,2},{2,4},{4,6},{6,0},{1,3},{3,5},{5,7},{7,1},{8,10},{10,12},{12... | collective-permute-start | bytes 786440 | tf_op jit(solution)/shard_map/ppermute | solution.py:223
  59.7 9.4 %collective-permute-start.5 = (bf16[2,128,1024]{2,1,0:T(8,128)(2,1)}, bf16[2,128,1024]{2,1,0:T(8,128)(2,1)}, u32[]{:S(2)}, u32[]{:S(2)}) collective-permute-start(bf16[2,128,1024]{2,1,0:T(8,128)(2,1)} %up_own.1), channel_id=1, source_target_pairs={{0,1},{1,0},{2,3},{3,2},{4,5},{5,4},{6,7},{7,6},{8,9},{9,8},{10,11... | collective-permute-start | bytes 1572872 | tf_op jit(solution)/shard_map/ppermute | solution.py:39
  62.3 6.8 %collective-permute-start.9 = (bf16[128,1024]{1,0:T(8,128)(2,1)}, bf16[128,1024]{1,0:T(8,128)(2,1)}, u32[]{:S(2)}, u32[]{:S(2)}) collective-permute-start(bf16[128,1024]{1,0:T(8,128)(2,1)} %collective-permute-done.7.near_values), channel_id=1, source_target_pairs={{0,1},{1,0},{2,3},{3,2},{4,5},{5,4},{6,7},{7,6},{8,9},{9,8},{10,11... | collective-permute-start | bytes 786440 | tf_op jit(solution)/shard_map/ppermute | solution.py:39
  62.3 6.8 %collective-permute-start.8 = (bf16[128,1024]{1,0:T(8,128)(2,1)}, bf16[128,1024]{1,0:T(8,128)(2,1)}, u32[]{:S(2)}, u32[]{:S(2)}) collective-permute-start(bf16[128,1024]{1,0:T(8,128)(2,1)} %collective-permute-done.6.near_keys), channel_id=1, source_target_pairs={{0,1},{1,0},{2,3},{3,2},{4,5},{5,4},{6,7},{7,6},{8,9},{9,8},{10,11... | collective-permute-start | bytes 786440 | tf_op jit(solution)/shard_map/ppermute | solution.py:39
  63.7 1.7 copy-start.1
  65.4 3.8 %copy-start.2 = (bf16[2,128,1024]{2,1,0:T(8,128)(2,1)S(1)}, bf16[2,128,1024]{2,1,0:T(8,128)(2,1)}, u32[]{:S(2)}) copy-start(bf16[2,128,1024]{2,1,0:T(8,128)(2,1)} %up_own.1) | copy-start | bytes 1572868
  65.4 3.8 %copy-start.3 = (f32[256,128]{1,0:T(8,128)S(1)}, f32[256,128]{1,0:T(8,128)}, u32[]{:S(2)}) copy-start(f32[256,128]{1,0:T(8,128)} %get-tuple-element.46.sine) | copy-start | bytes 393220
  98.8 19.4 %collective-permute-start.12 = (bf16[1280,256]{1,0:T(8,128)(2,1)S(1)}, bf16[1280,256]{1,0:T(8,128)(2,1)S(1)}, u32[]{:S(2)}, u32[]{:S(2)}) collective-permute-start(bf16[1280,256]{1,0:T(8,128)(2,1)S(1)} %bitcast.40), channel_id=1, source_target_pairs={{32,0},{0,96},{33,1},{1,97},{34,2},{2,98},{35,3},{3,99},{36,4},{4,... | collective-permute-start | bytes 1966088 | tf_op jit(solution)/shard_map/ppermute | solution.py:297
  100.2 12.2 %collective-permute-start.10 = (bf16[768,256]{1,0:T(8,128)(2,1)S(1)}, bf16[768,256]{1,0:T(8,128)(2,1)S(1)}, u32[]{:S(2)}, u32[]{:S(2)}) collective-permute-start(bf16[768,256]{1,0:T(8,128)(2,1)S(1)} %bitcast.42), channel_id=1, source_target_pairs={{0,32},{32,64},{64,96},{1,33},{33,65},{65,97},{2,34},{34,66},{66,9... | collective-permute-start | bytes 1179656 | tf_op jit(solution)/shard_map/ppermute | solution.py:296
  118.2 25.6 %collective-permute-start.13 = (bf16[1280,256]{1,0:T(8,128)(2,1)S(1)}, bf16[1280,256]{1,0:T(8,128)(2,1)S(1)}, u32[]{:S(2)}, u32[]{:S(2)}) collective-permute-start(bf16[1280,256]{1,0:T(8,128)(2,1)S(1)} %collective-permute-done.12), channel_id=1, source_target_pairs={{0,96},{96,64},{1,97},{97,65},{2,98},{98,66},{3,99},{99,67},{4,100... | collective-permute-start | bytes 1966088 | tf_op jit(solution)/shard_map/ppermute | solution.py:312
  120.1 13.9 %collective-permute-start.15 = (bf16[768,256]{1,0:T(8,128)(2,1)S(1)}, bf16[768,256]{1,0:T(8,128)(2,1)S(1)}, u32[]{:S(2)}, u32[]{:S(2)}) collective-permute-start(bf16[768,256]{1,0:T(8,128)(2,1)S(1)} %bitcast.41), channel_id=1, source_target_pairs={{0,32},{32,64},{64,96},{1,33},{33,65},{65,97},{2,34},{34,66},{66,9... | collective-permute-start | bytes 1179656 | tf_op jit(solution)/shard_map/ppermute | solution.py:298
  121.4 18.4 %collective-permute-start.14 = (bf16[512,256]{1,0:T(8,128)(2,1)S(1)}, bf16[512,256]{1,0:T(8,128)(2,1)S(1)}, u32[]{:S(2)}, u32[]{:S(2)}) collective-permute-start(bf16[512,256]{1,0:T(8,128)(2,1)S(1)} %bitcast.43), channel_id=1, source_target_pairs={{0,32},{32,64},{64,96},{1,33},{33,65},{65,97},{2,34},{34,66},{66,9... | collective-permute-start | bytes 786440 | tf_op jit(solution)/shard_map/ppermute | solution.py:299
  122.7 27.1 %collective-permute-start.11 = (bf16[768,256]{1,0:T(8,128)(2,1)S(1)}, bf16[768,256]{1,0:T(8,128)(2,1)S(1)}, u32[]{:S(2)}, u32[]{:S(2)}) collective-permute-start(bf16[768,256]{1,0:T(8,128)(2,1)S(1)} %collective-permute-done.10.pairs), channel_id=1, source_target_pairs={{32,64},{64,96},{33,65},{65,97},{34,66},{66,98},{35,67},{67,99},{3... | collective-permute-start | bytes 1179656 | tf_op jit(solution)/shard_map/ppermute | solution.py:300
  152.4 16.5 %all-to-all-start.2 = ((bf16[8,256,256]{2,1,0:T(8,128)(2,1)}), bf16[8,256,256]{2,1,0:T(8,128)(2,1)S(1)}, u32[]{:S(2)}, u32[]{:S(2)}) async-start(bf16[8,256,256]{2,1,0:T(8,128)(2,1)} %bitcast.15), calls=%async_computation.2 | async-start | bytes 2097152 | tf_op jit(solution)/shard_map/all_to_all | solution.py:322
where the time goes:
time: 172 us; the launch traced here: 171 us
  waiting for transfers between devices  72.2 us (42%)
  Pallas kernels  39.6 us (23%)
  starting transfers between devices  23.9 us (14%)
  blocking collectives  23.2 us (13%)
  local copies, waits for them, and re-layouts  8.09 us (5%)
  other arithmetic  2.52 us (1%)
    pallas_call x6, Pallas kernels, attention_call(): pl.pallas_call(kernel, out_shape=RESULT if result else (STATE, STATE), in...  29.5 us
    ppermute x1, waiting for transfers between devices, body(): near_right = lax.ppermute(down_weight[:, rank:], ('xh', 'xl'), backward)  25.8 us
    all_to_all x1, blocking collectives, body(): lax.all_to_all(pairs, PLANE, 0, 0, tiled=True).reshape(CHUNK, PAIR)  23.2 us
    all_to_all x1, waiting for transfers between devices, body(): lax.all_to_all(result.reshape(groups, rows, PAIR), PLANE, 0, 0, tiled=True)  12.9 us
    ppermute x1, waiting for transfers between devices, body(): near_values = lax.ppermute(up_weight[1], ('xh', 'xl'), backward)  12.6 us
    ppermute x1, waiting for transfers between devices, body(): near_middle = lax.ppermute(own_pairs[low:middle], 'z', up)  9.95 us
    pallas_call x1, Pallas kernels, body(): pl.pallas_call(project_kernel, out_shape=(jax.ShapeDtypeStruct((rows, ran...  6.4 us
    ppermute x1, waiting for transfers between devices, body(): near_low = lax.ppermute(own_pairs[:low], 'z', up)  5.33 us
  transfers between devices with their start and end apart: 18, of which 7 were waited for; matrix products, arithmetic and copies ran while one was open for 4% of the time, Pallas kernels for 18%

commit v1 on v0

v1 whole, which is shorter than its diff:
```python
import functools
import itertools

import jax
import jax.numpy as jnp
from jax import lax
from jax.experimental import pallas as pl
from jax.experimental.pallas import tpu as pltpu
from jax.sharding import Mesh
from jax.sharding import PartitionSpec as P


HEAD = 128
PAIR = 2 * HEAD
BLOCK = 256
CHUNK = 2048
BLOCKS = CHUNK // BLOCK
LOW, MIDDLE = 3, 6
RELAYED = 704
SIZES = {"z": 4, "y": 4, "xh": 2, "xl": 2, "core": 2}
SEQ_AXES = ("z", "y", "xh")
DP_AXES = ("xl", "core")
PLANE = ("y", "xh")

query_scale = 144.0 ** (-0.5)
soft_cap = 50.0
LOG2E = 1.4426950408889634
CONTRACT_LAST = (((1,), (1,)), ((), ()))


X_AXES = ("xh", "xl", "core")


def x_step(flip):
    pairs = []
    for x, core in itertools.product(range(4), range(2)):
        to = (x + (1 if core == 0 else -1)) % 4
        pairs.append((2 * x + core, 2 * to + (core ^ flip)))
    return pairs


def ring(step):
    return [(i, (i + step) % 4) for i in range(4)]


def to_partner(array):
    return lax.ppermute(array, "core", [(0, 1), (1, 0)])


def both_sequences(own, partner, weight):
    stacked = jnp.concatenate([own, partner], axis=0)
    return jnp.dot(stacked, weight, preferred_element_type=jnp.float32)


def half_product_kernel(info, own_0, own_1, partner_0, partner_1, weight_0, weight_1, out):
    out[...] = both_sequences(own_0[...], partner_0[...], weight_0[...]) + both_sequences(
        own_1[...], partner_1[...], weight_1[...]
    )


def project_kernel(
    info, partial, own_2, own_3, partner_2, partner_3, direct_a, direct_b,
    relay_0, relay_1, relay_2, relay_3, up_own, up_partner, cosine, sine,
    latent, pairs, weights, upper,
):
    mine, plane = info[0], info[1]
    core = mine % 2
    rows = own_2.shape[0]
    piece = up_own.shape[1]
    share = relay_0.shape[1]
    half = direct_a.shape[1]
    split = direct_a.shape[0] - 2 * piece
    for which, direct in ((0, direct_a), (1, direct_b)):
        weights[which, :split, :] = direct[:split, :]
        for step, relay in ((0, relay_0), (3, relay_1), (1, relay_2), (2, relay_3)):
            at = split + share * ((plane + step) % 4)
            weights[which, pl.ds(pl.multiple_of(at, 16), share), :] = relay[which]
        at = pl.ds(pl.multiple_of((mine ^ (2 + which)) * piece, piece), piece)
        upper[at, :half] = direct[split : split + piece, :]
        upper[at, half:] = direct[split + piece :, :]
    upper[pl.ds(pl.multiple_of(mine * piece, piece), piece), :] = up_own[0]
    upper[pl.ds(pl.multiple_of((mine ^ 1) * piece, piece), piece), :] = up_partner[0]
    total = partial[...] + both_sequences(own_2[...], partner_2[...], weights[0])
    total = total + both_sequences(own_3[...], partner_3[...], weights[1])
    rounded = total.astype(jnp.bfloat16)
    latent[...] = rounded
    raw = jnp.dot(rounded, upper[...], preferred_element_type=jnp.float32)
    for which, turn in ((0, core), (1, 1 - core)):
        for head in range(raw.shape[1] // HEAD):
            entry = raw[which * rows : (which + 1) * rows, head * HEAD : (head + 1) * HEAD]
            entry = entry * cosine[...] + pltpu.roll(entry, HEAD // 2, 1) * sine[...]
            pairs[2 * head + turn] = entry.astype(jnp.bfloat16)


def expo(raw):
    return jnp.exp2(jnp.tanh(raw * (query_scale / soft_cap)) * (soft_cap * LOG2E))


def folded(values):
    total = values[:, :HEAD]
    for t in range(1, values.shape[1] // HEAD):
        total = total + values[:, t * HEAD : (t + 1) * HEAD]
    return total


def triangle(newer):
    row = lax.broadcasted_iota(jnp.int32, (2 * BLOCK, BLOCK), 0) % BLOCK
    col = lax.broadcasted_iota(jnp.int32, (2 * BLOCK, BLOCK), 1)
    return col <= row if newer else col > row


def stacked_rows(queries, i):
    own = queries[pl.ds(pl.multiple_of(i * BLOCK, BLOCK), BLOCK), :]
    return jnp.concatenate([own[:, :HEAD], own[:, HEAD:]], axis=0)


def over_blocks(stacked, pairs, blocks):
    numer = denom = 0.0
    for j, mask in blocks:
        raw = lax.dot_general(
            stacked, pairs[2 * j], CONTRACT_LAST, preferred_element_type=jnp.float32
        )
        e = expo(raw)
        if mask is not None:
            e = jnp.where(mask, e, 0.0)
        denom = denom + folded(e)
        numer = numer + jnp.dot(
            e.astype(jnp.bfloat16), pairs[2 * j + 1], preferred_element_type=jnp.float32
        )
    return numer, denom


def state_rows(i):
    return pl.ds(pl.multiple_of(i * 2 * BLOCK, 2 * BLOCK), 2 * BLOCK)


def own_kernel(queries, pairs, numer, denom):
    mask = triangle(True)
    for i in range(BLOCKS):
        blocks = [(j, None) for j in range(i)] + [(i, mask)]
        numer[state_rows(i), :], denom[state_rows(i), :] = over_blocks(
            stacked_rows(queries, i), pairs, blocks
        )


def near_kernel(group, info, queries, pairs, numer_in, denom_in, numer, denom):
    blocks = [(j, None) for j in range(pairs.shape[0] // 2)]

    @pl.when(info[0] >= 1)
    def _():
        def step(t, carry):
            for u in range(group):
                i = t * group + u
                n, d = over_blocks(stacked_rows(queries, i), pairs, blocks)
                numer[state_rows(i), :] += n
                denom[state_rows(i), :] += d
            return carry

        lax.fori_loop(0, BLOCKS // group, step, 0)


def far_kernel(first, last, info, queries, pairs, numer_in, denom_in, *outs):
    end = first + pairs.shape[0] // 2
    mask = triangle(False)
    numer, denom = (numer_in, denom_in) if last else outs

    def finish(i, n, d):
        if last:
            n = n / jnp.sum(d, axis=1, keepdims=True)
            outs[0][i * BLOCK : (i + 1) * BLOCK, :] = jnp.concatenate(
                [n[:BLOCK], n[BLOCK:]], axis=1
            ).astype(jnp.bfloat16)
        else:
            numer[state_rows(i), :], denom[state_rows(i), :] = n, d

    @pl.when(info[0] >= 2)
    def _():
        for i in range(BLOCKS):
            blocks = [(j - first, mask if j == i else None) for j in range(max(i, first), end)]
            old_n, old_d = numer[state_rows(i), :], denom[state_rows(i), :]
            if blocks:
                n, d = over_blocks(stacked_rows(queries, i), pairs, blocks)
                finish(i, old_n + n, old_d + d)
            elif last:
                finish(i, old_n, old_d)

    if last:

        @pl.when(info[0] < 2)
        def _():
            for i in range(BLOCKS):
                finish(i, numer[state_rows(i), :], denom[state_rows(i), :])


IN_VMEM = pl.BlockSpec(memory_space=pltpu.VMEM)
IN_SMEM = pl.BlockSpec(memory_space=pltpu.SMEM)
STATE = jax.ShapeDtypeStruct((2 * CHUNK, HEAD), jnp.float32)
RESULT = jax.ShapeDtypeStruct((CHUNK, PAIR), jnp.bfloat16)


def attention_call(kernel, count, args, result=False, resume=True):
    single = BLOCK * 2 * BLOCK
    inputs = [IN_SMEM] + [IN_VMEM] * 4 if resume else [IN_VMEM] * 2
    return pl.pallas_call(
        kernel,
        out_shape=RESULT if result else (STATE, STATE),
        in_specs=inputs,
        out_specs=IN_VMEM if result else (IN_VMEM, IN_VMEM),
        input_output_aliases={3: 0, 4: 1} if resume and not result else {},
        compiler_params=pltpu.CompilerParams(vmem_limit_bytes=24 * 2**20),
        cost_estimate=pl.CostEstimate(
            flops=count * single * 4 * HEAD, bytes_accessed=2**22, transcendentals=2 * count * single
        ),
    )(*args)


def body(hidden, queries, down_weight, up_weight, lengths):
    _, rows, _ = hidden.shape
    depth, rank2 = down_weight.shape
    rank = rank2 // 2
    piece, kv_width = up_weight.shape[1:]
    groups = kv_width // HEAD
    hidden = hidden[0]
    core = lax.axis_index("core")
    mine = 2 * lax.axis_index("xl") + core
    plane = lax.axis_index("z")
    start = lax.axis_index(SEQ_AXES) * rows
    info = jnp.stack([mine, plane]).astype(jnp.int32)

    share = RELAYED // 4
    split = depth - RELAYED
    forward, crossed = x_step(0), x_step(1)

    def columns(which, first, count):
        return lax.dynamic_slice(down_weight, (first, rank * which), (count, rank))

    def direct_rows(which):
        upper = lax.dynamic_index_in_dim(up_weight, which, 0, keepdims=False)
        return jnp.concatenate(
            [columns(which, 0, split), upper[:, :rank], upper[:, rank:]], axis=0
        )

    first = split + share * plane
    relay_a = lax.ppermute(columns(core, first, share), X_AXES, forward)
    relay_b = lax.ppermute(columns(1 - core, first, share), X_AXES, crossed)
    direct_a = lax.ppermute(direct_rows(core), X_AXES, forward)
    direct_b = lax.ppermute(direct_rows(1 - core), X_AXES, crossed)
    relay_own = jnp.stack([relay_a, relay_b])
    relays = [lax.ppermute(relay_own, "z", ring(k)) for k in (1, -1, 2)]
    partner_hidden = to_partner(hidden)
    partner_weight = to_partner(down_weight)
    partner_upper = to_partner(up_weight)

    half = HEAD // 2
    places = (start + jnp.arange(rows, dtype=jnp.int32)).astype(jnp.float32)
    freqs = 10000.0 ** (-2.0 * jnp.arange(half, dtype=jnp.float32) / HEAD)
    angles = places[:, None] * freqs[None, :]
    cosine, sine = jnp.cos(angles), jnp.sin(angles)
    cosine = jnp.where(core == 0, jnp.concatenate([cosine, cosine], axis=1), 1.0)
    sine = jnp.where(core == 0, jnp.concatenate([-sine, sine], axis=1), 0.0)

    def hidden_part(flip):
        return pl.BlockSpec((rows, depth), lambda i, s: (0, s[0] ^ flip))

    def whole(shape):
        return pl.BlockSpec(shape, lambda i, s: (0,) * len(shape))

    half_weight = pl.BlockSpec((depth, rank), lambda i, s: (0, s[0] % 2))
    half_upper = pl.BlockSpec((1, piece, kv_width), lambda i, s: (s[0] % 2, 0, 0))

    def projection(kernel, **spec):
        out_shape = spec.pop("out_shape")
        return pl.pallas_call(
            kernel,
            out_shape=out_shape,
            grid_spec=pltpu.PrefetchScalarGridSpec(num_scalar_prefetch=1, grid=(1,), **spec),
            compiler_params=pltpu.CompilerParams(vmem_limit_bytes=40 * 2**20),
            cost_estimate=pl.CostEstimate(
                flops=4 * rows * depth * rank2, bytes_accessed=8 * 2**20, transcendentals=0
            ),
        )

    partial = projection(
        half_product_kernel,
        out_shape=jax.ShapeDtypeStruct((2 * rows, rank), jnp.float32),
        in_specs=[hidden_part(0), hidden_part(1)] * 2 + [half_weight] * 2,
        out_specs=whole((2 * rows, rank)),
    )(info, hidden, hidden, partner_hidden, partner_hidden, down_weight, partner_weight)

    latent, pairs = projection(
        project_kernel,
        out_shape=(
            jax.ShapeDtypeStruct((2 * rows, rank), jnp.bfloat16),
            jax.ShapeDtypeStruct((2 * groups, rows, HEAD), jnp.bfloat16),
        ),
        in_specs=[whole((2 * rows, rank))]
        + [hidden_part(2), hidden_part(3)] * 2
        + [whole((split + 2 * piece, rank))] * 2
        + [whole((2, share, rank))] * 4
        + [half_upper] * 2
        + [whole((rows, HEAD))] * 2,
        out_specs=[whole((2 * rows, rank)), whole((2 * groups, rows, HEAD))],
        scratch_shapes=[
            pltpu.VMEM((2, depth, rank), jnp.bfloat16),
            pltpu.VMEM((rank, kv_width), jnp.bfloat16),
        ],
    )(
        info, partial, hidden, hidden, partner_hidden, partner_hidden, direct_a, direct_b,
        relay_own, *relays, up_weight, partner_upper, cosine, sine,
    )

    sent = queries[0].reshape(rows, groups, PAIR).transpose(1, 0, 2)
    my_queries = lax.all_to_all(sent, PLANE, 0, 0, tiled=True).reshape(CHUNK, PAIR)
    pairs, my_queries = lax.optimization_barrier((pairs, my_queries))
    own_pairs = lax.all_to_all(pairs, PLANE + ("core",), 0, 0, tiled=True)
    other_half = to_partner(latent[rows:])

    low, middle = 2 * LOW, 2 * MIDDLE
    up = [(0, 1), (1, 2), (2, 3)]
    near_low = lax.ppermute(own_pairs[:low], "z", up)
    passing = lax.ppermute(own_pairs[low:], "z", [(1, 0), (0, 3)])
    near_middle = lax.ppermute(own_pairs[low:middle], "z", up)
    near_high = lax.ppermute(own_pairs[middle:], "z", up)
    far_low = lax.ppermute(near_low, "z", [(1, 2), (2, 3)])

    spot = plane.reshape(1).astype(jnp.int32)
    state = attention_call(own_kernel, 36, (my_queries, own_pairs), resume=False)
    for name, piece_pairs in (("low", near_low), ("middle", near_middle), ("high", near_high)):
        state = attention_call(
            functools.partial(near_kernel, 2),
            piece_pairs.shape[0] // 2 * BLOCKS,
            (spot, my_queries, piece_pairs, *state),
        )
        if name == "low":
            passing, state = lax.optimization_barrier((passing, state))
            far_high = lax.ppermute(passing, "z", [(0, 3), (3, 2)])
    state = attention_call(
        functools.partial(far_kernel, LOW, False), 30,
        (spot, my_queries, far_high, *state),
    )
    result = attention_call(
        functools.partial(far_kernel, 0, True), 6,
        (spot, my_queries, far_low, *state), result=True,
    )

    home = lax.all_to_all(result.reshape(groups, rows, PAIR), PLANE, 0, 0, tiled=True)
    home = home.transpose(1, 0, 2).reshape(rows, groups * PAIR)
    live = ((start + jnp.arange(rows, dtype=jnp.int32)) < lengths[0])[:, None]
    attended = jnp.where(live, home, jnp.zeros((), jnp.bfloat16))
    ours = latent[:rows]
    both = jnp.where(
        core == 0,
        jnp.concatenate([ours, other_half], axis=1),
        jnp.concatenate([other_half, ours], axis=1),
    )
    latent = jnp.where(live, both, jnp.zeros((), jnp.bfloat16))
    return latent[None], attended[None]


def solution(mesh):
    split = Mesh(mesh.devices.reshape(tuple(SIZES.values())), tuple(SIZES))
    rows = P(DP_AXES, SEQ_AXES, None)
    placed = (rows, rows, P(DP_AXES, None), P(None, DP_AXES, None), P(DP_AXES))

    return jax.shard_map(body, mesh=split, in_specs=placed, out_specs=(rows, rows), check_vma=False)
```

time: 172 us -> 151 us (0.88)
  waiting for transfers between devices: 72.2 us -> 36.6 us
  other arithmetic: 2.52 us -> 9.31 us
  local copies, waits for them, and re-layouts: 8.09 us -> 11.9 us
  starting transfers between devices: 23.9 us -> 27.1 us
  blocking collectives: 23.2 us -> 25.8 us
    ppermute x4 -> x7, waiting for transfers between devices: 44 us -> 9.04 us  [the longest x3 9.03 us: body(): relays = [lax.ppermute(relay_own, 'z', ring(k)) for k in (1, -1, 2)]]
    dynamic_slice x0 -> x2, local copies, waits for them, and re-layouts: none -> 3.75 us  [columns(): return lax.dynamic_slice(down_weight, (first, rank * which), (count, rank))]
    unnamed x11 -> x15, local copies, waits for them, and re-layouts: 1.98 us -> 4.97 us
    all_to_all x1, blocking collectives: 23.2 us -> 25.8 us  [body(): own_pairs = lax.all_to_all(pairs, PLANE + ('core',), 0, 0, tiled=True)]
    concatenate x1 -> x2, other arithmetic: 0.78 us -> 2.98 us  [direct_rows(): jnp.concatenate([columns(which, 0, split), upper[:, :rank], upper[:, rank...]
    select_n x1 -> x3, other arithmetic: 1.11 us -> 3.21 us  [the longest x1 1.16 us: body(): jnp.where(core == 0, jnp.concatenate([cosine, cosine], axis=1), 1.0)]
    ppermute x6 -> x4, starting transfers between devices: 0.61 us -> 2.53 us  [to_partner(): return lax.ppermute(array, 'core', [(0, 1), (1, 0)])]
    squeeze x1, local copies, waits for them, and re-layouts: 1.85 us -> 0.04 us  [direct_rows(): upper = lax.dynamic_index_in_dim(up_weight, which, 0, keepdims=False)]
  transfers between devices with their start and end apart: 18 -> 19, of which waited for: 7 -> 5; matrix products, arithmetic and copies ran while one was open for 4% -> 10% of each run, Pallas kernels for 18% -> 24%
where the time goes in v1:
time: 151 us
  Pallas kernels  38.4 us (25%)
  waiting for transfers between devices  36.6 us (24%)
  starting transfers between devices  27.1 us (18%)
  blocking collectives  25.8 us (17%)
  local copies, waits for them, and re-layouts  11.9 us (8%)
  other arithmetic  9.31 us (6%)
  between operations  1.58 us (1%)
    pallas_call x6, Pallas kernels, attention_call(): pl.pallas_call(kernel, out_shape=RESULT if result else (STATE, STATE), in...  29.5 us
    all_to_all x1, blocking collectives, body(): own_pairs = lax.all_to_all(pairs, PLANE + ('core',), 0, 0, tiled=True)  25.8 us
    all_to_all x1, waiting for transfers between devices, body(): lax.all_to_all(result.reshape(groups, rows, PAIR), PLANE, 0, 0, tiled=True)  11.4 us
    ppermute x1, waiting for transfers between devices, body(): near_middle = lax.ppermute(own_pairs[low:middle], 'z', up)  9.95 us
    ppermute x3, waiting for transfers between devices, body(): relays = [lax.ppermute(relay_own, 'z', ring(k)) for k in (1, -1, 2)]  9.03 us
    all_to_all x1, starting transfers between devices, body(): lax.all_to_all(sent, PLANE, 0, 0, tiled=True).reshape(CHUNK, PAIR)  5.72 us
    ppermute x1, waiting for transfers between devices, body(): near_low = lax.ppermute(own_pairs[:low], 'z', up)  5.32 us
    pallas_call x1, Pallas kernels, body(): projection(project_kernel, out_shape=(jax.ShapeDtypeStruct((2 * rows, ran...  5.19 us
  transfers between devices with their start and end apart: 19, of which 5 were waited for; matrix products, arithmetic and copies ran while one was open for 10% of the time, Pallas kernels for 24%

profile of v1, /device:TPU:96, one launch (start us, length us, event | category | flops | bytes accessed | tf_op | source)
XLA Modules:
  0.0 150.7 jit_solution(5976309056314055323)
XLA Ops:
  0.6 0.1 collective-permute-start
  0.7 0.5 collective-permute-start.1
  1.2 1.8 %fusion.4 = (bf16[176,512]{1,0:T(8,128)(2,1)}, bf16[176,512]{1,0:T(8,128)(2,1)}) fusion(bf16[1152,1024]{1,0:T(8,128)(2,1)} %weight_0.1, s32[]{:T(128)S(6)} %select_n.73, s32[]{:T(128)S(6)} %select_n.69, s32[]{:T(128)S(6)} %select_n.71), kind=kLoop, calls=%fused_computation.22 | loop fusion | bytes 720908 | tf_op jit(solution)/shard_map/dynamic_slice | solution.py:235
  3.0 1.5 collective-permute-start.4
  4.5 0.0 collective-permute-start.5
  4.5 1.9 %collective-permute-start.9 = (bf16[2,128,1024]{2,1,0:T(8,128)(2,1)}, bf16[2,128,1024]{2,1,0:T(8,128)(2,1)}, u32[]{:S(2)}, u32[]{:S(2)}) collective-permute-start(bf16[2,128,1024]{2,1,0:T(8,128)(2,1)} %up_own.1), channel_id=1, source_target_pairs={{0,1},{1,0},{2,3},{3,2},{4,5},{5,4},{6,7},{7,6},{8,9},{9,8},{10,11... | collective-permute-start | bytes 1572872 | tf_op jit(solution)/shard_map/ppermute | solution.py:47
  6.3 1.5 %copy.17 = bf16[32,8,8,256]{3,2,1,0:T(8,128)(2,1)S(1)} copy(bf16[32,8,8,256]{3,1,2,0:T(8,128)(2,1)} %bitcast.36) | data formatting | bytes 2097152
  7.9 0.0 copy-start.2
  7.9 1.2 copy.19
  9.0 5.7 %all-to-all-start = ((bf16[8,256,256]{2,1,0:T(8,128)(2,1)}), bf16[8,256,256]{2,1,0:T(8,128)(2,1)S(1)}, u32[]{:S(2)}, u32[]{:S(2)}) async-start(bf16[8,256,256]{2,1,0:T(8,128)(2,1)} %bitcast.21), calls=%async_computation | async-start | bytes 2097152 | tf_op jit(solution)/shard_map/all_to_all | solution.py:313
  14.8 2.0 %constant_dynamic-slice_fusion = (bf16[448,512]{1,0:T(8,128)(2,1)S(1)}, bf16[448,512]{1,0:T(8,128)(2,1)}) fusion(bf16[1152,1024]{1,0:T(8,128)(2,1)} %weight_0.1, s32[]{:T(128)S(6)} %select_n.71, s32[]{:T(128)S(6)} %select_n.69), kind=kLoop, calls=%fused_computation.15 | loop fusion | bytes 1835016 | tf_op jit(solution)/shard_map/dynamic_slice | solution.py:235
  16.8 0.7 fusion.6
  17.5 0.9 pad_maximum_fusion.1
  18.5 2.0 %pad_maximum_fusion = bf16[704,512]{1,0:T(8,128)(2,1)} fusion(bf16[128,512]{1,0:T(8,128)(2,1)S(1)} %get-tuple-element.53, bf16[128,512]{1,0:T(8,128)(2,1)} %get-tuple-element.54, bf16[448,512]{1,0:T(8,128)(2,1)} %get-tuple-element.39), kind=kLoop, calls=%fused_computation.2 | loop fusion | flops 2162688 | bytes 1441792 | tf_op jit(solution)/shard_map/concatenate | solution.py:239
  20.5 0.0 collective-permute-done.4
  20.5 1.1 collective-permute-start.2
  21.6 0.0 collective-permute-done.5
  21.6 0.0 collective-permute-start.3
  21.6 1.8 %pad_maximum_fusion.2.relay_0 = bf16[2,176,512]{2,1,0:T(8,128)(2,1)} fusion(bf16[1,176,512]{2,1,0:T(8,128)(2,1)} %bitcast.7, bf16[1,176,512]{2,1,0:T(8,128)(2,1)} %bitcast.6), kind=kLoop, calls=%fused_computation.6 | loop fusion | flops 180224 | bytes 720896 | tf_op jit(solution)/shard_map/stack | solution.py:248
  23.4 0.0 collective-permute-done.9.up_partner
  23.4 0.6 collective-permute-start.8
  24.0 0.0 collective-permute-done.partner_0.partner_1.partner_2.partner_3
  24.0 0.0 collective-permute-start.7
  24.0 0.0 collective-permute-done.1.weight_1
  24.0 3.2 %collective-permute-start.6 = (bf16[2,176,512]{2,1,0:T(8,128)(2,1)}, bf16[2,176,512]{2,1,0:T(8,128)(2,1)}, u32[]{:S(2)}, u32[]{:S(2)}) collective-permute-start(bf16[2,176,512]{2,1,0:T(8,128)(2,1)} %pad_maximum_fusion.2.relay_0), channel_id=1, source_target_pairs={{0,32},{32,64},{64,96},{96,0},{1,33},{33,65},{65,97},{97,1},{2,34}... | collective-permute-start | bytes 1081352 | tf_op jit(solution)/shard_map/ppermute | solution.py:249
  27.2 1.2 fusion.1
  28.4 0.1 pad_add_fusion.info
  28.5 1.2 maximum_select_fusion.1
  29.7 0.0 copy-start.1
  29.7 1.7 %copy-done.1 = bf16[1152,1024]{1,0:T(8,128)(2,1)S(1)} copy-done((bf16[1152,1024]{1,0:T(8,128)(2,1)S(1)}, bf16[1152,1024]{1,0:T(8,128)(2,1)}, u32[]{:S(2)}) %copy-start.1) | copy-done | bytes 2359320
  31.4 3.7 %shard_map.68.partial = f32[512,512]{1,0:T(8,128)S(1)} custom-call(s32[2]{0:T(128)S(1)} %pad_add_fusion.info, bf16[256,4608]{1,0:T(8,128)(2,1)S(1)} %bitcast.24, bf16[256,4608]{1,0:T(8,128)(2,1)S(1)} %bitcast.25, bf16[256,4608]{1,0:T(8,128)(2,1)} %collective-permute-done.partner_0.partner_1.partner_2.partner_3, ...), custom_call_target="tpu_custom_call" | custom-call | flops 1207959552 | bytes 8388608 | tf_op jit(solution)/shard_map/pallas_call | solution.py:283
  35.1 9.0 %collective-permute-done.7.relay_2 = bf16[2,176,512]{2,1,0:T(8,128)(2,1)} collective-permute-done((bf16[2,176,512]{2,1,0:T(8,128)(2,1)}, bf16[2,176,512]{2,1,0:T(8,128)(2,1)}, u32[]{:S(2)}, u32[]{:S(2)}) %collective-permute-start.7) | collective-permute-done | bytes 360480 | tf_op jit(solution)/shard_map/ppermute | solution.py:249
  44.1 0.0 collective-permute-done.6.relay_1
  44.1 0.0 collective-permute-done.2.direct_a
  44.1 0.0 collective-permute-done.3.direct_b
  44.2 5.2 %shard_map.69 = (bf16[512,512]{1,0:T(8,128)(2,1)S(1)}, bf16[16,256,128]{2,1,0:T(8,128)(2,1)S(1)}) custom-call(s32[2]{0:T(128)S(1)} %pad_add_fusion.info, f32[512,512]{1,0:T(8,128)S(1)} %shard_map.68.partial, bf16[256,4608]{1,0:T(8,128)(2,1)S(1)} %bitcast.26, bf16[256,4608]{1,0:T(8,128)(2,1)S(1)} %bitcast.27, ...), custom_call_target="tpu_custom_call" | custom-call | flops 1207959552 | bytes 8388608 | tf_op jit(solution)/shard_map/pallas_call | solution.py:290
  49.4 1.0 copy-done.4
  50.4 0.8 copy-done.5
  51.1 25.8 %all_to_all.15.pairs = bf16[16,256,128]{2,1,0:T(8,128)(2,1)S(1)} all-to-all(bf16[16,256,128]{2,1,0:T(8,128)(2,1)} %copy-done.4), channel_id=1, replica_groups=mesh['z'=4,'y'=4,'xh'=2,'xl'=2,'core'=2] {'y','xh','core'}, dimensions={0} | all-to-all | bytes 2097152 | tf_op jit(solution)/shard_map/all_to_all | solution.py:315
  77.0 1.3 collective-permute-start.13
  78.3 0.1 fusion.5
  78.4 1.5 collective-permute-start.11
  79.9 5.4 %shard_map.70 = (f32[4096,128]{1,0:T(8,128)S(1)}, f32[4096,128]{1,0:T(8,128)S(1)}) custom-call(bf16[2048,256]{1,0:T(8,128)(2,1)S(1)} %bitcast.28, bf16[16,256,128]{2,1,0:T(8,128)(2,1)S(1)} %all_to_all.15.pairs), custom_call_target="tpu_custom_call" | custom-call | flops 2415919104 | bytes 4194304 | tf_op jit(solution)/shard_map/pallas_call | solution.py:204
  85.2 5.3 %collective-permute-done.11.pairs = bf16[6,256,128]{2,1,0:T(8,128)(2,1)S(1)} collective-permute-done((bf16[6,256,128]{2,1,0:T(8,128)(2,1)S(1)}, bf16[6,256,128]{2,1,0:T(8,128)(2,1)S(1)}, u32[]{:S(2)}, u32[]{:S(2)}) %collective-permute-start.11) | collective-permute-done | bytes 393248 | tf_op jit(solution)/shard_map/ppermute | solution.py:320
  90.6 5.8 %shard_map.71 = (f32[4096,128]{1,0:T(8,128)S(1)}, f32[4096,128]{1,0:T(8,128)S(1)}) custom-call(s32[1]{0:T(128)} %bitcast.2.info, bf16[2048,256]{1,0:T(8,128)(2,1)S(1)} %bitcast.29, bf16[6,256,128]{2,1,0:T(8,128)(2,1)S(1)} %collective-permute-done.11.pairs, f32[4096,128]{1,0:T(8,128)S(1)} %get-tuple-element.23.numer_in, ...), custom_call_target="tpu_custom_call", output_to_operand_aliasing={{0}: (3, {}), {1}: (4, {})} | custom-call | flops 1610612736 | bytes 4194304 | tf_op jit(solution)/shard_map/pallas_call | solution.py:204
  96.4 0.0 collective-permute-done.13
  96.4 2.1 %collective-permute-start.14 = (bf16[10,256,128]{2,1,0:T(8,128)(2,1)S(1)}, bf16[10,256,128]{2,1,0:T(8,128)(2,1)S(1)}, u32[]{:S(2)}, u32[]{:S(2)}) collective-permute-start(bf16[10,256,128]{2,1,0:T(8,128)(2,1)S(1)} %collective-permute-done.13), channel_id=1, source_target_pairs={{0,96},{96,64},{1,97},{97,65},{2,98},{98,66},{3,99},{99,67},{4,100... | collective-permute-start | bytes 1966088 | tf_op jit(solution)/shard_map/ppermute | solution.py:336
  98.5 1.3 collective-permute-start.16
  99.9 1.3 collective-permute-start.15
  101.2 1.3 collective-permute-start.12
  102.5 10.0 %collective-permute-done.16.pairs = bf16[6,256,128]{2,1,0:T(8,128)(2,1)S(1)} collective-permute-done((bf16[6,256,128]{2,1,0:T(8,128)(2,1)S(1)}, bf16[6,256,128]{2,1,0:T(8,128)(2,1)S(1)}, u32[]{:S(2)}, u32[]{:S(2)}) %collective-permute-start.16) | collective-permute-done | bytes 393248 | tf_op jit(solution)/shard_map/ppermute | solution.py:322
  112.4 5.8 %shard_map.72 = (f32[4096,128]{1,0:T(8,128)S(1)}, f32[4096,128]{1,0:T(8,128)S(1)}) custom-call(s32[1]{0:T(128)} %bitcast.2.info, bf16[2048,256]{1,0:T(8,128)(2,1)S(1)} %bitcast.30, bf16[6,256,128]{2,1,0:T(8,128)(2,1)S(1)} %collective-permute-done.16.pairs, f32[4096,128]{1,0:T(8,128)S(1)} %get-tuple-element.28.numer_in, ...), custom_call_target="tpu_custom_call", output_to_operand_aliasing={{0}: (3, {}), {1}: (4, {})} | custom-call | flops 1610612736 | bytes 4194304 | tf_op jit(solution)/shard_map/pallas_call | solution.py:204
  118.3 4.0 %shard_map.73 = (f32[4096,128]{1,0:T(8,128)S(1)}, f32[4096,128]{1,0:T(8,128)S(1)}) custom-call(s32[1]{0:T(128)} %bitcast.2.info, bf16[2048,256]{1,0:T(8,128)(2,1)S(1)} %bitcast.31, bf16[4,256,128]{2,1,0:T(8,128)(2,1)S(1)} %collective-permute-done.15.pairs, f32[4096,128]{1,0:T(8,128)S(1)} %get-tuple-element.30.numer_in, ...), custom_call_target="tpu_custom_call", output_to_operand_aliasing={{0}: (3, {}), {1}: (4, {})} | custom-call | flops 1073741824 | bytes 4194304 | tf_op jit(solution)/shard_map/pallas_call | solution.py:204
  122.3 0.0 collective-permute-done.14.pairs
  122.3 6.0 %shard_map.74 = (f32[4096,128]{1,0:T(8,128)S(1)}, f32[4096,128]{1,0:T(8,128)S(1)}) custom-call(s32[1]{0:T(128)} %bitcast.2.info, bf16[2048,256]{1,0:T(8,128)(2,1)S(1)} %bitcast.32, bf16[10,256,128]{2,1,0:T(8,128)(2,1)S(1)} %collective-permute-done.14.pairs, ...), custom_call_target="tpu_custom_call", output_to_operand_aliasing={{0}: (3, {}), {1}: (4, {})} | custom-call | flops 2013265920 | bytes 4194304 | tf_op jit(solution)/shard_map/pallas_call | solution.py:204
  128.2 2.5 %shard_map.75 = bf16[2048,256]{1,0:T(8,128)(2,1)} custom-call(s32[1]{0:T(128)} %bitcast.2.info, bf16[2048,256]{1,0:T(8,128)(2,1)S(1)} %bitcast.33, bf16[6,256,128]{2,1,0:T(8,128)(2,1)S(1)} %collective-permute-done.12.pairs, f32[4096,128]{1,0:T(8,128)S(1)} %get-tuple-element.34.numer_in, f32[4096,128]{1,0:T(8,128)S(1)} %get-tuple-element.35.denom_in), custom_call_target="tpu_custom_call" | custom-call | flops 402653184 | bytes 4194304 | tf_op jit(solution)/shard_map/pallas_call | solution.py:204
  130.8 3.7 %all-to-all-start.2 = ((bf16[8,256,256]{2,1,0:T(8,128)(2,1)}), bf16[8,256,256]{2,1,0:T(8,128)(2,1)S(1)}, u32[]{:S(2)}, u32[]{:S(2)}) async-start(bf16[8,256,256]{2,1,0:T(8,128)(2,1)} %bitcast.12), calls=%async_computation.2 | async-start | bytes 2097152 | tf_op jit(solution)/shard_map/all_to_all | solution.py:346
  134.5 0.1 collective-permute-start.10
  135.3 0.9 collective-permute-done.10
  136.2 0.9 fusion
  137.1 11.4 %all-to-all-done.2 = bf16[8,256,256]{2,1,0:T(8,128)(2,1)S(1)} async-done(((bf16[8,256,256]{2,1,0:T(8,128)(2,1)}), bf16[8,256,256]{2,1,0:T(8,128)(2,1)S(1)}, u32[]{:S(2)}, u32[]{:S(2)}) %all-to-all-start.2) | async-done | bytes 1048608 | tf_op jit(solution)/shard_map/all_to_all | solution.py:346
  148.5 0.6 copy.16
  149.1 0.5 reshape.135
  149.6 1.1 broadcast_select_fusion
  (20 shorter events, 0.2 us)
Async XLA Ops:
  0.6 23.3 %collective-permute-start = (bf16[256,4608]{1,0:T(8,128)(2,1)}, bf16[256,4608]{1,0:T(8,128)(2,1)}, u32[]{:S(2)}, u32[]{:S(2)}) collective-permute-start(bf16[256,4608]{1,0:T(8,128)(2,1)} %bitcast.23), channel_id=1, source_target_pairs={{0,1},{1,0},{2,3},{3,2},{4,5},{5,4},{6,7},{7,6},{8,9},{9,8},{10,11... | collective-permute-start | bytes 7077896 | tf_op jit(solution)/shard_map/ppermute | solution.py:47
  0.7 23.2 %collective-permute-start.1 = (bf16[1152,1024]{1,0:T(8,128)(2,1)}, bf16[1152,1024]{1,0:T(8,128)(2,1)}, u32[]{:S(2)}, u32[]{:S(2)}) collective-permute-start(bf16[1152,1024]{1,0:T(8,128)(2,1)} %weight_0.1), channel_id=1, source_target_pairs={{0,1},{1,0},{2,3},{3,2},{4,5},{5,4},{6,7},{7,6},{8,9},{9,8},{10,11... | collective-permute-start | bytes 7077896 | tf_op jit(solution)/shard_map/ppermute | solution.py:47
  3.0 17.5 %collective-permute-start.4 = (bf16[176,512]{1,0:T(8,128)(2,1)}, bf16[176,512]{1,0:T(8,128)(2,1)}, u32[]{:S(2)}, u32[]{:S(2)}) collective-permute-start(bf16[176,512]{1,0:T(8,128)(2,1)} %get-tuple-element.36), channel_id=1, source_target_pairs={{0,2},{1,7},{2,4},{3,1},{4,6},{5,3},{6,0},{7,5},{8,10},{9,15},{10,... | collective-permute-start | bytes 540680 | tf_op jit(solution)/shard_map/ppermute | solution.py:244
  4.5 17.1 %collective-permute-start.5 = (bf16[176,512]{1,0:T(8,128)(2,1)}, bf16[176,512]{1,0:T(8,128)(2,1)}, u32[]{:S(2)}, u32[]{:S(2)}) collective-permute-start(bf16[176,512]{1,0:T(8,128)(2,1)} %get-tuple-element.37), channel_id=1, source_target_pairs={{0,3},{1,6},{2,5},{3,0},{4,7},{5,2},{6,1},{7,4},{8,11},{9,14},{10,... | collective-permute-start | bytes 540680 | tf_op jit(solution)/shard_map/ppermute | solution.py:245
  4.5 18.9 %collective-permute-start.9 = (bf16[2,128,1024]{2,1,0:T(8,128)(2,1)}, bf16[2,128,1024]{2,1,0:T(8,128)(2,1)}, u32[]{:S(2)}, u32[]{:S(2)}) collective-permute-start(bf16[2,128,1024]{2,1,0:T(8,128)(2,1)} %up_own.1), channel_id=1, source_target_pairs={{0,1},{1,0},{2,3},{3,2},{4,5},{5,4},{6,7},{7,6},{8,9},{9,8},{10,11... | collective-permute-start | bytes 1572872 | tf_op jit(solution)/shard_map/ppermute | solution.py:47
  7.9 6.9 %copy-start.2 = (bf16[2,128,1024]{2,1,0:T(8,128)(2,1)S(1)}, bf16[2,128,1024]{2,1,0:T(8,128)(2,1)}, u32[]{:S(2)}) copy-start(bf16[2,128,1024]{2,1,0:T(8,128)(2,1)} %up_own.1) | copy-start | bytes 1572868
  9.0 42.1 %all-to-all-start = ((bf16[8,256,256]{2,1,0:T(8,128)(2,1)}), bf16[8,256,256]{2,1,0:T(8,128)(2,1)S(1)}, u32[]{:S(2)}, u32[]{:S(2)}) async-start(bf16[8,256,256]{2,1,0:T(8,128)(2,1)} %bitcast.21), calls=%async_computation | async-start | bytes 2097152 | tf_op jit(solution)/shard_map/all_to_all | solution.py:313
  17.5 12.2 %copy-start = (bf16[1,256,4608]{2,1,0:T(8,128)(2,1)S(1)}, bf16[1,256,4608]{2,1,0:T(8,128)(2,1)}, u32[]{:S(2)}) copy-start(bf16[1,256,4608]{2,1,0:T(8,128)(2,1)} %param.5) | copy-start | bytes 7077892
  20.5 23.7 %collective-permute-start.2 = (bf16[704,512]{1,0:T(8,128)(2,1)}, bf16[704,512]{1,0:T(8,128)(2,1)}, u32[]{:S(2)}, u32[]{:S(2)}) collective-permute-start(bf16[704,512]{1,0:T(8,128)(2,1)} %pad_maximum_fusion), channel_id=1, source_target_pairs={{0,2},{1,7},{2,4},{3,1},{4,6},{5,3},{6,0},{7,5},{8,10},{9,15},{10,... | collective-permute-start | bytes 2162696 | tf_op jit(solution)/shard_map/ppermute | solution.py:246
  21.6 22.5 %collective-permute-start.3 = (bf16[704,512]{1,0:T(8,128)(2,1)}, bf16[704,512]{1,0:T(8,128)(2,1)}, u32[]{:S(2)}, u32[]{:S(2)}) collective-permute-start(bf16[704,512]{1,0:T(8,128)(2,1)} %pad_maximum_fusion.1), channel_id=1, source_target_pairs={{0,3},{1,6},{2,5},{3,0},{4,7},{5,2},{6,1},{7,4},{8,11},{9,14},{10,... | collective-permute-start | bytes 2162696 | tf_op jit(solution)/shard_map/ppermute | solution.py:247
  23.4 11.7 %collective-permute-start.8 = (bf16[2,176,512]{2,1,0:T(8,128)(2,1)}, bf16[2,176,512]{2,1,0:T(8,128)(2,1)}, u32[]{:S(2)}, u32[]{:S(2)}) collective-permute-start(bf16[2,176,512]{2,1,0:T(8,128)(2,1)} %pad_maximum_fusion.2.relay_0), channel_id=1, source_target_pairs={{0,64},{32,96},{64,0},{96,32},{1,65},{33,97},{65,1},{97,33},{2,66}... | collective-permute-start | bytes 1081352 | tf_op jit(solution)/shard_map/ppermute | solution.py:249
  24.0 20.2 %collective-permute-start.7 = (bf16[2,176,512]{2,1,0:T(8,128)(2,1)}, bf16[2,176,512]{2,1,0:T(8,128)(2,1)}, u32[]{:S(2)}, u32[]{:S(2)}) collective-permute-start(bf16[2,176,512]{2,1,0:T(8,128)(2,1)} %pad_maximum_fusion.2.relay_0), channel_id=1, source_target_pairs={{0,96},{32,0},{64,32},{96,64},{1,97},{33,1},{65,33},{97,65},{2,98}... | collective-permute-start | bytes 1081352 | tf_op jit(solution)/shard_map/ppermute | solution.py:249
  24.0 20.2 %collective-permute-start.6 = (bf16[2,176,512]{2,1,0:T(8,128)(2,1)}, bf16[2,176,512]{2,1,0:T(8,128)(2,1)}, u32[]{:S(2)}, u32[]{:S(2)}) collective-permute-start(bf16[2,176,512]{2,1,0:T(8,128)(2,1)} %pad_maximum_fusion.2.relay_0), channel_id=1, source_target_pairs={{0,32},{32,64},{64,96},{96,0},{1,33},{33,65},{65,97},{97,1},{2,34}... | collective-permute-start | bytes 1081352 | tf_op jit(solution)/shard_map/ppermute | solution.py:249
  29.7 1.7 %copy-start.1 = (bf16[1152,1024]{1,0:T(8,128)(2,1)S(1)}, bf16[1152,1024]{1,0:T(8,128)(2,1)}, u32[]{:S(2)}) copy-start(bf16[1152,1024]{1,0:T(8,128)(2,1)} %weight_0.1) | copy-start | bytes 7077892
  31.4 12.8 %copy-start.3 = (bf16[2,128,1024]{2,1,0:T(8,128)(2,1)S(1)}, bf16[2,128,1024]{2,1,0:T(8,128)(2,1)}, u32[]{:S(2)}) copy-start(bf16[2,128,1024]{2,1,0:T(8,128)(2,1)} %up_own.1) | copy-start | bytes 1572868
  49.4 1.0 copy-start.4
  50.4 0.8 copy-start.5
  77.0 19.3 %collective-permute-start.13 = (bf16[10,256,128]{2,1,0:T(8,128)(2,1)S(1)}, bf16[10,256,128]{2,1,0:T(8,128)(2,1)S(1)}, u32[]{:S(2)}, u32[]{:S(2)}) collective-permute-start(bf16[10,256,128]{2,1,0:T(8,128)(2,1)S(1)} %slice.45), channel_id=1, source_target_pairs={{32,0},{0,96},{33,1},{1,97},{34,2},{2,98},{35,3},{3,99},{36,4},{4,... | collective-permute-start | bytes 1966088 | tf_op jit(solution)/shard_map/ppermute | solution.py:321
  78.4 12.2 %collective-permute-start.11 = (bf16[6,256,128]{2,1,0:T(8,128)(2,1)S(1)}, bf16[6,256,128]{2,1,0:T(8,128)(2,1)S(1)}, u32[]{:S(2)}, u32[]{:S(2)}) collective-permute-start(bf16[6,256,128]{2,1,0:T(8,128)(2,1)S(1)} %get-tuple-element.41), channel_id=1, source_target_pairs={{0,32},{32,64},{64,96},{1,33},{33,65},{65,97},{2,34},{34,66},{66,9... | collective-permute-start | bytes 1179656 | tf_op jit(solution)/shard_map/ppermute | solution.py:320
  96.4 25.9 %collective-permute-start.14 = (bf16[10,256,128]{2,1,0:T(8,128)(2,1)S(1)}, bf16[10,256,128]{2,1,0:T(8,128)(2,1)S(1)}, u32[]{:S(2)}, u32[]{:S(2)}) collective-permute-start(bf16[10,256,128]{2,1,0:T(8,128)(2,1)S(1)} %collective-permute-done.13), channel_id=1, source_target_pairs={{0,96},{96,64},{1,97},{97,65},{2,98},{98,66},{3,99},{99,67},{4,100... | collective-permute-start | bytes 1966088 | tf_op jit(solution)/shard_map/ppermute | solution.py:336
  98.5 13.9 %collective-permute-start.16 = (bf16[6,256,128]{2,1,0:T(8,128)(2,1)S(1)}, bf16[6,256,128]{2,1,0:T(8,128)(2,1)S(1)}, u32[]{:S(2)}, u32[]{:S(2)}) collective-permute-start(bf16[6,256,128]{2,1,0:T(8,128)(2,1)S(1)} %get-tuple-element.40), channel_id=1, source_target_pairs={{0,32},{32,64},{64,96},{1,33},{33,65},{65,97},{2,34},{34,66},{66,9... | collective-permute-start | bytes 1179656 | tf_op jit(solution)/shard_map/ppermute | solution.py:322
  99.9 18.4 %collective-permute-start.15 = (bf16[4,256,128]{2,1,0:T(8,128)(2,1)S(1)}, bf16[4,256,128]{2,1,0:T(8,128)(2,1)S(1)}, u32[]{:S(2)}, u32[]{:S(2)}) collective-permute-start(bf16[4,256,128]{2,1,0:T(8,128)(2,1)S(1)} %slice.46), channel_id=1, source_target_pairs={{0,32},{32,64},{64,96},{1,33},{33,65},{65,97},{2,34},{34,66},{66,9... | collective-permute-start | bytes 786440 | tf_op jit(solution)/shard_map/ppermute | solution.py:323
  101.2 27.1 %collective-permute-start.12 = (bf16[6,256,128]{2,1,0:T(8,128)(2,1)S(1)}, bf16[6,256,128]{2,1,0:T(8,128)(2,1)S(1)}, u32[]{:S(2)}, u32[]{:S(2)}) collective-permute-start(bf16[6,256,128]{2,1,0:T(8,128)(2,1)S(1)} %collective-permute-done.11.pairs), channel_id=1, source_target_pairs={{32,64},{64,96},{33,65},{65,97},{34,66},{66,98},{35,67},{67,99},{3... | collective-permute-start | bytes 1179656 | tf_op jit(solution)/shard_map/ppermute | solution.py:324
  130.8 3.7 %copy-start.6 = (bf16[512,512]{1,0:T(8,128)(2,1)S(1)}, bf16[512,512]{1,0:T(8,128)(2,1)}, u32[]{:S(2)}) copy-start(bf16[512,512]{1,0:T(8,128)(2,1)} %copy-done.5) | copy-start | bytes 1572868
  130.8 17.7 %all-to-all-start.2 = ((bf16[8,256,256]{2,1,0:T(8,128)(2,1)}), bf16[8,256,256]{2,1,0:T(8,128)(2,1)S(1)}, u32[]{:S(2)}, u32[]{:S(2)}) async-start(bf16[8,256,256]{2,1,0:T(8,128)(2,1)} %bitcast.12), calls=%async_computation.2 | async-start | bytes 2097152 | tf_op jit(solution)/shard_map/all_to_all | solution.py:346
  134.5 1.6 %collective-permute-start.10 = (bf16[256,512]{1,0:T(8,128)(2,1)S(1)}, bf16[256,512]{1,0:T(8,128)(2,1)S(1)}, u32[]{:S(2)}, u32[]{:S(2)}) collective-permute-start(bf16[256,512]{1,0:T(8,128)(2,1)S(1)} %get-tuple-element.43), channel_id=1, source_target_pairs={{0,1},{1,0},{2,3},{3,2},{4,5},{5,4},{6,7},{7,6},{8,9},{9,8},{10,11... | collective-permute-start | bytes 786440 | tf_op jit(solution)/shard_map/ppermute | solution.py:47

commit v2 on v1

--- a/solution.py
+++ b/solution.py
@@ -45,6 +45,15 @@
 
 def to_partner(array):
     return lax.ppermute(array, "core", [(0, 1), (1, 0)])
+
+
+def pack_kernel(info, weight_a, upper_a, weight_b, upper_b, direct_a, direct_b):
+    split, width = weight_a.shape
+    piece = upper_a.shape[1]
+    for weight, upper, direct in ((weight_a, upper_a, direct_a), (weight_b, upper_b, direct_b)):
+        direct[:split, :] = weight[...]
+        direct[split : split + piece, :] = upper[0, :, :width]
+        direct[split + piece :, :] = upper[0, :, width:]
 
 
 def both_sequences(own, partner, weight):
@@ -207,7 +216,7 @@
         in_specs=inputs,
         out_specs=IN_VMEM if result else (IN_VMEM, IN_VMEM),
         input_output_aliases={3: 0, 4: 1} if resume and not result else {},
-        compiler_params=pltpu.CompilerParams(vmem_limit_bytes=24 * 2**20),
+        compiler_params=pltpu.CompilerParams(vmem_limit_bytes=12 * 2**20),
         cost_estimate=pl.CostEstimate(
             flops=count * single * 4 * HEAD, bytes_accessed=2**22, transcendentals=2 * count * single
         ),
@@ -234,22 +243,45 @@
     def columns(which, first, count):
         return lax.dynamic_slice(down_weight, (first, rank * which), (count, rank))
 
-    def direct_rows(which):
-        upper = lax.dynamic_index_in_dim(up_weight, which, 0, keepdims=False)
-        return jnp.concatenate(
-            [columns(which, 0, split), upper[:, :rank], upper[:, rank:]], axis=0
-        )
-
     first = split + share * plane
     relay_a = lax.ppermute(columns(core, first, share), X_AXES, forward)
     relay_b = lax.ppermute(columns(1 - core, first, share), X_AXES, crossed)
-    direct_a = lax.ppermute(direct_rows(core), X_AXES, forward)
-    direct_b = lax.ppermute(direct_rows(1 - core), X_AXES, crossed)
+    packed = jax.ShapeDtypeStruct((split + 2 * piece, rank), jnp.bfloat16)
+
+    def packing(flip):
+        return [
+            pl.BlockSpec((split, rank), lambda i, s: (0, (s[0] ^ flip) % 2)),
+            pl.BlockSpec((1, piece, kv_width), lambda i, s: ((s[0] ^ flip) % 2, 0, 0)),
+        ]
+
+    direct_a, direct_b = pl.pallas_call(
+        pack_kernel,
+        out_shape=(packed, packed),
+        grid_spec=pltpu.PrefetchScalarGridSpec(
+            num_scalar_prefetch=1,
+            grid=(1,),
+            in_specs=packing(0) + packing(1),
+            out_specs=[pl.BlockSpec(packed.shape, lambda i, s: (0, 0))] * 2,
+        ),
+        compiler_params=pltpu.CompilerParams(vmem_limit_bytes=16 * 2**20),
+        cost_estimate=pl.CostEstimate(flops=10**6, bytes_accessed=2**22, transcendentals=0),
+        name="pack",
+    )(info, down_weight, up_weight, down_weight, up_weight)
+    direct_a = lax.ppermute(direct_a, X_AXES, forward)
+    direct_b = lax.ppermute(direct_b, X_AXES, crossed)
     relay_own = jnp.stack([relay_a, relay_b])
     relays = [lax.ppermute(relay_own, "z", ring(k)) for k in (1, -1, 2)]
     partner_hidden = to_partner(hidden)
     partner_weight = to_partner(down_weight)
     partner_upper = to_partner(up_weight)
+
+    sent = queries[0].reshape(rows, 4, 2, PAIR).transpose(1, 2, 0, 3)
+    sent = lax.all_to_all(sent, "y", 0, 0, tiled=True)
+    here = lax.axis_index("xh")
+    kept_queries = lax.dynamic_index_in_dim(sent, here, 1, keepdims=False)
+    leaving = lax.dynamic_index_in_dim(sent, 1 - here, 1, keepdims=False)
+    leaving, direct_a, direct_b = lax.optimization_barrier((leaving, direct_a, direct_b))
+    crossing_queries = lax.ppermute(leaving, "xh", [(0, 1), (1, 0)])
 
     half = HEAD // 2
     places = (start + jnp.arange(rows, dtype=jnp.int32)).astype(jnp.float32)
@@ -274,7 +306,7 @@
             kernel,
             out_shape=out_shape,
             grid_spec=pltpu.PrefetchScalarGridSpec(num_scalar_prefetch=1, grid=(1,), **spec),
-            compiler_params=pltpu.CompilerParams(vmem_limit_bytes=40 * 2**20),
+            compiler_params=pltpu.CompilerParams(vmem_limit_bytes=26 * 2**20),
             cost_estimate=pl.CostEstimate(
                 flops=4 * rows * depth * rank2, bytes_accessed=8 * 2**20, transcendentals=0
             ),
@@ -290,8 +322,8 @@
     latent, pairs = projection(
         project_kernel,
         out_shape=(
-            jax.ShapeDtypeStruct((2 * rows, rank), jnp.bfloat16),
-            jax.ShapeDtypeStruct((2 * groups, rows, HEAD), jnp.bfloat16),
+            pltpu.HBM((2 * rows, rank), jnp.bfloat16),
+            pltpu.HBM((2 * groups, rows, HEAD), jnp.bfloat16),
         ),
         in_specs=[whole((2 * rows, rank))]
         + [hidden_part(2), hidden_part(3)] * 2
@@ -309,9 +341,9 @@
         relay_own, *relays, up_weight, partner_upper, cosine, sine,
     )
 
-    sent = queries[0].reshape(rows, groups, PAIR).transpose(1, 0, 2)
-    my_queries = lax.all_to_all(sent, PLANE, 0, 0, tiled=True).reshape(CHUNK, PAIR)
-    pairs, my_queries = lax.optimization_barrier((pairs, my_queries))
+    mixed = jnp.stack([kept_queries, crossing_queries], axis=1)
+    ordered = jnp.where(lax.axis_index("xh") == 0, mixed, mixed[:, ::-1])
+    my_queries = ordered.reshape(CHUNK, PAIR)
     own_pairs = lax.all_to_all(pairs, PLANE + ("core",), 0, 0, tiled=True)
     other_half = to_partner(latent[rows:])
 
@@ -325,15 +357,14 @@
 
     spot = plane.reshape(1).astype(jnp.int32)
     state = attention_call(own_kernel, 36, (my_queries, own_pairs), resume=False)
-    for name, piece_pairs in (("low", near_low), ("middle", near_middle), ("high", near_high)):
+    passing, state = lax.optimization_barrier((passing, state))
+    far_high = lax.ppermute(passing, "z", [(0, 3), (3, 2)])
+    for piece_pairs in (near_low, near_middle, near_high):
         state = attention_call(
-            functools.partial(near_kernel, 2),
+            functools.partial(near_kernel, 4),
             piece_pairs.shape[0] // 2 * BLOCKS,
             (spot, my_queries, piece_pairs, *state),
         )
-        if name == "low":
-            passing, state = lax.optimization_barrier((passing, state))
-            far_high = lax.ppermute(passing, "z", [(0, 3), (3, 2)])
     state = attention_call(
         functools.partial(far_kernel, LOW, False), 30,
         (spot, my_queries, far_high, *state),

time: 151 us -> 168 us (1.11)
  the two profiles are of different devices: /device:TPU:96 before, /device:TPU:66 now
where the time goes in v2:
time: 168 us; the launch traced here: 167 us
  waiting for transfers between devices  59.4 us (35%)
  starting transfers between devices  50.5 us (30%)
  Pallas kernels  39.6 us (24%)
  local copies, waits for them, and re-layouts  10.9 us (6%)
  other arithmetic  4.98 us (3%)
    pallas_call x6, Pallas kernels, attention_call(): pl.pallas_call(kernel, out_shape=RESULT if result else (STATE, STATE), in...  28 us
    ppermute x1, waiting for transfers between devices, body(): crossing_queries = lax.ppermute(leaving, 'xh', [(0, 1), (1, 0)])  23.6 us
    all_to_all x1, waiting for transfers between devices, body(): lax.all_to_all(result.reshape(groups, rows, PAIR), PLANE, 0, 0, tiled=True)  13 us
    ppermute x1, starting transfers between devices, body(): near_middle = lax.ppermute(own_pairs[low:middle], 'z', up)  12.7 us
    ppermute x1, waiting for transfers between devices, body(): relay_a = lax.ppermute(columns(core, first, share), X_AXES, forward)  10.7 us
    all_to_all x1, starting transfers between devices, body(): own_pairs = lax.all_to_all(pairs, PLANE + ('core',), 0, 0, tiled=True)  7.47 us
    ppermute x3, waiting for transfers between devices, body(): relays = [lax.ppermute(relay_own, 'z', ring(k)) for k in (1, -1, 2)]  6.37 us
    pallas_call x1, Pallas kernels, body(): projection(project_kernel, out_shape=(pltpu.HBM((2 * rows, rank), jnp.bfl...  6.04 us
  transfers between devices with their start and end apart: 21, of which 9 were waited for; matrix products, arithmetic and copies ran while one was open for 6% of the time, Pallas kernels for 19%

profile of v2, /device:TPU:66, one launch (start us, length us, event | category | flops | bytes accessed | tf_op | source)
XLA Modules:
  0.0 167.0 jit_solution(5709796063059732176)
XLA Ops:
  0.6 0.1 collective-permute-start
  0.7 0.5 collective-permute-start.1
  1.2 0.1 pad_add_fusion.info
  1.3 1.7 copy-done.1
  3.0 1.0 copy-done.3
  4.0 1.8 %pack.1 = (bf16[704,512]{1,0:T(8,128)(2,1)}, bf16[704,512]{1,0:T(8,128)(2,1)}) custom-call(s32[2]{0:T(128)S(1)} %pad_add_fusion.info, bf16[1152,1024]{1,0:T(8,128)(2,1)S(1)} %copy-done.1, bf16[2,128,1024]{2,1,0:T(8,128)(2,1)S(1)} %copy-done.3, bf16[1152,1024]{1,0:T(8,128)(2,1)S(1)} %copy-done.1, bf16[2,128,1024]{2,1,0:T(8,128)(2,1)S(1)} %copy-done.3), custom_call_target="tpu_custom_call" | custom-call | flops 1000000 | bytes 4194304 | tf_op jit(solution)/shard_map/pack/pallas_call | solution.py:257
  5.8 1.5 collective-permute-start.2
  7.3 0.0 collective-permute-start.3
  7.3 1.0 fusion.4
  8.3 1.5 collective-permute-start.4
  9.8 0.8 reshape_squeeze.3
  10.6 0.0 copy-start.4
  10.6 1.2 copy.18
  11.8 4.5 %all-to-all-start = ((bf16[4,2,256,256]{3,2,1,0:T(8,128)(2,1)}), bf16[4,2,256,256]{3,2,1,0:T(8,128)(2,1)}, u32[]{:S(2)}, u32[]{:S(2)}) async-start(bf16[4,2,256,256]{3,2,1,0:T(8,128)(2,1)} %bitcast.17), calls=%async_computation | async-start | bytes 2097152 | tf_op jit(solution)/shard_map/all_to_all | solution.py:279
  16.3 10.7 %collective-permute-done.4 = bf16[176,512]{1,0:T(8,128)(2,1)S(1)} collective-permute-done((bf16[176,512]{1,0:T(8,128)(2,1)S(1)}, bf16[176,512]{1,0:T(8,128)(2,1)S(1)}, u32[]{:S(2)}, u32[]{:S(2)}) %collective-permute-start.4) | collective-permute-done | bytes 180256 | tf_op jit(solution)/shard_map/ppermute | solution.py:247
  27.0 0.4 collective-permute-start.5
  27.4 4.5 %collective-permute-done.5 = bf16[176,512]{1,0:T(8,128)(2,1)S(1)} collective-permute-done((bf16[176,512]{1,0:T(8,128)(2,1)S(1)}, bf16[176,512]{1,0:T(8,128)(2,1)S(1)}, u32[]{:S(2)}, u32[]{:S(2)}) %collective-permute-start.5) | collective-permute-done | bytes 180256 | tf_op jit(solution)/shard_map/ppermute | solution.py:248
  31.9 0.5 collective-permute-start.9
  32.4 0.0 collective-permute-done.2.direct_a
  32.4 0.1 collective-permute-start.8
  32.5 0.0 collective-permute-done.3.direct_b
  32.6 3.1 %collective-permute-start.7 = (bf16[2,176,512]{2,1,0:T(8,128)(2,1)S(1)}, bf16[2,176,512]{2,1,0:T(8,128)(2,1)}, u32[]{:S(2)}, u32[]{:S(2)}) collective-permute-start(bf16[2,176,512]{2,1,0:T(8,128)(2,1)S(1)} %pad_maximum_fusion.1.relay_0), channel_id=1, source_target_pairs={{0,96},{32,0},{64,32},{96,64},{1,97},{33,1},{65,33},{97,65},{2,98}... | collective-permute-start | bytes 1081352 | tf_op jit(solution)/shard_map/ppermute | solution.py:273
  35.6 0.0 collective-permute-done.partner_0.partner_1.partner_2.partner_3
  35.6 0.0 collective-permute-start.6
  35.6 1.3 fusion.1
  36.9 1.2 maximum_select_fusion.1
  38.1 0.0 all-to-all-done
  38.1 2.2 %constant_dynamic-slice_fusion = (bf16[4,1,256,256]{3,2,1,0:T(8,128)(2,1)}, bf16[4,256,256]{2,1,0:T(8,128)(2,1)}) fusion(bf16[4,2,256,256]{3,2,1,0:T(8,128)(2,1)} %all-to-all-done, s32[]{:T(128)S(6)} %select_n.85, s32[]{:T(128)S(6)} %select_n.75), kind=kLoop, calls=%fused_computation.19 | loop fusion | bytes 2097160 | tf_op jit(solution)/shard_map/jit(dynamic_index_in_dim)/dynamic_slice | solution.py:281
  40.4 1.7 copy-done.2
  42.1 3.7 %shard_map.68.partial = f32[512,512]{1,0:T(8,128)S(1)} custom-call(s32[2]{0:T(128)S(1)} %pad_add_fusion.info, bf16[256,4608]{1,0:T(8,128)(2,1)S(1)} %bitcast.20, bf16[256,4608]{1,0:T(8,128)(2,1)S(1)} %bitcast.21, bf16[256,4608]{1,0:T(8,128)(2,1)} %collective-permute-done.partner_0.partner_1.partner_2.partner_3, ...), custom_call_target="tpu_custom_call" | custom-call | flops 1207959552 | bytes 8388608 | tf_op jit(solution)/shard_map/pallas_call | solution.py:315
  45.8 0.0 collective-permute-done.9.up_partner
  45.8 5.1 %collective-permute-done.7.relay_2 = bf16[2,176,512]{2,1,0:T(8,128)(2,1)} collective-permute-done((bf16[2,176,512]{2,1,0:T(8,128)(2,1)S(1)}, bf16[2,176,512]{2,1,0:T(8,128)(2,1)}, u32[]{:S(2)}, u32[]{:S(2)}) %collective-permute-start.7) | collective-permute-done | bytes 360480 | tf_op jit(solution)/shard_map/ppermute | solution.py:273
  50.9 1.3 collective-permute-done.6.relay_1
  52.2 6.0 %shard_map.69 = (bf16[512,512]{1,0:T(8,128)(2,1)}, bf16[16,256,128]{2,1,0:T(8,128)(2,1)}) custom-call(s32[2]{0:T(128)S(1)} %pad_add_fusion.info, f32[512,512]{1,0:T(8,128)S(1)} %shard_map.68.partial, bf16[256,4608]{1,0:T(8,128)(2,1)S(1)} %bitcast.22, bf16[256,4608]{1,0:T(8,128)(2,1)S(1)} %bitcast.23, ...), custom_call_target="tpu_custom_call" | custom-call | flops 1207959552 | bytes 8388608 | tf_op jit(solution)/shard_map/pallas_call | solution.py:322
  58.2 7.5 %all-to-all-start.1 = ((bf16[16,256,128]{2,1,0:T(8,128)(2,1)}), bf16[16,256,128]{2,1,0:T(8,128)(2,1)S(1)}, u32[]{:S(2)}, u32[]{:S(2)}) async-start(bf16[16,256,128]{2,1,0:T(8,128)(2,1)} %get-tuple-element.28), calls=%async_computation.1 | async-start | bytes 2097152 | tf_op jit(solution)/shard_map/all_to_all | solution.py:347
  65.7 3.5 %collective-permute-start.11 = (bf16[4,256,256]{2,1,0:T(8,128)(2,1)S(1)}, bf16[4,256,256]{2,1,0:T(8,128)(2,1)S(1)}, u32[]{:S(2)}, u32[]{:S(2)}) collective-permute-start(bf16[4,256,256]{2,1,0:T(8,128)(2,1)S(1)} %copy-done.8), channel_id=1, source_target_pairs={{0,4},{4,0},{1,5},{5,1},{2,6},{6,2},{3,7},{7,3},{8,12},{12,8},{9,1... | collective-permute-start | bytes 1572872 | tf_op jit(solution)/shard_map/ppermute | solution.py:284
  69.2 23.6 %collective-permute-done.11 = bf16[4,256,256]{2,1,0:T(8,128)(2,1)S(1)} collective-permute-done((bf16[4,256,256]{2,1,0:T(8,128)(2,1)S(1)}, bf16[4,256,256]{2,1,0:T(8,128)(2,1)S(1)}, u32[]{:S(2)}, u32[]{:S(2)}) %collective-permute-start.11) | collective-permute-done | bytes 524320 | tf_op jit(solution)/shard_map/ppermute | solution.py:284
  92.8 0.1 pad_maximum_fusion
  92.9 0.0 all-to-all-done.1.pairs
  93.0 0.7 collective-permute-start.14
  93.7 0.2 reverse_select_fusion
  93.9 0.1 fusion.5
  94.0 4.3 %collective-permute-start.12 = (bf16[6,256,128]{2,1,0:T(8,128)(2,1)S(1)}, bf16[6,256,128]{2,1,0:T(8,128)(2,1)S(1)}, u32[]{:S(2)}, u32[]{:S(2)}) collective-permute-start(bf16[6,256,128]{2,1,0:T(8,128)(2,1)S(1)} %get-tuple-element.45), channel_id=1, source_target_pairs={{0,32},{32,64},{64,96},{1,33},{33,65},{65,97},{2,34},{34,66},{66,9... | collective-permute-start | bytes 1179656 | tf_op jit(solution)/shard_map/ppermute | solution.py:352
  98.2 5.4 %shard_map.70 = (f32[4096,128]{1,0:T(8,128)S(1)}, f32[4096,128]{1,0:T(8,128)S(1)}) custom-call(bf16[2048,256]{1,0:T(8,128)(2,1)S(1)} %bitcast.24, bf16[16,256,128]{2,1,0:T(8,128)(2,1)S(1)} %all-to-all-done.1.pairs), custom_call_target="tpu_custom_call" | custom-call | flops 2415919104 | bytes 4194304 | tf_op jit(solution)/shard_map/pallas_call | solution.py:213
  103.6 1.3 collective-permute-start.15
  104.9 12.7 %collective-permute-start.17 = (bf16[6,256,128]{2,1,0:T(8,128)(2,1)S(1)}, bf16[6,256,128]{2,1,0:T(8,128)(2,1)S(1)}, u32[]{:S(2)}, u32[]{:S(2)}) collective-permute-start(bf16[6,256,128]{2,1,0:T(8,128)(2,1)S(1)} %get-tuple-element.44), channel_id=1, source_target_pairs={{0,32},{32,64},{64,96},{1,33},{33,65},{65,97},{2,34},{34,66},{66,9... | collective-permute-start | bytes 1179656 | tf_op jit(solution)/shard_map/ppermute | solution.py:354
  117.7 1.9 %collective-permute-start.16 = (bf16[4,256,128]{2,1,0:T(8,128)(2,1)S(1)}, bf16[4,256,128]{2,1,0:T(8,128)(2,1)S(1)}, u32[]{:S(2)}, u32[]{:S(2)}) collective-permute-start(bf16[4,256,128]{2,1,0:T(8,128)(2,1)S(1)} %slice.26), channel_id=1, source_target_pairs={{0,32},{32,64},{64,96},{1,33},{33,65},{65,97},{2,34},{34,66},{66,9... | collective-permute-start | bytes 786440 | tf_op jit(solution)/shard_map/ppermute | solution.py:355
  119.6 0.0 collective-permute-done.12.pairs
  119.6 1.9 %collective-permute-start.13 = (bf16[6,256,128]{2,1,0:T(8,128)(2,1)S(1)}, bf16[6,256,128]{2,1,0:T(8,128)(2,1)S(1)}, u32[]{:S(2)}, u32[]{:S(2)}) collective-permute-start(bf16[6,256,128]{2,1,0:T(8,128)(2,1)S(1)} %collective-permute-done.12.pairs), channel_id=1, source_target_pairs={{32,64},{64,96},{33,65},{65,97},{34,66},{66,98},{35,67},{67,99},{3... | collective-permute-start | bytes 1179656 | tf_op jit(solution)/shard_map/ppermute | solution.py:356
  121.6 5.4 %shard_map.71 = (f32[4096,128]{1,0:T(8,128)S(1)}, f32[4096,128]{1,0:T(8,128)S(1)}) custom-call(s32[1]{0:T(128)} %bitcast.2.info, bf16[2048,256]{1,0:T(8,128)(2,1)S(1)} %bitcast.25, bf16[6,256,128]{2,1,0:T(8,128)(2,1)S(1)} %collective-permute-done.12.pairs, f32[4096,128]{1,0:T(8,128)S(1)} %get-tuple-element.32.numer_in, ...), custom_call_target="tpu_custom_call", output_to_operand_aliasing={{0}: (3, {}), {1}: (4, {})} | custom-call | flops 1610612736 | bytes 4194304 | tf_op jit(solution)/shard_map/pallas_call | solution.py:213
  126.9 0.2 collective-permute-done.17.pairs
  127.1 5.4 %shard_map.72 = (f32[4096,128]{1,0:T(8,128)S(1)}, f32[4096,128]{1,0:T(8,128)S(1)}) custom-call(s32[1]{0:T(128)} %bitcast.2.info, bf16[2048,256]{1,0:T(8,128)(2,1)S(1)} %bitcast.26, bf16[6,256,128]{2,1,0:T(8,128)(2,1)S(1)} %collective-permute-done.17.pairs, f32[4096,128]{1,0:T(8,128)S(1)} %get-tuple-element.34.numer_in, ...), custom_call_target="tpu_custom_call", output_to_operand_aliasing={{0}: (3, {}), {1}: (4, {})} | custom-call | flops 1610612736 | bytes 4194304 | tf_op jit(solution)/shard_map/pallas_call | solution.py:213
  132.5 0.3 collective-permute-done.16.pairs
  132.8 3.7 %shard_map.73 = (f32[4096,128]{1,0:T(8,128)S(1)}, f32[4096,128]{1,0:T(8,128)S(1)}) custom-call(s32[1]{0:T(128)} %bitcast.2.info, bf16[2048,256]{1,0:T(8,128)(2,1)S(1)} %bitcast.27, bf16[4,256,128]{2,1,0:T(8,128)(2,1)S(1)} %collective-permute-done.16.pairs, f32[4096,128]{1,0:T(8,128)S(1)} %get-tuple-element.36.numer_in, ...), custom_call_target="tpu_custom_call", output_to_operand_aliasing={{0}: (3, {}), {1}: (4, {})} | custom-call | flops 1073741824 | bytes 4194304 | tf_op jit(solution)/shard_map/pallas_call | solution.py:213
  136.4 5.8 %shard_map.74 = (f32[4096,128]{1,0:T(8,128)S(1)}, f32[4096,128]{1,0:T(8,128)S(1)}) custom-call(s32[1]{0:T(128)} %bitcast.2.info, bf16[2048,256]{1,0:T(8,128)(2,1)S(1)} %bitcast.28, bf16[10,256,128]{2,1,0:T(8,128)(2,1)S(1)} %collective-permute-done.15.pairs, ...), custom_call_target="tpu_custom_call", output_to_operand_aliasing={{0}: (3, {}), {1}: (4, {})} | custom-call | flops 2013265920 | bytes 4194304 | tf_op jit(solution)/shard_map/pallas_call | solution.py:213
  142.2 2.5 %shard_map.75 = bf16[2048,256]{1,0:T(8,128)(2,1)} custom-call(s32[1]{0:T(128)} %bitcast.2.info, bf16[2048,256]{1,0:T(8,128)(2,1)S(1)} %bitcast.29, bf16[6,256,128]{2,1,0:T(8,128)(2,1)S(1)} %collective-permute-done.13.pairs, f32[4096,128]{1,0:T(8,128)S(1)} %get-tuple-element.40.numer_in, f32[4096,128]{1,0:T(8,128)S(1)} %get-tuple-element.41.denom_in), custom_call_target="tpu_custom_call" | custom-call | flops 402653184 | bytes 4194304 | tf_op jit(solution)/shard_map/pallas_call | solution.py:213
  144.8 4.4 %all-to-all-start.2 = ((bf16[8,256,256]{2,1,0:T(8,128)(2,1)}), bf16[8,256,256]{2,1,0:T(8,128)(2,1)S(1)}, u32[]{:S(2)}, u32[]{:S(2)}) async-start(bf16[8,256,256]{2,1,0:T(8,128)(2,1)} %bitcast.12), calls=%async_computation.2 | async-start | bytes 2097152 | tf_op jit(solution)/shard_map/all_to_all | solution.py:377
  149.2 0.1 collective-permute-start.10
  149.9 0.9 collective-permute-done.10
  150.8 0.9 fusion
  151.7 13.0 %all-to-all-done.2 = bf16[8,256,256]{2,1,0:T(8,128)(2,1)S(1)} async-done(((bf16[8,256,256]{2,1,0:T(8,128)(2,1)}), bf16[8,256,256]{2,1,0:T(8,128)(2,1)S(1)}, u32[]{:S(2)}, u32[]{:S(2)}) %all-to-all-start.2) | async-done | bytes 1048608 | tf_op jit(solution)/shard_map/all_to_all | solution.py:377
  164.7 0.6 copy.16
  165.3 0.5 reshape.135
  165.9 1.1 broadcast_select_fusion
  (26 shorter events, 0.2 us)
Async XLA Ops:
  0.6 35.0 %collective-permute-start = (bf16[256,4608]{1,0:T(8,128)(2,1)}, bf16[256,4608]{1,0:T(8,128)(2,1)}, u32[]{:S(2)}, u32[]{:S(2)}) collective-permute-start(bf16[256,4608]{1,0:T(8,128)(2,1)} %bitcast.19), channel_id=1, source_target_pairs={{0,1},{1,0},{2,3},{3,2},{4,5},{5,4},{6,7},{7,6},{8,9},{9,8},{10,11... | collective-permute-start | bytes 7077896 | tf_op jit(solution)/shard_map/ppermute | solution.py:47
  0.7 39.7 %collective-permute-start.1 = (bf16[1152,1024]{1,0:T(8,128)(2,1)}, bf16[1152,1024]{1,0:T(8,128)(2,1)}, u32[]{:S(2)}, u32[]{:S(2)}) collective-permute-start(bf16[1152,1024]{1,0:T(8,128)(2,1)} %weight_b.1), channel_id=1, source_target_pairs={{0,1},{1,0},{2,3},{3,2},{4,5},{5,4},{6,7},{7,6},{8,9},{9,8},{10,11... | collective-permute-start | bytes 7077896 | tf_op jit(solution)/shard_map/ppermute | solution.py:47
  1.3 1.7 copy-start.1
  3.0 1.0 copy-start.3
  4.0 5.8 %copy-start.6 = (bf16[1,256,2048]{2,1,0:T(8,128)(2,1)S(1)}, bf16[1,256,2048]{2,1,0:T(8,128)(2,1)}, u32[]{:S(2)}) copy-start(bf16[1,256,2048]{2,1,0:T(8,128)(2,1)} %param.6) | copy-start | bytes 3145732
  5.8 26.6 %collective-permute-start.2 = (bf16[704,512]{1,0:T(8,128)(2,1)}, bf16[704,512]{1,0:T(8,128)(2,1)}, u32[]{:S(2)}, u32[]{:S(2)}) collective-permute-start(bf16[704,512]{1,0:T(8,128)(2,1)} %get-tuple-element.22), channel_id=1, source_target_pairs={{0,2},{1,7},{2,4},{3,1},{4,6},{5,3},{6,0},{7,5},{8,10},{9,15},{10,... | collective-permute-start | bytes 2162696 | tf_op jit(solution)/shard_map/ppermute | solution.py:270
  7.3 25.2 %collective-permute-start.3 = (bf16[704,512]{1,0:T(8,128)(2,1)}, bf16[704,512]{1,0:T(8,128)(2,1)}, u32[]{:S(2)}, u32[]{:S(2)}) collective-permute-start(bf16[704,512]{1,0:T(8,128)(2,1)} %get-tuple-element.23), channel_id=1, source_target_pairs={{0,3},{1,6},{2,5},{3,0},{4,7},{5,2},{6,1},{7,4},{8,11},{9,14},{10,... | collective-permute-start | bytes 2162696 | tf_op jit(solution)/shard_map/ppermute | solution.py:271
  8.3 18.6 %collective-permute-start.4 = (bf16[176,512]{1,0:T(8,128)(2,1)S(1)}, bf16[176,512]{1,0:T(8,128)(2,1)S(1)}, u32[]{:S(2)}, u32[]{:S(2)}) collective-permute-start(bf16[176,512]{1,0:T(8,128)(2,1)S(1)} %get-tuple-element.42), channel_id=1, source_target_pairs={{0,2},{1,7},{2,4},{3,1},{4,6},{5,3},{6,0},{7,5},{8,10},{9,15},{10,... | collective-permute-start | bytes 540680 | tf_op jit(solution)/shard_map/ppermute | solution.py:247
  10.6 21.2 %copy-start.4 = (bf16[2,128,1024]{2,1,0:T(8,128)(2,1)S(1)}, bf16[2,128,1024]{2,1,0:T(8,128)(2,1)}, u32[]{:S(2)}) copy-start(bf16[2,128,1024]{2,1,0:T(8,128)(2,1)} %up_own.1) | copy-start | bytes 1572868
  11.8 26.3 %all-to-all-start = ((bf16[4,2,256,256]{3,2,1,0:T(8,128)(2,1)}), bf16[4,2,256,256]{3,2,1,0:T(8,128)(2,1)}, u32[]{:S(2)}, u32[]{:S(2)}) async-start(bf16[4,2,256,256]{3,2,1,0:T(8,128)(2,1)} %bitcast.17), calls=%async_computation | async-start | bytes 2097152 | tf_op jit(solution)/shard_map/all_to_all | solution.py:279
  16.3 24.1 %copy-start = (bf16[1,256,4608]{2,1,0:T(8,128)(2,1)S(1)}, bf16[1,256,4608]{2,1,0:T(8,128)(2,1)}, u32[]{:S(2)}) copy-start(bf16[1,256,4608]{2,1,0:T(8,128)(2,1)} %param.5) | copy-start | bytes 7077892
  27.0 4.9 %collective-permute-start.5 = (bf16[176,512]{1,0:T(8,128)(2,1)S(1)}, bf16[176,512]{1,0:T(8,128)(2,1)S(1)}, u32[]{:S(2)}, u32[]{:S(2)}) collective-permute-start(bf16[176,512]{1,0:T(8,128)(2,1)S(1)} %get-tuple-element.43), channel_id=1, source_target_pairs={{0,3},{1,6},{2,5},{3,0},{4,7},{5,2},{6,1},{7,4},{8,11},{9,14},{10,... | collective-permute-start | bytes 540680 | tf_op jit(solution)/shard_map/ppermute | solution.py:248
  31.9 13.9 %collective-permute-start.9 = (bf16[2,128,1024]{2,1,0:T(8,128)(2,1)S(1)}, bf16[2,128,1024]{2,1,0:T(8,128)(2,1)}, u32[]{:S(2)}, u32[]{:S(2)}) collective-permute-start(bf16[2,128,1024]{2,1,0:T(8,128)(2,1)S(1)} %copy-done.4), channel_id=1, source_target_pairs={{0,1},{1,0},{2,3},{3,2},{4,5},{5,4},{6,7},{7,6},{8,9},{9,8},{10,11... | collective-permute-start | bytes 1572872 | tf_op jit(solution)/shard_map/ppermute | solution.py:47
  32.4 13.4 %collective-permute-start.8 = (bf16[2,176,512]{2,1,0:T(8,128)(2,1)S(1)}, bf16[2,176,512]{2,1,0:T(8,128)(2,1)}, u32[]{:S(2)}, u32[]{:S(2)}) collective-permute-start(bf16[2,176,512]{2,1,0:T(8,128)(2,1)S(1)} %pad_maximum_fusion.1.relay_0), channel_id=1, source_target_pairs={{0,64},{32,96},{64,0},{96,32},{1,65},{33,97},{65,1},{97,33},{2,66}... | collective-permute-start | bytes 1081352 | tf_op jit(solution)/shard_map/ppermute | solution.py:273
  32.6 18.3 %collective-permute-start.7 = (bf16[2,176,512]{2,1,0:T(8,128)(2,1)S(1)}, bf16[2,176,512]{2,1,0:T(8,128)(2,1)}, u32[]{:S(2)}, u32[]{:S(2)}) collective-permute-start(bf16[2,176,512]{2,1,0:T(8,128)(2,1)S(1)} %pad_maximum_fusion.1.relay_0), channel_id=1, source_target_pairs={{0,96},{32,0},{64,32},{96,64},{1,97},{33,1},{65,33},{97,65},{2,98}... | collective-permute-start | bytes 1081352 | tf_op jit(solution)/shard_map/ppermute | solution.py:273
  35.6 16.6 %collective-permute-start.6 = (bf16[2,176,512]{2,1,0:T(8,128)(2,1)S(1)}, bf16[2,176,512]{2,1,0:T(8,128)(2,1)}, u32[]{:S(2)}, u32[]{:S(2)}) collective-permute-start(bf16[2,176,512]{2,1,0:T(8,128)(2,1)S(1)} %pad_maximum_fusion.1.relay_0), channel_id=1, source_target_pairs={{0,32},{32,64},{64,96},{96,0},{1,33},{33,65},{65,97},{97,1},{2,34}... | collective-permute-start | bytes 1081352 | tf_op jit(solution)/shard_map/ppermute | solution.py:273
  40.4 1.7 copy-start.2
  58.2 7.5 %copy-start.8 = (bf16[4,256,256]{2,1,0:T(8,128)(2,1)S(1)}, bf16[4,256,256]{2,1,0:T(8,128)(2,1)}, u32[]{:S(2)}) copy-start(bf16[4,256,256]{2,1,0:T(8,128)(2,1)} %get-tuple-element.27) | copy-start | bytes 1572868
  58.2 34.6 %copy-start.5 = (bf16[4,1,256,256]{3,2,1,0:T(8,128)(2,1)S(1)}, bf16[4,1,256,256]{3,2,1,0:T(8,128)(2,1)}, u32[]{:S(2)}) copy-start(bf16[4,1,256,256]{3,2,1,0:T(8,128)(2,1)} %get-tuple-element.46) | copy-start | bytes 1572868
  58.2 34.7 %all-to-all-start.1 = ((bf16[16,256,128]{2,1,0:T(8,128)(2,1)}), bf16[16,256,128]{2,1,0:T(8,128)(2,1)S(1)}, u32[]{:S(2)}, u32[]{:S(2)}) async-start(bf16[16,256,128]{2,1,0:T(8,128)(2,1)} %get-tuple-element.28), calls=%async_computation.1 | async-start | bytes 2097152 | tf_op jit(solution)/shard_map/all_to_all | solution.py:347
  65.7 27.1 %collective-permute-start.11 = (bf16[4,256,256]{2,1,0:T(8,128)(2,1)S(1)}, bf16[4,256,256]{2,1,0:T(8,128)(2,1)S(1)}, u32[]{:S(2)}, u32[]{:S(2)}) collective-permute-start(bf16[4,256,256]{2,1,0:T(8,128)(2,1)S(1)} %copy-done.8), channel_id=1, source_target_pairs={{0,4},{4,0},{1,5},{5,1},{2,6},{6,2},{3,7},{7,3},{8,12},{12,8},{9,1... | collective-permute-start | bytes 1572872 | tf_op jit(solution)/shard_map/ppermute | solution.py:284
  93.0 10.6 %collective-permute-start.14 = (bf16[10,256,128]{2,1,0:T(8,128)(2,1)S(1)}, bf16[10,256,128]{2,1,0:T(8,128)(2,1)S(1)}, u32[]{:S(2)}, u32[]{:S(2)}) collective-permute-start(bf16[10,256,128]{2,1,0:T(8,128)(2,1)S(1)} %slice.25), channel_id=1, source_target_pairs={{32,0},{0,96},{33,1},{1,97},{34,2},{2,98},{35,3},{3,99},{36,4},{4,... | collective-permute-start | bytes 1966088 | tf_op jit(solution)/shard_map/ppermute | solution.py:353
  94.0 25.7 %collective-permute-start.12 = (bf16[6,256,128]{2,1,0:T(8,128)(2,1)S(1)}, bf16[6,256,128]{2,1,0:T(8,128)(2,1)S(1)}, u32[]{:S(2)}, u32[]{:S(2)}) collective-permute-start(bf16[6,256,128]{2,1,0:T(8,128)(2,1)S(1)} %get-tuple-element.45), channel_id=1, source_target_pairs={{0,32},{32,64},{64,96},{1,33},{33,65},{65,97},{2,34},{34,66},{66,9... | collective-permute-start | bytes 1179656 | tf_op jit(solution)/shard_map/ppermute | solution.py:352
  103.6 32.8 %collective-permute-start.15 = (bf16[10,256,128]{2,1,0:T(8,128)(2,1)S(1)}, bf16[10,256,128]{2,1,0:T(8,128)(2,1)S(1)}, u32[]{:S(2)}, u32[]{:S(2)}) collective-permute-start(bf16[10,256,128]{2,1,0:T(8,128)(2,1)S(1)} %collective-permute-done.14), channel_id=1, source_target_pairs={{0,96},{96,64},{1,97},{97,65},{2,98},{98,66},{3,99},{99,67},{4,100... | collective-permute-start | bytes 1966088 | tf_op jit(solution)/shard_map/ppermute | solution.py:361
  104.9 22.2 %collective-permute-start.17 = (bf16[6,256,128]{2,1,0:T(8,128)(2,1)S(1)}, bf16[6,256,128]{2,1,0:T(8,128)(2,1)S(1)}, u32[]{:S(2)}, u32[]{:S(2)}) collective-permute-start(bf16[6,256,128]{2,1,0:T(8,128)(2,1)S(1)} %get-tuple-element.44), channel_id=1, source_target_pairs={{0,32},{32,64},{64,96},{1,33},{33,65},{65,97},{2,34},{34,66},{66,9... | collective-permute-start | bytes 1179656 | tf_op jit(solution)/shard_map/ppermute | solution.py:354
  117.7 15.1 %collective-permute-start.16 = (bf16[4,256,128]{2,1,0:T(8,128)(2,1)S(1)}, bf16[4,256,128]{2,1,0:T(8,128)(2,1)S(1)}, u32[]{:S(2)}, u32[]{:S(2)}) collective-permute-start(bf16[4,256,128]{2,1,0:T(8,128)(2,1)S(1)} %slice.26), channel_id=1, source_target_pairs={{0,32},{32,64},{64,96},{1,33},{33,65},{65,97},{2,34},{34,66},{66,9... | collective-permute-start | bytes 786440 | tf_op jit(solution)/shard_map/ppermute | solution.py:355
  119.6 22.6 %collective-permute-start.13 = (bf16[6,256,128]{2,1,0:T(8,128)(2,1)S(1)}, bf16[6,256,128]{2,1,0:T(8,128)(2,1)S(1)}, u32[]{:S(2)}, u32[]{:S(2)}) collective-permute-start(bf16[6,256,128]{2,1,0:T(8,128)(2,1)S(1)} %collective-permute-done.12.pairs), channel_id=1, source_target_pairs={{32,64},{64,96},{33,65},{65,97},{34,66},{66,98},{35,67},{67,99},{3... | collective-permute-start | bytes 1179656 | tf_op jit(solution)/shard_map/ppermute | solution.py:356
  144.8 4.4 %copy-start.7 = (bf16[512,512]{1,0:T(8,128)(2,1)S(1)}, bf16[512,512]{1,0:T(8,128)(2,1)}, u32[]{:S(2)}) copy-start(bf16[512,512]{1,0:T(8,128)(2,1)} %get-tuple-element.26) | copy-start | bytes 1572868
  144.8 20.0 %all-to-all-start.2 = ((bf16[8,256,256]{2,1,0:T(8,128)(2,1)}), bf16[8,256,256]{2,1,0:T(8,128)(2,1)S(1)}, u32[]{:S(2)}, u32[]{:S(2)}) async-start(bf16[8,256,256]{2,1,0:T(8,128)(2,1)} %bitcast.12), calls=%async_computation.2 | async-start | bytes 2097152 | tf_op jit(solution)/shard_map/all_to_all | solution.py:377
  149.2 1.6 collective-permute-start.10

commit v3 on v2

--- a/solution.py
+++ b/solution.py
@@ -15,8 +15,8 @@
 BLOCK = 256
 CHUNK = 2048
 BLOCKS = CHUNK // BLOCK
-LOW, MIDDLE = 3, 6
-RELAYED = 704
+LOW, MIDDLE = 4, 6
+RELAYED = 576
 SIZES = {"z": 4, "y": 4, "xh": 2, "xl": 2, "core": 2}
 SEQ_AXES = ("z", "y", "xh")
 DP_AXES = ("xl", "core")
@@ -118,8 +118,9 @@
     return col <= row if newer else col > row
 
 
-def stacked_rows(queries, i):
-    own = queries[pl.ds(pl.multiple_of(i * BLOCK, BLOCK), BLOCK), :]
+def stacked_rows(info, queries, pair, parity):
+    kept, crossed = queries
+    own = jnp.where(info[1] == parity, kept[pair], crossed[pair])
     return jnp.concatenate([own[:, :HEAD], own[:, HEAD:]], axis=0)
 
 
@@ -143,16 +144,16 @@
     return pl.ds(pl.multiple_of(i * 2 * BLOCK, 2 * BLOCK), 2 * BLOCK)
 
 
-def own_kernel(queries, pairs, numer, denom):
+def own_kernel(info, kept, crossed, pairs, numer, denom):
     mask = triangle(True)
     for i in range(BLOCKS):
         blocks = [(j, None) for j in range(i)] + [(i, mask)]
         numer[state_rows(i), :], denom[state_rows(i), :] = over_blocks(
-            stacked_rows(queries, i), pairs, blocks
+            stacked_rows(info, (kept, crossed), i // 2, i % 2), pairs, blocks
         )
 
 
-def near_kernel(group, info, queries, pairs, numer_in, denom_in, numer, denom):
+def near_kernel(group, info, kept, crossed, pairs, numer_in, denom_in, numer, denom):
     blocks = [(j, None) for j in range(pairs.shape[0] // 2)]
 
     @pl.when(info[0] >= 1)
@@ -160,7 +161,10 @@
         def step(t, carry):
             for u in range(group):
                 i = t * group + u
-                n, d = over_blocks(stacked_rows(queries, i), pairs, blocks)
+                stacked = stacked_rows(
+                    info, (kept, crossed), t * (group // 2) + u // 2, u % 2
+                )
+                n, d = over_blocks(stacked, pairs, blocks)
                 numer[state_rows(i), :] += n
                 denom[state_rows(i), :] += d
             return carry
@@ -168,7 +172,7 @@
         lax.fori_loop(0, BLOCKS // group, step, 0)
 
 
-def far_kernel(first, last, info, queries, pairs, numer_in, denom_in, *outs):
+def far_kernel(first, last, info, kept, crossed, pairs, numer_in, denom_in, *outs):
     end = first + pairs.shape[0] // 2
     mask = triangle(False)
     numer, denom = (numer_in, denom_in) if last else outs
@@ -188,7 +192,8 @@
             blocks = [(j - first, mask if j == i else None) for j in range(max(i, first), end)]
             old_n, old_d = numer[state_rows(i), :], denom[state_rows(i), :]
             if blocks:
-                n, d = over_blocks(stacked_rows(queries, i), pairs, blocks)
+                stacked = stacked_rows(info, (kept, crossed), i // 2, i % 2)
+                n, d = over_blocks(stacked, pairs, blocks)
                 finish(i, old_n + n, old_d + d)
             elif last:
                 finish(i, old_n, old_d)
@@ -209,13 +214,13 @@
 
 def attention_call(kernel, count, args, result=False, resume=True):
     single = BLOCK * 2 * BLOCK
-    inputs = [IN_SMEM] + [IN_VMEM] * 4 if resume else [IN_VMEM] * 2
+    inputs = [IN_SMEM] + [IN_VMEM] * (5 if resume else 3)
     return pl.pallas_call(
         kernel,
         out_shape=RESULT if result else (STATE, STATE),
         in_specs=inputs,
         out_specs=IN_VMEM if result else (IN_VMEM, IN_VMEM),
-        input_output_aliases={3: 0, 4: 1} if resume and not result else {},
+        input_output_aliases={4: 0, 5: 1} if resume and not result else {},
         compiler_params=pltpu.CompilerParams(vmem_limit_bytes=12 * 2**20),
         cost_estimate=pl.CostEstimate(
             flops=count * single * 4 * HEAD, bytes_accessed=2**22, transcendentals=2 * count * single
@@ -275,13 +280,13 @@
     partner_weight = to_partner(down_weight)
     partner_upper = to_partner(up_weight)
 
-    sent = queries[0].reshape(rows, 4, 2, PAIR).transpose(1, 2, 0, 3)
+    here = lax.axis_index("xh")
+    split_queries = queries[0].reshape(rows, 4, 2, PAIR)
+    kept_part = lax.dynamic_index_in_dim(split_queries, here, 2, keepdims=False)
+    other_part = lax.dynamic_index_in_dim(split_queries, 1 - here, 2, keepdims=False)
+    sent = jnp.stack([kept_part, other_part]).transpose(2, 0, 1, 3)
     sent = lax.all_to_all(sent, "y", 0, 0, tiled=True)
-    here = lax.axis_index("xh")
-    kept_queries = lax.dynamic_index_in_dim(sent, here, 1, keepdims=False)
-    leaving = lax.dynamic_index_in_dim(sent, 1 - here, 1, keepdims=False)
-    leaving, direct_a, direct_b = lax.optimization_barrier((leaving, direct_a, direct_b))
-    crossing_queries = lax.ppermute(leaving, "xh", [(0, 1), (1, 0)])
+    kept, leaving = sent[:, 0], sent[:, 1]
 
     half = HEAD // 2
     places = (start + jnp.arange(rows, dtype=jnp.int32)).astype(jnp.float32)
@@ -314,7 +319,7 @@
 
     partial = projection(
         half_product_kernel,
-        out_shape=jax.ShapeDtypeStruct((2 * rows, rank), jnp.float32),
+        out_shape=pltpu.HBM((2 * rows, rank), jnp.float32),
         in_specs=[hidden_part(0), hidden_part(1)] * 2 + [half_weight] * 2,
         out_specs=whole((2 * rows, rank)),
     )(info, hidden, hidden, partner_hidden, partner_hidden, down_weight, partner_weight)
@@ -341,9 +346,8 @@
         relay_own, *relays, up_weight, partner_upper, cosine, sine,
     )
 
-    mixed = jnp.stack([kept_queries, crossing_queries], axis=1)
-    ordered = jnp.where(lax.axis_index("xh") == 0, mixed, mixed[:, ::-1])
-    my_queries = ordered.reshape(CHUNK, PAIR)
+    leaving, pairs = lax.optimization_barrier((leaving, pairs))
+    crossed_queries = lax.ppermute(leaving, "xh", [(0, 1), (1, 0)])
     own_pairs = lax.all_to_all(pairs, PLANE + ("core",), 0, 0, tiled=True)
     other_half = to_partner(latent[rows:])
 
@@ -355,23 +359,23 @@
     near_high = lax.ppermute(own_pairs[middle:], "z", up)
     far_low = lax.ppermute(near_low, "z", [(1, 2), (2, 3)])
 
-    spot = plane.reshape(1).astype(jnp.int32)
-    state = attention_call(own_kernel, 36, (my_queries, own_pairs), resume=False)
+    common = (jnp.stack([plane, here]).astype(jnp.int32), kept, crossed_queries)
+    state = attention_call(own_kernel, 36, (*common, own_pairs), resume=False)
     passing, state = lax.optimization_barrier((passing, state))
     far_high = lax.ppermute(passing, "z", [(0, 3), (3, 2)])
     for piece_pairs in (near_low, near_middle, near_high):
         state = attention_call(
             functools.partial(near_kernel, 4),
             piece_pairs.shape[0] // 2 * BLOCKS,
-            (spot, my_queries, piece_pairs, *state),
+            (*common, piece_pairs, *state),
         )
     state = attention_call(
-        functools.partial(far_kernel, LOW, False), 30,
-        (spot, my_queries, far_high, *state),
+        functools.partial(far_kernel, LOW, False), 26,
+        (*common, far_high, *state),
     )
     result = attention_call(
-        functools.partial(far_kernel, 0, True), 6,
-        (spot, my_queries, far_low, *state), result=True,
+        functools.partial(far_kernel, 0, True), 10,
+        (*common, far_low, *state), result=True,
     )
 
     home = lax.all_to_all(result.reshape(groups, rows, PAIR), PLANE, 0, 0, tiled=True)

time: 168 us -> 149 us (0.89)
  the two profiles are of different devices: /device:TPU:66 before, /device:TPU:64 now
where the time goes in v3:
time: 149 us; the launch traced here: 148 us
  starting transfers between devices  44.6 us (30%)
  Pallas kernels  44.1 us (30%)
  waiting for transfers between devices  37.3 us (25%)
  local copies, waits for them, and re-layouts  12.3 us (8%)
  other arithmetic  8.08 us (5%)
  between operations  1.6 us (1%)
    pallas_call x6, Pallas kernels, attention_call(): pl.pallas_call(kernel, out_shape=RESULT if result else (STATE, STATE), in...  31.4 us
    all_to_all x1, waiting for transfers between devices, body(): own_pairs = lax.all_to_all(pairs, PLANE + ('core',), 0, 0, tiled=True)  15 us
    all_to_all x1, waiting for transfers between devices, body(): lax.all_to_all(result.reshape(groups, rows, PAIR), PLANE, 0, 0, tiled=True)  13.4 us
    ppermute x1, starting transfers between devices, body(): near_middle = lax.ppermute(own_pairs[low:middle], 'z', up)  6.88 us
    all_to_all x1, starting transfers between devices, body(): own_pairs = lax.all_to_all(pairs, PLANE + ('core',), 0, 0, tiled=True)  6.44 us
    pallas_call x1, Pallas kernels, body(): projection(project_kernel, out_shape=(pltpu.HBM((2 * rows, rank), jnp.bfl...  6.05 us
    ppermute x3, waiting for transfers between devices, body(): relays = [lax.ppermute(relay_own, 'z', ring(k)) for k in (1, -1, 2)]  5.79 us
    ppermute x1, starting transfers between devices, body(): near_low = lax.ppermute(own_pairs[:low], 'z', up)  5.51 us
  transfers between devices with their start and end apart: 21, of which 5 were waited for; matrix products, arithmetic and copies ran while one was open for 10% of the time, Pallas kernels for 23%

profile of v3, /device:TPU:64, one launch (start us, length us, event | category | flops | bytes accessed | tf_op | source)
XLA Modules:
  0.0 148.0 jit_solution(17612989215263853488)
XLA Ops:
  0.6 0.1 collective-permute-start
  0.7 0.5 collective-permute-start.1
  1.2 1.7 %fusion.4 = (bf16[144,512]{1,0:T(8,128)(2,1)}, bf16[144,512]{1,0:T(8,128)(2,1)}) fusion(bf16[1152,1024]{1,0:T(8,128)(2,1)} %weight_b.1, s32[]{:T(128)S(6)} %select_n.67, s32[]{:T(128)S(6)} %select_n.68, s32[]{:T(128)S(6)} %select_n.69), kind=kLoop, calls=%fused_computation.23 | loop fusion | bytes 589836 | tf_op jit(solution)/shard_map/dynamic_slice | solution.py:249
  2.9 1.5 %collective-permute-start.4 = (bf16[144,512]{1,0:T(8,128)(2,1)}, bf16[144,512]{1,0:T(8,128)(2,1)}, u32[]{:S(2)}, u32[]{:S(2)}) collective-permute-start(bf16[144,512]{1,0:T(8,128)(2,1)} %get-tuple-element.40), channel_id=1, source_target_pairs={{0,2},{1,7},{2,4},{3,1},{4,6},{5,3},{6,0},{7,5},{8,10},{9,15},{10,... | collective-permute-start | bytes 442376 | tf_op jit(solution)/shard_map/ppermute | solution.py:252
  4.4 0.0 collective-permute-start.5
  4.4 1.8 %reshape_squeeze.3 = bf16[256,4,2,256]{3,2,1,0:T(2,128)(2,1)S(1)} reshape(bf16[1,256,2048]{2,1,0:T(8,128)(2,1)} %param.6) | data formatting | bytes 2097152 | tf_op jit(solution)/shard_map/reshape;squeeze | solution.py:284
  6.3 2.2 %constant_dynamic-slice_fusion.1 = (bf16[256,4,1,256]{3,2,1,0:T(2,128)(2,1)S(1)}, bf16[256,4,1,256]{3,2,1,0:T(2,128)(2,1)S(1)}) fusion(bf16[256,4,2,256]{3,2,1,0:T(2,128)(2,1)S(1)} %reshape_squeeze.3, s32[]{:T(128)S(6)} %select_n.75, s32[]{:T(128)S(6)} %select_n.76), kind=kLoop, calls=%fused_computation.22 | loop fusion | bytes 2097160 | tf_op jit(solution)/shard_map/jit(dynamic_index_in_dim)/dynamic_slice | solution.py:285
  8.4 0.3 copy_bitcast_fusion
  8.8 0.0 copy-start.1
  8.8 0.0 copy-start.3
  8.8 1.1 maximum_bitcast_fusion
  9.9 4.6 %all-to-all-start = ((bf16[4,2,256,256]{3,2,1,0:T(8,128)(2,1)}), bf16[4,2,256,256]{3,2,1,0:T(8,128)(2,1)}, u32[]{:S(2)}, u32[]{:S(2)}) async-start(bf16[4,2,256,256]{3,2,1,0:T(8,128)(2,1)} %maximum_bitcast_fusion), calls=%async_computation | async-start | bytes 2097152 | tf_op jit(solution)/shard_map/all_to_all | solution.py:288
  14.5 1.7 %pad_maximum_fusion.relay_0 = bf16[2,144,512]{2,1,0:T(8,128)(2,1)} fusion(bf16[1,144,512]{2,1,0:T(8,128)(2,1)} %bitcast.5, bf16[1,144,512]{2,1,0:T(8,128)(2,1)} %bitcast.4), kind=kLoop, calls=%fused_computation.8 | loop fusion | flops 147456 | bytes 589824 | tf_op jit(solution)/shard_map/stack | solution.py:277
  16.2 0.1 pad_add_fusion.info
  16.3 1.9 %pack.1 = (bf16[832,512]{1,0:T(8,128)(2,1)}, bf16[832,512]{1,0:T(8,128)(2,1)}) custom-call(s32[2]{0:T(128)S(1)} %pad_add_fusion.info, bf16[1152,1024]{1,0:T(8,128)(2,1)S(1)} %copy-done.1, bf16[2,128,1024]{2,1,0:T(8,128)(2,1)S(1)} %copy-done.3, bf16[1152,1024]{1,0:T(8,128)(2,1)S(1)} %copy-done.1, bf16[2,128,1024]{2,1,0:T(8,128)(2,1)S(1)} %copy-done.3), custom_call_target="tpu_custom_call" | custom-call | flops 1000000 | bytes 4194304 | tf_op jit(solution)/shard_map/pack/pallas_call | solution.py:262
  18.2 1.5 %collective-permute-start.2 = (bf16[832,512]{1,0:T(8,128)(2,1)}, bf16[832,512]{1,0:T(8,128)(2,1)}, u32[]{:S(2)}, u32[]{:S(2)}) collective-permute-start(bf16[832,512]{1,0:T(8,128)(2,1)} %get-tuple-element.21), channel_id=1, source_target_pairs={{0,2},{1,7},{2,4},{3,1},{4,6},{5,3},{6,0},{7,5},{8,10},{9,15},{10,... | collective-permute-start | bytes 2555912 | tf_op jit(solution)/shard_map/ppermute | solution.py:275
  19.7 1.6 %collective-permute-start.3 = (bf16[832,512]{1,0:T(8,128)(2,1)}, bf16[832,512]{1,0:T(8,128)(2,1)}, u32[]{:S(2)}, u32[]{:S(2)}) collective-permute-start(bf16[832,512]{1,0:T(8,128)(2,1)} %get-tuple-element.22), channel_id=1, source_target_pairs={{0,3},{1,6},{2,5},{3,0},{4,7},{5,2},{6,1},{7,4},{8,11},{9,14},{10,... | collective-permute-start | bytes 2555912 | tf_op jit(solution)/shard_map/ppermute | solution.py:276
  21.3 5.8 %collective-permute-done.8.relay_3 = bf16[2,144,512]{2,1,0:T(8,128)(2,1)S(1)} collective-permute-done((bf16[2,144,512]{2,1,0:T(8,128)(2,1)}, bf16[2,144,512]{2,1,0:T(8,128)(2,1)S(1)}, u32[]{:S(2)}, u32[]{:S(2)}) %collective-permute-start.8) | collective-permute-done | bytes 294944 | tf_op jit(solution)/shard_map/ppermute | solution.py:278
  27.1 0.9 collective-permute-start.9
  28.0 1.3 fusion.1
  29.3 1.8 %maximum_select_fusion.1 = (f32[256,128]{1,0:T(8,128)S(1)}, f32[256,128]{1,0:T(8,128)}) fusion(f32[256,64]{1,0:T(8,128)} %get-tuple-element.54, pred[]{:T(512)S(6)} %eq.2, f32[256,64]{1,0:T(8,128)} %get-tuple-element.53, f32[256,64]{1,0:T(8,128)S(1)} %get-tuple-element.52), kind=kLoop, calls=%fused_computation.12 | loop fusion | flops 131072 | bytes 458753 | tf_op jit(solution)/shard_map/jit(_where)/select_n | solution.py:296
  31.1 0.1 collective-permute-start.7
  31.2 1.9 %collective-permute-start.6 = (bf16[2,144,512]{2,1,0:T(8,128)(2,1)}, bf16[2,144,512]{2,1,0:T(8,128)(2,1)}, u32[]{:S(2)}, u32[]{:S(2)}) collective-permute-start(bf16[2,144,512]{2,1,0:T(8,128)(2,1)} %pad_maximum_fusion.relay_0), channel_id=1, source_target_pairs={{0,32},{32,64},{64,96},{96,0},{1,33},{33,65},{65,97},{97,1},{2,34}... | collective-permute-start | bytes 884744 | tf_op jit(solution)/shard_map/ppermute | solution.py:278
  33.1 2.1 %slice_bitcast_fusion = (bf16[4,256,256]{2,1,0:T(8,128)(2,1)}, bf16[4,256,256]{2,1,0:T(8,128)(2,1)S(1)}) fusion(bf16[4,2,256,256]{3,2,1,0:T(8,128)(2,1)} %all-to-all-done), kind=kLoop, calls=%fused_computation.2 | loop fusion | bytes 2097152 | tf_op jit(solution)/shard_map/squeeze | solution.py:289
  35.2 1.7 %copy-done.2 = bf16[1152,1024]{1,0:T(8,128)(2,1)S(1)} copy-done((bf16[1152,1024]{1,0:T(8,128)(2,1)S(1)}, bf16[1152,1024]{1,0:T(8,128)(2,1)}, u32[]{:S(2)}) %copy-start.2) | copy-done | bytes 2359320
  36.9 4.7 %shard_map.68.partial = f32[512,512]{1,0:T(8,128)} custom-call(s32[2]{0:T(128)S(1)} %pad_add_fusion.info, bf16[256,4608]{1,0:T(8,128)(2,1)S(1)} %bitcast.28, bf16[256,4608]{1,0:T(8,128)(2,1)S(1)} %bitcast.29, bf16[256,4608]{1,0:T(8,128)(2,1)} %collective-permute-done.partner_0.partner_1.partner_2.partner_3, ...), custom_call_target="tpu_custom_call" | custom-call | flops 1207959552 | bytes 8388608 | tf_op jit(solution)/shard_map/pallas_call | solution.py:320
  41.6 0.0 collective-permute-done.7.relay_2
  41.6 0.0 collective-permute-done.6.relay_1
  41.6 0.0 collective-permute-done.9.up_partner
  41.6 0.0 collective-permute-done.2.direct_a
  41.6 0.0 copy-start.4
  41.7 1.2 copy-done.4
  42.9 6.0 %shard_map.69 = (bf16[512,512]{1,0:T(8,128)(2,1)}, bf16[16,256,128]{2,1,0:T(8,128)(2,1)}) custom-call(s32[2]{0:T(128)S(1)} %pad_add_fusion.info, f32[512,512]{1,0:T(8,128)S(1)} %copy-done.4, bf16[256,4608]{1,0:T(8,128)(2,1)S(1)} %bitcast.30, bf16[256,4608]{1,0:T(8,128)(2,1)S(1)} %bitcast.31, ...), custom_call_target="tpu_custom_call" | custom-call | flops 1207959552 | bytes 8388608 | tf_op jit(solution)/shard_map/pallas_call | solution.py:327
  48.9 6.4 %all-to-all-start.1 = ((bf16[16,256,128]{2,1,0:T(8,128)(2,1)}), bf16[16,256,128]{2,1,0:T(8,128)(2,1)S(1)}, u32[]{:S(2)}, u32[]{:S(2)}) async-start(bf16[16,256,128]{2,1,0:T(8,128)(2,1)} %get-tuple-element.26), calls=%async_computation.1 | async-start | bytes 2097152 | tf_op jit(solution)/shard_map/all_to_all | solution.py:351
  55.4 3.5 %collective-permute-start.11 = (bf16[4,256,256]{2,1,0:T(8,128)(2,1)S(1)}, bf16[4,256,256]{2,1,0:T(8,128)(2,1)S(1)}, u32[]{:S(2)}, u32[]{:S(2)}) collective-permute-start(bf16[4,256,256]{2,1,0:T(8,128)(2,1)S(1)} %copy-done.9), channel_id=1, source_target_pairs={{0,4},{4,0},{1,5},{5,1},{2,6},{6,2},{3,7},{7,3},{8,12},{12,8},{9,1... | collective-permute-start | bytes 1572872 | tf_op jit(solution)/shard_map/ppermute | solution.py:350
  58.9 15.0 %all-to-all-done.1.pairs = bf16[16,256,128]{2,1,0:T(8,128)(2,1)S(1)} async-done(((bf16[16,256,128]{2,1,0:T(8,128)(2,1)}), bf16[16,256,128]{2,1,0:T(8,128)(2,1)S(1)}, u32[]{:S(2)}, u32[]{:S(2)}) %all-to-all-start.1) | async-done | bytes 1048608 | tf_op jit(solution)/shard_map/all_to_all | solution.py:351
  73.9 0.1 fusion.6
  74.0 0.7 collective-permute-start.14
  74.7 0.1 pad_add_fusion.1.info
  74.8 5.5 %collective-permute-start.12 = (bf16[8,256,128]{2,1,0:T(8,128)(2,1)S(1)}, bf16[8,256,128]{2,1,0:T(8,128)(2,1)S(1)}, u32[]{:S(2)}, u32[]{:S(2)}) collective-permute-start(bf16[8,256,128]{2,1,0:T(8,128)(2,1)S(1)} %get-tuple-element.45), channel_id=1, source_target_pairs={{0,32},{32,64},{64,96},{1,33},{33,65},{65,97},{2,34},{34,66},{66,9... | collective-permute-start | bytes 1572872 | tf_op jit(solution)/shard_map/ppermute | solution.py:356
  80.3 2.1 %collective-permute-done.11.crossed = bf16[4,256,256]{2,1,0:T(8,128)(2,1)S(1)} collective-permute-done((bf16[4,256,256]{2,1,0:T(8,128)(2,1)S(1)}, bf16[4,256,256]{2,1,0:T(8,128)(2,1)S(1)}, u32[]{:S(2)}, u32[]{:S(2)}) %collective-permute-start.11) | collective-permute-done | bytes 524320 | tf_op jit(solution)/shard_map/ppermute | solution.py:350
  82.4 5.9 %shard_map.70 = (f32[4096,128]{1,0:T(8,128)S(1)}, f32[4096,128]{1,0:T(8,128)S(1)}) custom-call(s32[2]{0:T(128)S(1)} %pad_add_fusion.1.info, bf16[4,256,256]{2,1,0:T(8,128)(2,1)S(1)} %get-tuple-element.47.kept, bf16[4,256,256]{2,1,0:T(8,128)(2,1)S(1)} %collective-permute-done.11.crossed, bf16[16,256,128]{2,1,0:T(8,128)(2,1)S(1)} %all-to-all-done.1.pairs), custom_call_target="tpu_custom_call" | custom-call | flops 2415919104 | bytes 4194304 | tf_op jit(solution)/shard_map/pallas_call | solution.py:218
  88.3 0.0 collective-permute-done.14
  88.4 1.3 collective-permute-start.15
  89.7 6.9 %collective-permute-start.17 = (bf16[4,256,128]{2,1,0:T(8,128)(2,1)S(1)}, bf16[4,256,128]{2,1,0:T(8,128)(2,1)S(1)}, u32[]{:S(2)}, u32[]{:S(2)}) collective-permute-start(bf16[4,256,128]{2,1,0:T(8,128)(2,1)S(1)} %get-tuple-element.42), channel_id=1, source_target_pairs={{0,32},{32,64},{64,96},{1,33},{33,65},{65,97},{2,34},{34,66},{66,9... | collective-permute-start | bytes 786440 | tf_op jit(solution)/shard_map/ppermute | solution.py:358
  96.6 1.9 %collective-permute-start.16 = (bf16[4,256,128]{2,1,0:T(8,128)(2,1)S(1)}, bf16[4,256,128]{2,1,0:T(8,128)(2,1)S(1)}, u32[]{:S(2)}, u32[]{:S(2)}) collective-permute-start(bf16[4,256,128]{2,1,0:T(8,128)(2,1)S(1)} %get-tuple-element.43), channel_id=1, source_target_pairs={{0,32},{32,64},{64,96},{1,33},{33,65},{65,97},{2,34},{34,66},{66,9... | collective-permute-start | bytes 786440 | tf_op jit(solution)/shard_map/ppermute | solution.py:359
  98.5 0.0 collective-permute-done.12.pairs
  98.5 1.9 %collective-permute-start.13 = (bf16[8,256,128]{2,1,0:T(8,128)(2,1)S(1)}, bf16[8,256,128]{2,1,0:T(8,128)(2,1)S(1)}, u32[]{:S(2)}, u32[]{:S(2)}) collective-permute-start(bf16[8,256,128]{2,1,0:T(8,128)(2,1)S(1)} %collective-permute-done.12.pairs), channel_id=1, source_target_pairs={{32,64},{64,96},{33,65},{65,97},{34,66},{66,98},{35,67},{67,99},{3... | collective-permute-start | bytes 1572872 | tf_op jit(solution)/shard_map/ppermute | solution.py:360
  100.5 7.1 %shard_map.71 = (f32[4096,128]{1,0:T(8,128)S(1)}, f32[4096,128]{1,0:T(8,128)S(1)}) custom-call(s32[2]{0:T(128)S(1)} %pad_add_fusion.1.info, bf16[4,256,256]{2,1,0:T(8,128)(2,1)S(1)} %get-tuple-element.47.kept, bf16[4,256,256]{2,1,0:T(8,128)(2,1)S(1)} %collective-permute-done.11.crossed, ...), custom_call_target="tpu_custom_call", output_to_operand_aliasing={{0}: (4, {}), {1}: (5, {})} | custom-call | flops 2147483648 | bytes 4194304 | tf_op jit(solution)/shard_map/pallas_call | solution.py:218
  107.6 0.0 collective-permute-done.17.pairs
  107.6 4.2 %shard_map.72 = (f32[4096,128]{1,0:T(8,128)S(1)}, f32[4096,128]{1,0:T(8,128)S(1)}) custom-call(s32[2]{0:T(128)S(1)} %pad_add_fusion.1.info, bf16[4,256,256]{2,1,0:T(8,128)(2,1)S(1)} %get-tuple-element.47.kept, bf16[4,256,256]{2,1,0:T(8,128)(2,1)S(1)} %collective-permute-done.11.crossed, ...), custom_call_target="tpu_custom_call", output_to_operand_aliasing={{0}: (4, {}), {1}: (5, {})} | custom-call | flops 1073741824 | bytes 4194304 | tf_op jit(solution)/shard_map/pallas_call | solution.py:218
  111.8 4.4 %shard_map.73 = (f32[4096,128]{1,0:T(8,128)S(1)}, f32[4096,128]{1,0:T(8,128)S(1)}) custom-call(s32[2]{0:T(128)S(1)} %pad_add_fusion.1.info, bf16[4,256,256]{2,1,0:T(8,128)(2,1)S(1)} %get-tuple-element.47.kept, bf16[4,256,256]{2,1,0:T(8,128)(2,1)S(1)} %collective-permute-done.11.crossed, ...), custom_call_target="tpu_custom_call", output_to_operand_aliasing={{0}: (4, {}), {1}: (5, {})} | custom-call | flops 1073741824 | bytes 4194304 | tf_op jit(solution)/shard_map/pallas_call | solution.py:218
  116.3 0.0 collective-permute-done.15.pairs
  116.3 5.8 %shard_map.74 = (f32[4096,128]{1,0:T(8,128)S(1)}, f32[4096,128]{1,0:T(8,128)S(1)}) custom-call(s32[2]{0:T(128)S(1)} %pad_add_fusion.1.info, bf16[4,256,256]{2,1,0:T(8,128)(2,1)S(1)} %get-tuple-element.47.kept, bf16[4,256,256]{2,1,0:T(8,128)(2,1)S(1)} %collective-permute-done.11.crossed, ...), custom_call_target="tpu_custom_call", output_to_operand_aliasing={{0}: (4, {}), {1}: (5, {})} | custom-call | flops 1744830464 | bytes 4194304 | tf_op jit(solution)/shard_map/pallas_call | solution.py:218
  122.1 0.0 collective-permute-done.13.pairs
  122.1 3.9 %shard_map.75 = bf16[2048,256]{1,0:T(8,128)(2,1)} custom-call(s32[2]{0:T(128)S(1)} %pad_add_fusion.1.info, bf16[4,256,256]{2,1,0:T(8,128)(2,1)S(1)} %get-tuple-element.47.kept, bf16[4,256,256]{2,1,0:T(8,128)(2,1)S(1)} %collective-permute-done.11.crossed, bf16[8,256,128]{2,1,0:T(8,128)(2,1)S(1)} %collective-permute-done.13.pairs, ...), custom_call_target="tpu_custom_call" | custom-call | flops 671088640 | bytes 4194304 | tf_op jit(solution)/shard_map/pallas_call | solution.py:218
  126.0 3.7 %all-to-all-start.2 = ((bf16[8,256,256]{2,1,0:T(8,128)(2,1)}), bf16[8,256,256]{2,1,0:T(8,128)(2,1)S(1)}, u32[]{:S(2)}, u32[]{:S(2)}) async-start(bf16[8,256,256]{2,1,0:T(8,128)(2,1)} %bitcast.14), calls=%async_computation.2 | async-start | bytes 2097152 | tf_op jit(solution)/shard_map/all_to_all | solution.py:381
  129.8 0.1 collective-permute-start.10
  130.5 0.9 collective-permute-done.10
  131.4 0.9 fusion
  132.3 13.4 %all-to-all-done.2 = bf16[8,256,256]{2,1,0:T(8,128)(2,1)S(1)} async-done(((bf16[8,256,256]{2,1,0:T(8,128)(2,1)}), bf16[8,256,256]{2,1,0:T(8,128)(2,1)S(1)}, u32[]{:S(2)}, u32[]{:S(2)}) %all-to-all-start.2) | async-done | bytes 1048608 | tf_op jit(solution)/shard_map/all_to_all | solution.py:381
  145.8 0.6 copy.22
  146.3 0.5 reshape.132
  146.9 1.1 broadcast_select_fusion
  (28 shorter events, 0.1 us)
Async XLA Ops:
  0.6 30.5 %collective-permute-start = (bf16[256,4608]{1,0:T(8,128)(2,1)}, bf16[256,4608]{1,0:T(8,128)(2,1)}, u32[]{:S(2)}, u32[]{:S(2)}) collective-permute-start(bf16[256,4608]{1,0:T(8,128)(2,1)} %bitcast.27), channel_id=1, source_target_pairs={{0,1},{1,0},{2,3},{3,2},{4,5},{5,4},{6,7},{7,6},{8,9},{9,8},{10,11... | collective-permute-start | bytes 7077896 | tf_op jit(solution)/shard_map/ppermute | solution.py:47
  0.7 30.5 %collective-permute-start.1 = (bf16[1152,1024]{1,0:T(8,128)(2,1)}, bf16[1152,1024]{1,0:T(8,128)(2,1)}, u32[]{:S(2)}, u32[]{:S(2)}) collective-permute-start(bf16[1152,1024]{1,0:T(8,128)(2,1)} %weight_b.1), channel_id=1, source_target_pairs={{0,1},{1,0},{2,3},{3,2},{4,5},{5,4},{6,7},{7,6},{8,9},{9,8},{10,11... | collective-permute-start | bytes 7077896 | tf_op jit(solution)/shard_map/ppermute | solution.py:47
  2.9 11.5 %collective-permute-start.4 = (bf16[144,512]{1,0:T(8,128)(2,1)}, bf16[144,512]{1,0:T(8,128)(2,1)}, u32[]{:S(2)}, u32[]{:S(2)}) collective-permute-start(bf16[144,512]{1,0:T(8,128)(2,1)} %get-tuple-element.40), channel_id=1, source_target_pairs={{0,2},{1,7},{2,4},{3,1},{4,6},{5,3},{6,0},{7,5},{8,10},{9,15},{10,... | collective-permute-start | bytes 442376 | tf_op jit(solution)/shard_map/ppermute | solution.py:252
  4.4 10.0 %collective-permute-start.5 = (bf16[144,512]{1,0:T(8,128)(2,1)}, bf16[144,512]{1,0:T(8,128)(2,1)}, u32[]{:S(2)}, u32[]{:S(2)}) collective-permute-start(bf16[144,512]{1,0:T(8,128)(2,1)} %get-tuple-element.41), channel_id=1, source_target_pairs={{0,3},{1,6},{2,5},{3,0},{4,7},{5,2},{6,1},{7,4},{8,11},{9,14},{10,... | collective-permute-start | bytes 442376 | tf_op jit(solution)/shard_map/ppermute | solution.py:253
  8.8 7.5 %copy-start.1 = (bf16[1152,1024]{1,0:T(8,128)(2,1)S(1)}, bf16[1152,1024]{1,0:T(8,128)(2,1)}, u32[]{:S(2)}) copy-start(bf16[1152,1024]{1,0:T(8,128)(2,1)} %weight_b.1) | copy-start | bytes 7077892
  8.8 7.5 %copy-start.3 = (bf16[2,128,1024]{2,1,0:T(8,128)(2,1)S(1)}, bf16[2,128,1024]{2,1,0:T(8,128)(2,1)}, u32[]{:S(2)}) copy-start(bf16[2,128,1024]{2,1,0:T(8,128)(2,1)} %up_own.1) | copy-start | bytes 1572868
  9.9 23.3 %all-to-all-start = ((bf16[4,2,256,256]{3,2,1,0:T(8,128)(2,1)}), bf16[4,2,256,256]{3,2,1,0:T(8,128)(2,1)}, u32[]{:S(2)}, u32[]{:S(2)}) async-start(bf16[4,2,256,256]{3,2,1,0:T(8,128)(2,1)} %maximum_bitcast_fusion), calls=%async_computation | async-start | bytes 2097152 | tf_op jit(solution)/shard_map/all_to_all | solution.py:288
  16.2 10.9 %collective-permute-start.8 = (bf16[2,144,512]{2,1,0:T(8,128)(2,1)}, bf16[2,144,512]{2,1,0:T(8,128)(2,1)S(1)}, u32[]{:S(2)}, u32[]{:S(2)}) collective-permute-start(bf16[2,144,512]{2,1,0:T(8,128)(2,1)} %pad_maximum_fusion.relay_0), channel_id=1, source_target_pairs={{0,64},{32,96},{64,0},{96,32},{1,65},{33,97},{65,1},{97,33},{2,66}... | collective-permute-start | bytes 884744 | tf_op jit(solution)/shard_map/ppermute | solution.py:278
  18.2 17.0 %copy-start = (bf16[1,256,4608]{2,1,0:T(8,128)(2,1)S(1)}, bf16[1,256,4608]{2,1,0:T(8,128)(2,1)}, u32[]{:S(2)}) copy-start(bf16[1,256,4608]{2,1,0:T(8,128)(2,1)} %param.5) | copy-start | bytes 7077892
  18.2 23.4 %collective-permute-start.2 = (bf16[832,512]{1,0:T(8,128)(2,1)}, bf16[832,512]{1,0:T(8,128)(2,1)}, u32[]{:S(2)}, u32[]{:S(2)}) collective-permute-start(bf16[832,512]{1,0:T(8,128)(2,1)} %get-tuple-element.21), channel_id=1, source_target_pairs={{0,2},{1,7},{2,4},{3,1},{4,6},{5,3},{6,0},{7,5},{8,10},{9,15},{10,... | collective-permute-start | bytes 2555912 | tf_op jit(solution)/shard_map/ppermute | solution.py:275
  19.7 21.9 %collective-permute-start.3 = (bf16[832,512]{1,0:T(8,128)(2,1)}, bf16[832,512]{1,0:T(8,128)(2,1)}, u32[]{:S(2)}, u32[]{:S(2)}) collective-permute-start(bf16[832,512]{1,0:T(8,128)(2,1)} %get-tuple-element.22), channel_id=1, source_target_pairs={{0,3},{1,6},{2,5},{3,0},{4,7},{5,2},{6,1},{7,4},{8,11},{9,14},{10,... | collective-permute-start | bytes 2555912 | tf_op jit(solution)/shard_map/ppermute | solution.py:276
  27.1 6.0 %copy-start.6 = (bf16[2,144,512]{2,1,0:T(8,128)(2,1)}, bf16[2,144,512]{2,1,0:T(8,128)(2,1)S(1)}, u32[]{:S(2)}) copy-start(bf16[2,144,512]{2,1,0:T(8,128)(2,1)S(1)} %collective-permute-done.8.relay_3) | copy-start | bytes 884740
  27.1 14.5 %collective-permute-start.9 = (bf16[2,128,1024]{2,1,0:T(8,128)(2,1)S(1)}, bf16[2,128,1024]{2,1,0:T(8,128)(2,1)}, u32[]{:S(2)}, u32[]{:S(2)}) collective-permute-start(bf16[2,128,1024]{2,1,0:T(8,128)(2,1)S(1)} %copy-done.3), channel_id=1, source_target_pairs={{0,1},{1,0},{2,3},{3,2},{4,5},{5,4},{6,7},{7,6},{8,9},{9,8},{10,11... | collective-permute-start | bytes 1572872 | tf_op jit(solution)/shard_map/ppermute | solution.py:47
  31.1 10.5 %collective-permute-start.7 = (bf16[2,144,512]{2,1,0:T(8,128)(2,1)}, bf16[2,144,512]{2,1,0:T(8,128)(2,1)}, u32[]{:S(2)}, u32[]{:S(2)}) collective-permute-start(bf16[2,144,512]{2,1,0:T(8,128)(2,1)} %pad_maximum_fusion.relay_0), channel_id=1, source_target_pairs={{0,96},{32,0},{64,32},{96,64},{1,97},{33,1},{65,33},{97,65},{2,98}... | collective-permute-start | bytes 884744 | tf_op jit(solution)/shard_map/ppermute | solution.py:278
  31.2 10.4 %collective-permute-start.6 = (bf16[2,144,512]{2,1,0:T(8,128)(2,1)}, bf16[2,144,512]{2,1,0:T(8,128)(2,1)}, u32[]{:S(2)}, u32[]{:S(2)}) collective-permute-start(bf16[2,144,512]{2,1,0:T(8,128)(2,1)} %pad_maximum_fusion.relay_0), channel_id=1, source_target_pairs={{0,32},{32,64},{64,96},{96,0},{1,33},{33,65},{65,97},{97,1},{2,34}... | collective-permute-start | bytes 884744 | tf_op jit(solution)/shard_map/ppermute | solution.py:278
  35.2 1.7 %copy-start.2 = (bf16[1152,1024]{1,0:T(8,128)(2,1)S(1)}, bf16[1152,1024]{1,0:T(8,128)(2,1)}, u32[]{:S(2)}) copy-start(bf16[1152,1024]{1,0:T(8,128)(2,1)} %weight_b.1) | copy-start | bytes 7077892
  36.9 4.7 %copy-start.5 = (f32[256,128]{1,0:T(8,128)S(1)}, f32[256,128]{1,0:T(8,128)}, u32[]{:S(2)}) copy-start(f32[256,128]{1,0:T(8,128)} %get-tuple-element.56.sine) | copy-start | bytes 393220
  36.9 4.7 %copy-start.7 = (bf16[2,144,512]{2,1,0:T(8,128)(2,1)S(1)}, bf16[2,144,512]{2,1,0:T(8,128)(2,1)}, u32[]{:S(2)}) copy-start(bf16[2,144,512]{2,1,0:T(8,128)(2,1)} %copy-done.6) | copy-start | bytes 884740
  41.6 1.2 copy-start.4
  48.9 6.5 %copy-start.9 = (bf16[4,256,256]{2,1,0:T(8,128)(2,1)S(1)}, bf16[4,256,256]{2,1,0:T(8,128)(2,1)}, u32[]{:S(2)}) copy-start(bf16[4,256,256]{2,1,0:T(8,128)(2,1)} %get-tuple-element.25) | copy-start | bytes 1572868
  48.9 25.0 %all-to-all-start.1 = ((bf16[16,256,128]{2,1,0:T(8,128)(2,1)}), bf16[16,256,128]{2,1,0:T(8,128)(2,1)S(1)}, u32[]{:S(2)}, u32[]{:S(2)}) async-start(bf16[16,256,128]{2,1,0:T(8,128)(2,1)} %get-tuple-element.26), calls=%async_computation.1 | async-start | bytes 2097152 | tf_op jit(solution)/shard_map/all_to_all | solution.py:351
  55.4 27.1 %collective-permute-start.11 = (bf16[4,256,256]{2,1,0:T(8,128)(2,1)S(1)}, bf16[4,256,256]{2,1,0:T(8,128)(2,1)S(1)}, u32[]{:S(2)}, u32[]{:S(2)}) collective-permute-start(bf16[4,256,256]{2,1,0:T(8,128)(2,1)S(1)} %copy-done.9), channel_id=1, source_target_pairs={{0,4},{4,0},{1,5},{5,1},{2,6},{6,2},{3,7},{7,3},{8,12},{12,8},{9,1... | collective-permute-start | bytes 1572872 | tf_op jit(solution)/shard_map/ppermute | solution.py:350
  74.0 14.3 %collective-permute-start.14 = (bf16[8,256,128]{2,1,0:T(8,128)(2,1)S(1)}, bf16[8,256,128]{2,1,0:T(8,128)(2,1)S(1)}, u32[]{:S(2)}, u32[]{:S(2)}) collective-permute-start(bf16[8,256,128]{2,1,0:T(8,128)(2,1)S(1)} %get-tuple-element.44), channel_id=1, source_target_pairs={{32,0},{0,96},{33,1},{1,97},{34,2},{2,98},{35,3},{3,99},{36,4},{4,... | collective-permute-start | bytes 1572872 | tf_op jit(solution)/shard_map/ppermute | solution.py:357
  74.8 23.7 %collective-permute-start.12 = (bf16[8,256,128]{2,1,0:T(8,128)(2,1)S(1)}, bf16[8,256,128]{2,1,0:T(8,128)(2,1)S(1)}, u32[]{:S(2)}, u32[]{:S(2)}) collective-permute-start(bf16[8,256,128]{2,1,0:T(8,128)(2,1)S(1)} %get-tuple-element.45), channel_id=1, source_target_pairs={{0,32},{32,64},{64,96},{1,33},{33,65},{65,97},{2,34},{34,66},{66,9... | collective-permute-start | bytes 1572872 | tf_op jit(solution)/shard_map/ppermute | solution.py:356
  88.4 27.9 %collective-permute-start.15 = (bf16[8,256,128]{2,1,0:T(8,128)(2,1)S(1)}, bf16[8,256,128]{2,1,0:T(8,128)(2,1)S(1)}, u32[]{:S(2)}, u32[]{:S(2)}) collective-permute-start(bf16[8,256,128]{2,1,0:T(8,128)(2,1)S(1)} %collective-permute-done.14), channel_id=1, source_target_pairs={{0,96},{96,64},{1,97},{97,65},{2,98},{98,66},{3,99},{99,67},{4,100... | collective-permute-start | bytes 1572872 | tf_op jit(solution)/shard_map/ppermute | solution.py:365
  89.7 17.9 %collective-permute-start.17 = (bf16[4,256,128]{2,1,0:T(8,128)(2,1)S(1)}, bf16[4,256,128]{2,1,0:T(8,128)(2,1)S(1)}, u32[]{:S(2)}, u32[]{:S(2)}) collective-permute-start(bf16[4,256,128]{2,1,0:T(8,128)(2,1)S(1)} %get-tuple-element.42), channel_id=1, source_target_pairs={{0,32},{32,64},{64,96},{1,33},{33,65},{65,97},{2,34},{34,66},{66,9... | collective-permute-start | bytes 786440 | tf_op jit(solution)/shard_map/ppermute | solution.py:358
  96.6 15.2 %collective-permute-start.16 = (bf16[4,256,128]{2,1,0:T(8,128)(2,1)S(1)}, bf16[4,256,128]{2,1,0:T(8,128)(2,1)S(1)}, u32[]{:S(2)}, u32[]{:S(2)}) collective-permute-start(bf16[4,256,128]{2,1,0:T(8,128)(2,1)S(1)} %get-tuple-element.43), channel_id=1, source_target_pairs={{0,32},{32,64},{64,96},{1,33},{33,65},{65,97},{2,34},{34,66},{66,9... | collective-permute-start | bytes 786440 | tf_op jit(solution)/shard_map/ppermute | solution.py:359
  98.5 23.6 %collective-permute-start.13 = (bf16[8,256,128]{2,1,0:T(8,128)(2,1)S(1)}, bf16[8,256,128]{2,1,0:T(8,128)(2,1)S(1)}, u32[]{:S(2)}, u32[]{:S(2)}) collective-permute-start(bf16[8,256,128]{2,1,0:T(8,128)(2,1)S(1)} %collective-permute-done.12.pairs), channel_id=1, source_target_pairs={{32,64},{64,96},{33,65},{65,97},{34,66},{66,98},{35,67},{67,99},{3... | collective-permute-start | bytes 1572872 | tf_op jit(solution)/shard_map/ppermute | solution.py:360
  126.0 3.7 %copy-start.8 = (bf16[512,512]{1,0:T(8,128)(2,1)S(1)}, bf16[512,512]{1,0:T(8,128)(2,1)}, u32[]{:S(2)}) copy-start(bf16[512,512]{1,0:T(8,128)(2,1)} %get-tuple-element.23) | copy-start | bytes 1572868
  126.0 19.7 %all-to-all-start.2 = ((bf16[8,256,256]{2,1,0:T(8,128)(2,1)}), bf16[8,256,256]{2,1,0:T(8,128)(2,1)S(1)}, u32[]{:S(2)}, u32[]{:S(2)}) async-start(bf16[8,256,256]{2,1,0:T(8,128)(2,1)} %bitcast.14), calls=%async_computation.2 | async-start | bytes 2097152 | tf_op jit(solution)/shard_map/all_to_all | solution.py:381
  129.8 1.6 %collective-permute-start.10 = (bf16[256,512]{1,0:T(8,128)(2,1)S(1)}, bf16[256,512]{1,0:T(8,128)(2,1)S(1)}, u32[]{:S(2)}, u32[]{:S(2)}) collective-permute-start(bf16[256,512]{1,0:T(8,128)(2,1)S(1)} %get-tuple-element.51), channel_id=1, source_target_pairs={{0,1},{1,0},{2,3},{3,2},{4,5},{5,4},{6,7},{7,6},{8,9},{9,8},{10,11... | collective-permute-start | bytes 786440 | tf_op jit(solution)/shard_map/ppermute | solution.py:47

commit v4 on v3

v4 whole, which is shorter than its diff:
```python
import functools
import itertools

import jax
import jax.numpy as jnp
from jax import lax
from jax.experimental import pallas as pl
from jax.experimental.pallas import tpu as pltpu
from jax.sharding import Mesh
from jax.sharding import PartitionSpec as P


HEAD = 128
PAIR = 2 * HEAD
BLOCK = 256
CHUNK = 2048
KV_HEADS = 8
BLOCKS = CHUNK // BLOCK
LOW = 4
GRANT = {"collect": 60, "half": 49, "project": 46}
RELAYED = 576
SIZES = {"z": 4, "y": 4, "xh": 2, "xl": 2, "core": 2}
SEQ_AXES = ("z", "y", "xh")
DP_AXES = ("xl", "core")
PLANE = ("y", "xh")

query_scale = 144.0 ** (-0.5)
soft_cap = 50.0
LOG2E = 1.4426950408889634
CONTRACT_LAST = (((1,), (1,)), ((), ()))


X_AXES = ("xh", "xl", "core")


def x_step(flip):
    pairs = []
    for x, core in itertools.product(range(4), range(2)):
        to = (x + (1 if core == 0 else -1)) % 4
        pairs.append((2 * x + core, 2 * to + (core ^ flip)))
    return pairs


def ring(step):
    return [(i, (i + step) % 4) for i in range(4)]


def to_partner(array):
    return lax.ppermute(array, "core", [(0, 1), (1, 0)])


def begin(sems, *moves):
    copies = [pltpu.make_async_copy(a, b, sems.at[k]) for k, (a, b) in enumerate(moves)]
    for copy in copies:
        copy.start()
    return copies


def finish(copies):
    for copy in copies:
        copy.wait()


def chunk(index, size):
    return pl.ds(pl.multiple_of(index * size, size), size)


def collect_kernel(info, down, up, queries, relay_a, relay_b, direct_a, direct_b, sent, sems):
    share, rank = relay_a.shape
    piece = up.shape[1]
    split = down.shape[0] - 4 * share
    first = pl.ds(pl.multiple_of(split + share * info[1], 16), share)
    moves = []
    for flip, relay, direct in ((0, relay_a, direct_a), (1, relay_b, direct_b)):
        which = (info[0] ^ flip) % 2
        columns = chunk(which, rank)
        moves.append((down.at[first, columns], relay))
        moves.append((down.at[pl.ds(0, split), columns], direct.at[pl.ds(0, split)]))
        for k in range(2):
            at = pl.ds(split + k * piece, piece)
            moves.append((up.at[which, :, pl.ds(k * rank, rank)], direct.at[at]))
    for y, k in itertools.product(range(4), range(2)):
        pair = 2 * y + (info[2] ^ k)
        moves.append((queries.at[:, chunk(pair, PAIR)], sent.at[y, k]))
    finish(begin(sems, *moves))


def couple_kernel(a, b, out):
    out[0] = a[...]
    out[1] = b[...]


def hidden_moves(hidden, partner, shard, into):
    rows = hidden.shape[0]
    columns = chunk(shard, into.shape[1])
    return [
        (hidden.at[:, columns], into.at[pl.ds(0, rows)]),
        (partner.at[:, columns], into.at[pl.ds(rows, rows)]),
    ]


def half_kernel(info, hidden, partner, weight_0, weight_1, out, inputs, weights, sems):
    columns = chunk(info[0] % 2, weights.shape[2])
    moves = []
    for k, weight in enumerate((weight_0, weight_1)):
        moves += hidden_moves(hidden, partner, info[0] ^ k, inputs.at[k])
        moves.append((weight.at[:, columns], weights.at[k]))
    copies = begin(sems, *moves)
    finish(copies[:3])
    total = jnp.dot(inputs[0], weights[0], preferred_element_type=jnp.float32)
    finish(copies[3:])
    out[...] = total + jnp.dot(inputs[1], weights[1], preferred_element_type=jnp.float32)


def project_kernel(
    info, partial, hidden, partner, direct_a, direct_b, relay_0, relay_1, relay_2, relay_3,
    up_own, up_partner, cosine, sine, latent, pairs,
    inputs, weights, upper, rounded, ready, sems, out_sems,
):
    mine, plane = info[0], info[1]
    core = mine % 2
    rows = hidden.shape[0]
    piece = up_own.shape[1]
    share, rank = relay_0.shape[1:]
    split = weights.shape[1] - 4 * share
    moves = []
    for which, direct in ((0, direct_a), (1, direct_b)):
        moves += hidden_moves(hidden, partner, mine ^ (2 + which), inputs.at[which])
        moves.append((direct.at[pl.ds(0, split)], weights.at[which, pl.ds(0, split)]))
        for step, relay in ((0, relay_0), (3, relay_1), (1, relay_2), (2, relay_3)):
            at = pl.multiple_of(split + share * ((plane + step) % 4), 16)
            moves.append((relay.at[which], weights.at[which, pl.ds(at, share)]))
    count = len(moves) // 2
    moves.append((up_own.at[core], upper.at[chunk(mine, piece)]))
    moves.append((up_partner.at[core], upper.at[chunk(mine ^ 1, piece)]))
    for which, direct in ((0, direct_a), (1, direct_b)):
        for k in range(2):
            at = (chunk(mine ^ (2 + which), piece), pl.ds(k * rank, rank))
            moves.append((direct.at[pl.ds(split + k * piece, piece)], upper.at[at]))
    copies = begin(sems, *moves)
    finish(copies[:count])
    total = partial[...] + jnp.dot(inputs[0], weights[0], preferred_element_type=jnp.float32)
    finish(copies[count : 2 * count])
    total = total + jnp.dot(inputs[1], weights[1], preferred_element_type=jnp.float32)
    rounded[...] = total.astype(jnp.bfloat16)
    outgoing = [pltpu.make_async_copy(rounded, latent, out_sems.at[2 * KV_HEADS])]
    outgoing[0].start()
    finish(copies[2 * count :])
    for head in range(KV_HEADS):
        raw = jnp.dot(
            rounded[...], upper[:, head * HEAD : (head + 1) * HEAD],
            preferred_element_type=jnp.float32,
        )
        for which, turn in ((0, core), (1, 1 - core)):
            entry = raw[which * rows : (which + 1) * rows]
            entry = entry * cosine[...] + pltpu.roll(entry, HEAD // 2, 1) * sine[...]
            ready[2 * head + which] = entry.astype(jnp.bfloat16)
            copy = pltpu.make_async_copy(
                ready.at[2 * head + which],
                pairs.at[2 * head + turn],
                out_sems.at[2 * head + which],
            )
            copy.start()
            outgoing.append(copy)
    finish(outgoing)


def assemble_kernel(info, home, out):
    rows = out.shape[0]
    live = (info[3] + lax.broadcasted_iota(jnp.int32, (rows, PAIR), 0)) < info[4]
    for k in range(home.shape[0]):
        part = home[k]
        out[:, k * PAIR : (k + 1) * PAIR] = jnp.where(live, part, jnp.zeros_like(part))


def expo(raw):
    return jnp.exp2(jnp.tanh(raw * (query_scale / soft_cap)) * (soft_cap * LOG2E))


def folded(values):
    total = values[:, :HEAD]
    for t in range(1, values.shape[1] // HEAD):
        total = total + values[:, t * HEAD : (t + 1) * HEAD]
    return total


def triangle(newer):
    row = lax.broadcasted_iota(jnp.int32, (2 * BLOCK, BLOCK), 0) % BLOCK
    col = lax.broadcasted_iota(jnp.int32, (2 * BLOCK, BLOCK), 1)
    return col <= row if newer else col > row


def stacked_rows(info, queries, pair, parity):
    kept, crossed = queries
    own = jnp.where(info[2] == parity, kept[pair, 0], crossed[pair])
    return jnp.concatenate([own[:, :HEAD], own[:, HEAD:]], axis=0)


def over_blocks(stacked, pairs, blocks):
    numer = denom = 0.0
    for j, mask in blocks:
        raw = lax.dot_general(
            stacked, pairs[2 * j], CONTRACT_LAST, preferred_element_type=jnp.float32
        )
        e = expo(raw)
        if mask is not None:
            e = jnp.where(mask, e, 0.0)
        denom = denom + folded(e)
        numer = numer + jnp.dot(
            e.astype(jnp.bfloat16), pairs[2 * j + 1], preferred_element_type=jnp.float32
        )
    return numer, denom


def state_rows(i):
    return pl.ds(pl.multiple_of(i * 2 * BLOCK, 2 * BLOCK), 2 * BLOCK)


def own_kernel(info, kept, crossed, pairs, numer, denom):
    mask = triangle(True)
    for i in range(BLOCKS):
        blocks = [(j, None) for j in range(i)] + [(i, mask)]
        numer[state_rows(i), :], denom[state_rows(i), :] = over_blocks(
            stacked_rows(info, (kept, crossed), i // 2, i % 2), pairs, blocks
        )


def near_kernel(group, info, kept, crossed, pairs, numer_in, denom_in, numer, denom):
    blocks = [(j, None) for j in range(pairs.shape[0] // 2)]

    @pl.when(info[1] >= 1)
    def _():
        def step(t, carry):
            for u in range(group):
                i = t * group + u
                stacked = stacked_rows(
                    info, (kept, crossed), t * (group // 2) + u // 2, u % 2
                )
                n, d = over_blocks(stacked, pairs, blocks)
                numer[state_rows(i), :] += n
                denom[state_rows(i), :] += d
            return carry

        lax.fori_loop(0, BLOCKS // group, step, 0)


def far_kernel(first, last, info, kept, crossed, pairs, numer_in, denom_in, *outs):
    end = first + pairs.shape[0] // 2
    mask = triangle(False)
    numer, denom = (numer_in, denom_in) if last else outs

    def settle(i, n, d):
        if last:
            n = n / jnp.sum(d, axis=1, keepdims=True)
            outs[0][i * BLOCK : (i + 1) * BLOCK, :] = jnp.concatenate(
                [n[:BLOCK], n[BLOCK:]], axis=1
            ).astype(jnp.bfloat16)
        else:
            numer[state_rows(i), :], denom[state_rows(i), :] = n, d

    @pl.when(info[1] >= 2)
    def _():
        for i in range(BLOCKS):
            blocks = [(j - first, mask if j == i else None) for j in range(max(i, first), end)]
            old_n, old_d = numer[state_rows(i), :], denom[state_rows(i), :]
            if blocks:
                stacked = stacked_rows(info, (kept, crossed), i // 2, i % 2)
                n, d = over_blocks(stacked, pairs, blocks)
                settle(i, old_n + n, old_d + d)
            elif last:
                settle(i, old_n, old_d)

    if last:

        @pl.when(info[1] < 2)
        def _():
            for i in range(BLOCKS):
                settle(i, numer[state_rows(i), :], denom[state_rows(i), :])


IN_VMEM = pl.BlockSpec(memory_space=pltpu.VMEM)
IN_SMEM = pl.BlockSpec(memory_space=pltpu.SMEM)
ANYWHERE = pl.BlockSpec(memory_space=pl.ANY)
STATE = jax.ShapeDtypeStruct((2 * CHUNK, HEAD), jnp.float32)
RESULT = jax.ShapeDtypeStruct((CHUNK, PAIR), jnp.bfloat16)


def attention_call(kernel, count, args, result=False, resume=True):
    single = BLOCK * 2 * BLOCK
    inputs = [IN_SMEM] + [IN_VMEM] * (5 if resume else 3)
    return pl.pallas_call(
        kernel,
        out_shape=RESULT if result else (STATE, STATE),
        in_specs=inputs,
        out_specs=IN_VMEM if result else (IN_VMEM, IN_VMEM),
        input_output_aliases={4: 0, 5: 1} if resume and not result else {},
        compiler_params=pltpu.CompilerParams(vmem_limit_bytes=12 * 2**20),
        cost_estimate=pl.CostEstimate(
            flops=count * single * 4 * HEAD, bytes_accessed=2**22, transcendentals=2 * count * single
        ),
    )(*args)


def body(hidden, queries, down_weight, up_weight, lengths):
    _, rows, _ = hidden.shape
    depth, rank2 = down_weight.shape
    rank = rank2 // 2
    piece, kv_width = up_weight.shape[1:]
    groups = kv_width // HEAD
    hidden = hidden[0]
    core = lax.axis_index("core")
    mine = 2 * lax.axis_index("xl") + core
    plane = lax.axis_index("z")
    start = lax.axis_index(SEQ_AXES) * rows
    here = lax.axis_index("xh")
    info = jnp.stack([mine, plane, here, start, lengths[0]]).astype(jnp.int32)

    share = RELAYED // 4
    split = depth - RELAYED
    forward, crossed = x_step(0), x_step(1)

    def shape(*sizes):
        return jax.ShapeDtypeStruct(sizes, jnp.bfloat16)

    def scratch(*sizes):
        return pltpu.VMEM(sizes, jnp.bfloat16)

    def step(name, kernel, out_shape, in_specs, out_specs, scratch_shapes, flops):
        return pl.pallas_call(
            kernel,
            out_shape=out_shape,
            in_specs=in_specs,
            out_specs=out_specs,
            scratch_shapes=scratch_shapes,
            compiler_params=pltpu.CompilerParams(vmem_limit_bytes=GRANT.get(name, 20) * 2**20),
            cost_estimate=pl.CostEstimate(
                flops=flops, bytes_accessed=2**22, transcendentals=0
            ),
        )

    sems = pltpu.SemaphoreType.DMA
    relay_a, relay_b, direct_a, direct_b, sent = step(
        "collect",
        collect_kernel,
        (shape(share, rank),) * 2 + (shape(split + 2 * piece, rank),) * 2
        + (shape(4, 2, rows, PAIR),),
        [IN_SMEM] + [ANYWHERE] * 3,
        (IN_VMEM,) * 5,
        [sems((16,))],
        10**8,
    )(info, down_weight, up_weight, queries[0])
    relay_a = lax.ppermute(relay_a, X_AXES, forward)
    relay_b = lax.ppermute(relay_b, X_AXES, crossed)
    direct_a = lax.ppermute(direct_a, X_AXES, forward)
    direct_b = lax.ppermute(direct_b, X_AXES, crossed)
    relay_own = step(
        "couple", couple_kernel, shape(2, share, rank), [IN_VMEM] * 2, IN_VMEM, [], 10**7
    )(relay_a, relay_b)
    relays = [lax.ppermute(relay_own, "z", ring(k)) for k in (1, -1, 2)]
    partner_hidden = to_partner(hidden)
    partner_weight = to_partner(down_weight)
    partner_upper = to_partner(up_weight)
    sent = lax.all_to_all(sent, "y", 0, 0, tiled=True)
    leaving = sent[:, 1]

    half = HEAD // 2
    places = (start + jnp.arange(rows, dtype=jnp.int32)).astype(jnp.float32)
    freqs = 10000.0 ** (-2.0 * jnp.arange(half, dtype=jnp.float32) / HEAD)
    angles = places[:, None] * freqs[None, :]
    cosine, sine = jnp.cos(angles), jnp.sin(angles)
    cosine = jnp.where(core == 0, jnp.concatenate([cosine, cosine], axis=1), 1.0)
    sine = jnp.where(core == 0, jnp.concatenate([-sine, sine], axis=1), 0.0)

    flops = 4 * rows * depth * rank2
    partial = step(
        "half",
        half_kernel,
        jax.ShapeDtypeStruct((2 * rows, rank), jnp.float32),
        [IN_SMEM] + [ANYWHERE] * 4,
        IN_VMEM,
        [scratch(2, 2 * rows, depth), scratch(2, depth, rank), sems((6,))],
        flops,
    )(info, hidden, partner_hidden, down_weight, partner_weight)

    latent, pairs = step(
        "project",
        project_kernel,
        (
            pltpu.HBM((2 * rows, rank), jnp.bfloat16),
            pltpu.HBM((2 * groups, rows, HEAD), jnp.bfloat16),
        ),
        [IN_SMEM, IN_VMEM] + [ANYWHERE] * 10 + [IN_VMEM] * 2,
        (ANYWHERE, ANYWHERE),
        [
            scratch(2, 2 * rows, depth),
            scratch(2, depth, rank),
            scratch(rank, kv_width),
            scratch(2 * rows, rank),
            scratch(2 * groups, rows, HEAD),
            sems((20,)),
            sems((2 * groups + 1,)),
        ],
        flops,
    )(
        info, partial, hidden, partner_hidden, direct_a, direct_b,
        relay_own, *relays, up_weight, partner_upper, cosine, sine,
    )

    leaving, pairs = lax.optimization_barrier((leaving, pairs))
    crossed_queries = lax.ppermute(leaving, "xh", [(0, 1), (1, 0)])
    own_pairs = lax.all_to_all(pairs, PLANE + ("core",), 0, 0, tiled=True)
    other_half = to_partner(latent[rows:])

    low = 2 * LOW
    up = [(0, 1), (1, 2), (2, 3)]
    near_low = lax.ppermute(own_pairs[:low], "z", up)
    passing = lax.ppermute(own_pairs[low:], "z", [(1, 0), (0, 3)])
    near_high = lax.ppermute(own_pairs[low:], "z", up)
    far_low = lax.ppermute(near_low, "z", [(1, 2), (2, 3)])

    common = (info, sent, crossed_queries)
    state = attention_call(own_kernel, 36, (*common, own_pairs), resume=False)
    passing, state = lax.optimization_barrier((passing, state))
    far_high = lax.ppermute(passing, "z", [(0, 3), (3, 2)])
    for piece_pairs in (near_low, near_high):
        state = attention_call(
            functools.partial(near_kernel, 4),
            piece_pairs.shape[0] // 2 * BLOCKS,
            (*common, piece_pairs, *state),
        )
    state = attention_call(
        functools.partial(far_kernel, LOW, False), 26,
        (*common, far_high, *state),
    )
    result = attention_call(
        functools.partial(far_kernel, 0, True), 10,
        (*common, far_low, *state), result=True,
    )

    home = lax.all_to_all(result.reshape(groups, rows, PAIR), PLANE, 0, 0, tiled=True)
    each = 2
    attended = pl.pallas_call(
        assemble_kernel,
        out_shape=shape(rows, groups * PAIR),
        grid_spec=pltpu.PrefetchScalarGridSpec(
            num_scalar_prefetch=1,
            grid=(groups // each,),
            in_specs=[pl.BlockSpec((each, rows, PAIR), lambda i, s: (i, 0, 0))],
            out_specs=pl.BlockSpec((rows, each * PAIR), lambda i, s: (0, i)),
        ),
        compiler_params=pltpu.CompilerParams(vmem_limit_bytes=8 * 2**20),
        name="assemble",
    )(info, home)
    live = ((start + jnp.arange(rows, dtype=jnp.int32)) < lengths[0])[:, None]
    ours = latent[:rows]
    both = jnp.where(
        core == 0,
        jnp.concatenate([ours, other_half], axis=1),
        jnp.concatenate([other_half, ours], axis=1),
    )
    latent = jnp.where(live, both, jnp.zeros((), jnp.bfloat16))
    return latent[None], attended[None]


def solution(mesh):
    split = Mesh(mesh.devices.reshape(tuple(SIZES.values())), tuple(SIZES))
    rows = P(DP_AXES, SEQ_AXES, None)
    placed = (rows, rows, P(DP_AXES, None), P(None, DP_AXES, None), P(DP_AXES))

    return jax.shard_map(body, mesh=split, in_specs=placed, out_specs=(rows, rows), check_vma=False)
```

time: 149 us -> 145 us (0.973)
  local copies, waits for them, and re-layouts: 12.3 us -> 3.08 us
  starting transfers between devices: 44.6 us -> 48.8 us
  other arithmetic: 8.08 us -> 4.14 us
  Pallas kernels: 44.1 us -> 47.4 us
  waiting for transfers between devices: 37.3 us -> 39.6 us
    ppermute x4 -> x3, starting transfers between devices: 10.3 us -> 3.66 us  [the longest x1 2.1 us: body(): near_high = lax.ppermute(own_pairs[low:], 'z', up)]
    pallas_call x3 -> x5, Pallas kernels: 12.7 us -> 17.5 us  [the longest x1 6.05 us: body(): step('project', project_kernel, (pltpu.HBM((2 * rows, rank), jnp.bfloat16...]
    ppermute x1, starting transfers between devices: 5.51 us -> 9.97 us  [body(): near_low = lax.ppermute(own_pairs[:low], 'z', up)]
    dynamic_slice x2 -> x0, local copies, waits for them, and re-layouts: 3.87 us -> none  [the longest x1 2.17 us: body(): kept_part = lax.dynamic_index_in_dim(split_queries, here, 2, keepdims=False)]
    ppermute x3, starting transfers between devices: 2.03 us -> 5.31 us  [body(): relays = [lax.ppermute(relay_own, 'z', ring(k)) for k in (1, -1, 2)]]
    ppermute x1, waiting for transfers between devices: 0.01 us -> 3.05 us  [body(): near_low = lax.ppermute(own_pairs[:low], 'z', up)]
    ppermute x1, starting transfers between devices: 1.92 us -> 4.29 us  [body(): far_low = lax.ppermute(near_low, 'z', [(1, 2), (2, 3)])]
    ppermute x1, waiting for transfers between devices: 2.13 us -> 0.01 us  [body(): crossed_queries = lax.ppermute(leaving, 'xh', [(0, 1), (1, 0)])]
  transfers between devices with their start and end apart: 21 -> 20, of which waited for: 5 -> 8; matrix products, arithmetic and copies ran while one was open for 10% -> 4% of each run, Pallas kernels for 23% -> 24%
where the time goes in v4:
time: 145 us
  starting transfers between devices  48.8 us (34%)
  Pallas kernels  47.4 us (33%)
  waiting for transfers between devices  39.6 us (27%)
  other arithmetic  4.14 us (3%)
  local copies, waits for them, and re-layouts  3.08 us (2%)
  between operations  1.56 us (1%)
    pallas_call x5, Pallas kernels, attention_call(): pl.pallas_call(kernel, out_shape=RESULT if result else (STATE, STATE), in...  29.8 us
    all_to_all x1, waiting for transfers between devices, body(): own_pairs = lax.all_to_all(pairs, PLANE + ('core',), 0, 0, tiled=True)  15.1 us
    all_to_all x1, waiting for transfers between devices, body(): lax.all_to_all(result.reshape(groups, rows, PAIR), PLANE, 0, 0, tiled=True)  13.2 us
    ppermute x1, starting transfers between devices, body(): near_low = lax.ppermute(own_pairs[:low], 'z', up)  9.97 us
    all_to_all x1, starting transfers between devices, body(): own_pairs = lax.all_to_all(pairs, PLANE + ('core',), 0, 0, tiled=True)  6.65 us
    ppermute x3, waiting for transfers between devices, body(): relays = [lax.ppermute(relay_own, 'z', ring(k)) for k in (1, -1, 2)]  6.12 us
    pallas_call x1, Pallas kernels, body(): step('project', project_kernel, (pltpu.HBM((2 * rows, rank), jnp.bfloat16...  6.05 us
    ppermute x3, starting transfers between devices, body(): relays = [lax.ppermute(relay_own, 'z', ring(k)) for k in (1, -1, 2)]  5.31 us
  transfers between devices with their start and end apart: 20, of which 8 were waited for; matrix products, arithmetic and copies ran while one was open for 4% of the time, Pallas kernels for 24%

profile of v4, /device:TPU:64, one launch (start us, length us, event | category | flops | bytes accessed | tf_op | source)
XLA Modules:
  0.0 144.5 jit_solution(18258251607551609514)
XLA Ops:
  0.6 0.1 collective-permute-start
  0.7 0.5 collective-permute-start.1
  1.9 0.7 stack.19.info
  2.6 4.3 %shard_map.69 = (bf16[144,512]{1,0:T(8,128)(2,1)}, bf16[144,512]{1,0:T(8,128)(2,1)}, bf16[832,512]{1,0:T(8,128)(2,1)}, bf16[832,512]{1,0:T(8,128)(2,1)}, bf16[4,2,256,256]{3,2,1,0:T(8,128)(2,1)}) custom-call(s32[5]{0:T(128)} %stack.19.info, bf16[1152,1024]{1,0:T(8,128)(2,1)} %down.1, bf16[2,128,1024]{2,1,0:T(8,128)(2,1)} %up_own.1, bf16[256,2048]{1,0:T(8,128)(2,1)} %bitcast.21), custom_call_target="tpu_custom_call" | custom-call | flops 100000000 | bytes 4194304 | tf_op jit(solution)/shard_map/pallas_call | solution.py:342
  6.8 1.6 %collective-permute-start.4 = (bf16[144,512]{1,0:T(8,128)(2,1)}, bf16[144,512]{1,0:T(8,128)(2,1)S(1)}, u32[]{:S(2)}, u32[]{:S(2)}) collective-permute-start(bf16[144,512]{1,0:T(8,128)(2,1)} %get-tuple-element.24), channel_id=1, source_target_pairs={{0,2},{1,7},{2,4},{3,1},{4,6},{5,3},{6,0},{7,5},{8,10},{9,15},{10,... | collective-permute-start | bytes 442376 | tf_op jit(solution)/shard_map/ppermute | solution.py:352
  8.4 0.0 collective-permute-start.5
  8.4 4.6 %all-to-all-start = ((bf16[4,2,256,256]{3,2,1,0:T(8,128)(2,1)}), bf16[4,2,256,256]{3,2,1,0:T(8,128)(2,1)S(1)}, u32[]{:S(2)}, u32[]{:S(2)}) async-start(bf16[4,2,256,256]{3,2,1,0:T(8,128)(2,1)} %get-tuple-element.27), calls=%async_computation | async-start | bytes 2097152 | tf_op jit(solution)/shard_map/all_to_all | solution.py:363
  13.0 0.5 collective-permute-done.4.a
  13.5 0.0 collective-permute-done.5.b
  13.5 0.9 shard_map.70.relay_0
  14.4 0.0 copy-start.2
  14.4 0.7 copy-done.2
  15.1 1.6 %collective-permute-start.6 = (bf16[2,144,512]{2,1,0:T(8,128)(2,1)S(1)}, bf16[2,144,512]{2,1,0:T(8,128)(2,1)S(1)}, u32[]{:S(2)}, u32[]{:S(2)}) collective-permute-start(bf16[2,144,512]{2,1,0:T(8,128)(2,1)S(1)} %shard_map.70.relay_0), channel_id=1, source_target_pairs={{0,32},{32,64},{64,96},{96,0},{1,33},{33,65},{65,97},{97,1},{2,34}... | collective-permute-start | bytes 884744 | tf_op jit(solution)/shard_map/ppermute | solution.py:359
  16.8 1.3 collective-permute-start.2
  18.1 1.9 %collective-permute-start.3 = (bf16[832,512]{1,0:T(8,128)(2,1)}, bf16[832,512]{1,0:T(8,128)(2,1)}, u32[]{:S(2)}, u32[]{:S(2)}) collective-permute-start(bf16[832,512]{1,0:T(8,128)(2,1)} %get-tuple-element.23), channel_id=1, source_target_pairs={{0,3},{1,6},{2,5},{3,0},{4,7},{5,2},{6,1},{7,4},{8,11},{9,14},{10,... | collective-permute-start | bytes 2555912 | tf_op jit(solution)/shard_map/ppermute | solution.py:355
  19.9 3.9 %collective-permute-done.6.relay_1 = bf16[2,144,512]{2,1,0:T(8,128)(2,1)S(1)} collective-permute-done((bf16[2,144,512]{2,1,0:T(8,128)(2,1)S(1)}, bf16[2,144,512]{2,1,0:T(8,128)(2,1)S(1)}, u32[]{:S(2)}, u32[]{:S(2)}) %collective-permute-start.6) | collective-permute-done | bytes 294944 | tf_op jit(solution)/shard_map/ppermute | solution.py:359
  23.9 0.7 copy-done.5
  24.6 1.4 collective-permute-start.9
  26.0 1.3 fusion.1
  27.3 1.9 %maximum_select_fusion.1 = (f32[256,128]{1,0:T(8,128)S(1)}, f32[256,128]{1,0:T(8,128)}) fusion(f32[256,64]{1,0:T(8,128)} %get-tuple-element.48, pred[]{:T(512)S(6)} %eq.2, f32[256,64]{1,0:T(8,128)} %get-tuple-element.47, f32[256,64]{1,0:T(8,128)} %get-tuple-element.46), kind=kLoop, calls=%fused_computation.6 | loop fusion | flops 131072 | bytes 458753 | tf_op jit(solution)/shard_map/jit(_where)/select_n | solution.py:371
  29.1 0.0 collective-permute-done.partner
  29.1 0.1 collective-permute-start.7
  29.2 0.0 collective-permute-done.1.weight_1
  29.3 3.6 %collective-permute-start.8 = (bf16[2,144,512]{2,1,0:T(8,128)(2,1)}, bf16[2,144,512]{2,1,0:T(8,128)(2,1)}, u32[]{:S(2)}, u32[]{:S(2)}) collective-permute-start(bf16[2,144,512]{2,1,0:T(8,128)(2,1)} %copy-done.2), channel_id=1, source_target_pairs={{0,64},{32,96},{64,0},{96,32},{1,65},{33,97},{65,1},{97,33},{2,66}... | collective-permute-start | bytes 884744 | tf_op jit(solution)/shard_map/ppermute | solution.py:359
  32.8 0.0 all-to-all-done.kept
  32.8 0.8 slice_bitcast_fusion
  33.7 0.0 copy-done
  33.7 0.0 copy-done.7
  33.7 0.0 copy-start.4
  33.7 0.0 copy-start.6
  33.7 4.2 %shard_map.68.partial = f32[512,512]{1,0:T(8,128)S(1)} custom-call(s32[5]{0:T(128)S(1)} %copy-done.7, bf16[256,4608]{1,0:T(8,128)(2,1)S(1)} %bitcast.18, bf16[256,4608]{1,0:T(8,128)(2,1)} %collective-permute-done.partner, bf16[1152,1024]{1,0:T(8,128)(2,1)} %down.1, bf16[1152,1024]{1,0:T(8,128)(2,1)} %collective-permute-done.1.weight_1), custom_call_target="tpu_custom_call" | custom-call | flops 1207959552 | bytes 4194304 | tf_op jit(solution)/shard_map/pallas_call | solution.py:375
  37.9 1.4 %collective-permute-done.7.relay_2 = bf16[2,144,512]{2,1,0:T(8,128)(2,1)} collective-permute-done((bf16[2,144,512]{2,1,0:T(8,128)(2,1)}, bf16[2,144,512]{2,1,0:T(8,128)(2,1)}, u32[]{:S(2)}, u32[]{:S(2)}) %collective-permute-start.7) | collective-permute-done | bytes 294944 | tf_op jit(solution)/shard_map/ppermute | solution.py:359
  39.3 0.7 collective-permute-done.8.relay_3
  40.1 0.0 collective-permute-done.9.up_partner
  40.1 0.0 collective-permute-done.2.direct_a
  40.1 0.0 collective-permute-done.3.direct_b
  40.1 0.0 copy-done.1
  40.1 6.1 %shard_map.71 = (bf16[512,512]{1,0:T(8,128)(2,1)}, bf16[16,256,128]{2,1,0:T(8,128)(2,1)}) custom-call(s32[5]{0:T(128)S(1)} %copy-done.7, f32[512,512]{1,0:T(8,128)S(1)} %shard_map.68.partial, bf16[256,4608]{1,0:T(8,128)(2,1)S(1)} %bitcast.19, bf16[256,4608]{1,0:T(8,128)(2,1)} %collective-permute-done.partner, ...), custom_call_target="tpu_custom_call" | custom-call | flops 1207959552 | bytes 4194304 | tf_op jit(solution)/shard_map/pallas_call | solution.py:385
  46.2 6.7 %all-to-all-start.1 = ((bf16[16,256,128]{2,1,0:T(8,128)(2,1)}), bf16[16,256,128]{2,1,0:T(8,128)(2,1)S(1)}, u32[]{:S(2)}, u32[]{:S(2)}) async-start(bf16[16,256,128]{2,1,0:T(8,128)(2,1)} %get-tuple-element.30), calls=%async_computation.1 | async-start | bytes 2097152 | tf_op jit(solution)/shard_map/all_to_all | solution.py:411
  52.8 3.4 %collective-permute-start.11 = (bf16[4,256,256]{2,1,0:T(8,128)(2,1)}, bf16[4,256,256]{2,1,0:T(8,128)(2,1)S(1)}, u32[]{:S(2)}, u32[]{:S(2)}) collective-permute-start(bf16[4,256,256]{2,1,0:T(8,128)(2,1)} %slice_bitcast_fusion), channel_id=1, source_target_pairs={{0,4},{4,0},{1,5},{5,1},{2,6},{6,2},{3,7},{7,3},{8,12},{12,8},{9,1... | collective-permute-start | bytes 1572872 | tf_op jit(solution)/shard_map/ppermute | solution.py:410
  56.3 15.1 %all-to-all-done.1.pairs = bf16[16,256,128]{2,1,0:T(8,128)(2,1)S(1)} async-done(((bf16[16,256,128]{2,1,0:T(8,128)(2,1)}), bf16[16,256,128]{2,1,0:T(8,128)(2,1)S(1)}, u32[]{:S(2)}, u32[]{:S(2)}) %all-to-all-start.1) | async-done | bytes 1048608 | tf_op jit(solution)/shard_map/all_to_all | solution.py:411
  71.4 0.1 fusion.4
  71.5 0.7 collective-permute-start.14
  72.2 10.0 %collective-permute-start.12 = (bf16[8,256,128]{2,1,0:T(8,128)(2,1)S(1)}, bf16[8,256,128]{2,1,0:T(8,128)(2,1)S(1)}, u32[]{:S(2)}, u32[]{:S(2)}) collective-permute-start(bf16[8,256,128]{2,1,0:T(8,128)(2,1)S(1)} %get-tuple-element.43), channel_id=1, source_target_pairs={{0,32},{32,64},{64,96},{1,33},{33,65},{65,97},{2,34},{34,66},{66,9... | collective-permute-start | bytes 1572872 | tf_op jit(solution)/shard_map/ppermute | solution.py:416
  82.2 2.1 %collective-permute-start.16 = (bf16[8,256,128]{2,1,0:T(8,128)(2,1)S(1)}, bf16[8,256,128]{2,1,0:T(8,128)(2,1)S(1)}, u32[]{:S(2)}, u32[]{:S(2)}) collective-permute-start(bf16[8,256,128]{2,1,0:T(8,128)(2,1)S(1)} %get-tuple-element.42), channel_id=1, source_target_pairs={{0,32},{32,64},{64,96},{1,33},{33,65},{65,97},{2,34},{34,66},{66,9... | collective-permute-start | bytes 1572872 | tf_op jit(solution)/shard_map/ppermute | solution.py:418
  84.3 0.0 collective-permute-done.11.crossed
  84.3 5.9 %shard_map.72 = (f32[4096,128]{1,0:T(8,128)S(1)}, f32[4096,128]{1,0:T(8,128)S(1)}) custom-call(s32[5]{0:T(128)S(1)} %copy-done.7, bf16[4,2,256,256]{3,2,1,0:T(8,128)(2,1)S(1)} %all-to-all-done.kept, bf16[4,256,256]{2,1,0:T(8,128)(2,1)S(1)} %collective-permute-done.11.crossed, bf16[16,256,128]{2,1,0:T(8,128)(2,1)S(1)} %all-to-all-done.1.pairs), custom_call_target="tpu_custom_call" | custom-call | flops 2415919104 | bytes 4194304 | tf_op jit(solution)/shard_map/pallas_call | solution.py:291
  90.2 0.0 collective-permute-done.14
  90.2 1.3 collective-permute-start.15
  91.5 3.0 %collective-permute-done.12.pairs = bf16[8,256,128]{2,1,0:T(8,128)(2,1)S(1)} collective-permute-done((bf16[8,256,128]{2,1,0:T(8,128)(2,1)S(1)}, bf16[8,256,128]{2,1,0:T(8,128)(2,1)S(1)}, u32[]{:S(2)}, u32[]{:S(2)}) %collective-permute-start.12) | collective-permute-done | bytes 524320 | tf_op jit(solution)/shard_map/ppermute | solution.py:416
  94.5 4.3 %collective-permute-start.13 = (bf16[8,256,128]{2,1,0:T(8,128)(2,1)S(1)}, bf16[8,256,128]{2,1,0:T(8,128)(2,1)S(1)}, u32[]{:S(2)}, u32[]{:S(2)}) collective-permute-start(bf16[8,256,128]{2,1,0:T(8,128)(2,1)S(1)} %collective-permute-done.12.pairs), channel_id=1, source_target_pairs={{32,64},{64,96},{33,65},{65,97},{34,66},{66,98},{35,67},{67,99},{3... | collective-permute-start | bytes 1572872 | tf_op jit(solution)/shard_map/ppermute | solution.py:419
  98.8 7.1 %shard_map.73 = (f32[4096,128]{1,0:T(8,128)S(1)}, f32[4096,128]{1,0:T(8,128)S(1)}) custom-call(s32[5]{0:T(128)S(1)} %copy-done.7, bf16[4,2,256,256]{3,2,1,0:T(8,128)(2,1)S(1)} %all-to-all-done.kept, bf16[4,256,256]{2,1,0:T(8,128)(2,1)S(1)} %collective-permute-done.11.crossed, ...), custom_call_target="tpu_custom_call", output_to_operand_aliasing={{0}: (4, {}), {1}: (5, {})} | custom-call | flops 2147483648 | bytes 4194304 | tf_op jit(solution)/shard_map/pallas_call | solution.py:291
  105.9 0.0 collective-permute-done.16.pairs
  105.9 7.1 %shard_map.74 = (f32[4096,128]{1,0:T(8,128)S(1)}, f32[4096,128]{1,0:T(8,128)S(1)}) custom-call(s32[5]{0:T(128)S(1)} %copy-done.7, bf16[4,2,256,256]{3,2,1,0:T(8,128)(2,1)S(1)} %all-to-all-done.kept, bf16[4,256,256]{2,1,0:T(8,128)(2,1)S(1)} %collective-permute-done.11.crossed, ...), custom_call_target="tpu_custom_call", output_to_operand_aliasing={{0}: (4, {}), {1}: (5, {})} | custom-call | flops 2147483648 | bytes 4194304 | tf_op jit(solution)/shard_map/pallas_call | solution.py:291
  113.0 0.0 collective-permute-done.15.pairs
  113.0 6.0 %shard_map.75 = (f32[4096,128]{1,0:T(8,128)S(1)}, f32[4096,128]{1,0:T(8,128)S(1)}) custom-call(s32[5]{0:T(128)S(1)} %copy-done.7, bf16[4,2,256,256]{3,2,1,0:T(8,128)(2,1)S(1)} %all-to-all-done.kept, bf16[4,256,256]{2,1,0:T(8,128)(2,1)S(1)} %collective-permute-done.11.crossed, ...), custom_call_target="tpu_custom_call", output_to_operand_aliasing={{0}: (4, {}), {1}: (5, {})} | custom-call | flops 1744830464 | bytes 4194304 | tf_op jit(solution)/shard_map/pallas_call | solution.py:291
  119.0 0.0 collective-permute-done.13.pairs
  119.0 3.8 %shard_map.76 = bf16[2048,256]{1,0:T(8,128)(2,1)} custom-call(s32[5]{0:T(128)S(1)} %copy-done.7, bf16[4,2,256,256]{3,2,1,0:T(8,128)(2,1)S(1)} %all-to-all-done.kept, bf16[4,256,256]{2,1,0:T(8,128)(2,1)S(1)} %collective-permute-done.11.crossed, bf16[8,256,128]{2,1,0:T(8,128)(2,1)S(1)} %collective-permute-done.13.pairs, ...), custom_call_target="tpu_custom_call" | custom-call | flops 671088640 | bytes 4194304 | tf_op jit(solution)/shard_map/pallas_call | solution.py:291
  122.8 3.7 %all-to-all-start.2 = ((bf16[8,256,256]{2,1,0:T(8,128)(2,1)}), bf16[8,256,256]{2,1,0:T(8,128)(2,1)S(1)}, u32[]{:S(2)}, u32[]{:S(2)}) async-start(bf16[8,256,256]{2,1,0:T(8,128)(2,1)} %bitcast.10), calls=%async_computation.2 | async-start | bytes 2097152 | tf_op jit(solution)/shard_map/all_to_all | solution.py:440
  126.6 0.1 collective-permute-start.10
  126.7 1.5 %collective-permute-done.10 = bf16[256,512]{1,0:T(8,128)(2,1)S(1)} collective-permute-done((bf16[256,512]{1,0:T(8,128)(2,1)S(1)}, bf16[256,512]{1,0:T(8,128)(2,1)S(1)}, u32[]{:S(2)}, u32[]{:S(2)}) %collective-permute-start.10) | collective-permute-done | bytes 262176 | tf_op jit(solution)/shard_map/ppermute | solution.py:49
  128.2 0.9 fusion
  129.1 13.2 %all-to-all-done.2.home = bf16[8,256,256]{2,1,0:T(8,128)(2,1)S(1)} async-done(((bf16[8,256,256]{2,1,0:T(8,128)(2,1)}), bf16[8,256,256]{2,1,0:T(8,128)(2,1)S(1)}, u32[]{:S(2)}, u32[]{:S(2)}) %all-to-all-start.2) | async-done | bytes 1048608 | tf_op jit(solution)/shard_map/all_to_all | solution.py:440
  142.4 2.1 %assemble.1 = bf16[256,2048]{1,0:T(8,128)(2,1)} custom-call(s32[5]{0:T(128)S(1)} %copy-done.7, bf16[8,256,256]{2,1,0:T(8,128)(2,1)S(1)} %all-to-all-done.2.home), custom_call_target="tpu_custom_call" | custom-call | tf_op jit(solution)/shard_map/assemble/pallas_call | solution.py:442
  (14 shorter events, 0.1 us)
Async XLA Ops:
  0.6 28.5 %collective-permute-start = (bf16[256,4608]{1,0:T(8,128)(2,1)}, bf16[256,4608]{1,0:T(8,128)(2,1)}, u32[]{:S(2)}, u32[]{:S(2)}) collective-permute-start(bf16[256,4608]{1,0:T(8,128)(2,1)} %bitcast.17), channel_id=1, source_target_pairs={{0,1},{1,0},{2,3},{3,2},{4,5},{5,4},{6,7},{7,6},{8,9},{9,8},{10,11... | collective-permute-start | bytes 7077896 | tf_op jit(solution)/shard_map/ppermute | solution.py:49
  0.7 28.5 %collective-permute-start.1 = (bf16[1152,1024]{1,0:T(8,128)(2,1)}, bf16[1152,1024]{1,0:T(8,128)(2,1)}, u32[]{:S(2)}, u32[]{:S(2)}) collective-permute-start(bf16[1152,1024]{1,0:T(8,128)(2,1)} %down.1), channel_id=1, source_target_pairs={{0,1},{1,0},{2,3},{3,2},{4,5},{5,4},{6,7},{7,6},{8,9},{9,8},{10,11... | collective-permute-start | bytes 7077896 | tf_op jit(solution)/shard_map/ppermute | solution.py:49
  6.8 6.6 %collective-permute-start.4 = (bf16[144,512]{1,0:T(8,128)(2,1)}, bf16[144,512]{1,0:T(8,128)(2,1)S(1)}, u32[]{:S(2)}, u32[]{:S(2)}) collective-permute-start(bf16[144,512]{1,0:T(8,128)(2,1)} %get-tuple-element.24), channel_id=1, source_target_pairs={{0,2},{1,7},{2,4},{3,1},{4,6},{5,3},{6,0},{7,5},{8,10},{9,15},{10,... | collective-permute-start | bytes 442376 | tf_op jit(solution)/shard_map/ppermute | solution.py:352
  8.4 5.1 %collective-permute-start.5 = (bf16[144,512]{1,0:T(8,128)(2,1)}, bf16[144,512]{1,0:T(8,128)(2,1)}, u32[]{:S(2)}, u32[]{:S(2)}) collective-permute-start(bf16[144,512]{1,0:T(8,128)(2,1)} %get-tuple-element.25), channel_id=1, source_target_pairs={{0,3},{1,6},{2,5},{3,0},{4,7},{5,2},{6,1},{7,4},{8,11},{9,14},{10,... | collective-permute-start | bytes 442376 | tf_op jit(solution)/shard_map/ppermute | solution.py:353
  8.4 25.3 %copy-start = (bf16[1,256,4608]{2,1,0:T(8,128)(2,1)S(1)}, bf16[1,256,4608]{2,1,0:T(8,128)(2,1)}, u32[]{:S(2)}) copy-start(bf16[1,256,4608]{2,1,0:T(8,128)(2,1)} %param.5) | copy-start | bytes 7077892
  8.4 24.4 %all-to-all-start = ((bf16[4,2,256,256]{3,2,1,0:T(8,128)(2,1)}), bf16[4,2,256,256]{3,2,1,0:T(8,128)(2,1)S(1)}, u32[]{:S(2)}, u32[]{:S(2)}) async-start(bf16[4,2,256,256]{3,2,1,0:T(8,128)(2,1)} %get-tuple-element.27), calls=%async_computation | async-start | bytes 2097152 | tf_op jit(solution)/shard_map/all_to_all | solution.py:363
  14.4 0.7 copy-start.2
  15.1 18.6 %copy-start.7 = (s32[5]{0:T(128)S(1)}, s32[5]{0:T(128)}, u32[]{:S(2)}) copy-start(s32[5]{0:T(128)} %stack.19.info) | copy-start | bytes 64
  15.1 8.7 %collective-permute-start.6 = (bf16[2,144,512]{2,1,0:T(8,128)(2,1)S(1)}, bf16[2,144,512]{2,1,0:T(8,128)(2,1)S(1)}, u32[]{:S(2)}, u32[]{:S(2)}) collective-permute-start(bf16[2,144,512]{2,1,0:T(8,128)(2,1)S(1)} %shard_map.70.relay_0), channel_id=1, source_target_pairs={{0,32},{32,64},{64,96},{96,0},{1,33},{33,65},{65,97},{97,1},{2,34}... | collective-permute-start | bytes 884744 | tf_op jit(solution)/shard_map/ppermute | solution.py:359
  16.8 23.3 %collective-permute-start.2 = (bf16[832,512]{1,0:T(8,128)(2,1)}, bf16[832,512]{1,0:T(8,128)(2,1)}, u32[]{:S(2)}, u32[]{:S(2)}) collective-permute-start(bf16[832,512]{1,0:T(8,128)(2,1)} %get-tuple-element.22), channel_id=1, source_target_pairs={{0,2},{1,7},{2,4},{3,1},{4,6},{5,3},{6,0},{7,5},{8,10},{9,15},{10,... | collective-permute-start | bytes 2555912 | tf_op jit(solution)/shard_map/ppermute | solution.py:354
  18.1 22.0 %collective-permute-start.3 = (bf16[832,512]{1,0:T(8,128)(2,1)}, bf16[832,512]{1,0:T(8,128)(2,1)}, u32[]{:S(2)}, u32[]{:S(2)}) collective-permute-start(bf16[832,512]{1,0:T(8,128)(2,1)} %get-tuple-element.23), channel_id=1, source_target_pairs={{0,3},{1,6},{2,5},{3,0},{4,7},{5,2},{6,1},{7,4},{8,11},{9,14},{10,... | collective-permute-start | bytes 2555912 | tf_op jit(solution)/shard_map/ppermute | solution.py:355
  23.9 0.7 copy-start.5
  24.6 15.5 %collective-permute-start.9 = (bf16[2,128,1024]{2,1,0:T(8,128)(2,1)}, bf16[2,128,1024]{2,1,0:T(8,128)(2,1)}, u32[]{:S(2)}, u32[]{:S(2)}) collective-permute-start(bf16[2,128,1024]{2,1,0:T(8,128)(2,1)} %up_own.1), channel_id=1, source_target_pairs={{0,1},{1,0},{2,3},{3,2},{4,5},{5,4},{6,7},{7,6},{8,9},{9,8},{10,11... | collective-permute-start | bytes 1572872 | tf_op jit(solution)/shard_map/ppermute | solution.py:49
  29.1 10.2 %collective-permute-start.7 = (bf16[2,144,512]{2,1,0:T(8,128)(2,1)}, bf16[2,144,512]{2,1,0:T(8,128)(2,1)}, u32[]{:S(2)}, u32[]{:S(2)}) collective-permute-start(bf16[2,144,512]{2,1,0:T(8,128)(2,1)} %copy-done.2), channel_id=1, source_target_pairs={{0,96},{32,0},{64,32},{96,64},{1,97},{33,1},{65,33},{97,65},{2,98}... | collective-permute-start | bytes 884744 | tf_op jit(solution)/shard_map/ppermute | solution.py:359
  29.3 10.8 %collective-permute-start.8 = (bf16[2,144,512]{2,1,0:T(8,128)(2,1)}, bf16[2,144,512]{2,1,0:T(8,128)(2,1)}, u32[]{:S(2)}, u32[]{:S(2)}) collective-permute-start(bf16[2,144,512]{2,1,0:T(8,128)(2,1)} %copy-done.2), channel_id=1, source_target_pairs={{0,64},{32,96},{64,0},{96,32},{1,65},{33,97},{65,1},{97,33},{2,66}... | collective-permute-start | bytes 884744 | tf_op jit(solution)/shard_map/ppermute | solution.py:359
  33.7 6.4 %copy-start.1 = (bf16[2,128,1024]{2,1,0:T(8,128)(2,1)S(1)}, bf16[2,128,1024]{2,1,0:T(8,128)(2,1)}, u32[]{:S(2)}) copy-start(bf16[2,128,1024]{2,1,0:T(8,128)(2,1)} %up_own.1) | copy-start | bytes 1572868
  33.7 6.4 %copy-start.3 = (bf16[2,144,512]{2,1,0:T(8,128)(2,1)S(1)}, bf16[2,144,512]{2,1,0:T(8,128)(2,1)}, u32[]{:S(2)}) copy-start(bf16[2,144,512]{2,1,0:T(8,128)(2,1)} %copy-done.2) | copy-start | bytes 884740
  33.7 6.4 %copy-start.4 = (f32[256,128]{1,0:T(8,128)S(1)}, f32[256,128]{1,0:T(8,128)}, u32[]{:S(2)}) copy-start(f32[256,128]{1,0:T(8,128)} %get-tuple-element.50.sine) | copy-start | bytes 393220
  33.7 6.4 %copy-start.6 = (bf16[2,144,512]{2,1,0:T(8,128)(2,1)S(1)}, bf16[2,144,512]{2,1,0:T(8,128)(2,1)}, u32[]{:S(2)}) copy-start(bf16[2,144,512]{2,1,0:T(8,128)(2,1)} %copy-done.5) | copy-start | bytes 884740
  46.2 25.2 %all-to-all-start.1 = ((bf16[16,256,128]{2,1,0:T(8,128)(2,1)}), bf16[16,256,128]{2,1,0:T(8,128)(2,1)S(1)}, u32[]{:S(2)}, u32[]{:S(2)}) async-start(bf16[16,256,128]{2,1,0:T(8,128)(2,1)} %get-tuple-element.30), calls=%async_computation.1 | async-start | bytes 2097152 | tf_op jit(solution)/shard_map/all_to_all | solution.py:411
  52.8 31.4 %collective-permute-start.11 = (bf16[4,256,256]{2,1,0:T(8,128)(2,1)}, bf16[4,256,256]{2,1,0:T(8,128)(2,1)S(1)}, u32[]{:S(2)}, u32[]{:S(2)}) collective-permute-start(bf16[4,256,256]{2,1,0:T(8,128)(2,1)} %slice_bitcast_fusion), channel_id=1, source_target_pairs={{0,4},{4,0},{1,5},{5,1},{2,6},{6,2},{3,7},{7,3},{8,12},{12,8},{9,1... | collective-permute-start | bytes 1572872 | tf_op jit(solution)/shard_map/ppermute | solution.py:410
  71.5 18.7 %collective-permute-start.14 = (bf16[8,256,128]{2,1,0:T(8,128)(2,1)S(1)}, bf16[8,256,128]{2,1,0:T(8,128)(2,1)S(1)}, u32[]{:S(2)}, u32[]{:S(2)}) collective-permute-start(bf16[8,256,128]{2,1,0:T(8,128)(2,1)S(1)} %get-tuple-element.42), channel_id=1, source_target_pairs={{32,0},{0,96},{33,1},{1,97},{34,2},{2,98},{35,3},{3,99},{36,4},{4,... | collective-permute-start | bytes 1572872 | tf_op jit(solution)/shard_map/ppermute | solution.py:417
  72.2 22.4 %collective-permute-start.12 = (bf16[8,256,128]{2,1,0:T(8,128)(2,1)S(1)}, bf16[8,256,128]{2,1,0:T(8,128)(2,1)S(1)}, u32[]{:S(2)}, u32[]{:S(2)}) collective-permute-start(bf16[8,256,128]{2,1,0:T(8,128)(2,1)S(1)} %get-tuple-element.43), channel_id=1, source_target_pairs={{0,32},{32,64},{64,96},{1,33},{33,65},{65,97},{2,34},{34,66},{66,9... | collective-permute-start | bytes 1572872 | tf_op jit(solution)/shard_map/ppermute | solution.py:416
  82.2 23.7 %collective-permute-start.16 = (bf16[8,256,128]{2,1,0:T(8,128)(2,1)S(1)}, bf16[8,256,128]{2,1,0:T(8,128)(2,1)S(1)}, u32[]{:S(2)}, u32[]{:S(2)}) collective-permute-start(bf16[8,256,128]{2,1,0:T(8,128)(2,1)S(1)} %get-tuple-element.42), channel_id=1, source_target_pairs={{0,32},{32,64},{64,96},{1,33},{33,65},{65,97},{2,34},{34,66},{66,9... | collective-permute-start | bytes 1572872 | tf_op jit(solution)/shard_map/ppermute | solution.py:418
  90.2 22.8 %collective-permute-start.15 = (bf16[8,256,128]{2,1,0:T(8,128)(2,1)S(1)}, bf16[8,256,128]{2,1,0:T(8,128)(2,1)S(1)}, u32[]{:S(2)}, u32[]{:S(2)}) collective-permute-start(bf16[8,256,128]{2,1,0:T(8,128)(2,1)S(1)} %collective-permute-done.14), channel_id=1, source_target_pairs={{0,96},{96,64},{1,97},{97,65},{2,98},{98,66},{3,99},{99,67},{4,100... | collective-permute-start | bytes 1572872 | tf_op jit(solution)/shard_map/ppermute | solution.py:424
  94.5 24.5 %collective-permute-start.13 = (bf16[8,256,128]{2,1,0:T(8,128)(2,1)S(1)}, bf16[8,256,128]{2,1,0:T(8,128)(2,1)S(1)}, u32[]{:S(2)}, u32[]{:S(2)}) collective-permute-start(bf16[8,256,128]{2,1,0:T(8,128)(2,1)S(1)} %collective-permute-done.12.pairs), channel_id=1, source_target_pairs={{32,64},{64,96},{33,65},{65,97},{34,66},{66,98},{35,67},{67,99},{3... | collective-permute-start | bytes 1572872 | tf_op jit(solution)/shard_map/ppermute | solution.py:419
  122.8 3.7 %copy-start.8 = (bf16[512,512]{1,0:T(8,128)(2,1)S(1)}, bf16[512,512]{1,0:T(8,128)(2,1)}, u32[]{:S(2)}) copy-start(bf16[512,512]{1,0:T(8,128)(2,1)} %get-tuple-element.26) | copy-start | bytes 1572868
  122.8 19.5 %all-to-all-start.2 = ((bf16[8,256,256]{2,1,0:T(8,128)(2,1)}), bf16[8,256,256]{2,1,0:T(8,128)(2,1)S(1)}, u32[]{:S(2)}, u32[]{:S(2)}) async-start(bf16[8,256,256]{2,1,0:T(8,128)(2,1)} %bitcast.10), calls=%async_computation.2 | async-start | bytes 2097152 | tf_op jit(solution)/shard_map/all_to_all | solution.py:440
  126.6 1.6 %collective-permute-start.10 = (bf16[256,512]{1,0:T(8,128)(2,1)S(1)}, bf16[256,512]{1,0:T(8,128)(2,1)S(1)}, u32[]{:S(2)}, u32[]{:S(2)}) collective-permute-start(bf16[256,512]{1,0:T(8,128)(2,1)S(1)} %get-tuple-element.45), channel_id=1, source_target_pairs={{0,1},{1,0},{2,3},{3,2},{4,5},{5,4},{6,7},{7,6},{8,9},{9,8},{10,11... | collective-permute-start | bytes 786440 | tf_op jit(solution)/shard_map/ppermute | solution.py:49

commit v5 on v4

--- a/solution.py
+++ b/solution.py
@@ -16,8 +16,8 @@
 CHUNK = 2048
 KV_HEADS = 8
 BLOCKS = CHUNK // BLOCK
-LOW = 4
-GRANT = {"collect": 60, "half": 49, "project": 46}
+LOW, TOP, MIDDLE = 3, 5, 6
+GRANT = {"first": 60, "collect": 60, "half": 49, "project": 46}
 RELAYED = 576
 SIZES = {"z": 4, "y": 4, "xh": 2, "xl": 2, "core": 2}
 SEQ_AXES = ("z", "y", "xh")
@@ -65,16 +65,24 @@
     return pl.ds(pl.multiple_of(index * size, size), size)
 
 
-def collect_kernel(info, down, up, queries, relay_a, relay_b, direct_a, direct_b, sent, sems):
+def first_kernel(info, down, relay_a, relay_b, sems):
     share, rank = relay_a.shape
+    split = down.shape[0] - 4 * share
+    rows = pl.ds(pl.multiple_of(split + share * info[1], 16), share)
+    moves = []
+    for flip, relay in ((0, relay_a), (1, relay_b)):
+        moves.append((down.at[rows, chunk((info[0] ^ flip) % 2, rank)], relay))
+    finish(begin(sems, *moves))
+
+
+def collect_kernel(info, down, up, queries, direct_a, direct_b, sent, sems):
+    rank = direct_a.shape[1]
     piece = up.shape[1]
-    split = down.shape[0] - 4 * share
-    first = pl.ds(pl.multiple_of(split + share * info[1], 16), share)
+    split = direct_a.shape[0] - 2 * piece
     moves = []
-    for flip, relay, direct in ((0, relay_a, direct_a), (1, relay_b, direct_b)):
+    for flip, direct in ((0, direct_a), (1, direct_b)):
         which = (info[0] ^ flip) % 2
         columns = chunk(which, rank)
-        moves.append((down.at[first, columns], relay))
         moves.append((down.at[pl.ds(0, split), columns], direct.at[pl.ds(0, split)]))
         for k in range(2):
             at = pl.ds(split + k * piece, piece)
@@ -225,57 +233,85 @@
         )
 
 
-def near_kernel(group, info, kept, crossed, pairs, numer_in, denom_in, numer, denom):
+def two_blocks(info, queries, pair):
+    return jnp.concatenate(
+        [stacked_rows(info, queries, pair, 0), stacked_rows(info, queries, pair, 1)], axis=0
+    )
+
+
+def pair_rows(pair):
+    return chunk(pair, 4 * BLOCK)
+
+
+def near_kernel(info, kept, crossed, pairs, numer_in, denom_in, numer, denom):
     blocks = [(j, None) for j in range(pairs.shape[0] // 2)]
 
     @pl.when(info[1] >= 1)
     def _():
         def step(t, carry):
-            for u in range(group):
-                i = t * group + u
-                stacked = stacked_rows(
-                    info, (kept, crossed), t * (group // 2) + u // 2, u % 2
-                )
-                n, d = over_blocks(stacked, pairs, blocks)
-                numer[state_rows(i), :] += n
-                denom[state_rows(i), :] += d
+            for u in range(2):
+                pair = 2 * t + u
+                n, d = over_blocks(two_blocks(info, (kept, crossed), pair), pairs, blocks)
+                numer[pair_rows(pair), :] += n
+                denom[pair_rows(pair), :] += d
             return carry
 
-        lax.fori_loop(0, BLOCKS // group, step, 0)
-
-
-def far_kernel(first, last, info, kept, crossed, pairs, numer_in, denom_in, *outs):
-    end = first + pairs.shape[0] // 2
-    mask = triangle(False)
-    numer, denom = (numer_in, denom_in) if last else outs
-
-    def settle(i, n, d):
-        if last:
-            n = n / jnp.sum(d, axis=1, keepdims=True)
-            outs[0][i * BLOCK : (i + 1) * BLOCK, :] = jnp.concatenate(
-                [n[:BLOCK], n[BLOCK:]], axis=1
+        lax.fori_loop(0, BLOCKS // 4, step, 0)
+
+
+def far_kernel(pieces, last, info, kept, crossed, *refs):
+    inputs, refs = refs[: len(pieces)], refs[len(pieces) :]
+    if last:
+        numer, denom, out = refs
+    else:
+        _, _, numer, denom = refs
+    single = triangle(False)
+    row = lax.broadcasted_iota(jnp.int32, (4 * BLOCK, BLOCK), 0)
+    col = lax.broadcasted_iota(jnp.int32, (4 * BLOCK, BLOCK), 1)
+    double = (row < 2 * BLOCK) | (col > row % BLOCK)
+
+    def settle(pair, n, d):
+        at = pair_rows(pair)
+        if not last:
+            numer[at, :], denom[at, :] = n, d
+            return
+        result = n / jnp.sum(d, axis=1, keepdims=True)
+        for k in range(2):
+            own = result[2 * k * BLOCK : 2 * (k + 1) * BLOCK]
+            out[chunk(2 * pair + k, BLOCK), :] = jnp.concatenate(
+                [own[:BLOCK], own[BLOCK:]], axis=1
             ).astype(jnp.bfloat16)
-        else:
-            numer[state_rows(i), :], denom[state_rows(i), :] = n, d
 
     @pl.when(info[1] >= 2)
     def _():
-        for i in range(BLOCKS):
-            blocks = [(j - first, mask if j == i else None) for j in range(max(i, first), end)]
-            old_n, old_d = numer[state_rows(i), :], denom[state_rows(i), :]
-            if blocks:
-                stacked = stacked_rows(info, (kept, crossed), i // 2, i % 2)
-                n, d = over_blocks(stacked, pairs, blocks)
-                settle(i, old_n + n, old_d + d)
-            elif last:
-                settle(i, old_n, old_d)
+        for pair in range(BLOCKS // 2):
+            i = 2 * pair
+            n, d = numer[pair_rows(pair), :], denom[pair_rows(pair), :]
+            touched = False
+            for ref, (first, end) in zip(inputs, pieces):
+                shared = [
+                    (j - first, double if j == i + 1 else None)
+                    for j in range(max(i + 1, first), end)
+                ]
+                if shared:
+                    more = over_blocks(two_blocks(info, (kept, crossed), pair), ref, shared)
+                    n, d, touched = n + more[0], d + more[1], True
+                if first <= i < end:
+                    own = stacked_rows(info, (kept, crossed), pair, 0)
+                    more = over_blocks(own, ref, [(i - first, single)])
+                    rest = jnp.zeros((2 * BLOCK, HEAD), jnp.float32)
+                    n = n + jnp.concatenate([more[0], rest], axis=0)
+                    d = d + jnp.concatenate([more[1], rest], axis=0)
+                    touched = True
+            if touched or last:
+                settle(pair, n, d)
 
     if last:
 
         @pl.when(info[1] < 2)
         def _():
-            for i in range(BLOCKS):
-                settle(i, numer[state_rows(i), :], denom[state_rows(i), :])
+            for pair in range(BLOCKS // 2):
+                settle(pair, numer[pair_rows(pair), :], denom[pair_rows(pair), :])
 
 
 IN_VMEM = pl.BlockSpec(memory_space=pltpu.VMEM)
@@ -287,13 +323,13 @@
 
 def attention_call(kernel, count, args, result=False, resume=True):
     single = BLOCK * 2 * BLOCK
-    inputs = [IN_SMEM] + [IN_VMEM] * (5 if resume else 3)
+    state = len(args) - 2
     return pl.pallas_call(
         kernel,
         out_shape=RESULT if result else (STATE, STATE),
-        in_specs=inputs,
+        in_specs=[IN_SMEM] + [IN_VMEM] * (len(args) - 1),
         out_specs=IN_VMEM if result else (IN_VMEM, IN_VMEM),
-        input_output_aliases={4: 0, 5: 1} if resume and not result else {},
+        input_output_aliases={state: 0, state + 1: 1} if resume and not result else {},
         compiler_params=pltpu.CompilerParams(vmem_limit_bytes=12 * 2**20),
         cost_estimate=pl.CostEstimate(
             flops=count * single * 4 * HEAD, bytes_accessed=2**22, transcendentals=2 * count * single
@@ -339,14 +375,22 @@
         )
 
     sems = pltpu.SemaphoreType.DMA
-    relay_a, relay_b, direct_a, direct_b, sent = step(
+    relay_a, relay_b = step(
+        "first",
+        first_kernel,
+        (shape(share, rank),) * 2,
+        [IN_SMEM, ANYWHERE],
+        (IN_VMEM,) * 2,
+        [sems((2,))],
+        10**7,
+    )(info, down_weight)
+    direct_a, direct_b, sent = step(
         "collect",
         collect_kernel,
-        (shape(share, rank),) * 2 + (shape(split + 2 * piece, rank),) * 2
-        + (shape(4, 2, rows, PAIR),),
+        (shape(split + 2 * piece, rank),) * 2 + (shape(4, 2, rows, PAIR),),
         [IN_SMEM] + [ANYWHERE] * 3,
-        (IN_VMEM,) * 5,
-        [sems((16,))],
+        (IN_VMEM,) * 3,
+        [sems((14,))],
         10**8,
     )(info, down_weight, up_weight, queries[0])
     relay_a = lax.ppermute(relay_a, X_AXES, forward)
@@ -411,29 +455,32 @@
     own_pairs = lax.all_to_all(pairs, PLANE + ("core",), 0, 0, tiled=True)
     other_half = to_partner(latent[rows:])
 
-    low = 2 * LOW
-    up = [(0, 1), (1, 2), (2, 3)]
-    near_low = lax.ppermute(own_pairs[:low], "z", up)
-    passing = lax.ppermute(own_pairs[low:], "z", [(1, 0), (0, 3)])
-    near_high = lax.ppermute(own_pairs[low:], "z", up)
+    def part(first, end):
+        return own_pairs[2 * first : 2 * end]
+
+    up, down, on = [(0, 1), (1, 2), (2, 3)], [(1, 0), (0, 3)], [(0, 3), (3, 2)]
+    passing_2 = lax.ppermute(part(TOP, BLOCKS), "z", down)
+    near_low = lax.ppermute(part(0, LOW), "z", up)
+    passing_1 = lax.ppermute(part(LOW, TOP), "z", down)
+    near_mid = lax.ppermute(part(LOW, MIDDLE), "z", up)
+    near_high = lax.ppermute(part(MIDDLE, BLOCKS), "z", up)
     far_low = lax.ppermute(near_low, "z", [(1, 2), (2, 3)])
 
     common = (info, sent, crossed_queries)
     state = attention_call(own_kernel, 36, (*common, own_pairs), resume=False)
-    passing, state = lax.optimization_barrier((passing, state))
-    far_high = lax.ppermute(passing, "z", [(0, 3), (3, 2)])
-    for piece_pairs in (near_low, near_high):
-        state = attention_call(
-            functools.partial(near_kernel, 4),
-            piece_pairs.shape[0] // 2 * BLOCKS,
-            (*common, piece_pairs, *state),
-        )
+    passing_2, state = lax.optimization_barrier((passing_2, state))
+    far_2 = lax.ppermute(passing_2, "z", on)
+    state = attention_call(near_kernel, 8 * LOW, (*common, near_low, *state))
+    passing_1, state = lax.optimization_barrier((passing_1, state))
+    far_1 = lax.ppermute(passing_1, "z", on)
+    state = attention_call(near_kernel, 24, (*common, near_mid, *state))
+    state = attention_call(near_kernel, 16, (*common, near_high, *state))
+    pieces = ((TOP, BLOCKS), (LOW, TOP))
     state = attention_call(
-        functools.partial(far_kernel, LOW, False), 26,
-        (*common, far_high, *state),
+        functools.partial(far_kernel, pieces, False), 30, (*common, far_2, far_1, *state)
     )
     result = attention_call(
-        functools.partial(far_kernel, 0, True), 10,
+        functools.partial(far_kernel, ((0, LOW),), True), 6,
         (*common, far_low, *state), result=True,
     )
 

time: 145 us -> 145 us (level)
  starting transfers between devices: 48.8 us -> 44.4 us
  waiting for transfers between devices: 39.6 us -> 43.3 us
    ppermute x3, waiting for transfers between devices: 6.12 us -> 10.1 us  [body(): relays = [lax.ppermute(relay_own, 'z', ring(k)) for k in (1, -1, 2)]]
    ppermute x3, starting transfers between devices: 5.31 us -> 2.03 us  [body(): relays = [lax.ppermute(relay_own, 'z', ring(k)) for k in (1, -1, 2)]]
    ppermute x4 -> x7, waiting for transfers between devices: 3.05 us -> 5.24 us  [the longest x1 5.23 us: body(): near_low = lax.ppermute(part(0, LOW), 'z', up)]
    pallas_call x1 -> x2, Pallas kernels: 4.27 us -> 6.43 us  [the longest x1 4.03 us: body(): step('collect', collect_kernel, (shape(split + 2 * piece, rank),) * 2 + (...]
    all_to_all x1, waiting for transfers between devices: 13.2 us -> 11.4 us  [body(): lax.all_to_all(result.reshape(groups, rows, PAIR), PLANE, 0, 0, tiled=True)]
    ppermute x4 -> x7, starting transfers between devices: 14.1 us -> 12.6 us  [the longest x1 4.67 us: body(): near_mid = lax.ppermute(part(LOW, MIDDLE), 'z', up)]
    pallas_call x5 -> x6, Pallas kernels: 29.8 us -> 28.5 us  [attention_call(): pl.pallas_call(kernel, out_shape=RESULT if result else (STATE, STATE), in...]
  transfers between devices with their start and end apart: 20 -> 23, of which waited for: 8 -> 7; matrix products, arithmetic and copies ran while one was open for 4% -> 4% of each run, Pallas kernels for 24% -> 26%
where the time goes in v5:
time: 145 us
  Pallas kernels  48.2 us (33%)
  starting transfers between devices  44.4 us (31%)
  waiting for transfers between devices  43.3 us (30%)
  other arithmetic  4.13 us (3%)
  local copies, waits for them, and re-layouts  3.14 us (2%)
  between operations  1.65 us (1%)
    pallas_call x6, Pallas kernels, attention_call(): pl.pallas_call(kernel, out_shape=RESULT if result else (STATE, STATE), in...  28.5 us
    all_to_all x1, waiting for transfers between devices, body(): own_pairs = lax.all_to_all(pairs, PLANE + ('core',), 0, 0, tiled=True)  15 us
    all_to_all x1, waiting for transfers between devices, body(): lax.all_to_all(result.reshape(groups, rows, PAIR), PLANE, 0, 0, tiled=True)  11.4 us
    ppermute x3, waiting for transfers between devices, body(): relays = [lax.ppermute(relay_own, 'z', ring(k)) for k in (1, -1, 2)]  10.1 us
    all_to_all x1, starting transfers between devices, body(): own_pairs = lax.all_to_all(pairs, PLANE + ('core',), 0, 0, tiled=True)  6.91 us
    pallas_call x1, Pallas kernels, body(): step('project', project_kernel, (pltpu.HBM((2 * rows, rank), jnp.bfloat16...  5.98 us
    ppermute x1, waiting for transfers between devices, body(): near_low = lax.ppermute(part(0, LOW), 'z', up)  5.23 us
    ppermute x1, starting transfers between devices, body(): far_low = lax.ppermute(near_low, 'z', [(1, 2), (2, 3)])  5.02 us
  transfers between devices with their start and end apart: 23, of which 7 were waited for; matrix products, arithmetic and copies ran while one was open for 4% of the time, Pallas kernels for 26%

profile of v5, /device:TPU:64, one launch (start us, length us, event | category | flops | bytes accessed | tf_op | source)
XLA Modules:
  0.0 144.8 jit_solution(17030804944693889459)
XLA Ops:
  0.6 0.1 collective-permute-start
  0.7 0.5 collective-permute-start.1
  1.9 0.6 stack.19.info
  2.5 2.4 %shard_map.70 = (bf16[144,512]{1,0:T(8,128)(2,1)}, bf16[144,512]{1,0:T(8,128)(2,1)}) custom-call(s32[5]{0:T(128)} %stack.19.info, bf16[1152,1024]{1,0:T(8,128)(2,1)} %down.3), custom_call_target="tpu_custom_call" | custom-call | flops 10000000 | bytes 4194304 | tf_op jit(solution)/shard_map/pallas_call | solution.py:378
  4.9 1.6 %collective-permute-start.4 = (bf16[144,512]{1,0:T(8,128)(2,1)}, bf16[144,512]{1,0:T(8,128)(2,1)S(1)}, u32[]{:S(2)}, u32[]{:S(2)}) collective-permute-start(bf16[144,512]{1,0:T(8,128)(2,1)} %get-tuple-element.29), channel_id=1, source_target_pairs={{0,2},{1,7},{2,4},{3,1},{4,6},{5,3},{6,0},{7,5},{8,10},{9,15},{10,... | collective-permute-start | bytes 442376 | tf_op jit(solution)/shard_map/ppermute | solution.py:396
  6.5 0.0 collective-permute-start.5
  6.5 4.0 %shard_map.69 = (bf16[832,512]{1,0:T(8,128)(2,1)}, bf16[832,512]{1,0:T(8,128)(2,1)}, bf16[4,2,256,256]{3,2,1,0:T(8,128)(2,1)}) custom-call(s32[5]{0:T(128)} %stack.19.info, bf16[1152,1024]{1,0:T(8,128)(2,1)} %down.3, bf16[2,128,1024]{2,1,0:T(8,128)(2,1)} %up_own.1, bf16[256,2048]{1,0:T(8,128)(2,1)} %bitcast.21), custom_call_target="tpu_custom_call" | custom-call | flops 100000000 | bytes 4194304 | tf_op jit(solution)/shard_map/pallas_call | solution.py:387
  10.5 0.0 copy-start
  10.5 4.6 %all-to-all-start = ((bf16[4,2,256,256]{3,2,1,0:T(8,128)(2,1)}), bf16[4,2,256,256]{3,2,1,0:T(8,128)(2,1)S(1)}, u32[]{:S(2)}, u32[]{:S(2)}) async-start(bf16[4,2,256,256]{3,2,1,0:T(8,128)(2,1)} %get-tuple-element.32), calls=%async_computation | async-start | bytes 2097152 | tf_op jit(solution)/shard_map/all_to_all | solution.py:407
  15.1 0.0 collective-permute-done.4.a
  15.1 0.0 collective-permute-done.5.b
  15.1 0.9 shard_map.71.relay_0
  16.1 0.0 copy-start.2
  16.1 0.7 copy-done.2
  16.8 0.0 collective-permute-start.8
  16.8 1.5 %collective-permute-start.2 = (bf16[832,512]{1,0:T(8,128)(2,1)}, bf16[832,512]{1,0:T(8,128)(2,1)}, u32[]{:S(2)}, u32[]{:S(2)}) collective-permute-start(bf16[832,512]{1,0:T(8,128)(2,1)} %get-tuple-element.27), channel_id=1, source_target_pairs={{0,2},{1,7},{2,4},{3,1},{4,6},{5,3},{6,0},{7,5},{8,10},{9,15},{10,... | collective-permute-start | bytes 2555912 | tf_op jit(solution)/shard_map/ppermute | solution.py:398
  18.3 1.4 collective-permute-start.3
  19.7 7.8 %collective-permute-done.8.relay_3 = bf16[2,144,512]{2,1,0:T(8,128)(2,1)S(1)} collective-permute-done((bf16[2,144,512]{2,1,0:T(8,128)(2,1)S(1)}, bf16[2,144,512]{2,1,0:T(8,128)(2,1)S(1)}, u32[]{:S(2)}, u32[]{:S(2)}) %collective-permute-start.8) | collective-permute-done | bytes 294944 | tf_op jit(solution)/shard_map/ppermute | solution.py:403
  27.6 0.7 copy-done.5
  28.3 0.8 collective-permute-start.9
  29.1 1.3 fusion.1
  30.4 1.9 %maximum_select_fusion.1 = (f32[256,128]{1,0:T(8,128)S(1)}, f32[256,128]{1,0:T(8,128)}) fusion(f32[256,64]{1,0:T(8,128)} %get-tuple-element.61, pred[]{:T(512)S(6)} %eq.2, f32[256,64]{1,0:T(8,128)} %get-tuple-element.60, f32[256,64]{1,0:T(8,128)} %get-tuple-element.59), kind=kLoop, calls=%fused_computation.6 | loop fusion | flops 131072 | bytes 458753 | tf_op jit(solution)/shard_map/jit(_where)/select_n | solution.py:415
  32.3 0.0 collective-permute-done.partner
  32.3 0.1 collective-permute-start.7
  32.4 0.0 collective-permute-done.1.weight_1
  32.4 1.9 %collective-permute-start.6 = (bf16[2,144,512]{2,1,0:T(8,128)(2,1)}, bf16[2,144,512]{2,1,0:T(8,128)(2,1)}, u32[]{:S(2)}, u32[]{:S(2)}) collective-permute-start(bf16[2,144,512]{2,1,0:T(8,128)(2,1)} %copy-done.2), channel_id=1, source_target_pairs={{0,32},{32,64},{64,96},{96,0},{1,33},{33,65},{65,97},{97,1},{2,34}... | collective-permute-start | bytes 884744 | tf_op jit(solution)/shard_map/ppermute | solution.py:403
  34.3 0.0 all-to-all-done.kept
  34.3 0.8 slice_bitcast_fusion
  35.2 4.2 %shard_map.68.partial = f32[512,512]{1,0:T(8,128)S(1)} custom-call(s32[5]{0:T(128)S(1)} %copy-done.7, bf16[256,4608]{1,0:T(8,128)(2,1)S(1)} %bitcast.18, bf16[256,4608]{1,0:T(8,128)(2,1)} %collective-permute-done.partner, bf16[1152,1024]{1,0:T(8,128)(2,1)} %down.3, bf16[1152,1024]{1,0:T(8,128)(2,1)} %collective-permute-done.1.weight_1), custom_call_target="tpu_custom_call" | custom-call | flops 1207959552 | bytes 4194304 | tf_op jit(solution)/shard_map/pallas_call | solution.py:419
  39.4 2.1 %collective-permute-done.7.relay_2 = bf16[2,144,512]{2,1,0:T(8,128)(2,1)} collective-permute-done((bf16[2,144,512]{2,1,0:T(8,128)(2,1)}, bf16[2,144,512]{2,1,0:T(8,128)(2,1)}, u32[]{:S(2)}, u32[]{:S(2)}) %collective-permute-start.7) | collective-permute-done | bytes 294944 | tf_op jit(solution)/shard_map/ppermute | solution.py:403
  41.5 0.1 collective-permute-done.6.relay_1
  41.6 0.0 collective-permute-done.9.up_partner
  41.7 6.0 %shard_map.72 = (bf16[512,512]{1,0:T(8,128)(2,1)}, bf16[16,256,128]{2,1,0:T(8,128)(2,1)}) custom-call(s32[5]{0:T(128)S(1)} %copy-done.7, f32[512,512]{1,0:T(8,128)S(1)} %shard_map.68.partial, bf16[256,4608]{1,0:T(8,128)(2,1)S(1)} %bitcast.19, bf16[256,4608]{1,0:T(8,128)(2,1)} %collective-permute-done.partner, ...), custom_call_target="tpu_custom_call" | custom-call | flops 1207959552 | bytes 4194304 | tf_op jit(solution)/shard_map/pallas_call | solution.py:429
  47.7 6.9 %all-to-all-start.1 = ((bf16[16,256,128]{2,1,0:T(8,128)(2,1)}), bf16[16,256,128]{2,1,0:T(8,128)(2,1)S(1)}, u32[]{:S(2)}, u32[]{:S(2)}) async-start(bf16[16,256,128]{2,1,0:T(8,128)(2,1)} %get-tuple-element.35), calls=%async_computation.1 | async-start | bytes 2097152 | tf_op jit(solution)/shard_map/all_to_all | solution.py:455
  54.6 3.5 %collective-permute-start.11 = (bf16[4,256,256]{2,1,0:T(8,128)(2,1)S(1)}, bf16[4,256,256]{2,1,0:T(8,128)(2,1)S(1)}, u32[]{:S(2)}, u32[]{:S(2)}) collective-permute-start(bf16[4,256,256]{2,1,0:T(8,128)(2,1)S(1)} %copy-done.9), channel_id=1, source_target_pairs={{0,4},{4,0},{1,5},{5,1},{2,6},{6,2},{3,7},{7,3},{8,12},{12,8},{9,1... | collective-permute-start | bytes 1572872 | tf_op jit(solution)/shard_map/ppermute | solution.py:454
  58.1 15.0 %all-to-all-done.1.pairs = bf16[16,256,128]{2,1,0:T(8,128)(2,1)S(1)} async-done(((bf16[16,256,128]{2,1,0:T(8,128)(2,1)}), bf16[16,256,128]{2,1,0:T(8,128)(2,1)S(1)}, u32[]{:S(2)}, u32[]{:S(2)}) %all-to-all-start.1) | async-done | bytes 1048608 | tf_op jit(solution)/shard_map/all_to_all | solution.py:455
  73.1 0.1 fusion.4
  73.3 4.7 %collective-permute-start.19 = (bf16[6,256,128]{2,1,0:T(8,128)(2,1)S(1)}, bf16[6,256,128]{2,1,0:T(8,128)(2,1)S(1)}, u32[]{:S(2)}, u32[]{:S(2)}) collective-permute-start(bf16[6,256,128]{2,1,0:T(8,128)(2,1)S(1)} %get-tuple-element.52), channel_id=1, source_target_pairs={{0,32},{32,64},{64,96},{1,33},{33,65},{65,97},{2,34},{34,66},{66,9... | collective-permute-start | bytes 1179656 | tf_op jit(solution)/shard_map/ppermute | solution.py:465
  78.0 0.7 collective-permute-start.14
  78.7 1.9 %collective-permute-start.12 = (bf16[6,256,128]{2,1,0:T(8,128)(2,1)S(1)}, bf16[6,256,128]{2,1,0:T(8,128)(2,1)S(1)}, u32[]{:S(2)}, u32[]{:S(2)}) collective-permute-start(bf16[6,256,128]{2,1,0:T(8,128)(2,1)S(1)} %get-tuple-element.54), channel_id=1, source_target_pairs={{0,32},{32,64},{64,96},{1,33},{33,65},{65,97},{2,34},{34,66},{66,9... | collective-permute-start | bytes 1179656 | tf_op jit(solution)/shard_map/ppermute | solution.py:463
  80.6 1.9 %collective-permute-start.18 = (bf16[4,256,128]{2,1,0:T(8,128)(2,1)S(1)}, bf16[4,256,128]{2,1,0:T(8,128)(2,1)S(1)}, u32[]{:S(2)}, u32[]{:S(2)}) collective-permute-start(bf16[4,256,128]{2,1,0:T(8,128)(2,1)S(1)} %get-tuple-element.55), channel_id=1, source_target_pairs={{0,32},{32,64},{64,96},{1,33},{33,65},{65,97},{2,34},{34,66},{66,9... | collective-permute-start | bytes 786440 | tf_op jit(solution)/shard_map/ppermute | solution.py:466
  82.6 0.0 collective-permute-done.11.crossed
  82.6 0.9 collective-permute-start.16
  83.4 5.9 %shard_map.73 = (f32[4096,128]{1,0:T(8,128)S(1)}, f32[4096,128]{1,0:T(8,128)S(1)}) custom-call(s32[5]{0:T(128)S(1)} %copy-done.7, bf16[4,2,256,256]{3,2,1,0:T(8,128)(2,1)S(1)} %all-to-all-done.kept, bf16[4,256,256]{2,1,0:T(8,128)(2,1)S(1)} %collective-permute-done.11.crossed, bf16[16,256,128]{2,1,0:T(8,128)(2,1)S(1)} %all-to-all-done.1.pairs), custom_call_target="tpu_custom_call" | custom-call | flops 2415919104 | bytes 4194304 | tf_op jit(solution)/shard_map/pallas_call | solution.py:327
  89.4 1.3 collective-permute-start.15
  90.7 5.2 %collective-permute-done.12.pairs = bf16[6,256,128]{2,1,0:T(8,128)(2,1)S(1)} collective-permute-done((bf16[6,256,128]{2,1,0:T(8,128)(2,1)S(1)}, bf16[6,256,128]{2,1,0:T(8,128)(2,1)S(1)}, u32[]{:S(2)}, u32[]{:S(2)}) %collective-permute-start.12) | collective-permute-done | bytes 393248 | tf_op jit(solution)/shard_map/ppermute | solution.py:463
  95.9 5.2 %shard_map.74 = (f32[4096,128]{1,0:T(8,128)S(1)}, f32[4096,128]{1,0:T(8,128)S(1)}) custom-call(s32[5]{0:T(128)S(1)} %copy-done.7, bf16[4,2,256,256]{3,2,1,0:T(8,128)(2,1)S(1)} %all-to-all-done.kept, bf16[4,256,256]{2,1,0:T(8,128)(2,1)S(1)} %collective-permute-done.11.crossed, ...), custom_call_target="tpu_custom_call", output_to_operand_aliasing={{0}: (4, {}), {1}: (5, {})} | custom-call | flops 1610612736 | bytes 4194304 | tf_op jit(solution)/shard_map/pallas_call | solution.py:327
  101.0 0.0 collective-permute-done.16
  101.1 1.3 collective-permute-start.17
  102.4 5.0 %collective-permute-start.13 = (bf16[6,256,128]{2,1,0:T(8,128)(2,1)S(1)}, bf16[6,256,128]{2,1,0:T(8,128)(2,1)S(1)}, u32[]{:S(2)}, u32[]{:S(2)}) collective-permute-start(bf16[6,256,128]{2,1,0:T(8,128)(2,1)S(1)} %collective-permute-done.12.pairs), channel_id=1, source_target_pairs={{32,64},{64,96},{33,65},{65,97},{34,66},{66,98},{35,67},{67,99},{3... | collective-permute-start | bytes 1179656 | tf_op jit(solution)/shard_map/ppermute | solution.py:467
  107.4 0.0 collective-permute-done.19.pairs
  107.4 5.2 %shard_map.75 = (f32[4096,128]{1,0:T(8,128)S(1)}, f32[4096,128]{1,0:T(8,128)S(1)}) custom-call(s32[5]{0:T(128)S(1)} %copy-done.7, bf16[4,2,256,256]{3,2,1,0:T(8,128)(2,1)S(1)} %all-to-all-done.kept, bf16[4,256,256]{2,1,0:T(8,128)(2,1)S(1)} %collective-permute-done.11.crossed, ...), custom_call_target="tpu_custom_call", output_to_operand_aliasing={{0}: (4, {}), {1}: (5, {})} | custom-call | flops 1610612736 | bytes 4194304 | tf_op jit(solution)/shard_map/pallas_call | solution.py:327
  112.6 0.0 collective-permute-done.18.pairs
  112.6 3.8 %shard_map.76 = (f32[4096,128]{1,0:T(8,128)S(1)}, f32[4096,128]{1,0:T(8,128)S(1)}) custom-call(s32[5]{0:T(128)S(1)} %copy-done.7, bf16[4,2,256,256]{3,2,1,0:T(8,128)(2,1)S(1)} %all-to-all-done.kept, bf16[4,256,256]{2,1,0:T(8,128)(2,1)S(1)} %collective-permute-done.11.crossed, ...), custom_call_target="tpu_custom_call", output_to_operand_aliasing={{0}: (4, {}), {1}: (5, {})} | custom-call | flops 1073741824 | bytes 4194304 | tf_op jit(solution)/shard_map/pallas_call | solution.py:327
  116.3 0.0 collective-permute-done.15.refs_0_
  116.4 5.6 %shard_map.77 = (f32[4096,128]{1,0:T(8,128)S(1)}, f32[4096,128]{1,0:T(8,128)S(1)}) custom-call(s32[5]{0:T(128)S(1)} %copy-done.7, bf16[4,2,256,256]{3,2,1,0:T(8,128)(2,1)S(1)} %all-to-all-done.kept, bf16[4,256,256]{2,1,0:T(8,128)(2,1)S(1)} %collective-permute-done.11.crossed, ...), custom_call_target="tpu_custom_call", output_to_operand_aliasing={{0}: (5, {}), {1}: (6, {})} | custom-call | flops 2013265920 | bytes 4194304 | tf_op jit(solution)/shard_map/pallas_call | solution.py:327
  121.9 0.0 collective-permute-done.13.refs_0_
  121.9 3.0 %shard_map.78 = bf16[2048,256]{1,0:T(8,128)(2,1)} custom-call(s32[5]{0:T(128)S(1)} %copy-done.7, bf16[4,2,256,256]{3,2,1,0:T(8,128)(2,1)S(1)} %all-to-all-done.kept, bf16[4,256,256]{2,1,0:T(8,128)(2,1)S(1)} %collective-permute-done.11.crossed, bf16[6,256,128]{2,1,0:T(8,128)(2,1)S(1)} %collective-permute-done.13.refs_0_, ...), custom_call_target="tpu_custom_call" | custom-call | flops 402653184 | bytes 4194304 | tf_op jit(solution)/shard_map/pallas_call | solution.py:327
  124.9 3.7 %all-to-all-start.2 = ((bf16[8,256,256]{2,1,0:T(8,128)(2,1)}), bf16[8,256,256]{2,1,0:T(8,128)(2,1)S(1)}, u32[]{:S(2)}, u32[]{:S(2)}) async-start(bf16[8,256,256]{2,1,0:T(8,128)(2,1)} %bitcast.10), calls=%async_computation.2 | async-start | bytes 2097152 | tf_op jit(solution)/shard_map/all_to_all | solution.py:487
  128.7 0.1 collective-permute-start.10
  128.8 1.5 %collective-permute-done.10 = bf16[256,512]{1,0:T(8,128)(2,1)S(1)} collective-permute-done((bf16[256,512]{1,0:T(8,128)(2,1)S(1)}, bf16[256,512]{1,0:T(8,128)(2,1)S(1)}, u32[]{:S(2)}, u32[]{:S(2)}) %collective-permute-start.10) | collective-permute-done | bytes 262176 | tf_op jit(solution)/shard_map/ppermute | solution.py:49
  130.3 0.9 fusion
  131.3 11.4 %all-to-all-done.2.home = bf16[8,256,256]{2,1,0:T(8,128)(2,1)S(1)} async-done(((bf16[8,256,256]{2,1,0:T(8,128)(2,1)}), bf16[8,256,256]{2,1,0:T(8,128)(2,1)S(1)}, u32[]{:S(2)}, u32[]{:S(2)}) %all-to-all-start.2) | async-done | bytes 1048608 | tf_op jit(solution)/shard_map/all_to_all | solution.py:487
  142.6 2.1 %assemble.1 = bf16[256,2048]{1,0:T(8,128)(2,1)} custom-call(s32[5]{0:T(128)S(1)} %copy-done.7, bf16[8,256,256]{2,1,0:T(8,128)(2,1)S(1)} %all-to-all-done.2.home), custom_call_target="tpu_custom_call" | custom-call | tf_op jit(solution)/shard_map/assemble/pallas_call | solution.py:489
  (25 shorter events, 0.1 us)
Async XLA Ops:
  0.6 31.7 %collective-permute-start = (bf16[256,4608]{1,0:T(8,128)(2,1)}, bf16[256,4608]{1,0:T(8,128)(2,1)}, u32[]{:S(2)}, u32[]{:S(2)}) collective-permute-start(bf16[256,4608]{1,0:T(8,128)(2,1)} %bitcast.17), channel_id=1, source_target_pairs={{0,1},{1,0},{2,3},{3,2},{4,5},{5,4},{6,7},{7,6},{8,9},{9,8},{10,11... | collective-permute-start | bytes 7077896 | tf_op jit(solution)/shard_map/ppermute | solution.py:49
  0.7 31.7 %collective-permute-start.1 = (bf16[1152,1024]{1,0:T(8,128)(2,1)}, bf16[1152,1024]{1,0:T(8,128)(2,1)}, u32[]{:S(2)}, u32[]{:S(2)}) collective-permute-start(bf16[1152,1024]{1,0:T(8,128)(2,1)} %down.3), channel_id=1, source_target_pairs={{0,1},{1,0},{2,3},{3,2},{4,5},{5,4},{6,7},{7,6},{8,9},{9,8},{10,11... | collective-permute-start | bytes 7077896 | tf_op jit(solution)/shard_map/ppermute | solution.py:49
  4.9 10.2 %collective-permute-start.4 = (bf16[144,512]{1,0:T(8,128)(2,1)}, bf16[144,512]{1,0:T(8,128)(2,1)S(1)}, u32[]{:S(2)}, u32[]{:S(2)}) collective-permute-start(bf16[144,512]{1,0:T(8,128)(2,1)} %get-tuple-element.29), channel_id=1, source_target_pairs={{0,2},{1,7},{2,4},{3,1},{4,6},{5,3},{6,0},{7,5},{8,10},{9,15},{10,... | collective-permute-start | bytes 442376 | tf_op jit(solution)/shard_map/ppermute | solution.py:396
  6.5 8.7 %collective-permute-start.5 = (bf16[144,512]{1,0:T(8,128)(2,1)}, bf16[144,512]{1,0:T(8,128)(2,1)}, u32[]{:S(2)}, u32[]{:S(2)}) collective-permute-start(bf16[144,512]{1,0:T(8,128)(2,1)} %get-tuple-element.30), channel_id=1, source_target_pairs={{0,3},{1,6},{2,5},{3,0},{4,7},{5,2},{6,1},{7,4},{8,11},{9,14},{10,... | collective-permute-start | bytes 442376 | tf_op jit(solution)/shard_map/ppermute | solution.py:397
  10.5 24.7 %copy-start = (bf16[1,256,4608]{2,1,0:T(8,128)(2,1)S(1)}, bf16[1,256,4608]{2,1,0:T(8,128)(2,1)}, u32[]{:S(2)}) copy-start(bf16[1,256,4608]{2,1,0:T(8,128)(2,1)} %param.5) | copy-start | bytes 7077892
  10.5 23.8 %all-to-all-start = ((bf16[4,2,256,256]{3,2,1,0:T(8,128)(2,1)}), bf16[4,2,256,256]{3,2,1,0:T(8,128)(2,1)S(1)}, u32[]{:S(2)}, u32[]{:S(2)}) async-start(bf16[4,2,256,256]{3,2,1,0:T(8,128)(2,1)} %get-tuple-element.32), calls=%async_computation | async-start | bytes 2097152 | tf_op jit(solution)/shard_map/all_to_all | solution.py:407
  16.1 0.7 copy-start.2
  16.8 18.4 %copy-start.7 = (s32[5]{0:T(128)S(1)}, s32[5]{0:T(128)}, u32[]{:S(2)}) copy-start(s32[5]{0:T(128)} %stack.19.info) | copy-start | bytes 64
  16.8 10.8 %collective-permute-start.8 = (bf16[2,144,512]{2,1,0:T(8,128)(2,1)S(1)}, bf16[2,144,512]{2,1,0:T(8,128)(2,1)S(1)}, u32[]{:S(2)}, u32[]{:S(2)}) collective-permute-start(bf16[2,144,512]{2,1,0:T(8,128)(2,1)S(1)} %shard_map.71.relay_0), channel_id=1, source_target_pairs={{0,64},{32,96},{64,0},{96,32},{1,65},{33,97},{65,1},{97,33},{2,66}... | collective-permute-start | bytes 884744 | tf_op jit(solution)/shard_map/ppermute | solution.py:403
  16.8 24.8 %collective-permute-start.2 = (bf16[832,512]{1,0:T(8,128)(2,1)}, bf16[832,512]{1,0:T(8,128)(2,1)}, u32[]{:S(2)}, u32[]{:S(2)}) collective-permute-start(bf16[832,512]{1,0:T(8,128)(2,1)} %get-tuple-element.27), channel_id=1, source_target_pairs={{0,2},{1,7},{2,4},{3,1},{4,6},{5,3},{6,0},{7,5},{8,10},{9,15},{10,... | collective-permute-start | bytes 2555912 | tf_op jit(solution)/shard_map/ppermute | solution.py:398
  18.3 23.3 %collective-permute-start.3 = (bf16[832,512]{1,0:T(8,128)(2,1)}, bf16[832,512]{1,0:T(8,128)(2,1)}, u32[]{:S(2)}, u32[]{:S(2)}) collective-permute-start(bf16[832,512]{1,0:T(8,128)(2,1)} %get-tuple-element.28), channel_id=1, source_target_pairs={{0,3},{1,6},{2,5},{3,0},{4,7},{5,2},{6,1},{7,4},{8,11},{9,14},{10,... | collective-permute-start | bytes 2555912 | tf_op jit(solution)/shard_map/ppermute | solution.py:399
  27.6 0.7 copy-start.5
  28.3 13.3 %collective-permute-start.9 = (bf16[2,128,1024]{2,1,0:T(8,128)(2,1)}, bf16[2,128,1024]{2,1,0:T(8,128)(2,1)}, u32[]{:S(2)}, u32[]{:S(2)}) collective-permute-start(bf16[2,128,1024]{2,1,0:T(8,128)(2,1)} %up_own.1), channel_id=1, source_target_pairs={{0,1},{1,0},{2,3},{3,2},{4,5},{5,4},{6,7},{7,6},{8,9},{9,8},{10,11... | collective-permute-start | bytes 1572872 | tf_op jit(solution)/shard_map/ppermute | solution.py:49
  32.3 9.2 %collective-permute-start.7 = (bf16[2,144,512]{2,1,0:T(8,128)(2,1)}, bf16[2,144,512]{2,1,0:T(8,128)(2,1)}, u32[]{:S(2)}, u32[]{:S(2)}) collective-permute-start(bf16[2,144,512]{2,1,0:T(8,128)(2,1)} %copy-done.2), channel_id=1, source_target_pairs={{0,96},{32,0},{64,32},{96,64},{1,97},{33,1},{65,33},{97,65},{2,98}... | collective-permute-start | bytes 884744 | tf_op jit(solution)/shard_map/ppermute | solution.py:403
  32.4 9.2 %collective-permute-start.6 = (bf16[2,144,512]{2,1,0:T(8,128)(2,1)}, bf16[2,144,512]{2,1,0:T(8,128)(2,1)}, u32[]{:S(2)}, u32[]{:S(2)}) collective-permute-start(bf16[2,144,512]{2,1,0:T(8,128)(2,1)} %copy-done.2), channel_id=1, source_target_pairs={{0,32},{32,64},{64,96},{96,0},{1,33},{33,65},{65,97},{97,1},{2,34}... | collective-permute-start | bytes 884744 | tf_op jit(solution)/shard_map/ppermute | solution.py:403
  35.2 6.4 %copy-start.1 = (bf16[2,128,1024]{2,1,0:T(8,128)(2,1)S(1)}, bf16[2,128,1024]{2,1,0:T(8,128)(2,1)}, u32[]{:S(2)}) copy-start(bf16[2,128,1024]{2,1,0:T(8,128)(2,1)} %up_own.1) | copy-start | bytes 1572868
  35.2 6.5 %copy-start.3 = (bf16[2,144,512]{2,1,0:T(8,128)(2,1)S(1)}, bf16[2,144,512]{2,1,0:T(8,128)(2,1)}, u32[]{:S(2)}) copy-start(bf16[2,144,512]{2,1,0:T(8,128)(2,1)} %copy-done.2) | copy-start | bytes 884740
  35.2 6.5 %copy-start.4 = (f32[256,128]{1,0:T(8,128)S(1)}, f32[256,128]{1,0:T(8,128)}, u32[]{:S(2)}) copy-start(f32[256,128]{1,0:T(8,128)} %get-tuple-element.63.sine) | copy-start | bytes 393220
  35.2 6.5 %copy-start.6 = (bf16[2,144,512]{2,1,0:T(8,128)(2,1)S(1)}, bf16[2,144,512]{2,1,0:T(8,128)(2,1)}, u32[]{:S(2)}) copy-start(bf16[2,144,512]{2,1,0:T(8,128)(2,1)} %copy-done.5) | copy-start | bytes 884740
  47.6 6.9 %copy-start.9 = (bf16[4,256,256]{2,1,0:T(8,128)(2,1)S(1)}, bf16[4,256,256]{2,1,0:T(8,128)(2,1)}, u32[]{:S(2)}) copy-start(bf16[4,256,256]{2,1,0:T(8,128)(2,1)} %slice_bitcast_fusion) | copy-start | bytes 1572868
  47.7 25.5 %all-to-all-start.1 = ((bf16[16,256,128]{2,1,0:T(8,128)(2,1)}), bf16[16,256,128]{2,1,0:T(8,128)(2,1)S(1)}, u32[]{:S(2)}, u32[]{:S(2)}) async-start(bf16[16,256,128]{2,1,0:T(8,128)(2,1)} %get-tuple-element.35), calls=%async_computation.1 | async-start | bytes 2097152 | tf_op jit(solution)/shard_map/all_to_all | solution.py:455
  54.6 28.0 %collective-permute-start.11 = (bf16[4,256,256]{2,1,0:T(8,128)(2,1)S(1)}, bf16[4,256,256]{2,1,0:T(8,128)(2,1)S(1)}, u32[]{:S(2)}, u32[]{:S(2)}) collective-permute-start(bf16[4,256,256]{2,1,0:T(8,128)(2,1)S(1)} %copy-done.9), channel_id=1, source_target_pairs={{0,4},{4,0},{1,5},{5,1},{2,6},{6,2},{3,7},{7,3},{8,12},{12,8},{9,1... | collective-permute-start | bytes 1572872 | tf_op jit(solution)/shard_map/ppermute | solution.py:454
  73.3 34.1 %collective-permute-start.19 = (bf16[6,256,128]{2,1,0:T(8,128)(2,1)S(1)}, bf16[6,256,128]{2,1,0:T(8,128)(2,1)S(1)}, u32[]{:S(2)}, u32[]{:S(2)}) collective-permute-start(bf16[6,256,128]{2,1,0:T(8,128)(2,1)S(1)} %get-tuple-element.52), channel_id=1, source_target_pairs={{0,32},{32,64},{64,96},{1,33},{33,65},{65,97},{2,34},{34,66},{66,9... | collective-permute-start | bytes 1179656 | tf_op jit(solution)/shard_map/ppermute | solution.py:465
  78.0 11.4 %collective-permute-start.14 = (bf16[6,256,128]{2,1,0:T(8,128)(2,1)S(1)}, bf16[6,256,128]{2,1,0:T(8,128)(2,1)S(1)}, u32[]{:S(2)}, u32[]{:S(2)}) collective-permute-start(bf16[6,256,128]{2,1,0:T(8,128)(2,1)S(1)} %get-tuple-element.53), channel_id=1, source_target_pairs={{32,0},{0,96},{33,1},{1,97},{34,2},{2,98},{35,3},{3,99},{36,4},{4,... | collective-permute-start | bytes 1179656 | tf_op jit(solution)/shard_map/ppermute | solution.py:462
  78.7 17.2 %collective-permute-start.12 = (bf16[6,256,128]{2,1,0:T(8,128)(2,1)S(1)}, bf16[6,256,128]{2,1,0:T(8,128)(2,1)S(1)}, u32[]{:S(2)}, u32[]{:S(2)}) collective-permute-start(bf16[6,256,128]{2,1,0:T(8,128)(2,1)S(1)} %get-tuple-element.54), channel_id=1, source_target_pairs={{0,32},{32,64},{64,96},{1,33},{33,65},{65,97},{2,34},{34,66},{66,9... | collective-permute-start | bytes 1179656 | tf_op jit(solution)/shard_map/ppermute | solution.py:463
  80.6 31.9 %collective-permute-start.18 = (bf16[4,256,128]{2,1,0:T(8,128)(2,1)S(1)}, bf16[4,256,128]{2,1,0:T(8,128)(2,1)S(1)}, u32[]{:S(2)}, u32[]{:S(2)}) collective-permute-start(bf16[4,256,128]{2,1,0:T(8,128)(2,1)S(1)} %get-tuple-element.55), channel_id=1, source_target_pairs={{0,32},{32,64},{64,96},{1,33},{33,65},{65,97},{2,34},{34,66},{66,9... | collective-permute-start | bytes 786440 | tf_op jit(solution)/shard_map/ppermute | solution.py:466
  82.6 18.5 %collective-permute-start.16 = (bf16[4,256,128]{2,1,0:T(8,128)(2,1)S(1)}, bf16[4,256,128]{2,1,0:T(8,128)(2,1)S(1)}, u32[]{:S(2)}, u32[]{:S(2)}) collective-permute-start(bf16[4,256,128]{2,1,0:T(8,128)(2,1)S(1)} %get-tuple-element.56), channel_id=1, source_target_pairs={{32,0},{0,96},{33,1},{1,97},{34,2},{2,98},{35,3},{3,99},{36,4},{4,... | collective-permute-start | bytes 786440 | tf_op jit(solution)/shard_map/ppermute | solution.py:464
  89.4 27.0 %collective-permute-start.15 = (bf16[6,256,128]{2,1,0:T(8,128)(2,1)S(1)}, bf16[6,256,128]{2,1,0:T(8,128)(2,1)S(1)}, u32[]{:S(2)}, u32[]{:S(2)}) collective-permute-start(bf16[6,256,128]{2,1,0:T(8,128)(2,1)S(1)} %collective-permute-done.14), channel_id=1, source_target_pairs={{0,96},{96,64},{1,97},{97,65},{2,98},{98,66},{3,99},{99,67},{4,100... | collective-permute-start | bytes 1179656 | tf_op jit(solution)/shard_map/ppermute | solution.py:472
  101.1 15.3 %collective-permute-start.17 = (bf16[4,256,128]{2,1,0:T(8,128)(2,1)S(1)}, bf16[4,256,128]{2,1,0:T(8,128)(2,1)S(1)}, u32[]{:S(2)}, u32[]{:S(2)}) collective-permute-start(bf16[4,256,128]{2,1,0:T(8,128)(2,1)S(1)} %collective-permute-done.16), channel_id=1, source_target_pairs={{0,96},{96,64},{1,97},{97,65},{2,98},{98,66},{3,99},{99,67},{4,100... | collective-permute-start | bytes 786440 | tf_op jit(solution)/shard_map/ppermute | solution.py:475
  102.4 19.6 %collective-permute-start.13 = (bf16[6,256,128]{2,1,0:T(8,128)(2,1)S(1)}, bf16[6,256,128]{2,1,0:T(8,128)(2,1)S(1)}, u32[]{:S(2)}, u32[]{:S(2)}) collective-permute-start(bf16[6,256,128]{2,1,0:T(8,128)(2,1)S(1)} %collective-permute-done.12.pairs), channel_id=1, source_target_pairs={{32,64},{64,96},{33,65},{65,97},{34,66},{66,98},{35,67},{67,99},{3... | collective-permute-start | bytes 1179656 | tf_op jit(solution)/shard_map/ppermute | solution.py:467
  124.9 3.7 %copy-start.8 = (bf16[512,512]{1,0:T(8,128)(2,1)S(1)}, bf16[512,512]{1,0:T(8,128)(2,1)}, u32[]{:S(2)}) copy-start(bf16[512,512]{1,0:T(8,128)(2,1)} %get-tuple-element.31) | copy-start | bytes 1572868
  124.9 17.7 %all-to-all-start.2 = ((bf16[8,256,256]{2,1,0:T(8,128)(2,1)}), bf16[8,256,256]{2,1,0:T(8,128)(2,1)S(1)}, u32[]{:S(2)}, u32[]{:S(2)}) async-start(bf16[8,256,256]{2,1,0:T(8,128)(2,1)} %bitcast.10), calls=%async_computation.2 | async-start | bytes 2097152 | tf_op jit(solution)/shard_map/all_to_all | solution.py:487
  128.7 1.6 %collective-permute-start.10 = (bf16[256,512]{1,0:T(8,128)(2,1)S(1)}, bf16[256,512]{1,0:T(8,128)(2,1)S(1)}, u32[]{:S(2)}, u32[]{:S(2)}) collective-permute-start(bf16[256,512]{1,0:T(8,128)(2,1)S(1)} %get-tuple-element.58), channel_id=1, source_target_pairs={{0,1},{1,0},{2,3},{3,2},{4,5},{5,4},{6,7},{7,6},{8,9},{9,8},{10,11... | collective-permute-start | bytes 786440 | tf_op jit(solution)/shard_map/ppermute | solution.py:49

commit v6 on v5

--- a/solution.py
+++ b/solution.py
@@ -16,9 +16,9 @@
 CHUNK = 2048
 KV_HEADS = 8
 BLOCKS = CHUNK // BLOCK
-LOW, TOP, MIDDLE = 3, 5, 6
-GRANT = {"first": 60, "collect": 60, "half": 49, "project": 46}
-RELAYED = 576
+LOW = 4
+GRANT = {"first": 60, "collect": 60, "gather": 60, "half": 49, "project": 46}
+RELAYED = 640
 SIZES = {"z": 4, "y": 4, "xh": 2, "xl": 2, "core": 2}
 SEQ_AXES = ("z", "y", "xh")
 DP_AXES = ("xl", "core")
@@ -75,7 +75,7 @@
     finish(begin(sems, *moves))
 
 
-def collect_kernel(info, down, up, queries, direct_a, direct_b, sent, sems):
+def collect_kernel(info, down, up, direct_a, direct_b, sems):
     rank = direct_a.shape[1]
     piece = up.shape[1]
     split = direct_a.shape[0] - 2 * piece
@@ -87,6 +87,11 @@
         for k in range(2):
             at = pl.ds(split + k * piece, piece)
             moves.append((up.at[which, :, pl.ds(k * rank, rank)], direct.at[at]))
+    finish(begin(sems, *moves))
+
+
+def gather_kernel(info, queries, sent, sems):
+    moves = []
     for y, k in itertools.product(range(4), range(2)):
         pair = 2 * y + (info[2] ^ k)
         moves.append((queries.at[:, chunk(pair, PAIR)], sent.at[y, k]))
@@ -107,33 +112,37 @@
     ]
 
 
-def half_kernel(info, hidden, partner, weight_0, weight_1, out, inputs, weights, sems):
+def half_kernel(
+    info, hidden, partner, weight_0, weight_1, out, others, inputs, weights, sems
+):
     columns = chunk(info[0] % 2, weights.shape[2])
     moves = []
     for k, weight in enumerate((weight_0, weight_1)):
         moves += hidden_moves(hidden, partner, info[0] ^ k, inputs.at[k])
         moves.append((weight.at[:, columns], weights.at[k]))
+    for k in range(2):
+        moves += hidden_moves(hidden, partner, info[0] ^ (2 + k), others.at[k])
     copies = begin(sems, *moves)
     finish(copies[:3])
     total = jnp.dot(inputs[0], weights[0], preferred_element_type=jnp.float32)
-    finish(copies[3:])
+    finish(copies[3:6])
     out[...] = total + jnp.dot(inputs[1], weights[1], preferred_element_type=jnp.float32)
+    finish(copies[6:])
 
 
 def project_kernel(
-    info, partial, hidden, partner, direct_a, direct_b, relay_0, relay_1, relay_2, relay_3,
+    info, partial, inputs, direct_a, direct_b, relay_0, relay_1, relay_2, relay_3,
     up_own, up_partner, cosine, sine, latent, pairs,
-    inputs, weights, upper, rounded, ready, sems, out_sems,
+    weights, upper, rounded, ready, sems, out_sems,
 ):
     mine, plane = info[0], info[1]
     core = mine % 2
-    rows = hidden.shape[0]
+    rows = inputs.shape[1] // 2
     piece = up_own.shape[1]
     share, rank = relay_0.shape[1:]
     split = weights.shape[1] - 4 * share
     moves = []
     for which, direct in ((0, direct_a), (1, direct_b)):
-        moves += hidden_moves(hidden, partner, mine ^ (2 + which), inputs.at[which])
         moves.append((direct.at[pl.ds(0, split)], weights.at[which, pl.ds(0, split)]))
         for step, relay in ((0, relay_0), (3, relay_1), (1, relay_2), (2, relay_3)):
             at = pl.multiple_of(split + share * ((plane + step) % 4), 16)
@@ -173,12 +182,24 @@
     finish(outgoing)
 
 
-def assemble_kernel(info, home, out):
-    rows = out.shape[0]
-    live = (info[3] + lax.broadcasted_iota(jnp.int32, (rows, PAIR), 0)) < info[4]
-    for k in range(home.shape[0]):
-        part = home[k]
-        out[:, k * PAIR : (k + 1) * PAIR] = jnp.where(live, part, jnp.zeros_like(part))
+def assemble_kernel(info, home, out, masked, sems):
+    heads, rows, _ = home.shape
+    start, length = info[3], info[4]
+
+    def place(source):
+        moves = [(source.at[k], out.at[:, pl.ds(k * PAIR, PAIR)]) for k in range(heads)]
+        finish(begin(sems, *moves))
+
+    @pl.when(start + rows <= length)
+    def _():
+        place(home)
+
+    @pl.when(start + rows > length)
+    def _():
+        live = (start + lax.broadcasted_iota(jnp.int32, (rows, PAIR), 0)) < length
+        for k in range(heads):
+            masked[k] = jnp.where(live, home[k], jnp.zeros_like(home[k]))
+        place(masked)
 
 
 def expo(raw):
@@ -248,15 +269,10 @@
 
     @pl.when(info[1] >= 1)
     def _():
-        def step(t, carry):
-            for u in range(2):
-                pair = 2 * t + u
-                n, d = over_blocks(two_blocks(info, (kept, crossed), pair), pairs, blocks)
-                numer[pair_rows(pair), :] += n
-                denom[pair_rows(pair), :] += d
-            return carry
-
-        lax.fori_loop(0, BLOCKS // 4, step, 0)
+        for pair in range(BLOCKS // 2):
+            n, d = over_blocks(two_blocks(info, (kept, crossed), pair), pairs, blocks)
+            numer[pair_rows(pair), :] += n
+            denom[pair_rows(pair), :] += d
 
 
 def far_kernel(pieces, last, info, kept, crossed, *refs):
@@ -384,15 +400,15 @@
         [sems((2,))],
         10**7,
     )(info, down_weight)
-    direct_a, direct_b, sent = step(
+    direct_a, direct_b = step(
         "collect",
         collect_kernel,
-        (shape(split + 2 * piece, rank),) * 2 + (shape(4, 2, rows, PAIR),),
-        [IN_SMEM] + [ANYWHERE] * 3,
-        (IN_VMEM,) * 3,
-        [sems((14,))],
+        (shape(split + 2 * piece, rank),) * 2,
+        [IN_SMEM] + [ANYWHERE] * 2,
+        (IN_VMEM,) * 2,
+        [sems((6,))],
         10**8,
-    )(info, down_weight, up_weight, queries[0])
+    )(info, down_weight, up_weight)
     relay_a = lax.ppermute(relay_a, X_AXES, forward)
     relay_b = lax.ppermute(relay_b, X_AXES, crossed)
     direct_a = lax.ppermute(direct_a, X_AXES, forward)
@@ -404,6 +420,10 @@
     partner_hidden = to_partner(hidden)
     partner_weight = to_partner(down_weight)
     partner_upper = to_partner(up_weight)
+    sent = step(
+        "gather", gather_kernel, shape(4, 2, rows, PAIR), [IN_SMEM, ANYWHERE], IN_VMEM,
+        [sems((8,))], 10**7,
+    )(info, queries[0])
     sent = lax.all_to_all(sent, "y", 0, 0, tiled=True)
     leaving = sent[:, 1]
 
@@ -416,13 +436,16 @@
     sine = jnp.where(core == 0, jnp.concatenate([-sine, sine], axis=1), 0.0)
 
     flops = 4 * rows * depth * rank2
-    partial = step(
+    partial, others = step(
         "half",
         half_kernel,
-        jax.ShapeDtypeStruct((2 * rows, rank), jnp.float32),
+        (
+            jax.ShapeDtypeStruct((2 * rows, rank), jnp.float32),
+            shape(2, 2 * rows, depth),
+        ),
         [IN_SMEM] + [ANYWHERE] * 4,
-        IN_VMEM,
-        [scratch(2, 2 * rows, depth), scratch(2, depth, rank), sems((6,))],
+        (IN_VMEM, IN_VMEM),
+        [scratch(2, 2 * rows, depth), scratch(2, depth, rank), sems((10,))],
         flops,
     )(info, hidden, partner_hidden, down_weight, partner_weight)
 
@@ -433,20 +456,19 @@
             pltpu.HBM((2 * rows, rank), jnp.bfloat16),
             pltpu.HBM((2 * groups, rows, HEAD), jnp.bfloat16),
         ),
-        [IN_SMEM, IN_VMEM] + [ANYWHERE] * 10 + [IN_VMEM] * 2,
+        [IN_SMEM, IN_VMEM, IN_VMEM] + [ANYWHERE] * 8 + [IN_VMEM] * 2,
         (ANYWHERE, ANYWHERE),
         [
-            scratch(2, 2 * rows, depth),
             scratch(2, depth, rank),
             scratch(rank, kv_width),
             scratch(2 * rows, rank),
             scratch(2 * groups, rows, HEAD),
-            sems((20,)),
+            sems((16,)),
             sems((2 * groups + 1,)),
         ],
         flops,
     )(
-        info, partial, hidden, partner_hidden, direct_a, direct_b,
+        info, partial, others, direct_a, direct_b,
         relay_own, *relays, up_weight, partner_upper, cosine, sine,
     )
 
@@ -455,48 +477,32 @@
     own_pairs = lax.all_to_all(pairs, PLANE + ("core",), 0, 0, tiled=True)
     other_half = to_partner(latent[rows:])
 
-    def part(first, end):
-        return own_pairs[2 * first : 2 * end]
-
+    low = 2 * LOW
     up, down, on = [(0, 1), (1, 2), (2, 3)], [(1, 0), (0, 3)], [(0, 3), (3, 2)]
-    passing_2 = lax.ppermute(part(TOP, BLOCKS), "z", down)
-    near_low = lax.ppermute(part(0, LOW), "z", up)
-    passing_1 = lax.ppermute(part(LOW, TOP), "z", down)
-    near_mid = lax.ppermute(part(LOW, MIDDLE), "z", up)
-    near_high = lax.ppermute(part(MIDDLE, BLOCKS), "z", up)
+    passing = lax.ppermute(own_pairs[low:], "z", down)
+    near_low = lax.ppermute(own_pairs[:low], "z", up)
+    near_high = lax.ppermute(own_pairs[low:], "z", up)
     far_low = lax.ppermute(near_low, "z", [(1, 2), (2, 3)])
 
     common = (info, sent, crossed_queries)
     state = attention_call(own_kernel, 36, (*common, own_pairs), resume=False)
-    passing_2, state = lax.optimization_barrier((passing_2, state))
-    far_2 = lax.ppermute(passing_2, "z", on)
-    state = attention_call(near_kernel, 8 * LOW, (*common, near_low, *state))
-    passing_1, state = lax.optimization_barrier((passing_1, state))
-    far_1 = lax.ppermute(passing_1, "z", on)
-    state = attention_call(near_kernel, 24, (*common, near_mid, *state))
-    state = attention_call(near_kernel, 16, (*common, near_high, *state))
-    pieces = ((TOP, BLOCKS), (LOW, TOP))
+    passing, state = lax.optimization_barrier((passing, state))
+    far_high = lax.ppermute(passing, "z", on)
+    state = attention_call(near_kernel, 32, (*common, near_low, *state))
+    state = attention_call(near_kernel, 32, (*common, near_high, *state))
     state = attention_call(
-        functools.partial(far_kernel, pieces, False), 30, (*common, far_2, far_1, *state)
+        functools.partial(far_kernel, ((LOW, BLOCKS),), False), 26,
+        (*common, far_high, *state),
     )
     result = attention_call(
-        functools.partial(far_kernel, ((0, LOW),), True), 6,
+        functools.partial(far_kernel, ((0, LOW),), True), 10,
         (*common, far_low, *state), result=True,
     )
 
     home = lax.all_to_all(result.reshape(groups, rows, PAIR), PLANE, 0, 0, tiled=True)
-    each = 2
-    attended = pl.pallas_call(
-        assemble_kernel,
-        out_shape=shape(rows, groups * PAIR),
-        grid_spec=pltpu.PrefetchScalarGridSpec(
-            num_scalar_prefetch=1,
-            grid=(groups // each,),
-            in_specs=[pl.BlockSpec((each, rows, PAIR), lambda i, s: (i, 0, 0))],
-            out_specs=pl.BlockSpec((rows, each * PAIR), lambda i, s: (0, i)),
-        ),
-        compiler_params=pltpu.CompilerParams(vmem_limit_bytes=8 * 2**20),
-        name="assemble",
+    attended = step(
+        "assemble", assemble_kernel, pltpu.HBM((rows, groups * PAIR), jnp.bfloat16),
+        [IN_SMEM, IN_VMEM], ANYWHERE, [scratch(groups, rows, PAIR), sems((groups,))], 10**7,
     )(info, home)
     live = ((start + jnp.arange(rows, dtype=jnp.int32)) < lengths[0])[:, None]
     ours = latent[:rows]

time: 145 us -> 143 us (0.986)
  the two profiles are of different devices: /device:TPU:64 before, /device:TPU:96 now
where the time goes in v6:
time: 143 us
  waiting for transfers between devices  51.8 us (36%)
  Pallas kernels  47.9 us (33%)
  starting transfers between devices  34.6 us (24%)
  other arithmetic  4.19 us (3%)
  local copies, waits for them, and re-layouts  2.26 us (2%)
  between operations  1.76 us (1%)
    pallas_call x5, Pallas kernels, attention_call(): pl.pallas_call(kernel, out_shape=RESULT if result else (STATE, STATE), in...  27 us
    all_to_all x1, waiting for transfers between devices, body(): own_pairs = lax.all_to_all(pairs, PLANE + ('core',), 0, 0, tiled=True)  15 us
    ppermute x3, waiting for transfers between devices, body(): relays = [lax.ppermute(relay_own, 'z', ring(k)) for k in (1, -1, 2)]  13.5 us
    all_to_all x1, waiting for transfers between devices, body(): lax.all_to_all(result.reshape(groups, rows, PAIR), PLANE, 0, 0, tiled=True)  11.7 us
    all_to_all x1, starting transfers between devices, body(): own_pairs = lax.all_to_all(pairs, PLANE + ('core',), 0, 0, tiled=True)  7.02 us
    pallas_call x1, Pallas kernels, body(): step('project', project_kernel, (pltpu.HBM((2 * rows, rank), jnp.bfloat16...  5.96 us
    pallas_call x1, Pallas kernels, body(): step('half', half_kernel, (jax.ShapeDtypeStruct((2 * rows, rank), jnp.flo...  4.51 us
    all_to_all x1, starting transfers between devices, body(): sent = lax.all_to_all(sent, 'y', 0, 0, tiled=True)  4.47 us
  transfers between devices with their start and end apart: 20, of which 9 were waited for; matrix products, arithmetic and copies ran while one was open for 4% of the time, Pallas kernels for 26%

profile of v6, /device:TPU:96, one launch (start us, length us, event | category | flops | bytes accessed | tf_op | source)
XLA Modules:
  0.0 142.5 jit_solution(15536993519936549591)
XLA Ops:
  0.6 0.1 collective-permute-start
  0.7 0.5 collective-permute-start.1
  1.9 0.6 stack.19.info
  2.5 2.4 %shard_map.70 = (bf16[160,512]{1,0:T(8,128)(2,1)}, bf16[160,512]{1,0:T(8,128)(2,1)}) custom-call(s32[5]{0:T(128)} %stack.19.info, bf16[1152,1024]{1,0:T(8,128)(2,1)} %down.3), custom_call_target="tpu_custom_call" | custom-call | flops 10000000 | bytes 4194304 | tf_op jit(solution)/shard_map/pallas_call | solution.py:394
  4.9 1.6 %collective-permute-start.4 = (bf16[160,512]{1,0:T(8,128)(2,1)}, bf16[160,512]{1,0:T(8,128)(2,1)S(1)}, u32[]{:S(2)}, u32[]{:S(2)}) collective-permute-start(bf16[160,512]{1,0:T(8,128)(2,1)} %get-tuple-element.27), channel_id=1, source_target_pairs={{0,2},{1,7},{2,4},{3,1},{4,6},{5,3},{6,0},{7,5},{8,10},{9,15},{10,... | collective-permute-start | bytes 491528 | tf_op jit(solution)/shard_map/ppermute | solution.py:412
  6.4 0.0 collective-permute-start.5
  6.4 3.0 %shard_map.73 = bf16[4,2,256,256]{3,2,1,0:T(8,128)(2,1)} custom-call(s32[5]{0:T(128)} %stack.19.info, bf16[256,2048]{1,0:T(8,128)(2,1)} %bitcast.19), custom_call_target="tpu_custom_call" | custom-call | flops 10000000 | bytes 4194304 | tf_op jit(solution)/shard_map/pallas_call | solution.py:423
  9.4 4.5 %all-to-all-start = ((bf16[4,2,256,256]{3,2,1,0:T(8,128)(2,1)}), bf16[4,2,256,256]{3,2,1,0:T(8,128)(2,1)S(1)}, u32[]{:S(2)}, u32[]{:S(2)}) async-start(bf16[4,2,256,256]{3,2,1,0:T(8,128)(2,1)} %shard_map.73), calls=%async_computation | async-start | bytes 2097152 | tf_op jit(solution)/shard_map/all_to_all | solution.py:427
  13.9 0.0 collective-permute-done.4.a
  13.9 0.0 collective-permute-done.5.b
  13.9 0.0 copy-start.5
  14.0 0.1 collective-permute-start.6
  14.0 3.4 %shard_map.69 = (bf16[768,512]{1,0:T(8,128)(2,1)}, bf16[768,512]{1,0:T(8,128)(2,1)}) custom-call(s32[5]{0:T(128)} %stack.19.info, bf16[1152,1024]{1,0:T(8,128)(2,1)} %down.3, bf16[2,128,1024]{2,1,0:T(8,128)(2,1)} %up_own.1), custom_call_target="tpu_custom_call" | custom-call | flops 100000000 | bytes 4194304 | tf_op jit(solution)/shard_map/pallas_call | solution.py:403
  17.4 1.6 %collective-permute-start.2 = (bf16[768,512]{1,0:T(8,128)(2,1)}, bf16[768,512]{1,0:T(8,128)(2,1)S(1)}, u32[]{:S(2)}, u32[]{:S(2)}) collective-permute-start(bf16[768,512]{1,0:T(8,128)(2,1)} %get-tuple-element.25), channel_id=1, source_target_pairs={{0,2},{1,7},{2,4},{3,1},{4,6},{5,3},{6,0},{7,5},{8,10},{9,15},{10,... | collective-permute-start | bytes 2359304 | tf_op jit(solution)/shard_map/ppermute | solution.py:414
  19.0 1.4 %collective-permute-start.3 = (bf16[768,512]{1,0:T(8,128)(2,1)}, bf16[768,512]{1,0:T(8,128)(2,1)S(1)}, u32[]{:S(2)}, u32[]{:S(2)}) collective-permute-start(bf16[768,512]{1,0:T(8,128)(2,1)} %get-tuple-element.26), channel_id=1, source_target_pairs={{0,3},{1,6},{2,5},{3,0},{4,7},{5,2},{6,1},{7,4},{8,11},{9,14},{10,... | collective-permute-start | bytes 2359304 | tf_op jit(solution)/shard_map/ppermute | solution.py:415
  20.4 3.6 %collective-permute-done.6.relay_1 = bf16[2,160,512]{2,1,0:T(8,128)(2,1)S(1)} collective-permute-done((bf16[2,160,512]{2,1,0:T(8,128)(2,1)S(1)}, bf16[2,160,512]{2,1,0:T(8,128)(2,1)S(1)}, u32[]{:S(2)}, u32[]{:S(2)}) %collective-permute-start.6) | collective-permute-done | bytes 327712 | tf_op jit(solution)/shard_map/ppermute | solution.py:419
  24.0 0.7 copy-done.3
  24.7 0.0 copy-done
  24.7 0.7 collective-permute-start.9
  25.5 1.3 fusion.1
  26.7 1.9 %maximum_select_fusion.1 = (f32[256,128]{1,0:T(8,128)}, f32[256,128]{1,0:T(8,128)}) fusion(f32[256,64]{1,0:T(8,128)} %get-tuple-element.50, pred[]{:T(512)S(6)} %eq.2, f32[256,64]{1,0:T(8,128)} %get-tuple-element.49, f32[256,64]{1,0:T(8,128)} %get-tuple-element.48), kind=kLoop, calls=%fused_computation.6 | loop fusion | flops 131072 | bytes 458753 | tf_op jit(solution)/shard_map/jit(_where)/select_n | solution.py:435
  28.7 0.0 collective-permute-done.partner
  28.7 0.4 collective-permute-start.7
  29.1 0.0 collective-permute-done.1.weight_1
  29.1 2.3 %collective-permute-start.8 = (bf16[2,160,512]{2,1,0:T(8,128)(2,1)S(1)}, bf16[2,160,512]{2,1,0:T(8,128)(2,1)}, u32[]{:S(2)}, u32[]{:S(2)}) collective-permute-start(bf16[2,160,512]{2,1,0:T(8,128)(2,1)S(1)} %shard_map.71.relay_0), channel_id=1, source_target_pairs={{0,64},{32,96},{64,0},{96,32},{1,65},{33,97},{65,1},{97,33},{2,66}... | collective-permute-start | bytes 983048 | tf_op jit(solution)/shard_map/ppermute | solution.py:419
  31.4 0.0 all-to-all-done.kept
  31.4 0.8 slice_bitcast_fusion
  32.2 0.0 copy-done.5
  32.2 4.5 %shard_map.68 = (f32[512,512]{1,0:T(8,128)S(1)}, bf16[2,512,1152]{2,1,0:T(8,128)(2,1)S(1)}) custom-call(s32[5]{0:T(128)S(1)} %copy-done.5, bf16[256,4608]{1,0:T(8,128)(2,1)} %bitcast.18, bf16[256,4608]{1,0:T(8,128)(2,1)} %collective-permute-done.partner, bf16[1152,1024]{1,0:T(8,128)(2,1)} %down.3, bf16[1152,1024]{1,0:T(8,128)(2,1)} %collective-permute-done.1.weight_1), custom_call_target="tpu_custom_call" | custom-call | flops 1207959552 | bytes 4194304 | tf_op jit(solution)/shard_map/pallas_call | solution.py:439
  36.7 9.9 %collective-permute-done.7.relay_2 = bf16[2,160,512]{2,1,0:T(8,128)(2,1)} collective-permute-done((bf16[2,160,512]{2,1,0:T(8,128)(2,1)S(1)}, bf16[2,160,512]{2,1,0:T(8,128)(2,1)}, u32[]{:S(2)}, u32[]{:S(2)}) %collective-permute-start.7) | collective-permute-done | bytes 327712 | tf_op jit(solution)/shard_map/ppermute | solution.py:419
  46.6 0.0 collective-permute-done.8.relay_3
  46.6 0.0 collective-permute-done.9.up_partner
  46.7 0.0 collective-permute-done.2.direct_a
  46.7 0.0 collective-permute-done.3.direct_b
  46.7 0.0 copy-done.1
  46.7 0.0 copy-done.2
  46.7 0.0 copy-done.4
  46.7 6.0 %shard_map.72 = (bf16[512,512]{1,0:T(8,128)(2,1)}, bf16[16,256,128]{2,1,0:T(8,128)(2,1)}) custom-call(s32[5]{0:T(128)S(1)} %copy-done.5, f32[512,512]{1,0:T(8,128)S(1)} %get-tuple-element.23.partial, bf16[2,512,1152]{2,1,0:T(8,128)(2,1)S(1)} %get-tuple-element.24.inputs, bf16[768,512]{1,0:T(8,128)(2,1)S(1)} %collective-permute-done.2.direct_a, ...), custom_call_target="tpu_custom_call" | custom-call | flops 1207959552 | bytes 4194304 | tf_op jit(solution)/shard_map/pallas_call | solution.py:452
  52.7 7.0 %all-to-all-start.1 = ((bf16[16,256,128]{2,1,0:T(8,128)(2,1)}), bf16[16,256,128]{2,1,0:T(8,128)(2,1)S(1)}, u32[]{:S(2)}, u32[]{:S(2)}) async-start(bf16[16,256,128]{2,1,0:T(8,128)(2,1)} %get-tuple-element.32), calls=%async_computation.1 | async-start | bytes 2097152 | tf_op jit(solution)/shard_map/all_to_all | solution.py:477
  59.7 3.5 %collective-permute-start.11 = (bf16[4,256,256]{2,1,0:T(8,128)(2,1)S(1)}, bf16[4,256,256]{2,1,0:T(8,128)(2,1)S(1)}, u32[]{:S(2)}, u32[]{:S(2)}) collective-permute-start(bf16[4,256,256]{2,1,0:T(8,128)(2,1)S(1)} %copy-done.7), channel_id=1, source_target_pairs={{0,4},{4,0},{1,5},{5,1},{2,6},{6,2},{3,7},{7,3},{8,12},{12,8},{9,1... | collective-permute-start | bytes 1572872 | tf_op jit(solution)/shard_map/ppermute | solution.py:476
  63.2 15.0 %all-to-all-done.1.pairs = bf16[16,256,128]{2,1,0:T(8,128)(2,1)S(1)} async-done(((bf16[16,256,128]{2,1,0:T(8,128)(2,1)}), bf16[16,256,128]{2,1,0:T(8,128)(2,1)S(1)}, u32[]{:S(2)}, u32[]{:S(2)}) %all-to-all-start.1) | async-done | bytes 1048608 | tf_op jit(solution)/shard_map/all_to_all | solution.py:477
  78.3 0.1 fusion.4
  78.3 1.3 collective-permute-start.14
  79.6 1.3 collective-permute-start.12
  80.9 1.5 %collective-permute-start.16 = (bf16[8,256,128]{2,1,0:T(8,128)(2,1)S(1)}, bf16[8,256,128]{2,1,0:T(8,128)(2,1)S(1)}, u32[]{:S(2)}, u32[]{:S(2)}) collective-permute-start(bf16[8,256,128]{2,1,0:T(8,128)(2,1)S(1)} %get-tuple-element.44), channel_id=1, source_target_pairs={{0,32},{32,64},{64,96},{1,33},{33,65},{65,97},{2,34},{34,66},{66,9... | collective-permute-start | bytes 1572872 | tf_op jit(solution)/shard_map/ppermute | solution.py:484
  82.4 4.3 %collective-permute-done.11.crossed = bf16[4,256,256]{2,1,0:T(8,128)(2,1)S(1)} collective-permute-done((bf16[4,256,256]{2,1,0:T(8,128)(2,1)S(1)}, bf16[4,256,256]{2,1,0:T(8,128)(2,1)S(1)}, u32[]{:S(2)}, u32[]{:S(2)}) %collective-permute-start.11) | collective-permute-done | bytes 524320 | tf_op jit(solution)/shard_map/ppermute | solution.py:476
  86.8 6.0 %shard_map.74 = (f32[4096,128]{1,0:T(8,128)S(1)}, f32[4096,128]{1,0:T(8,128)S(1)}) custom-call(s32[5]{0:T(128)S(1)} %copy-done.5, bf16[4,2,256,256]{3,2,1,0:T(8,128)(2,1)S(1)} %all-to-all-done.kept, bf16[4,256,256]{2,1,0:T(8,128)(2,1)S(1)} %collective-permute-done.11.crossed, bf16[16,256,128]{2,1,0:T(8,128)(2,1)S(1)} %all-to-all-done.1.pairs), custom_call_target="tpu_custom_call" | custom-call | flops 2415919104 | bytes 4194304 | tf_op jit(solution)/shard_map/pallas_call | solution.py:343
  92.7 1.5 %collective-permute-done.14 = bf16[8,256,128]{2,1,0:T(8,128)(2,1)S(1)} collective-permute-done((bf16[8,256,128]{2,1,0:T(8,128)(2,1)S(1)}, bf16[8,256,128]{2,1,0:T(8,128)(2,1)S(1)}, u32[]{:S(2)}, u32[]{:S(2)}) %collective-permute-start.14) | collective-permute-done | bytes 524320 | tf_op jit(solution)/shard_map/ppermute | solution.py:482
  94.2 1.9 %collective-permute-start.15 = (bf16[8,256,128]{2,1,0:T(8,128)(2,1)S(1)}, bf16[8,256,128]{2,1,0:T(8,128)(2,1)S(1)}, u32[]{:S(2)}, u32[]{:S(2)}) collective-permute-start(bf16[8,256,128]{2,1,0:T(8,128)(2,1)S(1)} %collective-permute-done.14), channel_id=1, source_target_pairs={{0,96},{96,64},{1,97},{97,65},{2,98},{98,66},{3,99},{99,67},{4,100... | collective-permute-start | bytes 1572872 | tf_op jit(solution)/shard_map/ppermute | solution.py:490
  96.1 0.2 collective-permute-done.12.pairs
  96.3 1.3 collective-permute-start.13
  97.6 5.9 %shard_map.75 = (f32[4096,128]{1,0:T(8,128)S(1)}, f32[4096,128]{1,0:T(8,128)S(1)}) custom-call(s32[5]{0:T(128)S(1)} %copy-done.5, bf16[4,2,256,256]{3,2,1,0:T(8,128)(2,1)S(1)} %all-to-all-done.kept, bf16[4,256,256]{2,1,0:T(8,128)(2,1)S(1)} %collective-permute-done.11.crossed, ...), custom_call_target="tpu_custom_call", output_to_operand_aliasing={{0}: (4, {}), {1}: (5, {})} | custom-call | flops 2147483648 | bytes 4194304 | tf_op jit(solution)/shard_map/pallas_call | solution.py:343
  103.5 4.0 %collective-permute-done.16.pairs = bf16[8,256,128]{2,1,0:T(8,128)(2,1)S(1)} collective-permute-done((bf16[8,256,128]{2,1,0:T(8,128)(2,1)S(1)}, bf16[8,256,128]{2,1,0:T(8,128)(2,1)S(1)}, u32[]{:S(2)}, u32[]{:S(2)}) %collective-permute-start.16) | collective-permute-done | bytes 524320 | tf_op jit(solution)/shard_map/ppermute | solution.py:484
  107.6 6.1 %shard_map.76 = (f32[4096,128]{1,0:T(8,128)S(1)}, f32[4096,128]{1,0:T(8,128)S(1)}) custom-call(s32[5]{0:T(128)S(1)} %copy-done.5, bf16[4,2,256,256]{3,2,1,0:T(8,128)(2,1)S(1)} %all-to-all-done.kept, bf16[4,256,256]{2,1,0:T(8,128)(2,1)S(1)} %collective-permute-done.11.crossed, ...), custom_call_target="tpu_custom_call", output_to_operand_aliasing={{0}: (4, {}), {1}: (5, {})} | custom-call | flops 2147483648 | bytes 4194304 | tf_op jit(solution)/shard_map/pallas_call | solution.py:343
  113.7 0.0 collective-permute-done.15.refs_0_
  113.7 5.1 %shard_map.77 = (f32[4096,128]{1,0:T(8,128)S(1)}, f32[4096,128]{1,0:T(8,128)S(1)}) custom-call(s32[5]{0:T(128)S(1)} %copy-done.5, bf16[4,2,256,256]{3,2,1,0:T(8,128)(2,1)S(1)} %all-to-all-done.kept, bf16[4,256,256]{2,1,0:T(8,128)(2,1)S(1)} %collective-permute-done.11.crossed, ...), custom_call_target="tpu_custom_call", output_to_operand_aliasing={{0}: (4, {}), {1}: (5, {})} | custom-call | flops 1744830464 | bytes 4194304 | tf_op jit(solution)/shard_map/pallas_call | solution.py:343
  118.8 0.0 collective-permute-done.13.refs_0_
  118.8 4.0 %shard_map.78 = bf16[2048,256]{1,0:T(8,128)(2,1)} custom-call(s32[5]{0:T(128)S(1)} %copy-done.5, bf16[4,2,256,256]{3,2,1,0:T(8,128)(2,1)S(1)} %all-to-all-done.kept, bf16[4,256,256]{2,1,0:T(8,128)(2,1)S(1)} %collective-permute-done.11.crossed, bf16[8,256,128]{2,1,0:T(8,128)(2,1)S(1)} %collective-permute-done.13.refs_0_, ...), custom_call_target="tpu_custom_call" | custom-call | flops 671088640 | bytes 4194304 | tf_op jit(solution)/shard_map/pallas_call | solution.py:343
  122.8 3.7 %all-to-all-start.2 = ((bf16[8,256,256]{2,1,0:T(8,128)(2,1)}), bf16[8,256,256]{2,1,0:T(8,128)(2,1)S(1)}, u32[]{:S(2)}, u32[]{:S(2)}) async-start(bf16[8,256,256]{2,1,0:T(8,128)(2,1)} %bitcast.10), calls=%async_computation.2 | async-start | bytes 2097152 | tf_op jit(solution)/shard_map/all_to_all | solution.py:502
  126.5 0.1 collective-permute-start.10
  126.6 1.5 %collective-permute-done.10 = bf16[256,512]{1,0:T(8,128)(2,1)S(1)} collective-permute-done((bf16[256,512]{1,0:T(8,128)(2,1)S(1)}, bf16[256,512]{1,0:T(8,128)(2,1)S(1)}, u32[]{:S(2)}, u32[]{:S(2)}) %collective-permute-start.10) | collective-permute-done | bytes 262176 | tf_op jit(solution)/shard_map/ppermute | solution.py:49
  128.1 0.9 fusion
  129.1 11.7 %all-to-all-done.2.home = bf16[8,256,256]{2,1,0:T(8,128)(2,1)S(1)} async-done(((bf16[8,256,256]{2,1,0:T(8,128)(2,1)}), bf16[8,256,256]{2,1,0:T(8,128)(2,1)S(1)}, u32[]{:S(2)}, u32[]{:S(2)}) %all-to-all-start.2) | async-done | bytes 1048608 | tf_op jit(solution)/shard_map/all_to_all | solution.py:502
  140.8 1.6 %shard_map.79 = bf16[256,2048]{1,0:T(8,128)(2,1)} custom-call(s32[5]{0:T(128)S(1)} %copy-done.5, bf16[8,256,256]{2,1,0:T(8,128)(2,1)S(1)} %all-to-all-done.2.home), custom_call_target="tpu_custom_call" | custom-call | flops 10000000 | bytes 4194304 | tf_op jit(solution)/shard_map/pallas_call | solution.py:503
  (14 shorter events, 0.1 us)
Async XLA Ops:
  0.6 28.1 %collective-permute-start = (bf16[256,4608]{1,0:T(8,128)(2,1)}, bf16[256,4608]{1,0:T(8,128)(2,1)}, u32[]{:S(2)}, u32[]{:S(2)}) collective-permute-start(bf16[256,4608]{1,0:T(8,128)(2,1)} %bitcast.17), channel_id=1, source_target_pairs={{0,1},{1,0},{2,3},{3,2},{4,5},{5,4},{6,7},{7,6},{8,9},{9,8},{10,11... | collective-permute-start | bytes 7077896 | tf_op jit(solution)/shard_map/ppermute | solution.py:49
  0.7 28.4 %collective-permute-start.1 = (bf16[1152,1024]{1,0:T(8,128)(2,1)}, bf16[1152,1024]{1,0:T(8,128)(2,1)}, u32[]{:S(2)}, u32[]{:S(2)}) collective-permute-start(bf16[1152,1024]{1,0:T(8,128)(2,1)} %down.3), channel_id=1, source_target_pairs={{0,1},{1,0},{2,3},{3,2},{4,5},{5,4},{6,7},{7,6},{8,9},{9,8},{10,11... | collective-permute-start | bytes 7077896 | tf_op jit(solution)/shard_map/ppermute | solution.py:49
  4.9 9.1 %collective-permute-start.4 = (bf16[160,512]{1,0:T(8,128)(2,1)}, bf16[160,512]{1,0:T(8,128)(2,1)S(1)}, u32[]{:S(2)}, u32[]{:S(2)}) collective-permute-start(bf16[160,512]{1,0:T(8,128)(2,1)} %get-tuple-element.27), channel_id=1, source_target_pairs={{0,2},{1,7},{2,4},{3,1},{4,6},{5,3},{6,0},{7,5},{8,10},{9,15},{10,... | collective-permute-start | bytes 491528 | tf_op jit(solution)/shard_map/ppermute | solution.py:412
  6.4 7.5 %collective-permute-start.5 = (bf16[160,512]{1,0:T(8,128)(2,1)}, bf16[160,512]{1,0:T(8,128)(2,1)S(1)}, u32[]{:S(2)}, u32[]{:S(2)}) collective-permute-start(bf16[160,512]{1,0:T(8,128)(2,1)} %get-tuple-element.28), channel_id=1, source_target_pairs={{0,3},{1,6},{2,5},{3,0},{4,7},{5,2},{6,1},{7,4},{8,11},{9,14},{10,... | collective-permute-start | bytes 491528 | tf_op jit(solution)/shard_map/ppermute | solution.py:413
  9.4 21.9 %all-to-all-start = ((bf16[4,2,256,256]{3,2,1,0:T(8,128)(2,1)}), bf16[4,2,256,256]{3,2,1,0:T(8,128)(2,1)S(1)}, u32[]{:S(2)}, u32[]{:S(2)}) async-start(bf16[4,2,256,256]{3,2,1,0:T(8,128)(2,1)} %shard_map.73), calls=%async_computation | async-start | bytes 2097152 | tf_op jit(solution)/shard_map/all_to_all | solution.py:427
  13.9 10.8 %copy-start = (bf16[2,128,1024]{2,1,0:T(8,128)(2,1)S(1)}, bf16[2,128,1024]{2,1,0:T(8,128)(2,1)}, u32[]{:S(2)}) copy-start(bf16[2,128,1024]{2,1,0:T(8,128)(2,1)} %up_own.1) | copy-start | bytes 1572868
  13.9 18.3 %copy-start.5 = (s32[5]{0:T(128)S(1)}, s32[5]{0:T(128)}, u32[]{:S(2)}) copy-start(s32[5]{0:T(128)} %stack.19.info) | copy-start | bytes 64
  14.0 10.0 %collective-permute-start.6 = (bf16[2,160,512]{2,1,0:T(8,128)(2,1)S(1)}, bf16[2,160,512]{2,1,0:T(8,128)(2,1)S(1)}, u32[]{:S(2)}, u32[]{:S(2)}) collective-permute-start(bf16[2,160,512]{2,1,0:T(8,128)(2,1)S(1)} %shard_map.71.relay_0), channel_id=1, source_target_pairs={{0,32},{32,64},{64,96},{96,0},{1,33},{33,65},{65,97},{97,1},{2,34}... | collective-permute-start | bytes 983048 | tf_op jit(solution)/shard_map/ppermute | solution.py:419
  17.4 29.2 %collective-permute-start.2 = (bf16[768,512]{1,0:T(8,128)(2,1)}, bf16[768,512]{1,0:T(8,128)(2,1)S(1)}, u32[]{:S(2)}, u32[]{:S(2)}) collective-permute-start(bf16[768,512]{1,0:T(8,128)(2,1)} %get-tuple-element.25), channel_id=1, source_target_pairs={{0,2},{1,7},{2,4},{3,1},{4,6},{5,3},{6,0},{7,5},{8,10},{9,15},{10,... | collective-permute-start | bytes 2359304 | tf_op jit(solution)/shard_map/ppermute | solution.py:414
  19.0 27.7 %collective-permute-start.3 = (bf16[768,512]{1,0:T(8,128)(2,1)}, bf16[768,512]{1,0:T(8,128)(2,1)S(1)}, u32[]{:S(2)}, u32[]{:S(2)}) collective-permute-start(bf16[768,512]{1,0:T(8,128)(2,1)} %get-tuple-element.26), channel_id=1, source_target_pairs={{0,3},{1,6},{2,5},{3,0},{4,7},{5,2},{6,1},{7,4},{8,11},{9,14},{10,... | collective-permute-start | bytes 2359304 | tf_op jit(solution)/shard_map/ppermute | solution.py:415
  24.0 0.7 copy-start.3
  24.7 21.9 %collective-permute-start.9 = (bf16[2,128,1024]{2,1,0:T(8,128)(2,1)S(1)}, bf16[2,128,1024]{2,1,0:T(8,128)(2,1)}, u32[]{:S(2)}, u32[]{:S(2)}) collective-permute-start(bf16[2,128,1024]{2,1,0:T(8,128)(2,1)S(1)} %copy-done), channel_id=1, source_target_pairs={{0,1},{1,0},{2,3},{3,2},{4,5},{5,4},{6,7},{7,6},{8,9},{9,8},{10,11... | collective-permute-start | bytes 1572872 | tf_op jit(solution)/shard_map/ppermute | solution.py:49
  28.7 18.0 %collective-permute-start.7 = (bf16[2,160,512]{2,1,0:T(8,128)(2,1)S(1)}, bf16[2,160,512]{2,1,0:T(8,128)(2,1)}, u32[]{:S(2)}, u32[]{:S(2)}) collective-permute-start(bf16[2,160,512]{2,1,0:T(8,128)(2,1)S(1)} %shard_map.71.relay_0), channel_id=1, source_target_pairs={{0,96},{32,0},{64,32},{96,64},{1,97},{33,1},{65,33},{97,65},{2,98}... | collective-permute-start | bytes 983048 | tf_op jit(solution)/shard_map/ppermute | solution.py:419
  29.1 17.6 %collective-permute-start.8 = (bf16[2,160,512]{2,1,0:T(8,128)(2,1)S(1)}, bf16[2,160,512]{2,1,0:T(8,128)(2,1)}, u32[]{:S(2)}, u32[]{:S(2)}) collective-permute-start(bf16[2,160,512]{2,1,0:T(8,128)(2,1)S(1)} %shard_map.71.relay_0), channel_id=1, source_target_pairs={{0,64},{32,96},{64,0},{96,32},{1,65},{33,97},{65,1},{97,33},{2,66}... | collective-permute-start | bytes 983048 | tf_op jit(solution)/shard_map/ppermute | solution.py:419
  32.2 14.5 %copy-start.1 = (f32[256,128]{1,0:T(8,128)S(1)}, f32[256,128]{1,0:T(8,128)}, u32[]{:S(2)}) copy-start(f32[256,128]{1,0:T(8,128)} %get-tuple-element.51.cosine) | copy-start | bytes 393220
  32.2 14.5 %copy-start.2 = (f32[256,128]{1,0:T(8,128)S(1)}, f32[256,128]{1,0:T(8,128)}, u32[]{:S(2)}) copy-start(f32[256,128]{1,0:T(8,128)} %get-tuple-element.52.sine) | copy-start | bytes 393220
  32.2 14.5 %copy-start.4 = (bf16[2,160,512]{2,1,0:T(8,128)(2,1)S(1)}, bf16[2,160,512]{2,1,0:T(8,128)(2,1)}, u32[]{:S(2)}) copy-start(bf16[2,160,512]{2,1,0:T(8,128)(2,1)} %copy-done.3) | copy-start | bytes 983044
  52.7 7.0 %copy-start.7 = (bf16[4,256,256]{2,1,0:T(8,128)(2,1)S(1)}, bf16[4,256,256]{2,1,0:T(8,128)(2,1)}, u32[]{:S(2)}) copy-start(bf16[4,256,256]{2,1,0:T(8,128)(2,1)} %slice_bitcast_fusion) | copy-start | bytes 1572868
  52.7 25.6 %all-to-all-start.1 = ((bf16[16,256,128]{2,1,0:T(8,128)(2,1)}), bf16[16,256,128]{2,1,0:T(8,128)(2,1)S(1)}, u32[]{:S(2)}, u32[]{:S(2)}) async-start(bf16[16,256,128]{2,1,0:T(8,128)(2,1)} %get-tuple-element.32), calls=%async_computation.1 | async-start | bytes 2097152 | tf_op jit(solution)/shard_map/all_to_all | solution.py:477
  59.7 27.1 %collective-permute-start.11 = (bf16[4,256,256]{2,1,0:T(8,128)(2,1)S(1)}, bf16[4,256,256]{2,1,0:T(8,128)(2,1)S(1)}, u32[]{:S(2)}, u32[]{:S(2)}) collective-permute-start(bf16[4,256,256]{2,1,0:T(8,128)(2,1)S(1)} %copy-done.7), channel_id=1, source_target_pairs={{0,4},{4,0},{1,5},{5,1},{2,6},{6,2},{3,7},{7,3},{8,12},{12,8},{9,1... | collective-permute-start | bytes 1572872 | tf_op jit(solution)/shard_map/ppermute | solution.py:476
  78.3 15.9 %collective-permute-start.14 = (bf16[8,256,128]{2,1,0:T(8,128)(2,1)S(1)}, bf16[8,256,128]{2,1,0:T(8,128)(2,1)S(1)}, u32[]{:S(2)}, u32[]{:S(2)}) collective-permute-start(bf16[8,256,128]{2,1,0:T(8,128)(2,1)S(1)} %get-tuple-element.44), channel_id=1, source_target_pairs={{32,0},{0,96},{33,1},{1,97},{34,2},{2,98},{35,3},{3,99},{36,4},{4,... | collective-permute-start | bytes 1572872 | tf_op jit(solution)/shard_map/ppermute | solution.py:482
  79.6 16.7 %collective-permute-start.12 = (bf16[8,256,128]{2,1,0:T(8,128)(2,1)S(1)}, bf16[8,256,128]{2,1,0:T(8,128)(2,1)S(1)}, u32[]{:S(2)}, u32[]{:S(2)}) collective-permute-start(bf16[8,256,128]{2,1,0:T(8,128)(2,1)S(1)} %get-tuple-element.45), channel_id=1, source_target_pairs={{0,32},{32,64},{64,96},{1,33},{33,65},{65,97},{2,34},{34,66},{66,9... | collective-permute-start | bytes 1572872 | tf_op jit(solution)/shard_map/ppermute | solution.py:483
  80.9 26.6 %collective-permute-start.16 = (bf16[8,256,128]{2,1,0:T(8,128)(2,1)S(1)}, bf16[8,256,128]{2,1,0:T(8,128)(2,1)S(1)}, u32[]{:S(2)}, u32[]{:S(2)}) collective-permute-start(bf16[8,256,128]{2,1,0:T(8,128)(2,1)S(1)} %get-tuple-element.44), channel_id=1, source_target_pairs={{0,32},{32,64},{64,96},{1,33},{33,65},{65,97},{2,34},{34,66},{66,9... | collective-permute-start | bytes 1572872 | tf_op jit(solution)/shard_map/ppermute | solution.py:484
  94.2 19.5 %collective-permute-start.15 = (bf16[8,256,128]{2,1,0:T(8,128)(2,1)S(1)}, bf16[8,256,128]{2,1,0:T(8,128)(2,1)S(1)}, u32[]{:S(2)}, u32[]{:S(2)}) collective-permute-start(bf16[8,256,128]{2,1,0:T(8,128)(2,1)S(1)} %collective-permute-done.14), channel_id=1, source_target_pairs={{0,96},{96,64},{1,97},{97,65},{2,98},{98,66},{3,99},{99,67},{4,100... | collective-permute-start | bytes 1572872 | tf_op jit(solution)/shard_map/ppermute | solution.py:490
  96.3 22.4 %collective-permute-start.13 = (bf16[8,256,128]{2,1,0:T(8,128)(2,1)S(1)}, bf16[8,256,128]{2,1,0:T(8,128)(2,1)S(1)}, u32[]{:S(2)}, u32[]{:S(2)}) collective-permute-start(bf16[8,256,128]{2,1,0:T(8,128)(2,1)S(1)} %collective-permute-done.12.pairs), channel_id=1, source_target_pairs={{32,64},{64,96},{33,65},{65,97},{34,66},{66,98},{35,67},{67,99},{3... | collective-permute-start | bytes 1572872 | tf_op jit(solution)/shard_map/ppermute | solution.py:485
  122.8 3.7 %copy-start.6 = (bf16[512,512]{1,0:T(8,128)(2,1)S(1)}, bf16[512,512]{1,0:T(8,128)(2,1)}, u32[]{:S(2)}) copy-start(bf16[512,512]{1,0:T(8,128)(2,1)} %get-tuple-element.29) | copy-start | bytes 1572868
  122.8 18.0 %all-to-all-start.2 = ((bf16[8,256,256]{2,1,0:T(8,128)(2,1)}), bf16[8,256,256]{2,1,0:T(8,128)(2,1)S(1)}, u32[]{:S(2)}, u32[]{:S(2)}) async-start(bf16[8,256,256]{2,1,0:T(8,128)(2,1)} %bitcast.10), calls=%async_computation.2 | async-start | bytes 2097152 | tf_op jit(solution)/shard_map/all_to_all | solution.py:502
  126.5 1.6 %collective-permute-start.10 = (bf16[256,512]{1,0:T(8,128)(2,1)S(1)}, bf16[256,512]{1,0:T(8,128)(2,1)S(1)}, u32[]{:S(2)}, u32[]{:S(2)}) collective-permute-start(bf16[256,512]{1,0:T(8,128)(2,1)S(1)} %get-tuple-element.47), channel_id=1, source_target_pairs={{0,1},{1,0},{2,3},{3,2},{4,5},{5,4},{6,7},{7,6},{8,9},{9,8},{10,11... | collective-permute-start | bytes 786440 | tf_op jit(solution)/shard_map/ppermute | solution.py:49

commit v7 on v6

--- a/solution.py
+++ b/solution.py
@@ -163,19 +163,18 @@
     outgoing = [pltpu.make_async_copy(rounded, latent, out_sems.at[2 * KV_HEADS])]
     outgoing[0].start()
     finish(copies[2 * count :])
-    for head in range(KV_HEADS):
-        raw = jnp.dot(
-            rounded[...], upper[:, head * HEAD : (head + 1) * HEAD],
+    for couple in range(KV_HEADS // 2):
+        both = jnp.dot(
+            rounded[...], upper[:, couple * PAIR : (couple + 1) * PAIR],
             preferred_element_type=jnp.float32,
         )
-        for which, turn in ((0, core), (1, 1 - core)):
-            entry = raw[which * rows : (which + 1) * rows]
+        for head, (which, turn) in itertools.product(range(2), ((0, core), (1, 1 - core))):
+            slot = 2 * (2 * couple + head)
+            entry = both[which * rows : (which + 1) * rows, head * HEAD : (head + 1) * HEAD]
             entry = entry * cosine[...] + pltpu.roll(entry, HEAD // 2, 1) * sine[...]
-            ready[2 * head + which] = entry.astype(jnp.bfloat16)
+            ready[slot + which] = entry.astype(jnp.bfloat16)
             copy = pltpu.make_async_copy(
-                ready.at[2 * head + which],
-                pairs.at[2 * head + turn],
-                out_sems.at[2 * head + which],
+                ready.at[slot + which], pairs.at[slot + turn], out_sems.at[slot + which]
             )
             copy.start()
             outgoing.append(copy)
@@ -275,22 +274,14 @@
             denom[pair_rows(pair), :] += d
 
 
-def far_kernel(pieces, last, info, kept, crossed, *refs):
-    inputs, refs = refs[: len(pieces)], refs[len(pieces) :]
-    if last:
-        numer, denom, out = refs
-    else:
-        _, _, numer, denom = refs
+def far_kernel(pieces, info, kept, crossed, *refs):
+    inputs, (numer, denom, out) = refs[: len(pieces)], refs[len(pieces) :]
     single = triangle(False)
     row = lax.broadcasted_iota(jnp.int32, (4 * BLOCK, BLOCK), 0)
     col = lax.broadcasted_iota(jnp.int32, (4 * BLOCK, BLOCK), 1)
     double = (row < 2 * BLOCK) | (col > row % BLOCK)
 
     def settle(pair, n, d):
-        at = pair_rows(pair)
-        if not last:
-            numer[at, :], denom[at, :] = n, d
-            return
         result = n / jnp.sum(d, axis=1, keepdims=True)
         for k in range(2):
             own = result[2 * k * BLOCK : 2 * (k + 1) * BLOCK]
@@ -303,7 +294,6 @@
         for pair in range(BLOCKS // 2):
             i = 2 * pair
             n, d = numer[pair_rows(pair), :], denom[pair_rows(pair), :]
-            touched = False
             for ref, (first, end) in zip(inputs, pieces):
                 shared = [
                     (j - first, double if j == i + 1 else None)
@@ -311,23 +301,19 @@
                 ]
                 if shared:
                     more = over_blocks(two_blocks(info, (kept, crossed), pair), ref, shared)
-                    n, d, touched = n + more[0], d + more[1], True
+                    n, d = n + more[0], d + more[1]
                 if first <= i < end:
                     own = stacked_rows(info, (kept, crossed), pair, 0)
                     more = over_blocks(own, ref, [(i - first, single)])
                     rest = jnp.zeros((2 * BLOCK, HEAD), jnp.float32)
                     n = n + jnp.concatenate([more[0], rest], axis=0)
                     d = d + jnp.concatenate([more[1], rest], axis=0)
-                    touched = True
-            if touched or last:
-                settle(pair, n, d)
-
-    if last:
-
-        @pl.when(info[1] < 2)
-        def _():
-            for pair in range(BLOCKS // 2):
-                settle(pair, numer[pair_rows(pair), :], denom[pair_rows(pair), :])
+            settle(pair, n, d)
+
+    @pl.when(info[1] < 2)
+    def _():
+        for pair in range(BLOCKS // 2):
+            settle(pair, numer[pair_rows(pair), :], denom[pair_rows(pair), :])
 
 
 IN_VMEM = pl.BlockSpec(memory_space=pltpu.VMEM)
@@ -490,13 +476,9 @@
     far_high = lax.ppermute(passing, "z", on)
     state = attention_call(near_kernel, 32, (*common, near_low, *state))
     state = attention_call(near_kernel, 32, (*common, near_high, *state))
-    state = attention_call(
-        functools.partial(far_kernel, ((LOW, BLOCKS),), False), 26,
-        (*common, far_high, *state),
-    )
     result = attention_call(
-        functools.partial(far_kernel, ((0, LOW),), True), 10,
-        (*common, far_low, *state), result=True,
+        functools.partial(far_kernel, ((LOW, BLOCKS), (0, LOW))), 36,
+        (*common, far_high, far_low, *state), result=True,
     )
 
     home = lax.all_to_all(result.reshape(groups, rows, PAIR), PLANE, 0, 0, tiled=True)

time: 143 us -> 146 us (1.021)
  waiting for transfers between devices: 51.8 us -> 56.9 us
  Pallas kernels: 47.9 us -> 46.1 us
    ppermute x1, waiting for transfers between devices: 0.01 us -> 3.04 us  [body(): far_low = lax.ppermute(near_low, 'z', [(1, 2), (2, 3)])]
    all_to_all x1, waiting for transfers between devices: 11.7 us -> 13.7 us  [body(): lax.all_to_all(result.reshape(groups, rows, PAIR), PLANE, 0, 0, tiled=True)]
    pallas_call x5 -> x4, Pallas kernels: 27 us -> 25.5 us  [attention_call(): pl.pallas_call(kernel, out_shape=RESULT if result else (STATE, STATE), in...]
  transfers between devices with their start and end apart: 20 -> 20, of which waited for: 9 -> 10; matrix products, arithmetic and copies ran while one was open for 4% -> 3% of each run, Pallas kernels for 26% -> 22%
where the time goes in v7:
time: 146 us; the launch traced here: 145 us
  waiting for transfers between devices  56.9 us (39%)
  Pallas kernels  46.1 us (32%)
  starting transfers between devices  34.7 us (24%)
  other arithmetic  3.48 us (2%)
  local copies, waits for them, and re-layouts  2.27 us (2%)
  between operations  1.73 us (1%)
    pallas_call x4, Pallas kernels, attention_call(): pl.pallas_call(kernel, out_shape=RESULT if result else (STATE, STATE), in...  25.5 us
    all_to_all x1, waiting for transfers between devices, body(): own_pairs = lax.all_to_all(pairs, PLANE + ('core',), 0, 0, tiled=True)  15 us
    all_to_all x1, waiting for transfers between devices, body(): lax.all_to_all(result.reshape(groups, rows, PAIR), PLANE, 0, 0, tiled=True)  13.7 us
    ppermute x3, waiting for transfers between devices, body(): relays = [lax.ppermute(relay_own, 'z', ring(k)) for k in (1, -1, 2)]  13.5 us
    all_to_all x1, starting transfers between devices, body(): own_pairs = lax.all_to_all(pairs, PLANE + ('core',), 0, 0, tiled=True)  7.02 us
    pallas_call x1, Pallas kernels, body(): step('project', project_kernel, (pltpu.HBM((2 * rows, rank), jnp.bfloat16...  5.7 us
    pallas_call x1, Pallas kernels, body(): step('half', half_kernel, (jax.ShapeDtypeStruct((2 * rows, rank), jnp.flo...  4.51 us
    all_to_all x1, starting transfers between devices, body(): sent = lax.all_to_all(sent, 'y', 0, 0, tiled=True)  4.47 us
  transfers between devices with their start and end apart: 20, of which 10 were waited for; matrix products, arithmetic and copies ran while one was open for 3% of the time, Pallas kernels for 22%

profile of v7, /device:TPU:96, one launch (start us, length us, event | category | flops | bytes accessed | tf_op | source)
XLA Modules:
  0.0 145.2 jit_solution(8493905120241506917)
XLA Ops:
  0.6 0.1 collective-permute-start
  0.7 0.5 collective-permute-start.1
  1.9 0.6 stack.19.info
  2.5 2.4 %shard_map.70 = (bf16[160,512]{1,0:T(8,128)(2,1)}, bf16[160,512]{1,0:T(8,128)(2,1)}) custom-call(s32[5]{0:T(128)} %stack.19.info, bf16[1152,1024]{1,0:T(8,128)(2,1)} %down.3), custom_call_target="tpu_custom_call" | custom-call | flops 10000000 | bytes 4194304 | tf_op jit(solution)/shard_map/pallas_call | solution.py:380
  4.9 1.6 %collective-permute-start.4 = (bf16[160,512]{1,0:T(8,128)(2,1)}, bf16[160,512]{1,0:T(8,128)(2,1)S(1)}, u32[]{:S(2)}, u32[]{:S(2)}) collective-permute-start(bf16[160,512]{1,0:T(8,128)(2,1)} %get-tuple-element.25), channel_id=1, source_target_pairs={{0,2},{1,7},{2,4},{3,1},{4,6},{5,3},{6,0},{7,5},{8,10},{9,15},{10,... | collective-permute-start | bytes 491528 | tf_op jit(solution)/shard_map/ppermute | solution.py:398
  6.5 0.0 collective-permute-start.5
  6.5 3.0 %shard_map.73 = bf16[4,2,256,256]{3,2,1,0:T(8,128)(2,1)} custom-call(s32[5]{0:T(128)} %stack.19.info, bf16[256,2048]{1,0:T(8,128)(2,1)} %bitcast.19), custom_call_target="tpu_custom_call" | custom-call | flops 10000000 | bytes 4194304 | tf_op jit(solution)/shard_map/pallas_call | solution.py:409
  9.5 4.5 %all-to-all-start = ((bf16[4,2,256,256]{3,2,1,0:T(8,128)(2,1)}), bf16[4,2,256,256]{3,2,1,0:T(8,128)(2,1)S(1)}, u32[]{:S(2)}, u32[]{:S(2)}) async-start(bf16[4,2,256,256]{3,2,1,0:T(8,128)(2,1)} %shard_map.73), calls=%async_computation | async-start | bytes 2097152 | tf_op jit(solution)/shard_map/all_to_all | solution.py:413
  13.9 0.0 collective-permute-done.4.a
  13.9 0.0 collective-permute-done.5.b
  14.0 0.0 copy-start.3
  14.0 0.1 collective-permute-start.6
  14.1 3.4 %shard_map.69 = (bf16[768,512]{1,0:T(8,128)(2,1)}, bf16[768,512]{1,0:T(8,128)(2,1)}) custom-call(s32[5]{0:T(128)} %stack.19.info, bf16[1152,1024]{1,0:T(8,128)(2,1)} %down.3, bf16[2,128,1024]{2,1,0:T(8,128)(2,1)} %up_own.1), custom_call_target="tpu_custom_call" | custom-call | flops 100000000 | bytes 4194304 | tf_op jit(solution)/shard_map/pallas_call | solution.py:389
  17.5 1.6 %collective-permute-start.2 = (bf16[768,512]{1,0:T(8,128)(2,1)}, bf16[768,512]{1,0:T(8,128)(2,1)S(1)}, u32[]{:S(2)}, u32[]{:S(2)}) collective-permute-start(bf16[768,512]{1,0:T(8,128)(2,1)} %get-tuple-element.23), channel_id=1, source_target_pairs={{0,2},{1,7},{2,4},{3,1},{4,6},{5,3},{6,0},{7,5},{8,10},{9,15},{10,... | collective-permute-start | bytes 2359304 | tf_op jit(solution)/shard_map/ppermute | solution.py:400
  19.1 1.4 collective-permute-start.3
  20.5 3.5 %collective-permute-done.6.relay_1 = bf16[2,160,512]{2,1,0:T(8,128)(2,1)S(1)} collective-permute-done((bf16[2,160,512]{2,1,0:T(8,128)(2,1)S(1)}, bf16[2,160,512]{2,1,0:T(8,128)(2,1)S(1)}, u32[]{:S(2)}, u32[]{:S(2)}) %collective-permute-start.6) | collective-permute-done | bytes 327712 | tf_op jit(solution)/shard_map/ppermute | solution.py:405
  24.0 0.7 copy-done.1
  24.8 0.0 copy-done
  24.8 0.7 collective-permute-start.9
  25.5 1.3 fusion.1
  26.8 1.2 maximum_select_fusion.1
  28.0 0.0 collective-permute-done.partner
  28.0 0.5 collective-permute-start.7
  28.5 0.0 collective-permute-done.1.weight_1
  28.5 2.3 %collective-permute-start.8 = (bf16[2,160,512]{2,1,0:T(8,128)(2,1)S(1)}, bf16[2,160,512]{2,1,0:T(8,128)(2,1)}, u32[]{:S(2)}, u32[]{:S(2)}) collective-permute-start(bf16[2,160,512]{2,1,0:T(8,128)(2,1)S(1)} %shard_map.71.relay_0), channel_id=1, source_target_pairs={{0,64},{32,96},{64,0},{96,32},{1,65},{33,97},{65,1},{97,33},{2,66}... | collective-permute-start | bytes 983048 | tf_op jit(solution)/shard_map/ppermute | solution.py:405
  30.8 0.0 all-to-all-done.kept
  30.8 0.8 slice_bitcast_fusion
  31.6 0.0 copy-done.3
  31.6 4.5 %shard_map.68 = (f32[512,512]{1,0:T(8,128)S(1)}, bf16[2,512,1152]{2,1,0:T(8,128)(2,1)S(1)}) custom-call(s32[5]{0:T(128)S(1)} %copy-done.3, bf16[256,4608]{1,0:T(8,128)(2,1)} %bitcast.18, bf16[256,4608]{1,0:T(8,128)(2,1)} %collective-permute-done.partner, bf16[1152,1024]{1,0:T(8,128)(2,1)} %down.3, bf16[1152,1024]{1,0:T(8,128)(2,1)} %collective-permute-done.1.weight_1), custom_call_target="tpu_custom_call" | custom-call | flops 1207959552 | bytes 4194304 | tf_op jit(solution)/shard_map/pallas_call | solution.py:425
  36.1 9.9 %collective-permute-done.7.relay_2 = bf16[2,160,512]{2,1,0:T(8,128)(2,1)} collective-permute-done((bf16[2,160,512]{2,1,0:T(8,128)(2,1)S(1)}, bf16[2,160,512]{2,1,0:T(8,128)(2,1)}, u32[]{:S(2)}, u32[]{:S(2)}) %collective-permute-start.7) | collective-permute-done | bytes 327712 | tf_op jit(solution)/shard_map/ppermute | solution.py:405
  46.1 0.0 collective-permute-done.8.relay_3
  46.1 0.0 collective-permute-done.9.up_partner
  46.1 0.0 collective-permute-done.2.direct_a
  46.1 0.0 collective-permute-done.3.direct_b
  46.1 0.0 copy-done.2
  46.1 5.7 %shard_map.72 = (bf16[512,512]{1,0:T(8,128)(2,1)}, bf16[16,256,128]{2,1,0:T(8,128)(2,1)}) custom-call(s32[5]{0:T(128)S(1)} %copy-done.3, f32[512,512]{1,0:T(8,128)S(1)} %get-tuple-element.21.partial, bf16[2,512,1152]{2,1,0:T(8,128)(2,1)S(1)} %get-tuple-element.22.inputs, bf16[768,512]{1,0:T(8,128)(2,1)S(1)} %collective-permute-done.2.direct_a, ...), custom_call_target="tpu_custom_call" | custom-call | flops 1207959552 | bytes 4194304 | tf_op jit(solution)/shard_map/pallas_call | solution.py:438
  51.8 0.0 copy-start.5
  51.8 7.0 %all-to-all-start.1 = ((bf16[16,256,128]{2,1,0:T(8,128)(2,1)}), bf16[16,256,128]{2,1,0:T(8,128)(2,1)S(1)}, u32[]{:S(2)}, u32[]{:S(2)}) async-start(bf16[16,256,128]{2,1,0:T(8,128)(2,1)} %get-tuple-element.30), calls=%async_computation.1 | async-start | bytes 2097152 | tf_op jit(solution)/shard_map/all_to_all | solution.py:463
  58.8 0.0 copy-done.5
  58.9 3.5 %collective-permute-start.11 = (bf16[4,256,256]{2,1,0:T(8,128)(2,1)S(1)}, bf16[4,256,256]{2,1,0:T(8,128)(2,1)S(1)}, u32[]{:S(2)}, u32[]{:S(2)}) collective-permute-start(bf16[4,256,256]{2,1,0:T(8,128)(2,1)S(1)} %copy-done.5), channel_id=1, source_target_pairs={{0,4},{4,0},{1,5},{5,1},{2,6},{6,2},{3,7},{7,3},{8,12},{12,8},{9,1... | collective-permute-start | bytes 1572872 | tf_op jit(solution)/shard_map/ppermute | solution.py:462
  62.4 15.0 %all-to-all-done.1.pairs = bf16[16,256,128]{2,1,0:T(8,128)(2,1)S(1)} async-done(((bf16[16,256,128]{2,1,0:T(8,128)(2,1)}), bf16[16,256,128]{2,1,0:T(8,128)(2,1)S(1)}, u32[]{:S(2)}, u32[]{:S(2)}) %all-to-all-start.1) | async-done | bytes 1048608 | tf_op jit(solution)/shard_map/all_to_all | solution.py:463
  77.4 0.1 fusion.4
  77.5 1.3 collective-permute-start.12
  78.8 1.3 collective-permute-start.14
  80.1 1.5 %collective-permute-start.16 = (bf16[8,256,128]{2,1,0:T(8,128)(2,1)S(1)}, bf16[8,256,128]{2,1,0:T(8,128)(2,1)S(1)}, u32[]{:S(2)}, u32[]{:S(2)}) collective-permute-start(bf16[8,256,128]{2,1,0:T(8,128)(2,1)S(1)} %get-tuple-element.41), channel_id=1, source_target_pairs={{0,32},{32,64},{64,96},{1,33},{33,65},{65,97},{2,34},{34,66},{66,9... | collective-permute-start | bytes 1572872 | tf_op jit(solution)/shard_map/ppermute | solution.py:470
  81.6 4.3 %collective-permute-done.11.crossed = bf16[4,256,256]{2,1,0:T(8,128)(2,1)S(1)} collective-permute-done((bf16[4,256,256]{2,1,0:T(8,128)(2,1)S(1)}, bf16[4,256,256]{2,1,0:T(8,128)(2,1)S(1)}, u32[]{:S(2)}, u32[]{:S(2)}) %collective-permute-start.11) | collective-permute-done | bytes 524320 | tf_op jit(solution)/shard_map/ppermute | solution.py:462
  85.9 6.0 %shard_map.74 = (f32[4096,128]{1,0:T(8,128)S(1)}, f32[4096,128]{1,0:T(8,128)S(1)}) custom-call(s32[5]{0:T(128)S(1)} %copy-done.3, bf16[4,2,256,256]{3,2,1,0:T(8,128)(2,1)S(1)} %all-to-all-done.kept, bf16[4,256,256]{2,1,0:T(8,128)(2,1)S(1)} %collective-permute-done.11.crossed, bf16[16,256,128]{2,1,0:T(8,128)(2,1)S(1)} %all-to-all-done.1.pairs), custom_call_target="tpu_custom_call" | custom-call | flops 2415919104 | bytes 4194304 | tf_op jit(solution)/shard_map/pallas_call | solution.py:329
  91.9 1.5 %collective-permute-done.12 = bf16[8,256,128]{2,1,0:T(8,128)(2,1)S(1)} collective-permute-done((bf16[8,256,128]{2,1,0:T(8,128)(2,1)S(1)}, bf16[8,256,128]{2,1,0:T(8,128)(2,1)S(1)}, u32[]{:S(2)}, u32[]{:S(2)}) %collective-permute-start.12) | collective-permute-done | bytes 524320 | tf_op jit(solution)/shard_map/ppermute | solution.py:468
  93.3 1.9 %collective-permute-start.13 = (bf16[8,256,128]{2,1,0:T(8,128)(2,1)S(1)}, bf16[8,256,128]{2,1,0:T(8,128)(2,1)S(1)}, u32[]{:S(2)}, u32[]{:S(2)}) collective-permute-start(bf16[8,256,128]{2,1,0:T(8,128)(2,1)S(1)} %collective-permute-done.12), channel_id=1, source_target_pairs={{0,96},{96,64},{1,97},{97,65},{2,98},{98,66},{3,99},{99,67},{4,100... | collective-permute-start | bytes 1572872 | tf_op jit(solution)/shard_map/ppermute | solution.py:476
  95.3 0.2 collective-permute-done.14.pairs
  95.5 1.3 collective-permute-start.15
  96.8 5.9 %shard_map.75 = (f32[4096,128]{1,0:T(8,128)S(1)}, f32[4096,128]{1,0:T(8,128)S(1)}) custom-call(s32[5]{0:T(128)S(1)} %copy-done.3, bf16[4,2,256,256]{3,2,1,0:T(8,128)(2,1)S(1)} %all-to-all-done.kept, bf16[4,256,256]{2,1,0:T(8,128)(2,1)S(1)} %collective-permute-done.11.crossed, ...), custom_call_target="tpu_custom_call", output_to_operand_aliasing={{0}: (4, {}), {1}: (5, {})} | custom-call | flops 2147483648 | bytes 4194304 | tf_op jit(solution)/shard_map/pallas_call | solution.py:329
  102.7 4.0 %collective-permute-done.16.pairs = bf16[8,256,128]{2,1,0:T(8,128)(2,1)S(1)} collective-permute-done((bf16[8,256,128]{2,1,0:T(8,128)(2,1)S(1)}, bf16[8,256,128]{2,1,0:T(8,128)(2,1)S(1)}, u32[]{:S(2)}, u32[]{:S(2)}) %collective-permute-start.16) | collective-permute-done | bytes 524320 | tf_op jit(solution)/shard_map/ppermute | solution.py:470
  106.7 6.1 %shard_map.76 = (f32[4096,128]{1,0:T(8,128)S(1)}, f32[4096,128]{1,0:T(8,128)S(1)}) custom-call(s32[5]{0:T(128)S(1)} %copy-done.3, bf16[4,2,256,256]{3,2,1,0:T(8,128)(2,1)S(1)} %all-to-all-done.kept, bf16[4,256,256]{2,1,0:T(8,128)(2,1)S(1)} %collective-permute-done.11.crossed, ...), custom_call_target="tpu_custom_call", output_to_operand_aliasing={{0}: (4, {}), {1}: (5, {})} | custom-call | flops 2147483648 | bytes 4194304 | tf_op jit(solution)/shard_map/pallas_call | solution.py:329
  112.8 0.0 collective-permute-done.13.refs_0_
  112.9 3.0 %collective-permute-done.15.refs_1_ = bf16[8,256,128]{2,1,0:T(8,128)(2,1)S(1)} collective-permute-done((bf16[8,256,128]{2,1,0:T(8,128)(2,1)S(1)}, bf16[8,256,128]{2,1,0:T(8,128)(2,1)S(1)}, u32[]{:S(2)}, u32[]{:S(2)}) %collective-permute-start.15) | collective-permute-done | bytes 524320 | tf_op jit(solution)/shard_map/ppermute | solution.py:471
  115.9 7.5 %shard_map.77 = bf16[2048,256]{1,0:T(8,128)(2,1)} custom-call(s32[5]{0:T(128)S(1)} %copy-done.3, bf16[4,2,256,256]{3,2,1,0:T(8,128)(2,1)S(1)} %all-to-all-done.kept, bf16[4,256,256]{2,1,0:T(8,128)(2,1)S(1)} %collective-permute-done.11.crossed, bf16[8,256,128]{2,1,0:T(8,128)(2,1)S(1)} %collective-permute-done.13.refs_0_, ...), custom_call_target="tpu_custom_call" | custom-call | flops 2415919104 | bytes 4194304 | tf_op jit(solution)/shard_map/pallas_call | solution.py:329
  123.4 3.7 %all-to-all-start.2 = ((bf16[8,256,256]{2,1,0:T(8,128)(2,1)}), bf16[8,256,256]{2,1,0:T(8,128)(2,1)S(1)}, u32[]{:S(2)}, u32[]{:S(2)}) async-start(bf16[8,256,256]{2,1,0:T(8,128)(2,1)} %bitcast.10), calls=%async_computation.2 | async-start | bytes 2097152 | tf_op jit(solution)/shard_map/all_to_all | solution.py:484
  127.1 0.0 copy-done.4
  127.2 0.1 collective-permute-start.10
  127.3 1.5 %collective-permute-done.10 = bf16[256,512]{1,0:T(8,128)(2,1)S(1)} collective-permute-done((bf16[256,512]{1,0:T(8,128)(2,1)S(1)}, bf16[256,512]{1,0:T(8,128)(2,1)S(1)}, u32[]{:S(2)}, u32[]{:S(2)}) %collective-permute-start.10) | collective-permute-done | bytes 262176 | tf_op jit(solution)/shard_map/ppermute | solution.py:49
  128.8 0.9 fusion
  129.7 13.7 %all-to-all-done.2.home = bf16[8,256,256]{2,1,0:T(8,128)(2,1)S(1)} async-done(((bf16[8,256,256]{2,1,0:T(8,128)(2,1)}), bf16[8,256,256]{2,1,0:T(8,128)(2,1)S(1)}, u32[]{:S(2)}, u32[]{:S(2)}) %all-to-all-start.2) | async-done | bytes 1048608 | tf_op jit(solution)/shard_map/all_to_all | solution.py:484
  143.4 1.6 %shard_map.78 = bf16[256,2048]{1,0:T(8,128)(2,1)} custom-call(s32[5]{0:T(128)S(1)} %copy-done.3, bf16[8,256,256]{2,1,0:T(8,128)(2,1)S(1)} %all-to-all-done.2.home), custom_call_target="tpu_custom_call" | custom-call | flops 10000000 | bytes 4194304 | tf_op jit(solution)/shard_map/pallas_call | solution.py:485
  (9 shorter events, 0.1 us)
Async XLA Ops:
  0.6 27.4 %collective-permute-start = (bf16[256,4608]{1,0:T(8,128)(2,1)}, bf16[256,4608]{1,0:T(8,128)(2,1)}, u32[]{:S(2)}, u32[]{:S(2)}) collective-permute-start(bf16[256,4608]{1,0:T(8,128)(2,1)} %bitcast.17), channel_id=1, source_target_pairs={{0,1},{1,0},{2,3},{3,2},{4,5},{5,4},{6,7},{7,6},{8,9},{9,8},{10,11... | collective-permute-start | bytes 7077896 | tf_op jit(solution)/shard_map/ppermute | solution.py:49
  0.7 27.8 %collective-permute-start.1 = (bf16[1152,1024]{1,0:T(8,128)(2,1)}, bf16[1152,1024]{1,0:T(8,128)(2,1)}, u32[]{:S(2)}, u32[]{:S(2)}) collective-permute-start(bf16[1152,1024]{1,0:T(8,128)(2,1)} %down.3), channel_id=1, source_target_pairs={{0,1},{1,0},{2,3},{3,2},{4,5},{5,4},{6,7},{7,6},{8,9},{9,8},{10,11... | collective-permute-start | bytes 7077896 | tf_op jit(solution)/shard_map/ppermute | solution.py:49
  4.9 9.1 %collective-permute-start.4 = (bf16[160,512]{1,0:T(8,128)(2,1)}, bf16[160,512]{1,0:T(8,128)(2,1)S(1)}, u32[]{:S(2)}, u32[]{:S(2)}) collective-permute-start(bf16[160,512]{1,0:T(8,128)(2,1)} %get-tuple-element.25), channel_id=1, source_target_pairs={{0,2},{1,7},{2,4},{3,1},{4,6},{5,3},{6,0},{7,5},{8,10},{9,15},{10,... | collective-permute-start | bytes 491528 | tf_op jit(solution)/shard_map/ppermute | solution.py:398
  6.5 7.5 %collective-permute-start.5 = (bf16[160,512]{1,0:T(8,128)(2,1)}, bf16[160,512]{1,0:T(8,128)(2,1)S(1)}, u32[]{:S(2)}, u32[]{:S(2)}) collective-permute-start(bf16[160,512]{1,0:T(8,128)(2,1)} %get-tuple-element.26), channel_id=1, source_target_pairs={{0,3},{1,6},{2,5},{3,0},{4,7},{5,2},{6,1},{7,4},{8,11},{9,14},{10,... | collective-permute-start | bytes 491528 | tf_op jit(solution)/shard_map/ppermute | solution.py:399
  9.5 21.3 %all-to-all-start = ((bf16[4,2,256,256]{3,2,1,0:T(8,128)(2,1)}), bf16[4,2,256,256]{3,2,1,0:T(8,128)(2,1)S(1)}, u32[]{:S(2)}, u32[]{:S(2)}) async-start(bf16[4,2,256,256]{3,2,1,0:T(8,128)(2,1)} %shard_map.73), calls=%async_computation | async-start | bytes 2097152 | tf_op jit(solution)/shard_map/all_to_all | solution.py:413
  13.9 10.8 %copy-start = (bf16[2,128,1024]{2,1,0:T(8,128)(2,1)S(1)}, bf16[2,128,1024]{2,1,0:T(8,128)(2,1)}, u32[]{:S(2)}) copy-start(bf16[2,128,1024]{2,1,0:T(8,128)(2,1)} %up_own.1) | copy-start | bytes 1572868
  14.0 17.6 %copy-start.3 = (s32[5]{0:T(128)S(1)}, s32[5]{0:T(128)}, u32[]{:S(2)}) copy-start(s32[5]{0:T(128)} %stack.19.info) | copy-start | bytes 64
  14.0 10.0 %collective-permute-start.6 = (bf16[2,160,512]{2,1,0:T(8,128)(2,1)S(1)}, bf16[2,160,512]{2,1,0:T(8,128)(2,1)S(1)}, u32[]{:S(2)}, u32[]{:S(2)}) collective-permute-start(bf16[2,160,512]{2,1,0:T(8,128)(2,1)S(1)} %shard_map.71.relay_0), channel_id=1, source_target_pairs={{0,32},{32,64},{64,96},{96,0},{1,33},{33,65},{65,97},{97,1},{2,34}... | collective-permute-start | bytes 983048 | tf_op jit(solution)/shard_map/ppermute | solution.py:405
  17.5 28.6 %collective-permute-start.2 = (bf16[768,512]{1,0:T(8,128)(2,1)}, bf16[768,512]{1,0:T(8,128)(2,1)S(1)}, u32[]{:S(2)}, u32[]{:S(2)}) collective-permute-start(bf16[768,512]{1,0:T(8,128)(2,1)} %get-tuple-element.23), channel_id=1, source_target_pairs={{0,2},{1,7},{2,4},{3,1},{4,6},{5,3},{6,0},{7,5},{8,10},{9,15},{10,... | collective-permute-start | bytes 2359304 | tf_op jit(solution)/shard_map/ppermute | solution.py:400
  19.1 27.0 %collective-permute-start.3 = (bf16[768,512]{1,0:T(8,128)(2,1)}, bf16[768,512]{1,0:T(8,128)(2,1)}, u32[]{:S(2)}, u32[]{:S(2)}) collective-permute-start(bf16[768,512]{1,0:T(8,128)(2,1)} %get-tuple-element.24), channel_id=1, source_target_pairs={{0,3},{1,6},{2,5},{3,0},{4,7},{5,2},{6,1},{7,4},{8,11},{9,14},{10,... | collective-permute-start | bytes 2359304 | tf_op jit(solution)/shard_map/ppermute | solution.py:401
  24.0 0.7 copy-start.1
  24.8 21.3 %collective-permute-start.9 = (bf16[2,128,1024]{2,1,0:T(8,128)(2,1)S(1)}, bf16[2,128,1024]{2,1,0:T(8,128)(2,1)S(1)}, u32[]{:S(2)}, u32[]{:S(2)}) collective-permute-start(bf16[2,128,1024]{2,1,0:T(8,128)(2,1)S(1)} %copy-done), channel_id=1, source_target_pairs={{0,1},{1,0},{2,3},{3,2},{4,5},{5,4},{6,7},{7,6},{8,9},{9,8},{10,11... | collective-permute-start | bytes 1572872 | tf_op jit(solution)/shard_map/ppermute | solution.py:49
  28.0 18.0 %collective-permute-start.7 = (bf16[2,160,512]{2,1,0:T(8,128)(2,1)S(1)}, bf16[2,160,512]{2,1,0:T(8,128)(2,1)}, u32[]{:S(2)}, u32[]{:S(2)}) collective-permute-start(bf16[2,160,512]{2,1,0:T(8,128)(2,1)S(1)} %shard_map.71.relay_0), channel_id=1, source_target_pairs={{0,96},{32,0},{64,32},{96,64},{1,97},{33,1},{65,33},{97,65},{2,98}... | collective-permute-start | bytes 983048 | tf_op jit(solution)/shard_map/ppermute | solution.py:405
  28.5 17.6 %collective-permute-start.8 = (bf16[2,160,512]{2,1,0:T(8,128)(2,1)S(1)}, bf16[2,160,512]{2,1,0:T(8,128)(2,1)}, u32[]{:S(2)}, u32[]{:S(2)}) collective-permute-start(bf16[2,160,512]{2,1,0:T(8,128)(2,1)S(1)} %shard_map.71.relay_0), channel_id=1, source_target_pairs={{0,64},{32,96},{64,0},{96,32},{1,65},{33,97},{65,1},{97,33},{2,66}... | collective-permute-start | bytes 983048 | tf_op jit(solution)/shard_map/ppermute | solution.py:405
  31.6 14.5 %copy-start.2 = (bf16[2,160,512]{2,1,0:T(8,128)(2,1)S(1)}, bf16[2,160,512]{2,1,0:T(8,128)(2,1)}, u32[]{:S(2)}) copy-start(bf16[2,160,512]{2,1,0:T(8,128)(2,1)} %copy-done.1) | copy-start | bytes 983044
  51.8 7.0 %copy-start.5 = (bf16[4,256,256]{2,1,0:T(8,128)(2,1)S(1)}, bf16[4,256,256]{2,1,0:T(8,128)(2,1)}, u32[]{:S(2)}) copy-start(bf16[4,256,256]{2,1,0:T(8,128)(2,1)} %slice_bitcast_fusion) | copy-start | bytes 1572868
  51.8 25.6 %all-to-all-start.1 = ((bf16[16,256,128]{2,1,0:T(8,128)(2,1)}), bf16[16,256,128]{2,1,0:T(8,128)(2,1)S(1)}, u32[]{:S(2)}, u32[]{:S(2)}) async-start(bf16[16,256,128]{2,1,0:T(8,128)(2,1)} %get-tuple-element.30), calls=%async_computation.1 | async-start | bytes 2097152 | tf_op jit(solution)/shard_map/all_to_all | solution.py:463
  58.9 27.1 %collective-permute-start.11 = (bf16[4,256,256]{2,1,0:T(8,128)(2,1)S(1)}, bf16[4,256,256]{2,1,0:T(8,128)(2,1)S(1)}, u32[]{:S(2)}, u32[]{:S(2)}) collective-permute-start(bf16[4,256,256]{2,1,0:T(8,128)(2,1)S(1)} %copy-done.5), channel_id=1, source_target_pairs={{0,4},{4,0},{1,5},{5,1},{2,6},{6,2},{3,7},{7,3},{8,12},{12,8},{9,1... | collective-permute-start | bytes 1572872 | tf_op jit(solution)/shard_map/ppermute | solution.py:462
  77.5 15.9 %collective-permute-start.12 = (bf16[8,256,128]{2,1,0:T(8,128)(2,1)S(1)}, bf16[8,256,128]{2,1,0:T(8,128)(2,1)S(1)}, u32[]{:S(2)}, u32[]{:S(2)}) collective-permute-start(bf16[8,256,128]{2,1,0:T(8,128)(2,1)S(1)} %get-tuple-element.41), channel_id=1, source_target_pairs={{32,0},{0,96},{33,1},{1,97},{34,2},{2,98},{35,3},{3,99},{36,4},{4,... | collective-permute-start | bytes 1572872 | tf_op jit(solution)/shard_map/ppermute | solution.py:468
  78.8 16.7 %collective-permute-start.14 = (bf16[8,256,128]{2,1,0:T(8,128)(2,1)S(1)}, bf16[8,256,128]{2,1,0:T(8,128)(2,1)S(1)}, u32[]{:S(2)}, u32[]{:S(2)}) collective-permute-start(bf16[8,256,128]{2,1,0:T(8,128)(2,1)S(1)} %get-tuple-element.40), channel_id=1, source_target_pairs={{0,32},{32,64},{64,96},{1,33},{33,65},{65,97},{2,34},{34,66},{66,9... | collective-permute-start | bytes 1572872 | tf_op jit(solution)/shard_map/ppermute | solution.py:469
  80.1 26.6 %collective-permute-start.16 = (bf16[8,256,128]{2,1,0:T(8,128)(2,1)S(1)}, bf16[8,256,128]{2,1,0:T(8,128)(2,1)S(1)}, u32[]{:S(2)}, u32[]{:S(2)}) collective-permute-start(bf16[8,256,128]{2,1,0:T(8,128)(2,1)S(1)} %get-tuple-element.41), channel_id=1, source_target_pairs={{0,32},{32,64},{64,96},{1,33},{33,65},{65,97},{2,34},{34,66},{66,9... | collective-permute-start | bytes 1572872 | tf_op jit(solution)/shard_map/ppermute | solution.py:470
  93.3 19.5 %collective-permute-start.13 = (bf16[8,256,128]{2,1,0:T(8,128)(2,1)S(1)}, bf16[8,256,128]{2,1,0:T(8,128)(2,1)S(1)}, u32[]{:S(2)}, u32[]{:S(2)}) collective-permute-start(bf16[8,256,128]{2,1,0:T(8,128)(2,1)S(1)} %collective-permute-done.12), channel_id=1, source_target_pairs={{0,96},{96,64},{1,97},{97,65},{2,98},{98,66},{3,99},{99,67},{4,100... | collective-permute-start | bytes 1572872 | tf_op jit(solution)/shard_map/ppermute | solution.py:476
  95.5 20.4 %collective-permute-start.15 = (bf16[8,256,128]{2,1,0:T(8,128)(2,1)S(1)}, bf16[8,256,128]{2,1,0:T(8,128)(2,1)S(1)}, u32[]{:S(2)}, u32[]{:S(2)}) collective-permute-start(bf16[8,256,128]{2,1,0:T(8,128)(2,1)S(1)} %collective-permute-done.14.pairs), channel_id=1, source_target_pairs={{32,64},{64,96},{33,65},{65,97},{34,66},{66,98},{35,67},{67,99},{3... | collective-permute-start | bytes 1572872 | tf_op jit(solution)/shard_map/ppermute | solution.py:471
  123.4 3.7 %copy-start.4 = (bf16[512,512]{1,0:T(8,128)(2,1)S(1)}, bf16[512,512]{1,0:T(8,128)(2,1)}, u32[]{:S(2)}) copy-start(bf16[512,512]{1,0:T(8,128)(2,1)} %get-tuple-element.27) | copy-start | bytes 1572868
  123.4 20.0 %all-to-all-start.2 = ((bf16[8,256,256]{2,1,0:T(8,128)(2,1)}), bf16[8,256,256]{2,1,0:T(8,128)(2,1)S(1)}, u32[]{:S(2)}, u32[]{:S(2)}) async-start(bf16[8,256,256]{2,1,0:T(8,128)(2,1)} %bitcast.10), calls=%async_computation.2 | async-start | bytes 2097152 | tf_op jit(solution)/shard_map/all_to_all | solution.py:484
  127.2 1.6 %collective-permute-start.10 = (bf16[256,512]{1,0:T(8,128)(2,1)S(1)}, bf16[256,512]{1,0:T(8,128)(2,1)S(1)}, u32[]{:S(2)}, u32[]{:S(2)}) collective-permute-start(bf16[256,512]{1,0:T(8,128)(2,1)S(1)} %get-tuple-element.43), channel_id=1, source_target_pairs={{0,1},{1,0},{2,3},{3,2},{4,5},{5,4},{6,7},{7,6},{8,9},{9,8},{10,11... | collective-permute-start | bytes 786440 | tf_op jit(solution)/shard_map/ppermute | solution.py:49

commit v8 on v6

--- a/solution.py
+++ b/solution.py
@@ -17,7 +17,7 @@
 KV_HEADS = 8
 BLOCKS = CHUNK // BLOCK
 LOW = 4
-GRANT = {"first": 60, "collect": 60, "gather": 60, "half": 49, "project": 46}
+GRANT = {"first": 60, "collect": 60, "half": 49, "project": 46}
 RELAYED = 640
 SIZES = {"z": 4, "y": 4, "xh": 2, "xl": 2, "core": 2}
 SEQ_AXES = ("z", "y", "xh")
@@ -75,7 +75,7 @@
     finish(begin(sems, *moves))
 
 
-def collect_kernel(info, down, up, direct_a, direct_b, sems):
+def collect_kernel(info, down, up, queries, direct_a, direct_b, sent, sems):
     rank = direct_a.shape[1]
     piece = up.shape[1]
     split = direct_a.shape[0] - 2 * piece
@@ -87,11 +87,6 @@
         for k in range(2):
             at = pl.ds(split + k * piece, piece)
             moves.append((up.at[which, :, pl.ds(k * rank, rank)], direct.at[at]))
-    finish(begin(sems, *moves))
-
-
-def gather_kernel(info, queries, sent, sems):
-    moves = []
     for y, k in itertools.product(range(4), range(2)):
         pair = 2 * y + (info[2] ^ k)
         moves.append((queries.at[:, chunk(pair, PAIR)], sent.at[y, k]))
@@ -163,19 +158,18 @@
     outgoing = [pltpu.make_async_copy(rounded, latent, out_sems.at[2 * KV_HEADS])]
     outgoing[0].start()
     finish(copies[2 * count :])
-    for head in range(KV_HEADS):
-        raw = jnp.dot(
-            rounded[...], upper[:, head * HEAD : (head + 1) * HEAD],
+    for couple in range(KV_HEADS // 2):
+        both = jnp.dot(
+            rounded[...], upper[:, couple * PAIR : (couple + 1) * PAIR],
             preferred_element_type=jnp.float32,
         )
-        for which, turn in ((0, core), (1, 1 - core)):
-            entry = raw[which * rows : (which + 1) * rows]
+        for head, (which, turn) in itertools.product(range(2), ((0, core), (1, 1 - core))):
+            slot = 2 * (2 * couple + head)
+            entry = both[which * rows : (which + 1) * rows, head * HEAD : (head + 1) * HEAD]
             entry = entry * cosine[...] + pltpu.roll(entry, HEAD // 2, 1) * sine[...]
-            ready[2 * head + which] = entry.astype(jnp.bfloat16)
+            ready[slot + which] = entry.astype(jnp.bfloat16)
             copy = pltpu.make_async_copy(
-                ready.at[2 * head + which],
-                pairs.at[2 * head + turn],
-                out_sems.at[2 * head + which],
+                ready.at[slot + which], pairs.at[slot + turn], out_sems.at[slot + which]
             )
             copy.start()
             outgoing.append(copy)
@@ -400,15 +394,15 @@
         [sems((2,))],
         10**7,
     )(info, down_weight)
-    direct_a, direct_b = step(
+    direct_a, direct_b, sent = step(
         "collect",
         collect_kernel,
-        (shape(split + 2 * piece, rank),) * 2,
-        [IN_SMEM] + [ANYWHERE] * 2,
-        (IN_VMEM,) * 2,
-        [sems((6,))],
+        (shape(split + 2 * piece, rank),) * 2 + (shape(4, 2, rows, PAIR),),
+        [IN_SMEM] + [ANYWHERE] * 3,
+        (IN_VMEM,) * 3,
+        [sems((14,))],
         10**8,
-    )(info, down_weight, up_weight)
+    )(info, down_weight, up_weight, queries[0])
     relay_a = lax.ppermute(relay_a, X_AXES, forward)
     relay_b = lax.ppermute(relay_b, X_AXES, crossed)
     direct_a = lax.ppermute(direct_a, X_AXES, forward)
@@ -420,10 +414,6 @@
     partner_hidden = to_partner(hidden)
     partner_weight = to_partner(down_weight)
     partner_upper = to_partner(up_weight)
-    sent = step(
-        "gather", gather_kernel, shape(4, 2, rows, PAIR), [IN_SMEM, ANYWHERE], IN_VMEM,
-        [sems((8,))], 10**7,
-    )(info, queries[0])
     sent = lax.all_to_all(sent, "y", 0, 0, tiled=True)
     leaving = sent[:, 1]
 

time: 143 us -> 144 us (level)
  waiting for transfers between devices: 51.8 us -> 55.2 us
  Pallas kernels: 47.9 us -> 45.1 us
    ppermute x3, waiting for transfers between devices: 13.5 us -> 16.9 us  [body(): relays = [lax.ppermute(relay_own, 'z', ring(k)) for k in (1, -1, 2)]]
    pallas_call x2 -> x1, Pallas kernels: 6.39 us -> 3.94 us  [body(): step('collect', collect_kernel, (shape(split + 2 * piece, rank),) * 2 + (...]
  transfers between devices with their start and end apart: 20 -> 20, of which waited for: 9 -> 9; matrix products, arithmetic and copies ran while one was open for 4% -> 4% of each run, Pallas kernels for 26% -> 24%
where the time goes in v8:
time: 144 us; the launch traced here: 143 us
  waiting for transfers between devices  55.2 us (38%)
  Pallas kernels  45.1 us (31%)
  starting transfers between devices  34.8 us (24%)
  other arithmetic  4.19 us (3%)
  local copies, waits for them, and re-layouts  2.26 us (2%)
  between operations  1.76 us (1%)
    pallas_call x5, Pallas kernels, attention_call(): pl.pallas_call(kernel, out_shape=RESULT if result else (STATE, STATE), in...  27 us
    ppermute x3, waiting for transfers between devices, body(): relays = [lax.ppermute(relay_own, 'z', ring(k)) for k in (1, -1, 2)]  16.9 us
    all_to_all x1, waiting for transfers between devices, body(): own_pairs = lax.all_to_all(pairs, PLANE + ('core',), 0, 0, tiled=True)  15 us
    all_to_all x1, waiting for transfers between devices, body(): lax.all_to_all(result.reshape(groups, rows, PAIR), PLANE, 0, 0, tiled=True)  11.7 us
    all_to_all x1, starting transfers between devices, body(): own_pairs = lax.all_to_all(pairs, PLANE + ('core',), 0, 0, tiled=True)  7.01 us
    pallas_call x1, Pallas kernels, body(): step('project', project_kernel, (pltpu.HBM((2 * rows, rank), jnp.bfloat16...  5.66 us
    all_to_all x1, starting transfers between devices, body(): sent = lax.all_to_all(sent, 'y', 0, 0, tiled=True)  4.61 us
    pallas_call x1, Pallas kernels, body(): step('half', half_kernel, (jax.ShapeDtypeStruct((2 * rows, rank), jnp.flo...  4.51 us
  transfers between devices with their start and end apart: 20, of which 9 were waited for; matrix products, arithmetic and copies ran while one was open for 4% of the time, Pallas kernels for 24%

profile of v8, /device:TPU:96, one launch (start us, length us, event | category | flops | bytes accessed | tf_op | source)
XLA Modules:
  0.0 143.3 jit_solution(8280493918111373790)
XLA Ops:
  0.6 0.1 collective-permute-start
  0.7 0.5 collective-permute-start.1
  1.9 0.6 stack.19.info
  2.5 2.4 %shard_map.70 = (bf16[160,512]{1,0:T(8,128)(2,1)}, bf16[160,512]{1,0:T(8,128)(2,1)}) custom-call(s32[5]{0:T(128)} %stack.19.info, bf16[1152,1024]{1,0:T(8,128)(2,1)} %down.3), custom_call_target="tpu_custom_call" | custom-call | flops 10000000 | bytes 4194304 | tf_op jit(solution)/shard_map/pallas_call | solution.py:388
  4.8 1.6 %collective-permute-start.4 = (bf16[160,512]{1,0:T(8,128)(2,1)}, bf16[160,512]{1,0:T(8,128)(2,1)S(1)}, u32[]{:S(2)}, u32[]{:S(2)}) collective-permute-start(bf16[160,512]{1,0:T(8,128)(2,1)} %get-tuple-element.28), channel_id=1, source_target_pairs={{0,2},{1,7},{2,4},{3,1},{4,6},{5,3},{6,0},{7,5},{8,10},{9,15},{10,... | collective-permute-start | bytes 491528 | tf_op jit(solution)/shard_map/ppermute | solution.py:406
  6.4 0.0 collective-permute-start.5
  6.4 3.9 %shard_map.69 = (bf16[768,512]{1,0:T(8,128)(2,1)}, bf16[768,512]{1,0:T(8,128)(2,1)}, bf16[4,2,256,256]{3,2,1,0:T(8,128)(2,1)}) custom-call(s32[5]{0:T(128)} %stack.19.info, bf16[1152,1024]{1,0:T(8,128)(2,1)} %down.3, bf16[2,128,1024]{2,1,0:T(8,128)(2,1)} %up_own.1, bf16[256,2048]{1,0:T(8,128)(2,1)} %bitcast.20), custom_call_target="tpu_custom_call" | custom-call | flops 100000000 | bytes 4194304 | tf_op jit(solution)/shard_map/pallas_call | solution.py:397
  10.4 0.0 copy-start
  10.4 0.0 copy-start.5
  10.4 4.6 %all-to-all-start = ((bf16[4,2,256,256]{3,2,1,0:T(8,128)(2,1)}), bf16[4,2,256,256]{3,2,1,0:T(8,128)(2,1)S(1)}, u32[]{:S(2)}, u32[]{:S(2)}) async-start(bf16[4,2,256,256]{3,2,1,0:T(8,128)(2,1)} %get-tuple-element.31), calls=%async_computation | async-start | bytes 2097152 | tf_op jit(solution)/shard_map/all_to_all | solution.py:417
  15.0 0.0 collective-permute-done.4.a
  15.0 0.0 collective-permute-done.5.b
  15.0 0.1 collective-permute-start.6
  15.1 1.6 %collective-permute-start.2 = (bf16[768,512]{1,0:T(8,128)(2,1)}, bf16[768,512]{1,0:T(8,128)(2,1)S(1)}, u32[]{:S(2)}, u32[]{:S(2)}) collective-permute-start(bf16[768,512]{1,0:T(8,128)(2,1)} %get-tuple-element.26), channel_id=1, source_target_pairs={{0,2},{1,7},{2,4},{3,1},{4,6},{5,3},{6,0},{7,5},{8,10},{9,15},{10,... | collective-permute-start | bytes 2359304 | tf_op jit(solution)/shard_map/ppermute | solution.py:408
  16.7 1.4 %collective-permute-start.3 = (bf16[768,512]{1,0:T(8,128)(2,1)}, bf16[768,512]{1,0:T(8,128)(2,1)S(1)}, u32[]{:S(2)}, u32[]{:S(2)}) collective-permute-start(bf16[768,512]{1,0:T(8,128)(2,1)} %get-tuple-element.27), channel_id=1, source_target_pairs={{0,3},{1,6},{2,5},{3,0},{4,7},{5,2},{6,1},{7,4},{8,11},{9,14},{10,... | collective-permute-start | bytes 2359304 | tf_op jit(solution)/shard_map/ppermute | solution.py:409
  18.1 7.0 %collective-permute-done.6.relay_1 = bf16[2,160,512]{2,1,0:T(8,128)(2,1)S(1)} collective-permute-done((bf16[2,160,512]{2,1,0:T(8,128)(2,1)S(1)}, bf16[2,160,512]{2,1,0:T(8,128)(2,1)S(1)}, u32[]{:S(2)}, u32[]{:S(2)}) %collective-permute-start.6) | collective-permute-done | bytes 327712 | tf_op jit(solution)/shard_map/ppermute | solution.py:413
  25.1 0.7 copy-done.3
  25.8 0.0 copy-done
  25.8 0.7 collective-permute-start.9
  26.5 1.3 fusion.1
  27.8 1.9 %maximum_select_fusion.1 = (f32[256,128]{1,0:T(8,128)}, f32[256,128]{1,0:T(8,128)}) fusion(f32[256,64]{1,0:T(8,128)} %get-tuple-element.52, pred[]{:T(512)S(6)} %eq.2, f32[256,64]{1,0:T(8,128)} %get-tuple-element.51, f32[256,64]{1,0:T(8,128)} %get-tuple-element.50), kind=kLoop, calls=%fused_computation.6 | loop fusion | flops 131072 | bytes 458753 | tf_op jit(solution)/shard_map/jit(_where)/select_n | solution.py:425
  29.8 0.0 collective-permute-done.partner
  29.8 0.4 collective-permute-start.7
  30.2 0.0 collective-permute-done.1.weight_1
  30.2 2.3 %collective-permute-start.8 = (bf16[2,160,512]{2,1,0:T(8,128)(2,1)S(1)}, bf16[2,160,512]{2,1,0:T(8,128)(2,1)}, u32[]{:S(2)}, u32[]{:S(2)}) collective-permute-start(bf16[2,160,512]{2,1,0:T(8,128)(2,1)S(1)} %shard_map.71.relay_0), channel_id=1, source_target_pairs={{0,64},{32,96},{64,0},{96,32},{1,65},{33,97},{65,1},{97,33},{2,66}... | collective-permute-start | bytes 983048 | tf_op jit(solution)/shard_map/ppermute | solution.py:413
  32.4 0.0 all-to-all-done.kept
  32.5 0.8 slice_bitcast_fusion
  33.3 4.5 %shard_map.68 = (f32[512,512]{1,0:T(8,128)S(1)}, bf16[2,512,1152]{2,1,0:T(8,128)(2,1)S(1)}) custom-call(s32[5]{0:T(128)S(1)} %copy-done.5, bf16[256,4608]{1,0:T(8,128)(2,1)} %bitcast.18, bf16[256,4608]{1,0:T(8,128)(2,1)} %collective-permute-done.partner, bf16[1152,1024]{1,0:T(8,128)(2,1)} %down.3, bf16[1152,1024]{1,0:T(8,128)(2,1)} %collective-permute-done.1.weight_1), custom_call_target="tpu_custom_call" | custom-call | flops 1207959552 | bytes 4194304 | tf_op jit(solution)/shard_map/pallas_call | solution.py:429
  37.8 9.9 %collective-permute-done.7.relay_2 = bf16[2,160,512]{2,1,0:T(8,128)(2,1)} collective-permute-done((bf16[2,160,512]{2,1,0:T(8,128)(2,1)S(1)}, bf16[2,160,512]{2,1,0:T(8,128)(2,1)}, u32[]{:S(2)}, u32[]{:S(2)}) %collective-permute-start.7) | collective-permute-done | bytes 327712 | tf_op jit(solution)/shard_map/ppermute | solution.py:413
  47.7 0.0 collective-permute-done.8.relay_3
  47.7 0.0 collective-permute-done.9.up_partner
  47.7 0.0 collective-permute-done.2.direct_a
  47.7 0.0 collective-permute-done.3.direct_b
  47.7 0.0 copy-done.1
  47.8 0.0 copy-done.2
  47.8 0.0 copy-done.4
  47.8 5.7 %shard_map.72 = (bf16[512,512]{1,0:T(8,128)(2,1)}, bf16[16,256,128]{2,1,0:T(8,128)(2,1)}) custom-call(s32[5]{0:T(128)S(1)} %copy-done.5, f32[512,512]{1,0:T(8,128)S(1)} %get-tuple-element.24.partial, bf16[2,512,1152]{2,1,0:T(8,128)(2,1)S(1)} %get-tuple-element.25.inputs, bf16[768,512]{1,0:T(8,128)(2,1)S(1)} %collective-permute-done.2.direct_a, ...), custom_call_target="tpu_custom_call" | custom-call | flops 1207959552 | bytes 4194304 | tf_op jit(solution)/shard_map/pallas_call | solution.py:442
  53.5 7.0 %all-to-all-start.1 = ((bf16[16,256,128]{2,1,0:T(8,128)(2,1)}), bf16[16,256,128]{2,1,0:T(8,128)(2,1)S(1)}, u32[]{:S(2)}, u32[]{:S(2)}) async-start(bf16[16,256,128]{2,1,0:T(8,128)(2,1)} %get-tuple-element.34), calls=%async_computation.1 | async-start | bytes 2097152 | tf_op jit(solution)/shard_map/all_to_all | solution.py:467
  60.5 0.0 copy-done.7
  60.5 3.5 %collective-permute-start.11 = (bf16[4,256,256]{2,1,0:T(8,128)(2,1)S(1)}, bf16[4,256,256]{2,1,0:T(8,128)(2,1)S(1)}, u32[]{:S(2)}, u32[]{:S(2)}) collective-permute-start(bf16[4,256,256]{2,1,0:T(8,128)(2,1)S(1)} %copy-done.7), channel_id=1, source_target_pairs={{0,4},{4,0},{1,5},{5,1},{2,6},{6,2},{3,7},{7,3},{8,12},{12,8},{9,1... | collective-permute-start | bytes 1572872 | tf_op jit(solution)/shard_map/ppermute | solution.py:466
  64.0 15.0 %all-to-all-done.1.pairs = bf16[16,256,128]{2,1,0:T(8,128)(2,1)S(1)} async-done(((bf16[16,256,128]{2,1,0:T(8,128)(2,1)}), bf16[16,256,128]{2,1,0:T(8,128)(2,1)S(1)}, u32[]{:S(2)}, u32[]{:S(2)}) %all-to-all-start.1) | async-done | bytes 1048608 | tf_op jit(solution)/shard_map/all_to_all | solution.py:467
  79.0 0.1 fusion.4
  79.1 1.3 collective-permute-start.14
  80.4 1.3 collective-permute-start.12
  81.7 1.5 %collective-permute-start.16 = (bf16[8,256,128]{2,1,0:T(8,128)(2,1)S(1)}, bf16[8,256,128]{2,1,0:T(8,128)(2,1)S(1)}, u32[]{:S(2)}, u32[]{:S(2)}) collective-permute-start(bf16[8,256,128]{2,1,0:T(8,128)(2,1)S(1)} %get-tuple-element.46), channel_id=1, source_target_pairs={{0,32},{32,64},{64,96},{1,33},{33,65},{65,97},{2,34},{34,66},{66,9... | collective-permute-start | bytes 1572872 | tf_op jit(solution)/shard_map/ppermute | solution.py:474
  83.2 4.3 %collective-permute-done.11.crossed = bf16[4,256,256]{2,1,0:T(8,128)(2,1)S(1)} collective-permute-done((bf16[4,256,256]{2,1,0:T(8,128)(2,1)S(1)}, bf16[4,256,256]{2,1,0:T(8,128)(2,1)S(1)}, u32[]{:S(2)}, u32[]{:S(2)}) %collective-permute-start.11) | collective-permute-done | bytes 524320 | tf_op jit(solution)/shard_map/ppermute | solution.py:466
  87.5 6.0 %shard_map.73 = (f32[4096,128]{1,0:T(8,128)S(1)}, f32[4096,128]{1,0:T(8,128)S(1)}) custom-call(s32[5]{0:T(128)S(1)} %copy-done.5, bf16[4,2,256,256]{3,2,1,0:T(8,128)(2,1)S(1)} %all-to-all-done.kept, bf16[4,256,256]{2,1,0:T(8,128)(2,1)S(1)} %collective-permute-done.11.crossed, bf16[16,256,128]{2,1,0:T(8,128)(2,1)S(1)} %all-to-all-done.1.pairs), custom_call_target="tpu_custom_call" | custom-call | flops 2415919104 | bytes 4194304 | tf_op jit(solution)/shard_map/pallas_call | solution.py:337
  93.5 1.5 %collective-permute-done.14 = bf16[8,256,128]{2,1,0:T(8,128)(2,1)S(1)} collective-permute-done((bf16[8,256,128]{2,1,0:T(8,128)(2,1)S(1)}, bf16[8,256,128]{2,1,0:T(8,128)(2,1)S(1)}, u32[]{:S(2)}, u32[]{:S(2)}) %collective-permute-start.14) | collective-permute-done | bytes 524320 | tf_op jit(solution)/shard_map/ppermute | solution.py:472
  95.0 1.9 %collective-permute-start.15 = (bf16[8,256,128]{2,1,0:T(8,128)(2,1)S(1)}, bf16[8,256,128]{2,1,0:T(8,128)(2,1)S(1)}, u32[]{:S(2)}, u32[]{:S(2)}) collective-permute-start(bf16[8,256,128]{2,1,0:T(8,128)(2,1)S(1)} %collective-permute-done.14), channel_id=1, source_target_pairs={{0,96},{96,64},{1,97},{97,65},{2,98},{98,66},{3,99},{99,67},{4,100... | collective-permute-start | bytes 1572872 | tf_op jit(solution)/shard_map/ppermute | solution.py:480
  96.9 0.2 collective-permute-done.12.pairs
  97.1 1.3 collective-permute-start.13
  98.4 5.9 %shard_map.74 = (f32[4096,128]{1,0:T(8,128)S(1)}, f32[4096,128]{1,0:T(8,128)S(1)}) custom-call(s32[5]{0:T(128)S(1)} %copy-done.5, bf16[4,2,256,256]{3,2,1,0:T(8,128)(2,1)S(1)} %all-to-all-done.kept, bf16[4,256,256]{2,1,0:T(8,128)(2,1)S(1)} %collective-permute-done.11.crossed, ...), custom_call_target="tpu_custom_call", output_to_operand_aliasing={{0}: (4, {}), {1}: (5, {})} | custom-call | flops 2147483648 | bytes 4194304 | tf_op jit(solution)/shard_map/pallas_call | solution.py:337
  104.3 4.0 %collective-permute-done.16.pairs = bf16[8,256,128]{2,1,0:T(8,128)(2,1)S(1)} collective-permute-done((bf16[8,256,128]{2,1,0:T(8,128)(2,1)S(1)}, bf16[8,256,128]{2,1,0:T(8,128)(2,1)S(1)}, u32[]{:S(2)}, u32[]{:S(2)}) %collective-permute-start.16) | collective-permute-done | bytes 524320 | tf_op jit(solution)/shard_map/ppermute | solution.py:474
  108.3 6.1 %shard_map.75 = (f32[4096,128]{1,0:T(8,128)S(1)}, f32[4096,128]{1,0:T(8,128)S(1)}) custom-call(s32[5]{0:T(128)S(1)} %copy-done.5, bf16[4,2,256,256]{3,2,1,0:T(8,128)(2,1)S(1)} %all-to-all-done.kept, bf16[4,256,256]{2,1,0:T(8,128)(2,1)S(1)} %collective-permute-done.11.crossed, ...), custom_call_target="tpu_custom_call", output_to_operand_aliasing={{0}: (4, {}), {1}: (5, {})} | custom-call | flops 2147483648 | bytes 4194304 | tf_op jit(solution)/shard_map/pallas_call | solution.py:337
  114.5 0.0 collective-permute-done.15.refs_0_
  114.5 5.1 %shard_map.76 = (f32[4096,128]{1,0:T(8,128)S(1)}, f32[4096,128]{1,0:T(8,128)S(1)}) custom-call(s32[5]{0:T(128)S(1)} %copy-done.5, bf16[4,2,256,256]{3,2,1,0:T(8,128)(2,1)S(1)} %all-to-all-done.kept, bf16[4,256,256]{2,1,0:T(8,128)(2,1)S(1)} %collective-permute-done.11.crossed, ...), custom_call_target="tpu_custom_call", output_to_operand_aliasing={{0}: (4, {}), {1}: (5, {})} | custom-call | flops 1744830464 | bytes 4194304 | tf_op jit(solution)/shard_map/pallas_call | solution.py:337
  119.6 0.0 collective-permute-done.13.refs_0_
  119.6 4.0 %shard_map.77 = bf16[2048,256]{1,0:T(8,128)(2,1)} custom-call(s32[5]{0:T(128)S(1)} %copy-done.5, bf16[4,2,256,256]{3,2,1,0:T(8,128)(2,1)S(1)} %all-to-all-done.kept, bf16[4,256,256]{2,1,0:T(8,128)(2,1)S(1)} %collective-permute-done.11.crossed, bf16[8,256,128]{2,1,0:T(8,128)(2,1)S(1)} %collective-permute-done.13.refs_0_, ...), custom_call_target="tpu_custom_call" | custom-call | flops 671088640 | bytes 4194304 | tf_op jit(solution)/shard_map/pallas_call | solution.py:337
  123.5 3.7 %all-to-all-start.2 = ((bf16[8,256,256]{2,1,0:T(8,128)(2,1)}), bf16[8,256,256]{2,1,0:T(8,128)(2,1)S(1)}, u32[]{:S(2)}, u32[]{:S(2)}) async-start(bf16[8,256,256]{2,1,0:T(8,128)(2,1)} %bitcast.10), calls=%async_computation.2 | async-start | bytes 2097152 | tf_op jit(solution)/shard_map/all_to_all | solution.py:492
  127.3 0.1 collective-permute-start.10
  127.4 1.5 %collective-permute-done.10 = bf16[256,512]{1,0:T(8,128)(2,1)S(1)} collective-permute-done((bf16[256,512]{1,0:T(8,128)(2,1)S(1)}, bf16[256,512]{1,0:T(8,128)(2,1)S(1)}, u32[]{:S(2)}, u32[]{:S(2)}) %collective-permute-start.10) | collective-permute-done | bytes 262176 | tf_op jit(solution)/shard_map/ppermute | solution.py:49
  128.9 0.9 fusion
  129.8 11.7 %all-to-all-done.2.home = bf16[8,256,256]{2,1,0:T(8,128)(2,1)S(1)} async-done(((bf16[8,256,256]{2,1,0:T(8,128)(2,1)}), bf16[8,256,256]{2,1,0:T(8,128)(2,1)S(1)}, u32[]{:S(2)}, u32[]{:S(2)}) %all-to-all-start.2) | async-done | bytes 1048608 | tf_op jit(solution)/shard_map/all_to_all | solution.py:492
  141.5 1.6 %shard_map.78 = bf16[256,2048]{1,0:T(8,128)(2,1)} custom-call(s32[5]{0:T(128)S(1)} %copy-done.5, bf16[8,256,256]{2,1,0:T(8,128)(2,1)S(1)} %all-to-all-done.2.home), custom_call_target="tpu_custom_call" | custom-call | flops 10000000 | bytes 4194304 | tf_op jit(solution)/shard_map/pallas_call | solution.py:493
  (13 shorter events, 0.1 us)
Async XLA Ops:
  0.6 29.1 %collective-permute-start = (bf16[256,4608]{1,0:T(8,128)(2,1)}, bf16[256,4608]{1,0:T(8,128)(2,1)}, u32[]{:S(2)}, u32[]{:S(2)}) collective-permute-start(bf16[256,4608]{1,0:T(8,128)(2,1)} %bitcast.17), channel_id=1, source_target_pairs={{0,1},{1,0},{2,3},{3,2},{4,5},{5,4},{6,7},{7,6},{8,9},{9,8},{10,11... | collective-permute-start | bytes 7077896 | tf_op jit(solution)/shard_map/ppermute | solution.py:49
  0.7 29.4 %collective-permute-start.1 = (bf16[1152,1024]{1,0:T(8,128)(2,1)}, bf16[1152,1024]{1,0:T(8,128)(2,1)}, u32[]{:S(2)}, u32[]{:S(2)}) collective-permute-start(bf16[1152,1024]{1,0:T(8,128)(2,1)} %down.3), channel_id=1, source_target_pairs={{0,1},{1,0},{2,3},{3,2},{4,5},{5,4},{6,7},{7,6},{8,9},{9,8},{10,11... | collective-permute-start | bytes 7077896 | tf_op jit(solution)/shard_map/ppermute | solution.py:49
  4.8 10.1 %collective-permute-start.4 = (bf16[160,512]{1,0:T(8,128)(2,1)}, bf16[160,512]{1,0:T(8,128)(2,1)S(1)}, u32[]{:S(2)}, u32[]{:S(2)}) collective-permute-start(bf16[160,512]{1,0:T(8,128)(2,1)} %get-tuple-element.28), channel_id=1, source_target_pairs={{0,2},{1,7},{2,4},{3,1},{4,6},{5,3},{6,0},{7,5},{8,10},{9,15},{10,... | collective-permute-start | bytes 491528 | tf_op jit(solution)/shard_map/ppermute | solution.py:406
  6.4 8.6 %collective-permute-start.5 = (bf16[160,512]{1,0:T(8,128)(2,1)}, bf16[160,512]{1,0:T(8,128)(2,1)S(1)}, u32[]{:S(2)}, u32[]{:S(2)}) collective-permute-start(bf16[160,512]{1,0:T(8,128)(2,1)} %get-tuple-element.29), channel_id=1, source_target_pairs={{0,3},{1,6},{2,5},{3,0},{4,7},{5,2},{6,1},{7,4},{8,11},{9,14},{10,... | collective-permute-start | bytes 491528 | tf_op jit(solution)/shard_map/ppermute | solution.py:407
  10.4 15.4 %copy-start = (bf16[2,128,1024]{2,1,0:T(8,128)(2,1)S(1)}, bf16[2,128,1024]{2,1,0:T(8,128)(2,1)}, u32[]{:S(2)}) copy-start(bf16[2,128,1024]{2,1,0:T(8,128)(2,1)} %up_own.1) | copy-start | bytes 1572868
  10.4 22.9 %copy-start.5 = (s32[5]{0:T(128)S(1)}, s32[5]{0:T(128)}, u32[]{:S(2)}) copy-start(s32[5]{0:T(128)} %stack.19.info) | copy-start | bytes 64
  10.4 22.1 %all-to-all-start = ((bf16[4,2,256,256]{3,2,1,0:T(8,128)(2,1)}), bf16[4,2,256,256]{3,2,1,0:T(8,128)(2,1)S(1)}, u32[]{:S(2)}, u32[]{:S(2)}) async-start(bf16[4,2,256,256]{3,2,1,0:T(8,128)(2,1)} %get-tuple-element.31), calls=%async_computation | async-start | bytes 2097152 | tf_op jit(solution)/shard_map/all_to_all | solution.py:417
  15.0 10.0 %collective-permute-start.6 = (bf16[2,160,512]{2,1,0:T(8,128)(2,1)S(1)}, bf16[2,160,512]{2,1,0:T(8,128)(2,1)S(1)}, u32[]{:S(2)}, u32[]{:S(2)}) collective-permute-start(bf16[2,160,512]{2,1,0:T(8,128)(2,1)S(1)} %shard_map.71.relay_0), channel_id=1, source_target_pairs={{0,32},{32,64},{64,96},{96,0},{1,33},{33,65},{65,97},{97,1},{2,34}... | collective-permute-start | bytes 983048 | tf_op jit(solution)/shard_map/ppermute | solution.py:413
  15.1 32.6 %collective-permute-start.2 = (bf16[768,512]{1,0:T(8,128)(2,1)}, bf16[768,512]{1,0:T(8,128)(2,1)S(1)}, u32[]{:S(2)}, u32[]{:S(2)}) collective-permute-start(bf16[768,512]{1,0:T(8,128)(2,1)} %get-tuple-element.26), channel_id=1, source_target_pairs={{0,2},{1,7},{2,4},{3,1},{4,6},{5,3},{6,0},{7,5},{8,10},{9,15},{10,... | collective-permute-start | bytes 2359304 | tf_op jit(solution)/shard_map/ppermute | solution.py:408
  16.7 31.1 %collective-permute-start.3 = (bf16[768,512]{1,0:T(8,128)(2,1)}, bf16[768,512]{1,0:T(8,128)(2,1)S(1)}, u32[]{:S(2)}, u32[]{:S(2)}) collective-permute-start(bf16[768,512]{1,0:T(8,128)(2,1)} %get-tuple-element.27), channel_id=1, source_target_pairs={{0,3},{1,6},{2,5},{3,0},{4,7},{5,2},{6,1},{7,4},{8,11},{9,14},{10,... | collective-permute-start | bytes 2359304 | tf_op jit(solution)/shard_map/ppermute | solution.py:409
  25.1 0.7 copy-start.3
  25.8 21.9 %collective-permute-start.9 = (bf16[2,128,1024]{2,1,0:T(8,128)(2,1)S(1)}, bf16[2,128,1024]{2,1,0:T(8,128)(2,1)}, u32[]{:S(2)}, u32[]{:S(2)}) collective-permute-start(bf16[2,128,1024]{2,1,0:T(8,128)(2,1)S(1)} %copy-done), channel_id=1, source_target_pairs={{0,1},{1,0},{2,3},{3,2},{4,5},{5,4},{6,7},{7,6},{8,9},{9,8},{10,11... | collective-permute-start | bytes 1572872 | tf_op jit(solution)/shard_map/ppermute | solution.py:49
  29.8 18.0 %collective-permute-start.7 = (bf16[2,160,512]{2,1,0:T(8,128)(2,1)S(1)}, bf16[2,160,512]{2,1,0:T(8,128)(2,1)}, u32[]{:S(2)}, u32[]{:S(2)}) collective-permute-start(bf16[2,160,512]{2,1,0:T(8,128)(2,1)S(1)} %shard_map.71.relay_0), channel_id=1, source_target_pairs={{0,96},{32,0},{64,32},{96,64},{1,97},{33,1},{65,33},{97,65},{2,98}... | collective-permute-start | bytes 983048 | tf_op jit(solution)/shard_map/ppermute | solution.py:413
  30.2 17.6 %collective-permute-start.8 = (bf16[2,160,512]{2,1,0:T(8,128)(2,1)S(1)}, bf16[2,160,512]{2,1,0:T(8,128)(2,1)}, u32[]{:S(2)}, u32[]{:S(2)}) collective-permute-start(bf16[2,160,512]{2,1,0:T(8,128)(2,1)S(1)} %shard_map.71.relay_0), channel_id=1, source_target_pairs={{0,64},{32,96},{64,0},{96,32},{1,65},{33,97},{65,1},{97,33},{2,66}... | collective-permute-start | bytes 983048 | tf_op jit(solution)/shard_map/ppermute | solution.py:413
  33.3 14.5 %copy-start.1 = (f32[256,128]{1,0:T(8,128)S(1)}, f32[256,128]{1,0:T(8,128)}, u32[]{:S(2)}) copy-start(f32[256,128]{1,0:T(8,128)} %get-tuple-element.53.cosine) | copy-start | bytes 393220
  33.3 14.5 %copy-start.2 = (f32[256,128]{1,0:T(8,128)S(1)}, f32[256,128]{1,0:T(8,128)}, u32[]{:S(2)}) copy-start(f32[256,128]{1,0:T(8,128)} %get-tuple-element.54.sine) | copy-start | bytes 393220
  33.3 14.5 %copy-start.4 = (bf16[2,160,512]{2,1,0:T(8,128)(2,1)S(1)}, bf16[2,160,512]{2,1,0:T(8,128)(2,1)}, u32[]{:S(2)}) copy-start(bf16[2,160,512]{2,1,0:T(8,128)(2,1)} %copy-done.3) | copy-start | bytes 983044
  53.4 7.0 %copy-start.7 = (bf16[4,256,256]{2,1,0:T(8,128)(2,1)S(1)}, bf16[4,256,256]{2,1,0:T(8,128)(2,1)}, u32[]{:S(2)}) copy-start(bf16[4,256,256]{2,1,0:T(8,128)(2,1)} %slice_bitcast_fusion) | copy-start | bytes 1572868
  53.5 25.6 %all-to-all-start.1 = ((bf16[16,256,128]{2,1,0:T(8,128)(2,1)}), bf16[16,256,128]{2,1,0:T(8,128)(2,1)S(1)}, u32[]{:S(2)}, u32[]{:S(2)}) async-start(bf16[16,256,128]{2,1,0:T(8,128)(2,1)} %get-tuple-element.34), calls=%async_computation.1 | async-start | bytes 2097152 | tf_op jit(solution)/shard_map/all_to_all | solution.py:467
  60.5 27.1 %collective-permute-start.11 = (bf16[4,256,256]{2,1,0:T(8,128)(2,1)S(1)}, bf16[4,256,256]{2,1,0:T(8,128)(2,1)S(1)}, u32[]{:S(2)}, u32[]{:S(2)}) collective-permute-start(bf16[4,256,256]{2,1,0:T(8,128)(2,1)S(1)} %copy-done.7), channel_id=1, source_target_pairs={{0,4},{4,0},{1,5},{5,1},{2,6},{6,2},{3,7},{7,3},{8,12},{12,8},{9,1... | collective-permute-start | bytes 1572872 | tf_op jit(solution)/shard_map/ppermute | solution.py:466
  79.1 15.9 %collective-permute-start.14 = (bf16[8,256,128]{2,1,0:T(8,128)(2,1)S(1)}, bf16[8,256,128]{2,1,0:T(8,128)(2,1)S(1)}, u32[]{:S(2)}, u32[]{:S(2)}) collective-permute-start(bf16[8,256,128]{2,1,0:T(8,128)(2,1)S(1)} %get-tuple-element.46), channel_id=1, source_target_pairs={{32,0},{0,96},{33,1},{1,97},{34,2},{2,98},{35,3},{3,99},{36,4},{4,... | collective-permute-start | bytes 1572872 | tf_op jit(solution)/shard_map/ppermute | solution.py:472
  80.4 16.7 %collective-permute-start.12 = (bf16[8,256,128]{2,1,0:T(8,128)(2,1)S(1)}, bf16[8,256,128]{2,1,0:T(8,128)(2,1)S(1)}, u32[]{:S(2)}, u32[]{:S(2)}) collective-permute-start(bf16[8,256,128]{2,1,0:T(8,128)(2,1)S(1)} %get-tuple-element.47), channel_id=1, source_target_pairs={{0,32},{32,64},{64,96},{1,33},{33,65},{65,97},{2,34},{34,66},{66,9... | collective-permute-start | bytes 1572872 | tf_op jit(solution)/shard_map/ppermute | solution.py:473
  81.7 26.6 %collective-permute-start.16 = (bf16[8,256,128]{2,1,0:T(8,128)(2,1)S(1)}, bf16[8,256,128]{2,1,0:T(8,128)(2,1)S(1)}, u32[]{:S(2)}, u32[]{:S(2)}) collective-permute-start(bf16[8,256,128]{2,1,0:T(8,128)(2,1)S(1)} %get-tuple-element.46), channel_id=1, source_target_pairs={{0,32},{32,64},{64,96},{1,33},{33,65},{65,97},{2,34},{34,66},{66,9... | collective-permute-start | bytes 1572872 | tf_op jit(solution)/shard_map/ppermute | solution.py:474
  95.0 19.5 %collective-permute-start.15 = (bf16[8,256,128]{2,1,0:T(8,128)(2,1)S(1)}, bf16[8,256,128]{2,1,0:T(8,128)(2,1)S(1)}, u32[]{:S(2)}, u32[]{:S(2)}) collective-permute-start(bf16[8,256,128]{2,1,0:T(8,128)(2,1)S(1)} %collective-permute-done.14), channel_id=1, source_target_pairs={{0,96},{96,64},{1,97},{97,65},{2,98},{98,66},{3,99},{99,67},{4,100... | collective-permute-start | bytes 1572872 | tf_op jit(solution)/shard_map/ppermute | solution.py:480
  97.1 22.4 %collective-permute-start.13 = (bf16[8,256,128]{2,1,0:T(8,128)(2,1)S(1)}, bf16[8,256,128]{2,1,0:T(8,128)(2,1)S(1)}, u32[]{:S(2)}, u32[]{:S(2)}) collective-permute-start(bf16[8,256,128]{2,1,0:T(8,128)(2,1)S(1)} %collective-permute-done.12.pairs), channel_id=1, source_target_pairs={{32,64},{64,96},{33,65},{65,97},{34,66},{66,98},{35,67},{67,99},{3... | collective-permute-start | bytes 1572872 | tf_op jit(solution)/shard_map/ppermute | solution.py:475
  123.5 3.7 %copy-start.6 = (bf16[512,512]{1,0:T(8,128)(2,1)S(1)}, bf16[512,512]{1,0:T(8,128)(2,1)}, u32[]{:S(2)}) copy-start(bf16[512,512]{1,0:T(8,128)(2,1)} %get-tuple-element.30) | copy-start | bytes 1572868
  123.5 18.0 %all-to-all-start.2 = ((bf16[8,256,256]{2,1,0:T(8,128)(2,1)}), bf16[8,256,256]{2,1,0:T(8,128)(2,1)S(1)}, u32[]{:S(2)}, u32[]{:S(2)}) async-start(bf16[8,256,256]{2,1,0:T(8,128)(2,1)} %bitcast.10), calls=%async_computation.2 | async-start | bytes 2097152 | tf_op jit(solution)/shard_map/all_to_all | solution.py:492
  127.3 1.6 %collective-permute-start.10 = (bf16[256,512]{1,0:T(8,128)(2,1)S(1)}, bf16[256,512]{1,0:T(8,128)(2,1)S(1)}, u32[]{:S(2)}, u32[]{:S(2)}) collective-permute-start(bf16[256,512]{1,0:T(8,128)(2,1)S(1)} %get-tuple-element.49), channel_id=1, source_target_pairs={{0,1},{1,0},{2,3},{3,2},{4,5},{5,4},{6,7},{7,6},{8,9},{9,8},{10,11... | collective-permute-start | bytes 786440 | tf_op jit(solution)/shard_map/ppermute | solution.py:49
